TPU v7x, 8 devices: a whole 2x2x1 slice. The times are simulated.
8 devices in a mesh: replica: 1 (over z), model: 8 (over y, x, core).
Axes of the slice: x: 2, y: 2, z: 1, core: 2. Of those that a mesh axis runs over, the one named last changes fastest.
Arguments:
- prompt: bfloat16 [8, 1024, 4096], P('replica', 'model')
- lengths: int32 [8], P('replica')
- new_tok: bfloat16 [8, 4096], P('replica')
- norm_attn: bfloat16 [1, 4096], replicated
- w_q: bfloat16 [1, 4096, 4096], P(None, None, 'model')
- w_k: bfloat16 [1, 4096, 4096], P(None, None, 'model')
- w_v: bfloat16 [1, 4096, 4096], P(None, None, 'model')
- w_o: bfloat16 [1, 4096, 4096], P(None, 'model')
- norm_mlp: bfloat16 [1, 4096], replicated
- w_gate: bfloat16 [1, 4096, 11008], P(None, None, 'model')
- w_up: bfloat16 [1, 4096, 11008], P(None, None, 'model')
- w_down: bfloat16 [1, 11008, 4096], P(None, 'model')
Outputs:
- output 1: bfloat16 [8, 4096], P('replica')
- output 2: bfloat16 [8, 4096], P('replica')
- output 3: bfloat16 [1, 8, 1025, 32, 128], P(None, 'replica', None, 'model')
- output 4: bfloat16 [1, 8, 1025, 32, 128], P(None, 'replica', None, 'model')
All inputs are finite; a program needn't handle non-finite values.
Results may differ from a plain program's by a relative error of at most 0.0108766.
Values are sent between devices in bfloat16 or wider.
A program may use at most 1 GiB of HBM per device.

v0:
```python
import jax
import jax.numpy as jnp
from jax import lax
from jax.sharding import PartitionSpec as P

HEAD_DIM = 128
NEG_BIG = -1e30


def rms_norm(hidden, gain_vec):
    hid_f32 = hidden.astype(jnp.float32)
    inv_rms = lax.rsqrt(jnp.mean(hid_f32 * hid_f32, axis=-1, keepdims=True) + 1e-5)
    return (hid_f32 * inv_rms * gain_vec.astype(jnp.float32)).astype(jnp.bfloat16)


def rotary(heads_f32, positions):
    half_dim = HEAD_DIM // 2
    inv_freq = 10000.0 ** (-2.0 * jnp.arange(half_dim, dtype=jnp.float32) / HEAD_DIM)
    angles = positions.astype(jnp.float32)[..., None] * inv_freq
    cos_tab = jnp.cos(angles)[..., None, :]
    sin_tab = jnp.sin(angles)[..., None, :]
    lo_half = heads_f32[..., :half_dim]
    hi_half = heads_f32[..., half_dim:]
    return jnp.concatenate([lo_half * cos_tab - hi_half * sin_tab, hi_half * cos_tab + lo_half * sin_tab], axis=-1)


def block_attention(q_block, key_blocks, val_blocks, lengths, q_start, n_used):
    n_batch, blk_len, n_heads, _ = q_block.shape
    kv_heads = key_blocks.shape[3]
    n_group = n_heads // kv_heads
    q_grouped = q_block.reshape(n_batch, blk_len, kv_heads, n_group, HEAD_DIM)
    q_pos = q_start + jnp.arange(blk_len)
    score_scale = HEAD_DIM ** -0.5

    def step_fn(blk_idx, loop_state):
        run_max, run_sum, run_acc = loop_state
        key_blk = lax.dynamic_index_in_dim(key_blocks, blk_idx, axis=0, keepdims=False)
        val_blk = lax.dynamic_index_in_dim(val_blocks, blk_idx, axis=0, keepdims=False)
        k_pos = blk_idx * blk_len + jnp.arange(blk_len)
        scores = jnp.einsum('bqhgd,bkhd->bqhgk', q_grouped, key_blk, preferred_element_type=jnp.float32) * score_scale
        visible = (k_pos[None, None, :] <= q_pos[None, :, None]) & (k_pos[None, None, :] < lengths[:, None, None])
        scores = jnp.where(visible[:, :, None, None, :], scores, NEG_BIG)
        new_max = jnp.maximum(run_max, jnp.max(scores, axis=-1))
        rescale = jnp.exp(run_max - new_max)
        attn_prob = jnp.exp(scores - new_max[..., None])
        run_sum = run_sum * rescale + jnp.sum(attn_prob, axis=-1)
        run_acc = run_acc * rescale[..., None] + jnp.einsum('bqhgk,bkhd->bqhgd', attn_prob.astype(jnp.bfloat16), val_blk, preferred_element_type=jnp.float32)
        return new_max, run_sum, run_acc

    stat_shape = (n_batch, blk_len, kv_heads, n_group)
    init_state = (jnp.full(stat_shape, NEG_BIG, jnp.float32), jnp.zeros(stat_shape, jnp.float32), jnp.zeros(stat_shape + (HEAD_DIM,), jnp.float32))
    run_max, run_sum, run_acc = lax.fori_loop(0, n_used, step_fn, init_state)
    return (run_acc / run_sum[..., None]).reshape(n_batch, blk_len, n_heads * HEAD_DIM).astype(jnp.bfloat16)


def decode_attention(q_new, key_cache, val_cache, lengths):
    n_batch, n_heads, _ = q_new.shape
    kv_heads = key_cache.shape[2]
    cache_len = key_cache.shape[1]
    q_grouped = q_new.reshape(n_batch, kv_heads, n_heads // kv_heads, HEAD_DIM)
    scores = jnp.einsum('bhgd,bkhd->bhgk', q_grouped, key_cache, preferred_element_type=jnp.float32) * (HEAD_DIM ** -0.5)
    cache_pos = jnp.arange(cache_len)
    visible = (cache_pos[None, :] < lengths[:, None]) | (cache_pos[None, :] == cache_len - 1)
    scores = jnp.where(visible[:, None, None, :], scores, NEG_BIG)
    attn_prob = jax.nn.softmax(scores, axis=-1)
    out_f32 = jnp.einsum('bhgk,bkhd->bhgd', attn_prob.astype(jnp.bfloat16), val_cache, preferred_element_type=jnp.float32)
    return out_f32.reshape(n_batch, n_heads * HEAD_DIM).astype(jnp.bfloat16)


def decode_layer(dec_hidden, key_mine, val_mine, lengths, gain_attn, wq_loc, wk_loc, wv_loc, wo_loc, gain_mlp, wg_loc, wu_loc, wd_loc):
    n_batch = dec_hidden.shape[0]
    heads_loc = wq_loc.shape[1] // HEAD_DIM
    kv_loc = wk_loc.shape[1] // HEAD_DIM
    tok_norm = rms_norm(dec_hidden, gain_attn)
    q_new = rotary(jnp.dot(tok_norm, wq_loc, preferred_element_type=jnp.float32).reshape(n_batch, heads_loc, HEAD_DIM), lengths).astype(jnp.bfloat16)
    k_new = rotary(jnp.dot(tok_norm, wk_loc, preferred_element_type=jnp.float32).reshape(n_batch, kv_loc, HEAD_DIM), lengths).astype(jnp.bfloat16)
    v_new = jnp.dot(tok_norm, wv_loc, preferred_element_type=jnp.float32).astype(jnp.bfloat16).reshape(n_batch, kv_loc, HEAD_DIM)
    key_cache = jnp.concatenate([key_mine, k_new[:, None]], axis=1)
    val_cache = jnp.concatenate([val_mine, v_new[:, None]], axis=1)
    tok_attn = decode_attention(q_new, key_cache, val_cache, lengths)
    attn_part = jnp.dot(tok_attn, wo_loc, preferred_element_type=jnp.float32)
    dec_hidden = (dec_hidden.astype(jnp.float32) + lax.psum(attn_part, 'model')).astype(jnp.bfloat16)
    tok_norm = rms_norm(dec_hidden, gain_mlp)
    tok_mid = (jax.nn.silu(jnp.dot(tok_norm, wg_loc, preferred_element_type=jnp.float32)) * jnp.dot(tok_norm, wu_loc, preferred_element_type=jnp.float32)).astype(jnp.bfloat16)
    mlp_part = jnp.dot(tok_mid, wd_loc, preferred_element_type=jnp.float32)
    dec_hidden = (dec_hidden.astype(jnp.float32) + lax.psum(mlp_part, 'model')).astype(jnp.bfloat16)
    return dec_hidden, key_cache, val_cache


def solution(mesh):
    n_dev = mesh.shape['model']
    seq_spec = P('replica', 'model', None)
    col_spec = P(None, None, 'model')
    row_spec = P(None, 'model', None)
    gain_spec = P(None, None)
    tok_spec = P('replica', None)
    cache_spec = P(None, 'replica', None, 'model', None)
    in_specs = (seq_spec, P('replica'), tok_spec, gain_spec, col_spec, col_spec, col_spec, row_spec, gain_spec, col_spec, col_spec, row_spec)
    out_specs = (tok_spec, tok_spec, cache_spec, cache_spec)

    def per_device(prompt, lengths, new_tok, norm_attn, w_q, w_k, w_v, w_o, norm_mlp, w_gate, w_up, w_down):
        my_idx = lax.axis_index('model')
        n_batch, seq_loc, d_model = prompt.shape
        n_tok = n_batch * seq_loc
        kv_loc = w_k.shape[2] // HEAD_DIM
        n_heads = (w_q.shape[2] // HEAD_DIM) * n_dev
        kv_heads = kv_loc * n_dev
        seq_len = seq_loc * n_dev
        seq_pos = my_idx * seq_loc + jnp.arange(seq_loc)
        hidden = prompt
        dec_hidden = new_tok
        key_layers = []
        val_layers = []
        for layer_idx in range(w_q.shape[0]):
            wq_full = lax.all_gather(w_q[layer_idx], 'model', axis=1, tiled=True)
            wk_full = lax.all_gather(w_k[layer_idx], 'model', axis=1, tiled=True)
            wv_full = lax.all_gather(w_v[layer_idx], 'model', axis=1, tiled=True)
            wo_full = lax.all_gather(w_o[layer_idx], 'model', axis=0, tiled=True)
            wg_full = lax.all_gather(w_gate[layer_idx], 'model', axis=1, tiled=True)
            wu_full = lax.all_gather(w_up[layer_idx], 'model', axis=1, tiled=True)
            wd_full = lax.all_gather(w_down[layer_idx], 'model', axis=0, tiled=True)
            normed = rms_norm(hidden, norm_attn[layer_idx]).reshape(n_tok, d_model)
            q_rot = rotary(jnp.dot(normed, wq_full, preferred_element_type=jnp.float32).reshape(n_batch, seq_loc, n_heads, HEAD_DIM), seq_pos).astype(jnp.bfloat16)
            k_rot = rotary(jnp.dot(normed, wk_full, preferred_element_type=jnp.float32).reshape(n_batch, seq_loc, kv_heads, HEAD_DIM), seq_pos).astype(jnp.bfloat16)
            v_proj = jnp.dot(normed, wv_full, preferred_element_type=jnp.float32).astype(jnp.bfloat16).reshape(n_batch, seq_loc, kv_heads, HEAD_DIM)
            key_blocks = lax.all_gather(k_rot, 'model', axis=0)
            val_blocks = lax.all_gather(v_proj, 'model', axis=0)
            attn_out = block_attention(q_rot, key_blocks, val_blocks, lengths, my_idx * seq_loc, my_idx + 1).reshape(n_tok, n_heads * HEAD_DIM)
            hidden = (hidden.astype(jnp.float32) + jnp.dot(attn_out, wo_full, preferred_element_type=jnp.float32).reshape(n_batch, seq_loc, d_model)).astype(jnp.bfloat16)
            normed = rms_norm(hidden, norm_mlp[layer_idx]).reshape(n_tok, d_model)
            mlp_mid = (jax.nn.silu(jnp.dot(normed, wg_full, preferred_element_type=jnp.float32)) * jnp.dot(normed, wu_full, preferred_element_type=jnp.float32)).astype(jnp.bfloat16)
            hidden = (hidden.astype(jnp.float32) + jnp.dot(mlp_mid, wd_full, preferred_element_type=jnp.float32).reshape(n_batch, seq_loc, d_model)).astype(jnp.bfloat16)
            key_mine = jnp.moveaxis(lax.dynamic_slice_in_dim(key_blocks, my_idx * kv_loc, kv_loc, axis=3), 0, 1).reshape(n_batch, seq_len, kv_loc, HEAD_DIM)
            val_mine = jnp.moveaxis(lax.dynamic_slice_in_dim(val_blocks, my_idx * kv_loc, kv_loc, axis=3), 0, 1).reshape(n_batch, seq_len, kv_loc, HEAD_DIM)
            dec_hidden, key_cache, val_cache = decode_layer(dec_hidden, key_mine, val_mine, lengths, norm_attn[layer_idx], w_q[layer_idx], w_k[layer_idx], w_v[layer_idx], w_o[layer_idx], norm_mlp[layer_idx], w_gate[layer_idx], w_up[layer_idx], w_down[layer_idx])
            key_layers.append(key_cache)
            val_layers.append(val_cache)
        last_sel = (seq_pos[None, :] == (lengths - 1)[:, None]).astype(jnp.bfloat16)
        last_part = jnp.einsum('bs,bsd->bd', last_sel, hidden, preferred_element_type=jnp.float32)
        last_hidden = lax.psum(last_part, 'model').astype(jnp.bfloat16)
        return dec_hidden, last_hidden, jnp.stack(key_layers), jnp.stack(val_layers)

    return jax.shard_map(per_device, mesh=mesh, in_specs=in_specs, out_specs=out_specs, check_vma=False)
```

profile of v0, /device:TPU:0, one launch (start us, length us, event | category | flops | bytes accessed | tf_op | source)
XLA Modules:
  0.0 2685.6 jit_solution(15666044401025018990)
XLA Ops:
  14.6 10.5 fusion.33
  25.1 149.5 %all-gather.23.cloned.1.call-done = bf16[1,4096,4096]{2,1,0:T(8,128)(2,1)} async-done(((bf16[1,4096,512]{2,1,0:T(8,128)(2,1)}), bf16[1,4096,4096]{2,1,0:T(8,128)(2,1)}) %all-gather.23.cloned.1.call-update) | async-done | bytes 33554448 | tf_op jit(solution)/shard_map/all_gather | solution.py:117
  174.6 42.6 %convert_bitcast_fusion = bf16[128,8,32,128]{3,1,2,0:T(8,128)(2,1)} fusion(bf16[1024,4096]{1,0:T(8,128)(2,1)} %bitcast.232, bf16[1,4096,4096]{2,1,0:T(8,128)(2,1)} %all-gather.23.cloned.1.call-done), kind=kOutput, calls=%fused_computation.74 | convolution fusion | flops 34363932672 | bytes 50331648 | tf_op jit(solution)/shard_map/dot_general | solution.py:125
  217.2 9.5 copy.103
  228.2 110.1 %all-gather.25.cloned.1.call-done = bf16[1,4096,4096]{2,1,0:T(8,128)(2,1)} async-done(((bf16[1,4096,512]{2,1,0:T(8,128)(2,1)}), bf16[1,4096,4096]{2,1,0:T(8,128)(2,1)}) %all-gather.25.cloned.1.call-update) | async-done | bytes 33554448 | tf_op jit(solution)/shard_map/all_gather | solution.py:115
  338.3 42.7 %copy.81 = bf16[4096,4096]{1,0:T(8,128)(2,1)} copy(bf16[4096,4096]{0,1:T(8,128)(2,1)} %bitcast.222) | data formatting | bytes 67108864 | tf_op jit(solution)/shard_map/dot_general | solution.py:123
  381.0 121.1 %all-gather.21.cloned.1.call-done = bf16[1,4096,4096]{2,1,0:T(8,128)(2,1)} async-done(((bf16[1,4096,512]{2,1,0:T(8,128)(2,1)}), bf16[1,4096,4096]{2,1,0:T(8,128)(2,1)}) %all-gather.21.cloned.1.call-update) | async-done | bytes 33554448 | tf_op jit(solution)/shard_map/all_gather | solution.py:116
  502.0 39.9 %copy.74 = bf16[4096,4096]{1,0:T(8,128)(2,1)} copy(bf16[4096,4096]{0,1:T(8,128)(2,1)} %bitcast.223) | data formatting | bytes 67108864 | tf_op jit(solution)/shard_map/dot_general | solution.py:124
  542.0 43.3 %fusion.47 = f32[8,128,32,128]{1,3,2,0:T(8,128)} fusion(bf16[32,128,4096,1]{2,1,0,3:T(8,128)(2,1)} %bitcast.224, bf16[8,128,4096]{2,1,0:T(8,128)(2,1)} %fusion.33), kind=kOutput, calls=%fused_computation.68 | convolution fusion | flops 34359738368 | bytes 58720256 | tf_op jit(solution)/shard_map/dot_general | solution.py:123
  585.2 43.4 %fusion.49 = f32[8,128,32,128]{1,3,2,0:T(8,128)} fusion(bf16[32,128,4096,1]{2,1,0,3:T(8,128)(2,1)} %bitcast.225, bf16[8,128,4096]{2,1,0:T(8,128)(2,1)} %fusion.33), kind=kOutput, calls=%fused_computation.70 | convolution fusion | flops 34359738368 | bytes 58720256 | tf_op jit(solution)/shard_map/dot_general | solution.py:124
  628.7 19.5 fusion.61
  648.2 10.1 pad_maximum_fusion.2
  658.3 12.6 copy.75
  677.7 6.3 copy.97
  684.1 6.5 copy.98
  699.1 10.1 pad_maximum_fusion.3
  709.2 12.0 copy.83
  721.2 79.8 %all-gather.19.cloned.1.call-done = bf16[8,8,128,32,128]{4,3,2,1,0:T(8,128)(2,1)} async-done(((bf16[1,8,128,32,128]{4,3,2,1,0:T(8,128)(2,1)}), bf16[8,8,128,32,128]{4,3,2,1,0:T(8,128)(2,1)}) %all-gather.19.cloned.1.call-update) | async-done | bytes 67108880 | tf_op jit(solution)/shard_map/all_gather | solution.py:127
  800.9 299.5 %all-gather.17.cloned.1.call-done = bf16[8,8,128,32,128]{4,3,2,1,0:T(8,128)(2,1)} async-done(((bf16[1,8,128,32,128]{4,3,2,1,0:T(8,128)(2,1)}), bf16[8,8,128,32,128]{4,3,2,1,0:T(8,128)(2,1)}) %all-gather.17.cloned.1.call-update) | async-done | bytes 67108880 | tf_op jit(solution)/shard_map/all_gather | solution.py:126
  1100.4 21.2 constant_dynamic-slice_fusion.2
  1121.6 9.0 copy.102
  1130.5 9.0 copy.101
  1146.1 7.9 broadcast_in_dim.37
  1154.0 67.1 %while.15 = (s32[]{:T(128)}, f32[8,128,32,1]{1,2,0,3:T(8,128)S(1)}, f32[8,128,32,1]{1,2,0,3:T(8,128)S(1)}, f32[8,128,32,1,128]{1,4,2,0,3:T(8,128)}, s32[]{:T(128...) while((s32[]{:T(128)}, f32[8,128,32,1]{1,2,0,3:T(8,128)S(1)}, ...), condition=%wide.region_10.11_spmd.clone, body=%wide.region_7.10_spmd.clone.sunk | while | flops 2202256640 | bytes 162042608 | solution.py:52
  1154.9 10.0 constant_dynamic-slice_fusion.5
  1164.8 11.9 fusion.149
  1176.8 10.4 fusion.151
  1187.2 12.8 copy.130
  1200.0 21.1 bitcast_add_fusion.5
  1221.2 9.6 divide_convert_fusion
  1230.8 26.5 all-gather.27.cloned.1.call-done
  1257.3 43.4 %fusion.35 = (f32[8,128]{1,0:T(8,128)S(1)}, bf16[8,128,4096]{2,1,0:T(8,128)(2,1)}) fusion(bf16[8,128,4096]{1,2,0:T(8,128)(2,1)} %bitcast.217, bf16[1,4096,4096]{2,1,0:T(8,128)(2,1)} %all-gather.27.cloned.1.call-done, bf16[8,128,4096]{2,1,0:T(8,128)(2,1)} %param.14), kind=kOutput, calls=%fused_computation.52 | convolution fusion | flops 34384904192 | bytes 58724352 | tf_op jit(solution)/shard_map/dot_general | solution.py:129
  1304.3 7.3 fusion.57
  1311.6 10.5 fusion.37
  1322.1 332.0 %all-gather.29.cloned.1.call-done = bf16[1,4096,11008]{1,2,0:T(8,128)(2,1)} async-done(((bf16[1,4096,1376]{1,2,0:T(8,128)(2,1)}), bf16[1,4096,11008]{1,2,0:T(8,128)(2,1)}) %all-gather.29.cloned.1.call-update) | async-done | bytes 90177552 | tf_op jit(solution)/shard_map/all_gather | solution.py:119
  1654.1 105.0 %fusion.23 = f32[1024,11008]{1,0:T(8,128)} fusion(bf16[1024,4096]{1,0:T(8,128)(2,1)} %bitcast.233, bf16[1,4096,11008]{1,2,0:T(8,128)(2,1)} %all-gather.29.cloned.1.call-done), kind=kOutput, calls=%fused_computation.35 | convolution fusion | flops 92341796864 | bytes 143654912 | tf_op jit(solution)/shard_map/dot_general | solution.py:131
  1759.1 291.9 %all-gather.31.cloned.1.call-done = bf16[1,4096,11008]{1,2,0:T(8,128)(2,1)} async-done(((bf16[1,4096,1376]{1,2,0:T(8,128)(2,1)}), bf16[1,4096,11008]{1,2,0:T(8,128)(2,1)}) %all-gather.31.cloned.1.call-update) | async-done | bytes 90177552 | tf_op jit(solution)/shard_map/all_gather | solution.py:120
  2050.9 109.2 %multiply_convert_fusion = bf16[1024,11008]{1,0:T(8,128)(2,1)} fusion(f32[1024,11008]{1,0:T(8,128)} %fusion.23, bf16[1024,4096]{1,0:T(8,128)(2,1)} %bitcast.234, bf16[1,4096,11008]{1,2,0:T(8,128)(2,1)} %all-gather.31.cloned.1.call-done), kind=kOutput, calls=%fused_computation.37 | convolution fusion | flops 92409430016 | bytes 166199296 | tf_op jit(solution)/shard_map/dot_general | solution.py:131
  2160.1 287.6 %all-gather.33.cloned.1.call-done = bf16[1,11008,4096]{2,1,0:T(8,128)(2,1)} async-done(((bf16[1,1376,4096]{2,1,0:T(8,128)(2,1)}), bf16[1,11008,4096]{2,1,0:T(8,128)(2,1)}) %all-gather.33.cloned.1.call-update) | async-done | bytes 90177552 | tf_op jit(solution)/shard_map/all_gather | solution.py:121
  2447.7 106.6 %fusion.19 = f32[1024,4096]{1,0:T(8,128)} fusion(bf16[1024,11008]{1,0:T(8,128)(2,1)} %multiply_convert_fusion, bf16[1,11008,4096]{2,1,0:T(8,128)(2,1)} %all-gather.33.cloned.1.call-done), kind=kOutput, calls=%fused_computation.31 | convolution fusion | flops 92341796864 | bytes 129499136 | tf_op jit(solution)/shard_map/dot_general | solution.py:132
  2554.4 9.6 fusion.45
  2564.0 7.3 fusion.55
  2571.4 22.2 copy.86
  2593.6 19.7 copy.87
  2614.5 7.2 fusion.43
  2621.7 13.3 fusion.39
  2635.0 23.8 all-reduce.7
  2658.7 18.6 all-reduce.6.cloned.1.call-done
  (114 shorter events, 37.3 us)
Async XLA Ops:
  7.2 2.3 copy-start.16
  7.2 167.4 %all-gather.23.cloned.1.call-start = ((), (), s32[]{:S(2)}) async-start(), calls=%async_computation.5 | async-start | bytes 37748736 | tf_op jit(solution)/shard_map/all_gather | solution.py:117
  7.9 330.4 %all-gather.25.cloned.1.call-start = ((), (), s32[]{:S(2)}) async-start(), calls=%async_computation.6 | async-start | bytes 37748736 | tf_op jit(solution)/shard_map/all_gather | solution.py:115
  8.7 493.4 %all-gather.21.cloned.1.call-start = ((), (), s32[]{:S(2)}) async-start(), calls=%async_computation.4 | async-start | bytes 37748736 | tf_op jit(solution)/shard_map/all_gather | solution.py:116
  9.4 791.5 %all-gather.19.cloned.1.call-start = ((), (), s32[]{:S(2)}) async-start(), calls=%async_computation.1 | async-start | bytes 75497472 | tf_op jit(solution)/shard_map/all_gather | solution.py:127
  9.5 5.1 copy-start.4
  226.7 873.7 %all-gather.17.cloned.1.call-start = ((), (), s32[]{:S(2)}) async-start(), calls=%async_computation | async-start | bytes 75497472 | tf_op jit(solution)/shard_map/all_gather | solution.py:126
  226.8 0.6 copy-start.18
  585.2 43.4 %copy-start.8 = (f32[128,64]{0,1:T(8,128)S(1)}, f32[128,64]{0,1:T(8,128)}, u32[]{:S(2)}) copy-start(f32[128,64]{0,1:T(8,128)} %get-tuple-element.192) | copy-start | bytes 98308
  585.2 43.4 %copy-start.9 = (f32[128,64]{0,1:T(8,128)S(1)}, f32[128,64]{0,1:T(8,128)}, u32[]{:S(2)}) copy-start(f32[128,64]{0,1:T(8,128)} %get-tuple-element.193) | copy-start | bytes 98308
  670.9 586.4 %all-gather.27.cloned.1.call-start = ((), (), s32[]{:S(2)}) async-start(), calls=%async_computation.7 | async-start | bytes 37748736 | tf_op jit(solution)/shard_map/all_gather | solution.py:118
  671.5 982.6 %all-gather.29.cloned.1.call-start = ((), (), s32[]{:S(2)}) async-start(), calls=%async_computation.8 | async-start | bytes 101449728 | tf_op jit(solution)/shard_map/all_gather | solution.py:119
  672.3 1.8 copy-start.2
  672.3 1.9 copy-start.5
  672.3 1378.6 %all-gather.31.cloned.1.call-start = ((), (), s32[]{:S(2)}) async-start(), calls=%async_computation.9 | async-start | bytes 101449728 | tf_op jit(solution)/shard_map/all_gather | solution.py:120
  673.0 1774.7 %all-gather.33.cloned.1.call-start = ((), (), s32[]{:S(2)}) async-start(), calls=%async_computation.10 | async-start | bytes 101449728 | tf_op jit(solution)/shard_map/all_gather | solution.py:121
  673.8 16.8 copy-start.15
  673.8 16.7 copy-start.19
  673.8 1939.6 %all-reduce.4.cloned.1.call-start = ((), (), s32[]{:S(2)}) async-start(), calls=%async_computation.2 | async-start | bytes 262144 | tf_op jit(solution)/shard_map/psum | solution.py:82
  677.7 19.9 copy-start.17
  697.6 442.0 %copy-start.12 = (bf16[8,1,4,128]{3,1,2,0:T(2,128)(2,1)}, bf16[8,1,4,128]{3,1,2,0:T(2,128)(2,1)S(1)}, u32[]{:S(2)}) copy-start(bf16[8,1,4,128]{3,1,2,0:T(2,128)(2,1)S(1)} %copy.78) | copy-start | bytes 24580
  1257.3 43.4 %copy-start = (bf16[8,8,128,4,128]{4,2,0,3,1:T(8,128)(2,1)S(1)}, bf16[8,8,128,4,128]{4,2,0,3,1:T(8,128)(2,1)}, u32[]{:S(2)}) copy-start(bf16[8,8,128,4,128]{4,2,0,3,1:T(8,128)(2,1)} %copy.102) | copy-start | bytes 25165828
  1257.3 43.4 %copy-start.10 = (bf16[8,1,4,128]{3,1,2,0:T(2,128)(2,1)S(1)}, bf16[8,1,4,128]{3,1,2,0:T(2,128)(2,1)}, u32[]{:S(2)}) copy-start(bf16[8,1,4,128]{3,1,2,0:T(2,128)(2,1)} %copy.80) | copy-start | bytes 24580
  1257.3 43.5 %copy-start.20 = (bf16[8,4,1025,1]{2,0,1,3:T(8,128)(2,1)S(1)}, bf16[8,4,1025,1]{2,0,1,3:T(8,128)(2,1)}, u32[]{:S(2)}) copy-start(bf16[8,4,1025,1]{2,0,1,3:T(8,128)(2,1)} %fusion.71) | copy-start | bytes 196804
  1300.7 2.2 copy-start.1
  1300.7 3.5 copy-start.13
  1302.1 9.6 copy-start.6
  1311.6 1365.7 %all-reduce.6.cloned.1.call-start = ((), (), s32[]{:S(2)}) async-start(), calls=%async_computation.3 | async-start | bytes 262144 | tf_op jit(solution)/shard_map/psum | solution.py:86
  2447.7 106.6 %copy-start.14 = (pred[8,128,1]{1,0,2:T(8,128)(4,1)S(1)}, pred[8,128,1]{1,0,2:T(8,128)(4,1)}, u32[]{:S(2)}) copy-start(pred[8,128,1]{1,0,2:T(8,128)(4,1)} %compare_bitcast_fusion) | copy-start | bytes 3076
  2554.4 9.7 copy-start.11
  2571.3 22.3 slice-start
  2571.4 22.2 slice-start.1
  2571.4 22.2 slice-start.2
  2593.6 19.8 copy-start.3
  2593.6 20.8 copy-start.7
Sparse Core Ops, SparseCore 0:
  9.8 164.7 all-gather.22
  176.4 161.8 all-gather.24
  340.1 161.8 all-gather.20
  503.7 297.1 all-gather.18
  803.2 297.1 all-gather.16
  1102.1 155.1 all-gather.26
  1259.2 394.9 all-gather.28
  1656.0 394.9 all-gather.30
  2052.8 394.9 all-gather.32
  2450.6 42.1 all-reduce.3
  2635.1 42.1 all-reduce.5
where the time goes:
time: 2700 us; the launch traced here: 2690 us
  waiting for transfers between devices  1720 us (64%)
  matrix products  575 us (21%)
  local copies, waits for them, and re-layouts  243 us (9%)
  other arithmetic  107 us (4%)
    all_gather x1, waiting for transfers between devices, per_device(): wg_full = lax.all_gather(w_gate[layer_idx], 'model', axis=1, tiled=True)  332 us
    all_gather x1, waiting for transfers between devices, per_device(): key_blocks = lax.all_gather(k_rot, 'model', axis=0)  299 us
    all_gather x1, waiting for transfers between devices, per_device(): wu_full = lax.all_gather(w_up[layer_idx], 'model', axis=1, tiled=True)  292 us
    all_gather x1, waiting for transfers between devices, per_device(): wd_full = lax.all_gather(w_down[layer_idx], 'model', axis=0, tiled=True)  288 us
    all_gather x1, waiting for transfers between devices, per_device(): wv_full = lax.all_gather(w_v[layer_idx], 'model', axis=1, tiled=True)  149 us
    all_gather x1, waiting for transfers between devices, per_device(): wk_full = lax.all_gather(w_k[layer_idx], 'model', axis=1, tiled=True)  121 us
    all_gather x1, waiting for transfers between devices, per_device(): wq_full = lax.all_gather(w_q[layer_idx], 'model', axis=1, tiled=True)  110 us
    dot_general x1, matrix products, per_device(): jnp.dot(normed, wu_full, preferred_element_type=jnp.float32)  109 us
  transfers between devices with their start and end apart: 11, of which 10 were waited for; matrix products, arithmetic and copies ran while one was open for 34% of the time, Pallas kernels for 0%

commit v1 on v0

v1 whole, which is shorter than its diff:
```python
import functools

import jax
import jax.numpy as jnp
from jax import lax
from jax.experimental import pallas as pl
from jax.experimental.pallas import tpu as pltpu
from jax.sharding import PartitionSpec as P


HEAD_DIM = 128
NEG_BIG = -1e30
STAT_ROWS = 8
MESH = pl.DeviceIdType.MESH


def rms_norm(hidden, gain_vec):
    hid_f32 = hidden.astype(jnp.float32)
    inv_rms = lax.rsqrt(jnp.mean(hid_f32 * hid_f32, axis=-1, keepdims=True) + 1e-5)
    return (hid_f32 * inv_rms * gain_vec.astype(jnp.float32)).astype(jnp.bfloat16)


def rotary_tables(positions):
    half_dim = HEAD_DIM // 2
    inv_freq = 10000.0 ** (-2.0 * jnp.arange(half_dim, dtype=jnp.float32) / HEAD_DIM)
    angles = positions.astype(jnp.float32)[..., None] * inv_freq
    cos_tab = jnp.cos(angles)
    sin_tab = jnp.sin(angles)
    return jnp.concatenate([cos_tab, cos_tab], axis=-1), jnp.concatenate([-sin_tab, sin_tab], axis=-1)


def rotate(heads_f32, cos_tab, sin_tab):
    half_dim = HEAD_DIM // 2
    swapped = jnp.concatenate([heads_f32[..., half_dim:], heads_f32[..., :half_dim]], axis=-1)
    return heads_f32 * cos_tab + swapped * sin_tab


def kv_kernel(n_in, with_new, sc_ref, *refs):
    x_refs = refs[:n_in]
    cos_refs = refs[n_in:2 * n_in]
    sin_refs = refs[2 * n_in:3 * n_in]
    rest = refs[3 * n_in:]
    wk_ref, wv_ref, gain_ref, q_ref = rest[:4]
    rest = rest[4:]
    if with_new:
        knew_ref, vnew_ref, _ = rest[:3]
        rest = rest[3:]
    else:
        rest = rest[3:]
    kc_ref, vc_ref, st_ref, n_buf, k_buf, v_buf, k_out, v_out, s_out, sems, new_sem = rest
    step = pl.program_id(0)
    n_steps = pl.num_programs(0)
    slot = lax.rem(step, 2)
    blk = x_refs[0].shape[1]
    width = wk_ref.shape[1]
    heads = width // HEAD_DIM

    def out_copies(which, at_step):
        copies = []
        for i in range(n_in):
            shard = sc_ref[i]
            bat = sc_ref[n_in + i] + at_step
            rows = pl.ds(shard * blk, blk)
            copies.append(pltpu.make_async_copy(k_out.at[which, i], kc_ref.at[bat, rows], sems.at[which, i, 0]))
            copies.append(pltpu.make_async_copy(v_out.at[which, i], vc_ref.at[bat, rows], sems.at[which, i, 1]))
            copies.append(pltpu.make_async_copy(s_out.at[which, i], st_ref.at[shard, bat], sems.at[which, i, 2]))
        return copies

    if with_new:
        @pl.when(step == 0)
        def _():
            for idx, (src, dst) in enumerate(((knew_ref, kc_ref), (vnew_ref, vc_ref))):
                for b in range(src.shape[0]):
                    pltpu.make_async_copy(src.at[b], dst.at[b, pl.ds(dst.shape[1] - 1, 1)], new_sem.at[idx, b]).start()

    @pl.when(step >= 2)
    def _():
        for copy in out_copies(slot, step - 2):
            copy.wait()

    gain = gain_ref[...]
    for i in range(n_in):
        def norm_rows(r, carry, i=i):
            rows = pl.ds(pl.multiple_of(r * 16, 16), 16)
            xf = x_refs[i][0, rows, :].astype(jnp.float32)
            inv_rms = lax.rsqrt(jnp.mean(xf * xf, axis=-1, keepdims=True) + 1e-5)
            n_buf[pl.ds(pl.multiple_of(i * blk + r * 16, 16), 16), :] = (xf * inv_rms * gain).astype(jnp.bfloat16)
            return carry

        lax.fori_loop(0, blk // 16, norm_rows, 0)

    def col_tile(c, carry):
        cols = pl.ds(pl.multiple_of(c * 256, 256), 256)
        kf = jnp.dot(n_buf[...], wk_ref[:, cols], preferred_element_type=jnp.float32)
        parts = []
        for i in range(n_in):
            cos_tab = cos_refs[i][0]
            sin_tab = sin_refs[i][0]
            halves = []
            for h in range(2):
                kh = kf[i * blk:(i + 1) * blk, h * HEAD_DIM:(h + 1) * HEAD_DIM]
                halves.append(kh * cos_tab + pltpu.roll(kh, HEAD_DIM // 2, 1) * sin_tab)
            parts.append(jnp.concatenate(halves, axis=1))
        k_buf[:, cols] = jnp.concatenate(parts, axis=0).astype(jnp.bfloat16)
        vf = jnp.dot(n_buf[...], wv_ref[:, cols], preferred_element_type=jnp.float32)
        v_buf[:, cols] = vf.astype(jnp.bfloat16)
        return carry

    lax.fori_loop(0, width // 256, col_tile, 0)

    head_of_row = lax.broadcasted_iota(jnp.int32, (STAT_ROWS, HEAD_DIM), 0) // (STAT_ROWS // heads)
    for i in range(n_in):
        shard = sc_ref[i]
        bat = sc_ref[n_in + i] + step
        seq_len = sc_ref[2 * n_in + bat]
        k_blk = k_buf[i * blk:(i + 1) * blk, :]
        v_blk = v_buf[i * blk:(i + 1) * blk, :]
        k_out[slot, i] = k_blk.reshape(blk, heads, HEAD_DIM)
        v_out[slot, i] = v_blk.reshape(blk, heads, HEAD_DIM)
        scores = lax.dot_general(q_ref[bat], k_blk, (((1,), (1,)), ((), ())), preferred_element_type=jnp.float32) * (HEAD_DIM ** -0.5)
        pos = shard * blk + lax.broadcasted_iota(jnp.int32, scores.shape, 1)
        visible = pos < seq_len
        scores = jnp.where(visible, scores, NEG_BIG)
        blk_max = jnp.max(scores, axis=-1, keepdims=True)
        prob = jnp.where(visible, jnp.exp(scores - blk_max), 0.0)
        blk_sum = jnp.sum(prob, axis=-1, keepdims=True)
        full = jnp.dot(prob.astype(jnp.bfloat16), v_blk, preferred_element_type=jnp.float32)
        acc = jnp.zeros((STAT_ROWS, HEAD_DIM), jnp.float32)
        for h in range(heads):
            acc = jnp.where(head_of_row == h, full[:, h * HEAD_DIM:(h + 1) * HEAD_DIM], acc)
        s_out[slot, i, 0] = acc
        s_out[slot, i, 1] = jnp.broadcast_to(blk_max, (STAT_ROWS, HEAD_DIM))
        s_out[slot, i, 2] = jnp.broadcast_to(blk_sum, (STAT_ROWS, HEAD_DIM))

    for copy in out_copies(slot, step):
        copy.start()

    @pl.when(step == n_steps - 1)
    def _():
        for copy in out_copies(slot, step):
            copy.wait()
        if with_new:
            for idx, (src, dst) in enumerate(((knew_ref, kc_ref), (vnew_ref, vc_ref))):
                for b in range(src.shape[0]):
                    pltpu.make_async_copy(src.at[b], dst.at[b, pl.ds(dst.shape[1] - 1, 1)], new_sem.at[idx, b]).wait()

    @pl.when((step == n_steps - 1) & (n_steps >= 2))
    def _():
        for copy in out_copies(1 - slot, step - 1):
            copy.wait()


def kv_call(inputs, shards, batches, lengths, tabs, w_k, w_v, gain, q_diag, caches, new_rows=None):
    n_in = len(inputs)
    n_steps = inputs[0][2]
    cos_tab, sin_tab = tabs
    blk, d_model = inputs[0][0].shape[1:]
    width = w_k.shape[1]
    heads = width // HEAD_DIM
    scalars = jnp.concatenate([jnp.stack([jnp.int32(s) for s in shards]), jnp.array(batches, jnp.int32), lengths])
    in_specs = []
    operands = []
    for arr, first, _ in inputs:
        in_specs.append(pl.BlockSpec((1, blk, d_model), lambda g, sc, first=first: (first + g, 0, 0)))
        operands.append(arr)
    for tab in (cos_tab, sin_tab):
        for i in range(n_in):
            in_specs.append(pl.BlockSpec((1, blk, HEAD_DIM), lambda g, sc, i=i: (sc[i], 0, 0)))
            operands.append(tab)
    once = pl.Buffered(1)
    in_specs += [
        pl.BlockSpec((d_model, width), lambda g, sc: (0, 0), pipeline_mode=once),
        pl.BlockSpec((d_model, width), lambda g, sc: (0, 0), pipeline_mode=once),
        pl.BlockSpec((1, d_model), lambda g, sc: (0, 0)),
        pl.BlockSpec(q_diag.shape, lambda g, sc: (0, 0, 0)),
    ]
    operands += [w_k, w_v, gain, q_diag]
    any_spec = pl.BlockSpec(memory_space=pl.ANY)
    with_new = new_rows is not None
    if with_new:
        operands += [*new_rows, caches[2]]
        in_specs += [any_spec] * 3
        aliases = {len(operands): 2}
    else:
        operands += list(caches)
        in_specs += [any_spec] * 3
        aliases = {len(operands) - 2: 0, len(operands) - 1: 1, len(operands): 2}
    cache_shape = caches[0].shape
    tokens = n_in * blk
    flops = 2 * n_steps * tokens * d_model * 2 * width
    return pl.pallas_call(
        functools.partial(kv_kernel, n_in, with_new),
        grid_spec=pltpu.PrefetchScalarGridSpec(
            num_scalar_prefetch=1,
            grid=(n_steps,),
            in_specs=in_specs,
            out_specs=[any_spec] * 3,
            scratch_shapes=[
                pltpu.VMEM((tokens, d_model), jnp.bfloat16),
                pltpu.VMEM((tokens, width), jnp.bfloat16),
                pltpu.VMEM((tokens, width), jnp.bfloat16),
                pltpu.VMEM((2, n_in, blk, heads, HEAD_DIM), jnp.bfloat16),
                pltpu.VMEM((2, n_in, blk, heads, HEAD_DIM), jnp.bfloat16),
                pltpu.VMEM((2, n_in, 3, STAT_ROWS, HEAD_DIM), jnp.float32),
                pltpu.SemaphoreType.DMA((2, n_in, 3)),
                pltpu.SemaphoreType.DMA((2, cache_shape[0])),
            ],
        ),
        out_shape=[
            jax.ShapeDtypeStruct(cache_shape, jnp.bfloat16),
            jax.ShapeDtypeStruct(cache_shape, jnp.bfloat16),
            jax.ShapeDtypeStruct(caches[2].shape, jnp.float32),
        ],
        input_output_aliases=aliases,
        compiler_params=pltpu.CompilerParams(vmem_limit_bytes=28 * 2 ** 20),
        cost_estimate=pl.CostEstimate(flops=flops, bytes_accessed=2 * 2 * d_model * width + 2 * n_steps * tokens * (d_model + 2 * width), transcendentals=0),
        name="kv_chunk",
    )(scalars, *operands)


def tail_kernel(n_dev, n_part, st_ref, xs_ref, gain_ref, wo_hbm, wg_hbm, wu_hbm, wd_hbm, dec_ref, last_ref,
                wo, wg, wu, wd, stv, rows, a_buf, n_buf, ps1, pr1, ps2, pr2, xo1, xg1, xo2, xg2,
                w_sem, send_sem, recv_sem):
    me = lax.axis_index("model")
    n_batch = dec_ref.shape[0]
    n_rows = 2 * n_batch
    d_model = dec_ref.shape[1]
    cols = d_model // n_dev
    heads = STAT_ROWS // 2
    loads = [pltpu.make_async_copy(src, dst, w_sem.at[i]) for i, (src, dst) in enumerate(
        ((st_ref, stv), (wo_hbm, wo), (wg_hbm, wg), (wu_hbm, wu), (wd_hbm, wd)))]
    for load in loads:
        load.start()
    barrier = pltpu.get_barrier_semaphore()
    for k in range(1, n_dev):
        peer = lax.rem(me + k, n_dev)
        pl.semaphore_signal(barrier, inc=1, device_id={"model": peer}, device_id_type=MESH)
    pl.semaphore_wait(barrier, n_dev - 1)

    def send(phase, k, src, dst):
        peer = lax.rem(me + k, n_dev)
        return pltpu.make_async_remote_copy(
            src_ref=src, dst_ref=dst, send_sem=send_sem.at[phase, k - 1], recv_sem=recv_sem.at[phase, k - 1],
            device_id={"model": peer}, device_id_type=MESH)

    loads[0].wait()
    for b in range(n_batch):
        top = stv[0, b, 1]
        for j in range(1, n_part):
            top = jnp.maximum(top, stv[j, b, 1])
        den = jnp.zeros((STAT_ROWS, HEAD_DIM), jnp.float32)
        num = jnp.zeros((STAT_ROWS, HEAD_DIM), jnp.float32)
        for j in range(n_part):
            scale = jnp.exp(stv[j, b, 1] - top)
            den += scale * stv[j, b, 2]
            num += scale * stv[j, b, 0]
        rows[:, b, :] = num / den
    for h in range(heads):
        for t in range(2):
            a_buf[t * n_batch:(t + 1) * n_batch, h * HEAD_DIM:(h + 1) * HEAD_DIM] = rows[2 * h + t]
    att = a_buf[...].astype(jnp.bfloat16)

    def all_reduce(phase, partial, base, ps, pr, xo, xg):
        copies = []
        for k in range(1, n_dev):
            peer = lax.rem(me + k, n_dev)
            ps[k - 1] = partial(peer)
            copies.append(send(phase, k, ps.at[k - 1], pr.at[k - 1]))
            copies[-1].start()
        total = base + partial(me)
        for k in range(1, n_dev):
            copies[k - 1].wait_recv()
            total = total + pr[k - 1]
        xo[...] = total.astype(jnp.bfloat16)
        outs = []
        for k in range(1, n_dev):
            outs.append(send(phase + 1, k, xo, xg.at[me]))
            outs[-1].start()
        xg[me] = xo[...]
        for k in range(1, n_dev):
            outs[k - 1].wait_recv()
        return copies + outs

    def col_block(p):
        return pl.ds(pl.multiple_of(p * cols, cols), cols)

    loads[1].wait()
    sent = all_reduce(0, lambda p: jnp.dot(att, wo[:, col_block(p)], preferred_element_type=jnp.float32),
                      xs_ref[...].astype(jnp.float32), ps1, pr1, xo1, xg1)
    sq = jnp.zeros((n_rows, 1), jnp.float32)
    for j in range(n_dev):
        xf = xg1[j].astype(jnp.float32)
        sq += jnp.sum(xf * xf, axis=-1, keepdims=True)
    inv_rms = lax.rsqrt(sq / d_model + 1e-5)
    for j in range(n_dev):
        xf = xg1[j].astype(jnp.float32)
        n_buf[:, j * cols:(j + 1) * cols] = (xf * inv_rms * gain_ref[:, j * cols:(j + 1) * cols]).astype(jnp.bfloat16)
    loads[2].wait()
    nt = (((1,), (1,)), ((), ()))
    gate = lax.dot_general(wg[...], n_buf[...], nt, preferred_element_type=jnp.float32)
    loads[3].wait()
    up = lax.dot_general(wu[...], n_buf[...], nt, preferred_element_type=jnp.float32)
    mid_t = gate * (1.0 / (1.0 + jnp.exp(-gate))) * up
    mid = mid_t.T.astype(jnp.bfloat16)
    loads[4].wait()
    sent += all_reduce(2, lambda p: jnp.dot(mid, wd[:, col_block(p)], preferred_element_type=jnp.float32),
                       xo1[...].astype(jnp.float32), ps2, pr2, xo2, xg2)
    for j in range(n_dev):
        dec_ref[:, j * cols:(j + 1) * cols] = xg2[j, :n_batch]
        last_ref[:, j * cols:(j + 1) * cols] = xg2[j, n_batch:]
    for copy in sent:
        copy.wait_send()


def tail_call(n_dev, stats, x_mine, gain, w_o, w_gate_t, w_up_t, w_down, n_batch):
    n_rows, cols = x_mine.shape
    d_model = w_o.shape[1]
    n_part = stats.shape[0]
    vmem = pl.BlockSpec(memory_space=pltpu.VMEM)
    hbm = pl.BlockSpec(memory_space=pl.ANY)
    return pl.pallas_call(
        functools.partial(tail_kernel, n_dev, n_part),
        out_shape=[jax.ShapeDtypeStruct((n_batch, d_model), jnp.bfloat16)] * 2,
        in_specs=[hbm, vmem, vmem, hbm, hbm, hbm, hbm],
        out_specs=[vmem, vmem],
        scratch_shapes=[
            pltpu.VMEM(w_o.shape, jnp.bfloat16),
            pltpu.VMEM(w_gate_t.shape, jnp.bfloat16),
            pltpu.VMEM(w_up_t.shape, jnp.bfloat16),
            pltpu.VMEM(w_down.shape, jnp.bfloat16),
            pltpu.VMEM(stats.shape, jnp.float32),
            pltpu.VMEM((STAT_ROWS, n_batch, HEAD_DIM), jnp.float32),
            pltpu.VMEM((n_rows, w_o.shape[0]), jnp.float32),
            pltpu.VMEM((n_rows, d_model), jnp.bfloat16),
            pltpu.VMEM((n_dev - 1, n_rows, cols), jnp.float32),
            pltpu.VMEM((n_dev - 1, n_rows, cols), jnp.float32),
            pltpu.VMEM((n_dev - 1, n_rows, cols), jnp.float32),
            pltpu.VMEM((n_dev - 1, n_rows, cols), jnp.float32),
            pltpu.VMEM((n_rows, cols), jnp.bfloat16),
            pltpu.VMEM((n_dev, n_rows, cols), jnp.bfloat16),
            pltpu.VMEM((n_rows, cols), jnp.bfloat16),
            pltpu.VMEM((n_dev, n_rows, cols), jnp.bfloat16),
            pltpu.SemaphoreType.DMA((5,)),
            pltpu.SemaphoreType.DMA((4, n_dev - 1)),
            pltpu.SemaphoreType.DMA((4, n_dev - 1)),
        ],
        compiler_params=pltpu.CompilerParams(collective_id=0, has_side_effects=True, vmem_limit_bytes=52 * 2 ** 20),
        name="tail",
    )(stats, x_mine, gain, w_o, w_gate_t, w_up_t, w_down)


def solution(mesh):
    n_dev = mesh.shape['model']
    seq_spec = P('replica', 'model', None)
    col_spec = P(None, None, 'model')
    row_spec = P(None, 'model', None)
    gain_spec = P(None, None)
    tok_spec = P('replica', None)
    cache_spec = P(None, 'replica', None, 'model', None)
    in_specs = (seq_spec, P('replica'), tok_spec, gain_spec, col_spec, col_spec, col_spec, row_spec, gain_spec, col_spec, col_spec, row_spec)
    out_specs = (tok_spec, tok_spec, cache_spec, cache_spec)

    def swap(arr, bit):
        return lax.ppermute(arr, 'model', [(i, i ^ bit) for i in range(n_dev)])

    def per_device(prompt, lengths, new_tok, norm_attn, w_q, w_k, w_v, w_o, norm_mlp, w_gate, w_up, w_down):
        my_idx = lax.axis_index('model')
        n_batch, blk, d_model = prompt.shape
        seq_len = blk * n_dev
        width = w_k.shape[2]
        heads = width // HEAD_DIM
        half = n_batch // 2
        wq, wk, wv = w_q[0], w_k[0], w_v[0]

        y_parts = [(0, 1), (1, half), (half, n_batch)]
        x_parts = [(half, half + 1), (half + 1, n_batch), (0, half)]
        seq_pos = my_idx * blk + jnp.arange(blk)
        sel = (seq_pos[None, :] == (lengths - 1)[:, None]).astype(jnp.bfloat16)
        from_y, from_x = {}, {}
        from_y[y_parts[0]] = swap(prompt[0:1], 4)
        from_x[x_parts[0]] = swap(prompt[half:half + 1], 2)
        last_x = jnp.einsum('bs,bsd->bd', sel, prompt, preferred_element_type=jnp.float32).astype(jnp.bfloat16)
        last_x = last_x + swap(last_x, 1)
        rest, last_x = lax.optimization_barrier((prompt, last_x))
        last_x = (last_x + swap(last_x, 2)) + (swap(last_x, 4) + swap(last_x, 6))
        for y_part, x_part in zip(y_parts[1:], x_parts[1:]):
            from_y[y_part] = swap(rest[y_part[0]:y_part[1]], 4)
            from_x[x_part] = swap(rest[x_part[0]:x_part[1]], 2)
        core_all = swap(rest, 1)
        x_rows = jnp.concatenate([new_tok, last_x], axis=0)
        n_rows = rms_norm(x_rows, norm_attn[0])
        row_cos, row_sin = rotary_tables(jnp.stack([lengths, lengths - 1]))
        q_rows = jnp.dot(n_rows, wq, preferred_element_type=jnp.float32).reshape(2, n_batch, heads, HEAD_DIM)
        q_rows = rotate(q_rows, row_cos[:, :, None], row_sin[:, :, None]).astype(jnp.bfloat16)
        k_new = jnp.dot(n_rows[:n_batch], wk, preferred_element_type=jnp.float32).reshape(n_batch, heads, HEAD_DIM)
        k_new = rotate(k_new, row_cos[0][:, None], row_sin[0][:, None]).astype(jnp.bfloat16)
        v_new = jnp.dot(n_rows[:n_batch], wv, preferred_element_type=jnp.float32).astype(jnp.bfloat16).reshape(n_batch, heads, HEAD_DIM)

        q_bht = jnp.moveaxis(q_rows, 0, 2)
        q_diag = (q_bht[:, :, :, None, :] * jnp.eye(heads, dtype=jnp.bfloat16)[None, :, None, :, None]).reshape(n_batch, STAT_ROWS, width)
        self_score = jnp.sum(q_rows[0].astype(jnp.float32) * k_new.astype(jnp.float32), axis=-1) * (HEAD_DIM ** -0.5)
        is_new = (jnp.arange(2) == 0)[None, None, :, None]
        full = (n_batch, heads, 2, HEAD_DIM)
        self_max = jnp.where(is_new, jnp.broadcast_to(self_score[:, :, None, None], full), NEG_BIG)
        self_sum = jnp.broadcast_to(jnp.where(is_new, 1.0, 0.0), full)
        self_acc = jnp.where(is_new, v_new.astype(jnp.float32)[:, :, None, :], 0.0)
        self_stat = jnp.stack([a.reshape(n_batch, STAT_ROWS, HEAD_DIM) for a in (self_acc, self_max, self_sum)], axis=1)
        stats = jnp.zeros((n_dev + 1, n_batch, 3, STAT_ROWS, HEAD_DIM), jnp.float32).at[n_dev].set(self_stat)

        tabs = tuple(tab.reshape(n_dev, blk, HEAD_DIM) for tab in rotary_tables(jnp.arange(seq_len)))
        gain = norm_attn.astype(jnp.float32)
        cache_shape = jax.ShapeDtypeStruct((n_batch, seq_len + 1, heads, HEAD_DIM), jnp.bfloat16)
        caches = (cache_shape, cache_shape, stats)

        def run(streams, shards, batches, caches, new_rows=None):
            return kv_call(streams, shards, batches, lengths, tabs, wk, wv, gain, q_diag, caches, new_rows)

        def shard_of(bits):
            idx = my_idx
            for bit in (1, 2, 4):
                if bits & bit:
                    idx = idx + jnp.where((my_idx // bit) % 2 == 0, bit, -bit)
            return idx

        def after(caches, *arrays):
            out = lax.optimization_barrier((caches[2], *arrays))
            return (caches[0], caches[1], out[0]), out[1:]

        s_own, s_core = my_idx, shard_of(1)
        caches = run([(prompt, 0, half), (prompt, half, half)], [s_own] * 2, [0, half], caches,
                     (k_new[:, None], v_new[:, None]))
        caches, (core_all,) = after(caches, core_all)
        caches = run([(core_all, 0, half), (core_all, half, half)], [s_core] * 2, [0, half], caches)
        diag = {}
        for step, (y_part, x_part) in enumerate(zip(y_parts, x_parts)):
            n = y_part[1] - y_part[0]
            caches, (got_y, got_x) = after(caches, from_y[y_part], from_x[x_part])
            other_y, other_x = swap(got_y, 1), swap(got_x, 1)
            if step < 2:
                diag[step] = (swap(got_y, 2), swap(got_x, 4))
            caches = run([(got_y, 0, n), (got_x, 0, n)], [shard_of(4), shard_of(2)], [y_part[0], x_part[0]], caches)
            caches, (other_y, other_x) = after(caches, other_y, other_x)
            caches = run([(other_y, 0, n), (other_x, 0, n)], [shard_of(5), shard_of(3)], [y_part[0], x_part[0]], caches)
        for step in (1, 0):
            y_part, x_part = y_parts[step], x_parts[step]
            n = y_part[1] - y_part[0]
            caches, (via_x, via_y) = after(caches, *diag[step])
            other_x, other_y = swap(via_x, 1), swap(via_y, 1)
            caches = run([(via_x, 0, n), (via_y, 0, n)], [shard_of(6)] * 2, [y_part[0], x_part[0]], caches)
            caches, (other_x, other_y) = after(caches, other_x, other_y)
            caches = run([(other_x, 0, n), (other_y, 0, n)], [shard_of(7)] * 2, [y_part[0], x_part[0]], caches)

        k_cache, v_cache, stats = caches
        x_mine = lax.dynamic_slice_in_dim(x_rows, my_idx * (d_model // n_dev), d_model // n_dev, axis=1)
        dec_hidden, last_hidden = tail_call(n_dev, stats, x_mine, norm_mlp.astype(jnp.float32), w_o[0],
                                            w_gate[0].T, w_up[0].T, w_down[0], n_batch)
        return dec_hidden, last_hidden, k_cache[None], v_cache[None]

    return jax.shard_map(per_device, mesh=mesh, in_specs=in_specs, out_specs=out_specs, check_vma=False)
```

time: 2700 us -> 392 us (0.15)
  waiting for transfers between devices: 1720 us -> 68.6 us
  matrix products: 575 us -> 12 us
  Pallas kernels: 0 us -> 245 us
  local copies, waits for them, and re-layouts: 243 us -> 40.2 us
  other arithmetic: 107 us -> 4.37 us
    all_gather x9 -> x0, waiting for transfers between devices: 1700 us -> none  [the longest x1 332 us: per_device(): wg_full = lax.all_gather(w_gate[layer_idx], 'model', axis=1, tiled=True)]
    dot_general x18 -> x4, matrix products: 575 us -> 12 us  [the longest x1 4.57 us: per_device(): jnp.einsum('bs,bsd->bd', sel, prompt, preferred_element_type=jnp.float32)]
    pallas_call x0 -> x13, Pallas kernels: none -> 245 us  [the longest x12 212 us: kv_call(): pl.pallas_call(functools.partial(kv_kernel, n_in, with_new), grid_spec=pl...]
    dot_general x5 -> x3, local copies, waits for them, and re-layouts: 95.5 us -> 12.7 us  [the longest x1 6.33 us: per_device(): jnp.dot(n_rows, wq, preferred_element_type=jnp.float32)]
    unnamed x54 -> x39, local copies, waits for them, and re-layouts: 82.9 us -> 13.5 us
    ppermute x0 -> x25, waiting for transfers between devices: none -> 68.6 us  [swap(): return lax.ppermute(arr, 'model', [(i, i ^ bit) for i in range(n_dev)])]
    dynamic_slice x3 -> x0, local copies, waits for them, and re-layouts: 43.9 us -> none  [the longest x2 22.8 us: step_fn(): lax.dynamic_index_in_dim(val_blocks, blk_idx, axis=0, keepdims=False)]
    concatenate x5 -> x7, other arithmetic: 39.9 us -> 0.74 us  [the longest x2 0.41 us: rotary_tables(): jnp.concatenate([cos_tab, cos_tab], axis=-1)]
  transfers between devices with their start and end apart: 11 -> 25, of which waited for: 10 -> 5; matrix products, arithmetic and copies ran while one was open for 34% -> 10% of each run, Pallas kernels for 0% -> 52%
where the time goes in v1:
time: 392 us
  Pallas kernels  245 us (62%)
  waiting for transfers between devices  68.6 us (17%)
  local copies, waits for them, and re-layouts  40.2 us (10%)
  starting transfers between devices  20.5 us (5%)
  matrix products  12 us (3%)
  other arithmetic  4.37 us (1%)
    pallas_call x12, Pallas kernels, kv_call(): pl.pallas_call(functools.partial(kv_kernel, n_in, with_new), grid_spec=pl...  212 us
    ppermute x25, waiting for transfers between devices, swap(): return lax.ppermute(arr, 'model', [(i, i ^ bit) for i in range(n_dev)])  68.6 us
    pallas_call x1, Pallas kernels, tail_call(): pl.pallas_call(functools.partial(tail_kernel, n_dev, n_part), out_shape=[...  32.6 us
    ppermute x25, starting transfers between devices, swap(): return lax.ppermute(arr, 'model', [(i, i ^ bit) for i in range(n_dev)])  20.5 us
    unnamed x39, local copies, waits for them, and re-layouts  13.5 us
    slice x2, local copies, waits for them, and re-layouts, per_device(): from_x[x_part] = swap(rest[x_part[0]:x_part[1]], 2)  10.1 us
  transfers between devices with their start and end apart: 25, of which 5 were waited for; matrix products, arithmetic and copies ran while one was open for 10% of the time, Pallas kernels for 52%

profile of v1, /device:TPU:0, one launch (start us, length us, event | category | flops | bytes accessed | tf_op | source)
XLA Modules:
  0.0 391.6 jit_solution(885631268081661737)
XLA Ops:
  0.7 0.7 fusion.31
  1.4 4.6 %fusion.16 = bf16[8,1,4096]{2,1,0:T(2,128)(2,1)S(1)} fusion(bf16[8,128,4096]{2,1,0:T(8,128)(2,1)} %refs_1_.1, pred[8,128,1]{1,0,2:T(8,128)(4,1)S(1)} %compare_bitcast_fusion), kind=kOutput, calls=%fused_computation.35 | convolution fusion | flops 8388608 | bytes 8455168 | tf_op jit(solution)/shard_map/bs,bsd->bd/dot_general | solution.py:382
  6.1 0.9 collective-permute-start
  6.9 3.1 fusion.35
  10.0 2.5 collective-permute-start.5
  12.6 6.3 %copy.99 = bf16[512,4096]{1,0:T(8,128)(2,1)} copy(bf16[512,4096]{0,1:T(8,128)(2,1)} %bitcast.119) | data formatting | bytes 8388608 | tf_op jit(solution)/shard_map/dot_general | solution.py:393
  19.0 6.3 %copy.100 = bf16[512,4096]{1,0:T(8,128)(2,1)} copy(bf16[512,4096]{0,1:T(8,128)(2,1)} %bitcast.82) | data formatting | bytes 8388608 | tf_op jit(solution)/shard_map/dot_general | solution.py:395
  26.3 1.9 fusion.3
  28.9 2.7 collective-permute-start.3
  31.5 0.5 collective-permute-start.1
  32.1 6.3 %fusion.34 = (bf16[3,128,4096]{2,1,0:T(8,128)(2,1)}, bf16[3,128,4096]{2,1,0:T(8,128)(2,1)}) fusion(bf16[8,128,4096]{2,1,0:T(8,128)(2,1)} %refs_1_.1), kind=kLoop, calls=%fused_computation.91 | loop fusion | bytes 12582912 | tf_op jit(solution)/shard_map/slice | solution.py:388
  38.3 1.0 collective-permute-done.2
  39.4 1.7 collective-permute-start.6
  41.1 1.5 collective-permute-start.9
  42.6 0.5 collective-permute-start.10
  43.4 1.2 fusion.4
  44.9 3.4 fusion.6
  48.4 2.8 bitcast_convert_fusion.1
  51.9 2.2 copy-done
  54.1 2.2 copy-done.3
  56.3 3.4 copy-done.6
  59.7 24.8 %kv_chunk.12 = (bf16[8,1025,4,128]{3,2,1,0:T(4,128)(2,1)}, bf16[8,1025,4,128]{3,2,1,0:T(4,128)(2,1)}, f32[9,8,3,8,128]{4,3,2,1,0:T(8,128)S(1)}) custom-call(s32[12]{0:T(128)S(1)} %get-tuple-element.178.sc_ref, bf16[8,128,4096]{2,1,0:T(8,128)(2,1)S(1)} %copy-done.6, bf16[8,128,4096]{2,1,0:T(8,128)(2,1)S(1)} %copy-done.6, ...), custom_call_target="tpu_custom_call", output_to_operand_aliasing={{2}: (13, {})} | custom-call | flops 8589934592 | bytes 18874368 | tf_op jit(solution)/shard_map/kv_chunk/pallas_call | solution.py:191
  84.5 26.5 %kv_chunk.13 = (bf16[8,1025,4,128]{3,2,1,0:T(4,128)(2,1)}, bf16[8,1025,4,128]{3,2,1,0:T(4,128)(2,1)}, f32[9,8,3,8,128]{4,3,2,1,0:T(8,128)S(1)}) custom-call(s32[12]{0:T(128)S(1)} %get-tuple-element.181.sc_ref, bf16[8,128,4096]{2,1,0:T(8,128)(2,1)} %collective-permute-done.4.refs_0_.refs_1_, ...), custom_call_target="tpu_custom_call", output_to_operand_aliasing={{0}: (11, {}), {1}: (12, {}), {2}: (13, {})} | custom-call | flops 8589934592 | bytes 18874368 | tf_op jit(solution)/shard_map/kv_chunk/pallas_call | solution.py:191
  111.6 3.8 fusion.33
  115.7 1.7 collective-permute-start.14
  117.4 8.5 %kv_chunk.14 = (bf16[8,1025,4,128]{3,2,1,0:T(4,128)(2,1)}, bf16[8,1025,4,128]{3,2,1,0:T(4,128)(2,1)}, f32[9,8,3,8,128]{4,3,2,1,0:T(8,128)S(1)}) custom-call(s32[12]{0:T(128)S(1)} %get-tuple-element.182.sc_ref, bf16[1,128,4096]{2,1,0:T(8,128)(2,1)S(1)} %collective-permute-done.5.refs_0_, ...), custom_call_target="tpu_custom_call", output_to_operand_aliasing={{0}: (11, {}), {1}: (12, {}), {2}: (13, {})} | custom-call | flops 2147483648 | bytes 11010048 | tf_op jit(solution)/shard_map/kv_chunk/pallas_call | solution.py:191
  125.9 7.4 %kv_chunk.15 = (bf16[8,1025,4,128]{3,2,1,0:T(4,128)(2,1)}, bf16[8,1025,4,128]{3,2,1,0:T(4,128)(2,1)}, f32[9,8,3,8,128]{4,3,2,1,0:T(8,128)S(1)}) custom-call(s32[12]{0:T(128)S(1)} %get-tuple-element.180.sc_ref, bf16[1,128,4096]{2,1,0:T(8,128)(2,1)S(1)} %collective-permute-done.7.refs_0_, ...), custom_call_target="tpu_custom_call", output_to_operand_aliasing={{0}: (11, {}), {1}: (12, {}), {2}: (13, {})} | custom-call | flops 2147483648 | bytes 11010048 | tf_op jit(solution)/shard_map/kv_chunk/pallas_call | solution.py:191
  134.0 20.4 %kv_chunk.16 = (bf16[8,1025,4,128]{3,2,1,0:T(4,128)(2,1)}, bf16[8,1025,4,128]{3,2,1,0:T(4,128)(2,1)}, f32[9,8,3,8,128]{4,3,2,1,0:T(8,128)S(1)}) custom-call(s32[12]{0:T(128)S(1)} %get-tuple-element.184.sc_ref, bf16[3,128,4096]{2,1,0:T(8,128)(2,1)} %collective-permute-done.9.refs_0_, ...), custom_call_target="tpu_custom_call", output_to_operand_aliasing={{0}: (11, {}), {1}: (12, {}), {2}: (13, {})} | custom-call | flops 6442450944 | bytes 16252928 | tf_op jit(solution)/shard_map/kv_chunk/pallas_call | solution.py:191
  154.4 18.9 %kv_chunk.17 = (bf16[8,1025,4,128]{3,2,1,0:T(4,128)(2,1)}, bf16[8,1025,4,128]{3,2,1,0:T(4,128)(2,1)}, f32[9,8,3,8,128]{4,3,2,1,0:T(8,128)S(1)}) custom-call(s32[12]{0:T(128)S(1)} %get-tuple-element.186.sc_ref, bf16[3,128,4096]{2,1,0:T(8,128)(2,1)S(1)} %collective-permute-done.11.refs_0_, ...), custom_call_target="tpu_custom_call", output_to_operand_aliasing={{0}: (11, {}), {1}: (12, {}), {2}: (13, {})} | custom-call | flops 6442450944 | bytes 16252928 | tf_op jit(solution)/shard_map/kv_chunk/pallas_call | solution.py:191
  173.3 34.8 %collective-permute-done.13.refs_0_ = bf16[4,128,4096]{2,1,0:T(8,128)(2,1)S(1)} collective-permute-done((bf16[4,128,4096]{2,1,0:T(8,128)(2,1)}, bf16[4,128,4096]{2,1,0:T(8,128)(2,1)S(1)}, u32[]{:S(2)}, u32[]{:S(2)}) %collective-permute-start.13) | collective-permute-done | bytes 4194336 | tf_op jit(solution)/shard_map/ppermute | solution.py:364
  208.2 13.7 %collective-permute-done.14.refs_1_ = bf16[4,128,4096]{2,1,0:T(8,128)(2,1)S(1)} collective-permute-done((bf16[4,128,4096]{2,1,0:T(8,128)(2,1)}, bf16[4,128,4096]{2,1,0:T(8,128)(2,1)S(1)}, u32[]{:S(2)}, u32[]{:S(2)}) %collective-permute-start.14) | collective-permute-done | bytes 4194336 | tf_op jit(solution)/shard_map/ppermute | solution.py:364
  222.4 1.4 collective-permute-start.17
  223.8 1.5 collective-permute-start.18
  225.4 24.7 %kv_chunk.18 = (bf16[8,1025,4,128]{3,2,1,0:T(4,128)(2,1)}, bf16[8,1025,4,128]{3,2,1,0:T(4,128)(2,1)}, f32[9,8,3,8,128]{4,3,2,1,0:T(8,128)S(1)}) custom-call(s32[12]{0:T(128)S(1)} %get-tuple-element.187.sc_ref, bf16[4,128,4096]{2,1,0:T(8,128)(2,1)S(1)} %collective-permute-done.13.refs_0_, ...), custom_call_target="tpu_custom_call", output_to_operand_aliasing={{0}: (11, {}), {1}: (12, {}), {2}: (13, {})} | custom-call | flops 8589934592 | bytes 18874368 | tf_op jit(solution)/shard_map/kv_chunk/pallas_call | solution.py:191
  250.1 24.7 %kv_chunk.19 = (bf16[8,1025,4,128]{3,2,1,0:T(4,128)(2,1)}, bf16[8,1025,4,128]{3,2,1,0:T(4,128)(2,1)}, f32[9,8,3,8,128]{4,3,2,1,0:T(8,128)S(1)}) custom-call(s32[12]{0:T(128)S(1)} %get-tuple-element.188.sc_ref, bf16[4,128,4096]{2,1,0:T(8,128)(2,1)S(1)} %collective-permute-done.15.refs_0_, ...), custom_call_target="tpu_custom_call", output_to_operand_aliasing={{0}: (11, {}), {1}: (12, {}), {2}: (13, {})} | custom-call | flops 8589934592 | bytes 18874368 | tf_op jit(solution)/shard_map/kv_chunk/pallas_call | solution.py:191
  274.8 17.9 %collective-permute-done.17.refs_0_ = bf16[3,128,4096]{2,1,0:T(8,128)(2,1)} collective-permute-done((bf16[3,128,4096]{2,1,0:T(8,128)(2,1)}, bf16[3,128,4096]{2,1,0:T(8,128)(2,1)}, u32[]{:S(2)}, u32[]{:S(2)}) %collective-permute-start.17) | collective-permute-done | bytes 3145760 | tf_op jit(solution)/shard_map/ppermute | solution.py:364
  292.7 1.0 collective-permute-done.18.refs_1_
  294.2 0.6 collective-permute-start.21
  294.8 1.5 collective-permute-start.22
  296.3 20.1 %kv_chunk.20 = (bf16[8,1025,4,128]{3,2,1,0:T(4,128)(2,1)}, bf16[8,1025,4,128]{3,2,1,0:T(4,128)(2,1)}, f32[9,8,3,8,128]{4,3,2,1,0:T(8,128)S(1)}) custom-call(s32[12]{0:T(128)S(1)} %get-tuple-element.185.sc_ref, bf16[3,128,4096]{2,1,0:T(8,128)(2,1)} %collective-permute-done.17.refs_0_, ...), custom_call_target="tpu_custom_call", output_to_operand_aliasing={{0}: (11, {}), {1}: (12, {}), {2}: (13, {})} | custom-call | flops 6442450944 | bytes 16252928 | tf_op jit(solution)/shard_map/kv_chunk/pallas_call | solution.py:191
  316.4 18.9 %kv_chunk.21 = (bf16[8,1025,4,128]{3,2,1,0:T(4,128)(2,1)}, bf16[8,1025,4,128]{3,2,1,0:T(4,128)(2,1)}, f32[9,8,3,8,128]{4,3,2,1,0:T(8,128)S(1)}) custom-call(s32[12]{0:T(128)S(1)} %get-tuple-element.193.sc_ref, bf16[3,128,4096]{2,1,0:T(8,128)(2,1)S(1)} %collective-permute-done.19.refs_0_, ...), custom_call_target="tpu_custom_call", output_to_operand_aliasing={{0}: (11, {}), {1}: (12, {}), {2}: (13, {})} | custom-call | flops 6442450944 | bytes 16252928 | tf_op jit(solution)/shard_map/kv_chunk/pallas_call | solution.py:191
  335.9 2.2 copy-done.2
  338.1 2.2 copy-done.5
  340.3 8.8 %kv_chunk.22 = (bf16[8,1025,4,128]{3,2,1,0:T(4,128)(2,1)}, bf16[8,1025,4,128]{3,2,1,0:T(4,128)(2,1)}, f32[9,8,3,8,128]{4,3,2,1,0:T(8,128)S(1)}) custom-call(s32[12]{0:T(128)S(1)} %get-tuple-element.179.sc_ref, bf16[1,128,4096]{2,1,0:T(8,128)(2,1)} %collective-permute-done.21.refs_0_, ...), custom_call_target="tpu_custom_call", output_to_operand_aliasing={{0}: (11, {}), {1}: (12, {}), {2}: (13, {})} | custom-call | flops 2147483648 | bytes 11010048 | tf_op jit(solution)/shard_map/kv_chunk/pallas_call | solution.py:191
  349.1 8.7 %kv_chunk.23 = (bf16[8,1025,4,128]{3,2,1,0:T(4,128)(2,1)}, bf16[8,1025,4,128]{3,2,1,0:T(4,128)(2,1)}, f32[9,8,3,8,128]{4,3,2,1,0:T(8,128)S(1)}) custom-call(s32[12]{0:T(128)S(1)} %get-tuple-element.183.sc_ref, bf16[1,128,4096]{2,1,0:T(8,128)(2,1)S(1)} %collective-permute-done.23.refs_0_, ...), custom_call_target="tpu_custom_call", output_to_operand_aliasing={{0}: (11, {}), {1}: (12, {}), {2}: (13, {})} | custom-call | flops 2147483648 | bytes 11010048 | tf_op jit(solution)/shard_map/kv_chunk/pallas_call | solution.py:191
  357.8 32.6 %tail.1 = (bf16[8,4096]{1,0:T(8,128)(2,1)S(1)}, bf16[8,4096]{1,0:T(8,128)(2,1)S(1)}) custom-call(f32[9,8,3,8,128]{4,3,2,1,0:T(8,128)S(1)} %get-tuple-element.155.st_ref, bf16[16,512]{1,0:T(8,128)(2,1)S(1)} %fusion.12.xs_ref, f32[1,4096]{1,0:T(1,128)S(1)} %convert_element_type.115.gain_ref, bf16[512,4096]{1,0:T(8,128)(2,1)} %bitcast.118, ...), custom_call_target="tpu_custom_call" | custom-call | tf_op jit(solution)/shard_map/tail/pallas_call | solution.py:321
  390.4 0.6 copy.153
  391.0 0.6 copy.154
  (116 shorter events, 6.3 us)
Async XLA Ops:
  0.6 11.9 %copy-start.9 = (bf16[1,4096]{1,0:T(2,128)(2,1)S(1)}, bf16[1,4096]{1,0:T(2,128)(2,1)}, u32[]{:S(2)}) copy-start(bf16[1,4096]{1,0:T(2,128)(2,1)} %param.29) | copy-start | bytes 24580
  6.1 19.2 %collective-permute-start = (bf16[8,4096]{1,0:T(8,128)(2,1)S(1)}, bf16[8,4096]{1,0:T(8,128)(2,1)S(1)}, u32[]{:S(2)}, u32[]{:S(2)}) collective-permute-start(bf16[8,4096]{1,0:T(8,128)(2,1)S(1)} %bitcast.122), channel_id=1, source_target_pairs={{0,1},{1,0},{2,3},{3,2},{4,5},{5,4},{6,7},{7,6}} | collective-permute-start | bytes 196616 | tf_op jit(solution)/shard_map/ppermute | solution.py:364
  10.0 101.0 %collective-permute-start.5 = (bf16[1,128,4096]{2,1,0:T(8,128)(2,1)}, bf16[1,128,4096]{2,1,0:T(8,128)(2,1)S(1)}, u32[]{:S(2)}, u32[]{:S(2)}) collective-permute-start(bf16[1,128,4096]{2,1,0:T(8,128)(2,1)} %get-tuple-element.167), channel_id=1, source_target_pairs={{0,4},{1,5},{2,6},{3,7},{4,0},{5,1},{6,2},{7,3}} | collective-permute-start | bytes 3145736 | tf_op jit(solution)/shard_map/ppermute | solution.py:364
  12.5 13.3 %copy-start.11 = (s32[8]{0:T(128)S(1)}, s32[8]{0:T(128)}, u32[]{:S(2)}) copy-start(s32[8]{0:T(128)} %param.27) | copy-start | bytes 100
  25.4 59.1 %collective-permute-start.4 = (bf16[8,128,4096]{2,1,0:T(8,128)(2,1)}, bf16[8,128,4096]{2,1,0:T(8,128)(2,1)}, u32[]{:S(2)}, u32[]{:S(2)}) collective-permute-start(bf16[8,128,4096]{2,1,0:T(8,128)(2,1)} %refs_1_.1), channel_id=1, source_target_pairs={{0,1},{1,0},{2,3},{3,2},{4,5},{5,4},{6,7},{7,6}} | collective-permute-start | bytes 25165832 | tf_op jit(solution)/shard_map/ppermute | solution.py:364
  26.3 16.9 %copy-start.8 = (bf16[8,4096]{1,0:T(8,128)(2,1)S(1)}, bf16[8,4096]{1,0:T(8,128)(2,1)}, u32[]{:S(2)}) copy-start(bf16[8,4096]{1,0:T(8,128)(2,1)} %param.28) | copy-start | bytes 196612
  26.3 17.1 %copy-start.7 = (bf16[512,4096]{1,0:T(8,128)(2,1)S(1)}, bf16[512,4096]{1,0:T(8,128)(2,1)}, u32[]{:S(2)}) copy-start(bf16[512,4096]{1,0:T(8,128)(2,1)} %copy.99) | copy-start | bytes 12582916
  28.6 10.8 %collective-permute-start.2 = (bf16[8,4096]{1,0:T(8,128)(2,1)S(1)}, bf16[8,4096]{1,0:T(8,128)(2,1)S(1)}, u32[]{:S(2)}, u32[]{:S(2)}) collective-permute-start(bf16[8,4096]{1,0:T(8,128)(2,1)S(1)} %fusion.41), channel_id=1, source_target_pairs={{0,4},{1,5},{2,6},{3,7},{4,0},{5,1},{6,2},{7,3}} | collective-permute-start | bytes 196616 | tf_op jit(solution)/shard_map/ppermute | solution.py:364
  28.9 12.2 %collective-permute-start.3 = (bf16[8,4096]{1,0:T(8,128)(2,1)S(1)}, bf16[8,4096]{1,0:T(8,128)(2,1)S(1)}, u32[]{:S(2)}, u32[]{:S(2)}) collective-permute-start(bf16[8,4096]{1,0:T(8,128)(2,1)S(1)} %fusion.41), channel_id=1, source_target_pairs={{0,6},{1,7},{2,4},{3,5},{4,2},{5,3},{6,0},{7,1}} | collective-permute-start | bytes 196616 | tf_op jit(solution)/shard_map/ppermute | solution.py:364
  31.5 11.1 %collective-permute-start.1 = (bf16[8,4096]{1,0:T(8,128)(2,1)S(1)}, bf16[8,4096]{1,0:T(8,128)(2,1)S(1)}, u32[]{:S(2)}, u32[]{:S(2)}) collective-permute-start(bf16[8,4096]{1,0:T(8,128)(2,1)S(1)} %fusion.41), channel_id=1, source_target_pairs={{0,2},{1,3},{2,0},{3,1},{4,6},{5,7},{6,4},{7,5}} | collective-permute-start | bytes 196616 | tf_op jit(solution)/shard_map/ppermute | solution.py:364
  39.4 71.7 %collective-permute-start.6 = (bf16[1,128,4096]{2,1,0:T(8,128)(2,1)}, bf16[1,128,4096]{2,1,0:T(8,128)(2,1)}, u32[]{:S(2)}, u32[]{:S(2)}) collective-permute-start(bf16[1,128,4096]{2,1,0:T(8,128)(2,1)} %get-tuple-element.166), channel_id=1, source_target_pairs={{0,2},{1,3},{2,0},{3,1},{4,6},{5,7},{6,4},{7,5}} | collective-permute-start | bytes 3145736 | tf_op jit(solution)/shard_map/ppermute | solution.py:364
  41.1 92.3 %collective-permute-start.9 = (bf16[3,128,4096]{2,1,0:T(8,128)(2,1)}, bf16[3,128,4096]{2,1,0:T(8,128)(2,1)}, u32[]{:S(2)}, u32[]{:S(2)}) collective-permute-start(bf16[3,128,4096]{2,1,0:T(8,128)(2,1)} %get-tuple-element.165), channel_id=1, source_target_pairs={{0,4},{1,5},{2,6},{3,7},{4,0},{5,1},{6,2},{7,3}} | collective-permute-start | bytes 9437192 | tf_op jit(solution)/shard_map/ppermute | solution.py:364
  42.6 90.8 %collective-permute-start.10 = (bf16[3,128,4096]{2,1,0:T(8,128)(2,1)}, bf16[3,128,4096]{2,1,0:T(8,128)(2,1)}, u32[]{:S(2)}, u32[]{:S(2)}) collective-permute-start(bf16[3,128,4096]{2,1,0:T(8,128)(2,1)} %get-tuple-element.164), channel_id=1, source_target_pairs={{0,2},{1,3},{2,0},{3,1},{4,6},{5,7},{6,4},{7,5}} | collective-permute-start | bytes 9437192 | tf_op jit(solution)/shard_map/ppermute | solution.py:364
  51.9 2.2 copy-start
  54.1 2.2 copy-start.3
  56.3 3.4 copy-start.6
  59.7 51.9 %slice-start = ((s8[8388608]{0:T(1024)(128)(4,1)}), s8[4194304]{0:T(1024)(128)(4,1)S(1)}, s32[]{:S(2)}) async-start(s8[8388608]{0:T(1024)(128)(4,1)} %bitcast.107), calls=%async_computation | async-start | bytes 8388608
  84.5 27.1 %slice-start.1 = ((s8[8388608]{0:T(1024)(128)(4,1)}), s8[4194304]{0:T(1024)(128)(4,1)S(1)}, s32[]{:S(2)}) async-start(s8[8388608]{0:T(1024)(128)(4,1)} %bitcast.107), calls=%async_computation.1 | async-start | bytes 8388608
  111.0 6.4 %copy-start.4 = (bf16[1,4096,512]{2,1,0:T(8,128)(2,1)S(1)}, bf16[1,4096,512]{2,1,0:T(8,128)(2,1)}, u32[]{:S(2)}) copy-start(bf16[1,4096,512]{2,1,0:T(8,128)(2,1)} %param.32) | copy-start | bytes 12582916
  111.0 4.7 %collective-permute-start.7 = (bf16[1,128,4096]{2,1,0:T(8,128)(2,1)S(1)}, bf16[1,128,4096]{2,1,0:T(8,128)(2,1)S(1)}, u32[]{:S(2)}, u32[]{:S(2)}) collective-permute-start(bf16[1,128,4096]{2,1,0:T(8,128)(2,1)S(1)} %collective-permute-done.5.refs_0_), channel_id=1, source_target_pairs={{0,1},{1,0},{2,3},{3,2},{4,5},{5,4},{6,7},{7,6}} | collective-permute-start | bytes 3145736 | tf_op jit(solution)/shard_map/ppermute | solution.py:364
  111.1 14.8 %collective-permute-start.8 = (bf16[1,128,4096]{2,1,0:T(8,128)(2,1)}, bf16[1,128,4096]{2,1,0:T(8,128)(2,1)S(1)}, u32[]{:S(2)}, u32[]{:S(2)}) collective-permute-start(bf16[1,128,4096]{2,1,0:T(8,128)(2,1)} %collective-permute-done.6.refs_1_), channel_id=1, source_target_pairs={{0,1},{1,0},{2,3},{3,2},{4,5},{5,4},{6,7},{7,6}} | collective-permute-start | bytes 3145736 | tf_op jit(solution)/shard_map/ppermute | solution.py:364
  115.4 92.7 %collective-permute-start.13 = (bf16[4,128,4096]{2,1,0:T(8,128)(2,1)}, bf16[4,128,4096]{2,1,0:T(8,128)(2,1)S(1)}, u32[]{:S(2)}, u32[]{:S(2)}) collective-permute-start(bf16[4,128,4096]{2,1,0:T(8,128)(2,1)} %get-tuple-element.163), channel_id=1, source_target_pairs={{0,4},{1,5},{2,6},{3,7},{4,0},{5,1},{6,2},{7,3}} | collective-permute-start | bytes 12582920 | tf_op jit(solution)/shard_map/ppermute | solution.py:364
  115.7 106.1 %collective-permute-start.14 = (bf16[4,128,4096]{2,1,0:T(8,128)(2,1)}, bf16[4,128,4096]{2,1,0:T(8,128)(2,1)S(1)}, u32[]{:S(2)}, u32[]{:S(2)}) collective-permute-start(bf16[4,128,4096]{2,1,0:T(8,128)(2,1)} %get-tuple-element.162), channel_id=1, source_target_pairs={{0,2},{1,3},{2,0},{3,1},{4,6},{5,7},{6,4},{7,5}} | collective-permute-start | bytes 12582920 | tf_op jit(solution)/shard_map/ppermute | solution.py:364
  125.9 8.0 %copy-start.12 = (s32[2]{0:T(128)S(1)}, s32[2]{0:T(128)}, u32[]{:S(2)}) copy-start(s32[2]{0:T(128)} %constant.232.clone) | copy-start | bytes 28
  125.9 8.1 %copy-start.1 = (bf16[1,4096,512]{2,1,0:T(8,128)(2,1)S(1)}, bf16[1,4096,512]{2,1,0:T(8,128)(2,1)}, u32[]{:S(2)}) copy-start(bf16[1,4096,512]{2,1,0:T(8,128)(2,1)} %param.31) | copy-start | bytes 12582916
  133.4 21.0 %collective-permute-start.11 = (bf16[3,128,4096]{2,1,0:T(8,128)(2,1)}, bf16[3,128,4096]{2,1,0:T(8,128)(2,1)S(1)}, u32[]{:S(2)}, u32[]{:S(2)}) collective-permute-start(bf16[3,128,4096]{2,1,0:T(8,128)(2,1)} %collective-permute-done.9.refs_0_), channel_id=1, source_target_pairs={{0,1},{1,0},{2,3},{3,2},{4,5},{5,4},{6,7},{7,6}} | collective-permute-start | bytes 9437192 | tf_op jit(solution)/shard_map/ppermute | solution.py:364
  133.4 21.0 %collective-permute-start.12 = (bf16[3,128,4096]{2,1,0:T(8,128)(2,1)}, bf16[3,128,4096]{2,1,0:T(8,128)(2,1)S(1)}, u32[]{:S(2)}, u32[]{:S(2)}) collective-permute-start(bf16[3,128,4096]{2,1,0:T(8,128)(2,1)} %collective-permute-done.10.refs_1_), channel_id=1, source_target_pairs={{0,1},{1,0},{2,3},{3,2},{4,5},{5,4},{6,7},{7,6}} | collective-permute-start | bytes 9437192 | tf_op jit(solution)/shard_map/ppermute | solution.py:364
  154.4 70.9 %copy-start.13 = (s32[2]{0:T(128)S(1)}, s32[2]{0:T(128)}, u32[]{:S(2)}) copy-start(s32[2]{0:T(128)} %constant.233.clone) | copy-start | bytes 28
  221.8 28.2 %collective-permute-start.15 = (bf16[4,128,4096]{2,1,0:T(8,128)(2,1)S(1)}, bf16[4,128,4096]{2,1,0:T(8,128)(2,1)S(1)}, u32[]{:S(2)}, u32[]{:S(2)}) collective-permute-start(bf16[4,128,4096]{2,1,0:T(8,128)(2,1)S(1)} %collective-permute-done.13.refs_0_), channel_id=1, source_target_pairs={{0,1},{1,0},{2,3},{3,2},{4,5},{5,4},{6,7},{7,6}} | collective-permute-start | bytes 12582920 | tf_op jit(solution)/shard_map/ppermute | solution.py:364
  221.8 28.2 %collective-permute-start.16 = (bf16[4,128,4096]{2,1,0:T(8,128)(2,1)S(1)}, bf16[4,128,4096]{2,1,0:T(8,128)(2,1)S(1)}, u32[]{:S(2)}, u32[]{:S(2)}) collective-permute-start(bf16[4,128,4096]{2,1,0:T(8,128)(2,1)S(1)} %collective-permute-done.14.refs_1_), channel_id=1, source_target_pairs={{0,1},{1,0},{2,3},{3,2},{4,5},{5,4},{6,7},{7,6}} | collective-permute-start | bytes 12582920 | tf_op jit(solution)/shard_map/ppermute | solution.py:364
  222.4 70.3 %collective-permute-start.17 = (bf16[3,128,4096]{2,1,0:T(8,128)(2,1)}, bf16[3,128,4096]{2,1,0:T(8,128)(2,1)}, u32[]{:S(2)}, u32[]{:S(2)}) collective-permute-start(bf16[3,128,4096]{2,1,0:T(8,128)(2,1)} %collective-permute-done.9.refs_0_), channel_id=1, source_target_pairs={{0,2},{1,3},{2,0},{3,1},{4,6},{5,7},{6,4},{7,5}} | collective-permute-start | bytes 9437192 | tf_op jit(solution)/shard_map/ppermute | solution.py:364
  223.8 69.9 %collective-permute-start.18 = (bf16[3,128,4096]{2,1,0:T(8,128)(2,1)}, bf16[3,128,4096]{2,1,0:T(8,128)(2,1)S(1)}, u32[]{:S(2)}, u32[]{:S(2)}) collective-permute-start(bf16[3,128,4096]{2,1,0:T(8,128)(2,1)} %collective-permute-done.10.refs_1_), channel_id=1, source_target_pairs={{0,4},{1,5},{2,6},{3,7},{4,0},{5,1},{6,2},{7,3}} | collective-permute-start | bytes 9437192 | tf_op jit(solution)/shard_map/ppermute | solution.py:364
  293.7 22.7 %collective-permute-start.19 = (bf16[3,128,4096]{2,1,0:T(8,128)(2,1)}, bf16[3,128,4096]{2,1,0:T(8,128)(2,1)S(1)}, u32[]{:S(2)}, u32[]{:S(2)}) collective-permute-start(bf16[3,128,4096]{2,1,0:T(8,128)(2,1)} %collective-permute-done.17.refs_0_), channel_id=1, source_target_pairs={{0,1},{1,0},{2,3},{3,2},{4,5},{5,4},{6,7},{7,6}} | collective-permute-start | bytes 9437192 | tf_op jit(solution)/shard_map/ppermute | solution.py:364
  293.7 22.7 %collective-permute-start.20 = (bf16[3,128,4096]{2,1,0:T(8,128)(2,1)S(1)}, bf16[3,128,4096]{2,1,0:T(8,128)(2,1)S(1)}, u32[]{:S(2)}, u32[]{:S(2)}) collective-permute-start(bf16[3,128,4096]{2,1,0:T(8,128)(2,1)S(1)} %collective-permute-done.18.refs_1_), channel_id=1, source_target_pairs={{0,1},{1,0},{2,3},{3,2},{4,5},{5,4},{6,7},{7,6}} | collective-permute-start | bytes 9437192 | tf_op jit(solution)/shard_map/ppermute | solution.py:364
  294.2 41.1 %collective-permute-start.21 = (bf16[1,128,4096]{2,1,0:T(8,128)(2,1)S(1)}, bf16[1,128,4096]{2,1,0:T(8,128)(2,1)}, u32[]{:S(2)}, u32[]{:S(2)}) collective-permute-start(bf16[1,128,4096]{2,1,0:T(8,128)(2,1)S(1)} %collective-permute-done.5.refs_0_), channel_id=1, source_target_pairs={{0,2},{1,3},{2,0},{3,1},{4,6},{5,7},{6,4},{7,5}} | collective-permute-start | bytes 3145736 | tf_op jit(solution)/shard_map/ppermute | solution.py:364
  294.8 40.5 %collective-permute-start.22 = (bf16[1,128,4096]{2,1,0:T(8,128)(2,1)}, bf16[1,128,4096]{2,1,0:T(8,128)(2,1)}, u32[]{:S(2)}, u32[]{:S(2)}) collective-permute-start(bf16[1,128,4096]{2,1,0:T(8,128)(2,1)} %collective-permute-done.6.refs_1_), channel_id=1, source_target_pairs={{0,4},{1,5},{2,6},{3,7},{4,0},{5,1},{6,2},{7,3}} | collective-permute-start | bytes 3145736 | tf_op jit(solution)/shard_map/ppermute | solution.py:364
  316.4 19.4 %copy-start.10 = (bf16[1,4096]{1,0:T(2,128)(2,1)S(1)}, bf16[1,4096]{1,0:T(2,128)(2,1)}, u32[]{:S(2)}) copy-start(bf16[1,4096]{1,0:T(2,128)(2,1)} %param.34) | copy-start | bytes 24580
  335.3 13.7 %collective-permute-start.23 = (bf16[1,128,4096]{2,1,0:T(8,128)(2,1)}, bf16[1,128,4096]{2,1,0:T(8,128)(2,1)S(1)}, u32[]{:S(2)}, u32[]{:S(2)}) collective-permute-start(bf16[1,128,4096]{2,1,0:T(8,128)(2,1)} %collective-permute-done.21.refs_0_), channel_id=1, source_target_pairs={{0,1},{1,0},{2,3},{3,2},{4,5},{5,4},{6,7},{7,6}} | collective-permute-start | bytes 3145736 | tf_op jit(solution)/shard_map/ppermute | solution.py:364
  335.4 13.7 %collective-permute-start.24 = (bf16[1,128,4096]{2,1,0:T(8,128)(2,1)}, bf16[1,128,4096]{2,1,0:T(8,128)(2,1)}, u32[]{:S(2)}, u32[]{:S(2)}) collective-permute-start(bf16[1,128,4096]{2,1,0:T(8,128)(2,1)} %collective-permute-done.22.refs_1_), channel_id=1, source_target_pairs={{0,1},{1,0},{2,3},{3,2},{4,5},{5,4},{6,7},{7,6}} | collective-permute-start | bytes 3145736 | tf_op jit(solution)/shard_map/ppermute | solution.py:364
  335.9 2.2 copy-start.2
  338.1 2.2 copy-start.5

commit v2 on v1

--- a/solution.py
+++ b/solution.py
@@ -11,6 +11,8 @@
 HEAD_DIM = 128
 NEG_BIG = -1e30
 STAT_ROWS = 8
+NORM_ROWS = 32
+COL_TILE = 256
 MESH = pl.DeviceIdType.MESH
 
 
@@ -35,102 +37,144 @@
     return heads_f32 * cos_tab + swapped * sin_tab
 
 
-def kv_kernel(n_in, with_new, sc_ref, *refs):
-    x_refs = refs[:n_in]
-    cos_refs = refs[n_in:2 * n_in]
-    sin_refs = refs[2 * n_in:3 * n_in]
-    rest = refs[3 * n_in:]
-    wk_ref, wv_ref, gain_ref, q_ref = rest[:4]
-    rest = rest[4:]
+def kv_kernel(n_in, n_groups, with_new, sc_ref, *refs):
+    n_arr = n_in * n_groups
+    x_refs = refs[:n_arr]
+    cos_refs = refs[n_arr:n_arr + n_in]
+    sin_refs = refs[n_arr + n_in:n_arr + 2 * n_in]
+    wk_hbm, wv_hbm, gain_ref, q_ref = refs[n_arr + 2 * n_in:n_arr + 2 * n_in + 4]
+    rest = refs[n_arr + 2 * n_in + 4:]
     if with_new:
-        knew_ref, vnew_ref, _ = rest[:3]
-        rest = rest[3:]
-    else:
-        rest = rest[3:]
-    kc_ref, vc_ref, st_ref, n_buf, k_buf, v_buf, k_out, v_out, s_out, sems, new_sem = rest
+        new_refs = rest[:2]
+    (kc_ref, vc_ref, st_ref, wk, wv, n_buf, ss_buf, k_buf, v_buf, k_out, v_out, s_out, w_sem, sems, new_sem) = rest[3:]
     step = pl.program_id(0)
     n_steps = pl.num_programs(0)
     slot = lax.rem(step, 2)
+    per_group = n_steps // n_groups
     blk = x_refs[0].shape[1]
-    width = wk_ref.shape[1]
+    d_model = n_buf.shape[1]
+    width = wk.shape[1]
     heads = width // HEAD_DIM
+    n_tok = n_in * blk
+
+    def w_copy(c, which):
+        cols = pl.ds(pl.multiple_of(c * COL_TILE, COL_TILE), COL_TILE)
+        src, dst = ((wk_hbm, wk), (wv_hbm, wv))[which]
+        return pltpu.make_async_copy(src.at[:, cols], dst.at[:, cols], w_sem.at[c, which])
+
+    def place(i, at_step):
+        group = at_step // per_group
+        return sc_ref[group * n_in + i], sc_ref[n_arr + group * n_in + i] + lax.rem(at_step, per_group)
 
     def out_copies(which, at_step):
         copies = []
         for i in range(n_in):
-            shard = sc_ref[i]
-            bat = sc_ref[n_in + i] + at_step
+            shard, bat = place(i, at_step)
             rows = pl.ds(shard * blk, blk)
             copies.append(pltpu.make_async_copy(k_out.at[which, i], kc_ref.at[bat, rows], sems.at[which, i, 0]))
             copies.append(pltpu.make_async_copy(v_out.at[which, i], vc_ref.at[bat, rows], sems.at[which, i, 1]))
             copies.append(pltpu.make_async_copy(s_out.at[which, i], st_ref.at[shard, bat], sems.at[which, i, 2]))
         return copies
 
-    if with_new:
-        @pl.when(step == 0)
-        def _():
-            for idx, (src, dst) in enumerate(((knew_ref, kc_ref), (vnew_ref, vc_ref))):
-                for b in range(src.shape[0]):
-                    pltpu.make_async_copy(src.at[b], dst.at[b, pl.ds(dst.shape[1] - 1, 1)], new_sem.at[idx, b]).start()
+    def new_copies():
+        return [pltpu.make_async_copy(src.at[b], dst.at[b, pl.ds(dst.shape[1] - 1, 1)], new_sem.at[idx, b])
+                for idx, (src, dst) in enumerate(zip(new_refs, (kc_ref, vc_ref))) for b in range(src.shape[0])]
+
+    @pl.when(step == 0)
+    def _():
+        for c in range(width // COL_TILE):
+            for which in range(2):
+                w_copy(c, which).start()
+        if with_new:
+            for copy in new_copies():
+                copy.start()
 
     @pl.when(step >= 2)
     def _():
         for copy in out_copies(slot, step - 2):
             copy.wait()
 
-    gain = gain_ref[...]
-    for i in range(n_in):
-        def norm_rows(r, carry, i=i):
-            rows = pl.ds(pl.multiple_of(r * 16, 16), 16)
-            xf = x_refs[i][0, rows, :].astype(jnp.float32)
-            inv_rms = lax.rsqrt(jnp.mean(xf * xf, axis=-1, keepdims=True) + 1e-5)
-            n_buf[pl.ds(pl.multiple_of(i * blk + r * 16, 16), 16), :] = (xf * inv_rms * gain).astype(jnp.bfloat16)
-            return carry
-
-        lax.fori_loop(0, blk // 16, norm_rows, 0)
+    lanes = [slice(c * HEAD_DIM, (c + 1) * HEAD_DIM) for c in range(d_model // HEAD_DIM)]
+    for group in range(n_groups):
+        @pl.when(step // per_group == group)
+        def _(group=group):
+            for i in range(n_in):
+                x_ref = x_refs[group * n_in + i]
+
+                def square_rows(r, carry):
+                    rows = pl.ds(pl.multiple_of(r * NORM_ROWS, NORM_ROWS), NORM_ROWS)
+                    acc = [jnp.zeros((NORM_ROWS, HEAD_DIM), jnp.float32) for _ in range(2)]
+                    for c, lane in enumerate(lanes):
+                        xf = x_ref[0, rows, lane].astype(jnp.float32)
+                        acc[c % 2] += xf * xf
+                    ss_buf[pl.ds(pl.multiple_of(i * blk + r * NORM_ROWS, NORM_ROWS), NORM_ROWS), :] = acc[0] + acc[1]
+                    return carry
+
+                lax.fori_loop(0, blk // NORM_ROWS, square_rows, 0)
+            total = jnp.sum(ss_buf[...], axis=-1, keepdims=True)
+            ss_buf[...] = jnp.broadcast_to(lax.rsqrt(total / d_model + 1e-5), (n_tok, HEAD_DIM))
+            for i in range(n_in):
+                x_ref = x_refs[group * n_in + i]
+
+                def norm_rows(r, carry):
+                    rows = pl.ds(pl.multiple_of(r * NORM_ROWS, NORM_ROWS), NORM_ROWS)
+                    out_rows = pl.ds(pl.multiple_of(i * blk + r * NORM_ROWS, NORM_ROWS), NORM_ROWS)
+                    inv_rms = ss_buf[out_rows, :]
+                    for lane in lanes:
+                        xf = x_ref[0, rows, lane].astype(jnp.float32)
+                        n_buf[out_rows, lane] = (xf * inv_rms * gain_ref[:, lane]).astype(jnp.bfloat16)
+                    return carry
+
+                lax.fori_loop(0, blk // NORM_ROWS, norm_rows, 0)
 
     def col_tile(c, carry):
-        cols = pl.ds(pl.multiple_of(c * 256, 256), 256)
-        kf = jnp.dot(n_buf[...], wk_ref[:, cols], preferred_element_type=jnp.float32)
+        @pl.when(step == 0)
+        def _():
+            w_copy(c, 0).wait()
+            w_copy(c, 1).wait()
+
+        cols = pl.ds(pl.multiple_of(c * COL_TILE, COL_TILE), COL_TILE)
+        kf = jnp.dot(n_buf[...], wk[:, cols], preferred_element_type=jnp.float32)
+        vf = jnp.dot(n_buf[...], wv[:, cols], preferred_element_type=jnp.float32)
+        v_buf[:, cols] = vf.astype(jnp.bfloat16)
         parts = []
         for i in range(n_in):
             cos_tab = cos_refs[i][0]
             sin_tab = sin_refs[i][0]
             halves = []
-            for h in range(2):
+            for h in range(COL_TILE // HEAD_DIM):
                 kh = kf[i * blk:(i + 1) * blk, h * HEAD_DIM:(h + 1) * HEAD_DIM]
                 halves.append(kh * cos_tab + pltpu.roll(kh, HEAD_DIM // 2, 1) * sin_tab)
             parts.append(jnp.concatenate(halves, axis=1))
         k_buf[:, cols] = jnp.concatenate(parts, axis=0).astype(jnp.bfloat16)
-        vf = jnp.dot(n_buf[...], wv_ref[:, cols], preferred_element_type=jnp.float32)
-        v_buf[:, cols] = vf.astype(jnp.bfloat16)
         return carry
 
-    lax.fori_loop(0, width // 256, col_tile, 0)
+    lax.fori_loop(0, width // COL_TILE, col_tile, 0)
 
     head_of_row = lax.broadcasted_iota(jnp.int32, (STAT_ROWS, HEAD_DIM), 0) // (STAT_ROWS // heads)
+    probs = []
     for i in range(n_in):
-        shard = sc_ref[i]
-        bat = sc_ref[n_in + i] + step
-        seq_len = sc_ref[2 * n_in + bat]
-        k_blk = k_buf[i * blk:(i + 1) * blk, :]
-        v_blk = v_buf[i * blk:(i + 1) * blk, :]
-        k_out[slot, i] = k_blk.reshape(blk, heads, HEAD_DIM)
-        v_out[slot, i] = v_blk.reshape(blk, heads, HEAD_DIM)
-        scores = lax.dot_general(q_ref[bat], k_blk, (((1,), (1,)), ((), ())), preferred_element_type=jnp.float32) * (HEAD_DIM ** -0.5)
+        shard, bat = place(i, step)
+        scores = lax.dot_general(q_ref[bat], k_buf[i * blk:(i + 1) * blk, :], (((1,), (1,)), ((), ())),
+                                 preferred_element_type=jnp.float32) * (HEAD_DIM ** -0.5)
         pos = shard * blk + lax.broadcasted_iota(jnp.int32, scores.shape, 1)
-        visible = pos < seq_len
+        visible = pos < sc_ref[2 * n_arr + bat]
         scores = jnp.where(visible, scores, NEG_BIG)
         blk_max = jnp.max(scores, axis=-1, keepdims=True)
         prob = jnp.where(visible, jnp.exp(scores - blk_max), 0.0)
-        blk_sum = jnp.sum(prob, axis=-1, keepdims=True)
-        full = jnp.dot(prob.astype(jnp.bfloat16), v_blk, preferred_element_type=jnp.float32)
+        probs.append((blk_max, prob))
+    stats = []
+    for i, (blk_max, prob) in enumerate(probs):
+        full = jnp.dot(prob.astype(jnp.bfloat16), v_buf[i * blk:(i + 1) * blk, :], preferred_element_type=jnp.float32)
         acc = jnp.zeros((STAT_ROWS, HEAD_DIM), jnp.float32)
         for h in range(heads):
             acc = jnp.where(head_of_row == h, full[:, h * HEAD_DIM:(h + 1) * HEAD_DIM], acc)
-        s_out[slot, i, 0] = acc
-        s_out[slot, i, 1] = jnp.broadcast_to(blk_max, (STAT_ROWS, HEAD_DIM))
-        s_out[slot, i, 2] = jnp.broadcast_to(blk_sum, (STAT_ROWS, HEAD_DIM))
+        stats.append((acc, blk_max, jnp.sum(prob, axis=-1, keepdims=True)))
+    for i in range(n_in):
+        k_out[slot, i] = k_buf[i * blk:(i + 1) * blk, :].reshape(blk, heads, HEAD_DIM)
+        v_out[slot, i] = v_buf[i * blk:(i + 1) * blk, :].reshape(blk, heads, HEAD_DIM)
+        for k, stat in enumerate(stats[i]):
+            s_out[slot, i, k] = jnp.broadcast_to(stat, (STAT_ROWS, HEAD_DIM))
 
     for copy in out_copies(slot, step):
         copy.start()
@@ -140,9 +184,8 @@
         for copy in out_copies(slot, step):
             copy.wait()
         if with_new:
-            for idx, (src, dst) in enumerate(((knew_ref, kc_ref), (vnew_ref, vc_ref))):
-                for b in range(src.shape[0]):
-                    pltpu.make_async_copy(src.at[b], dst.at[b, pl.ds(dst.shape[1] - 1, 1)], new_sem.at[idx, b]).wait()
+            for copy in new_copies():
+                copy.wait()
 
     @pl.when((step == n_steps - 1) & (n_steps >= 2))
     def _():
@@ -150,31 +193,35 @@
             copy.wait()
 
 
-def kv_call(inputs, shards, batches, lengths, tabs, w_k, w_v, gain, q_diag, caches, new_rows=None):
-    n_in = len(inputs)
-    n_steps = inputs[0][2]
+def kv_call(groups, per_group, shards, batches, lengths, tabs, w_k, w_v, gain, q_diag, caches, new_rows=None):
+    n_groups = len(groups)
+    n_in = len(groups[0])
+    n_steps = n_groups * per_group
     cos_tab, sin_tab = tabs
-    blk, d_model = inputs[0][0].shape[1:]
+    blk, d_model = groups[0][0][0].shape[1:]
     width = w_k.shape[1]
     heads = width // HEAD_DIM
-    scalars = jnp.concatenate([jnp.stack([jnp.int32(s) for s in shards]), jnp.array(batches, jnp.int32), lengths])
+    scalars = jnp.concatenate([jnp.stack([jnp.int32(s) for group in shards for s in group]),
+                               jnp.array([b for group in batches for b in group], jnp.int32), lengths])
     in_specs = []
     operands = []
-    for arr, first, _ in inputs:
-        in_specs.append(pl.BlockSpec((1, blk, d_model), lambda g, sc, first=first: (first + g, 0, 0)))
-        operands.append(arr)
+    for p, group in enumerate(groups):
+        for arr, first in group:
+            in_specs.append(pl.BlockSpec((1, blk, d_model), lambda g, sc, p=p, first=first: (
+                first + jnp.clip(g - p * per_group, 0, per_group - 1), 0, 0)))
+            operands.append(arr)
     for tab in (cos_tab, sin_tab):
         for i in range(n_in):
-            in_specs.append(pl.BlockSpec((1, blk, HEAD_DIM), lambda g, sc, i=i: (sc[i], 0, 0)))
+            in_specs.append(pl.BlockSpec((1, blk, HEAD_DIM), lambda g, sc, i=i: (sc[g // per_group * n_in + i], 0, 0)))
             operands.append(tab)
-    once = pl.Buffered(1)
+    hbm_spec = pl.BlockSpec(memory_space=pltpu.HBM)
     in_specs += [
-        pl.BlockSpec((d_model, width), lambda g, sc: (0, 0), pipeline_mode=once),
-        pl.BlockSpec((d_model, width), lambda g, sc: (0, 0), pipeline_mode=once),
+        hbm_spec,
+        hbm_spec,
         pl.BlockSpec((1, d_model), lambda g, sc: (0, 0)),
         pl.BlockSpec(q_diag.shape, lambda g, sc: (0, 0, 0)),
     ]
-    operands += [w_k, w_v, gain, q_diag]
+    operands += [pltpu.with_memory_space_constraint(w, pltpu.HBM) for w in (w_k, w_v)] + [gain, q_diag]
     any_spec = pl.BlockSpec(memory_space=pl.ANY)
     with_new = new_rows is not None
     if with_new:
@@ -189,19 +236,23 @@
     tokens = n_in * blk
     flops = 2 * n_steps * tokens * d_model * 2 * width
     return pl.pallas_call(
-        functools.partial(kv_kernel, n_in, with_new),
+        functools.partial(kv_kernel, n_in, n_groups, with_new),
         grid_spec=pltpu.PrefetchScalarGridSpec(
             num_scalar_prefetch=1,
             grid=(n_steps,),
             in_specs=in_specs,
             out_specs=[any_spec] * 3,
             scratch_shapes=[
+                pltpu.VMEM((d_model, width), jnp.bfloat16),
+                pltpu.VMEM((d_model, width), jnp.bfloat16),
                 pltpu.VMEM((tokens, d_model), jnp.bfloat16),
+                pltpu.VMEM((tokens, HEAD_DIM), jnp.float32),
                 pltpu.VMEM((tokens, width), jnp.bfloat16),
                 pltpu.VMEM((tokens, width), jnp.bfloat16),
                 pltpu.VMEM((2, n_in, blk, heads, HEAD_DIM), jnp.bfloat16),
                 pltpu.VMEM((2, n_in, blk, heads, HEAD_DIM), jnp.bfloat16),
                 pltpu.VMEM((2, n_in, 3, STAT_ROWS, HEAD_DIM), jnp.float32),
+                pltpu.SemaphoreType.DMA((width // COL_TILE, 2)),
                 pltpu.SemaphoreType.DMA((2, n_in, 3)),
                 pltpu.SemaphoreType.DMA((2, cache_shape[0])),
             ],
@@ -212,14 +263,14 @@
             jax.ShapeDtypeStruct(caches[2].shape, jnp.float32),
         ],
         input_output_aliases=aliases,
-        compiler_params=pltpu.CompilerParams(vmem_limit_bytes=28 * 2 ** 20),
+        compiler_params=pltpu.CompilerParams(vmem_limit_bytes=30 * 2 ** 20),
         cost_estimate=pl.CostEstimate(flops=flops, bytes_accessed=2 * 2 * d_model * width + 2 * n_steps * tokens * (d_model + 2 * width), transcendentals=0),
         name="kv_chunk",
     )(scalars, *operands)
 
 
 def tail_kernel(n_dev, n_part, st_ref, xs_ref, gain_ref, wo_hbm, wg_hbm, wu_hbm, wd_hbm, dec_ref, last_ref,
-                wo, wg, wu, wd, stv, rows, a_buf, n_buf, ps1, pr1, ps2, pr2, xo1, xg1, xo2, xg2,
+                wo, wg, wu, wd, stv, rows, a_buf, n_buf, mid_buf, ps1, pr1, ps2, pr2, xo1, xg1, xo2, xg2,
                 w_sem, send_sem, recv_sem):
     me = lax.axis_index("model")
     n_batch = dec_ref.shape[0]
@@ -229,13 +280,12 @@
     heads = STAT_ROWS // 2
     loads = [pltpu.make_async_copy(src, dst, w_sem.at[i]) for i, (src, dst) in enumerate(
         ((st_ref, stv), (wo_hbm, wo), (wg_hbm, wg), (wu_hbm, wu), (wd_hbm, wd)))]
-    for load in loads:
-        load.start()
+    loads[0].start()
+    loads[1].start()
     barrier = pltpu.get_barrier_semaphore()
     for k in range(1, n_dev):
         peer = lax.rem(me + k, n_dev)
         pl.semaphore_signal(barrier, inc=1, device_id={"model": peer}, device_id_type=MESH)
-    pl.semaphore_wait(barrier, n_dev - 1)
 
     def send(phase, k, src, dst):
         peer = lax.rem(me + k, n_dev)
@@ -244,6 +294,8 @@
             device_id={"model": peer}, device_id_type=MESH)
 
     loads[0].wait()
+    for load in loads[2:]:
+        load.start()
     for b in range(n_batch):
         top = stv[0, b, 1]
         for j in range(1, n_part):
@@ -285,6 +337,7 @@
         return pl.ds(pl.multiple_of(p * cols, cols), cols)
 
     loads[1].wait()
+    pl.semaphore_wait(barrier, n_dev - 1)
     sent = all_reduce(0, lambda p: jnp.dot(att, wo[:, col_block(p)], preferred_element_type=jnp.float32),
                       xs_ref[...].astype(jnp.float32), ps1, pr1, xo1, xg1)
     sq = jnp.zeros((n_rows, 1), jnp.float32)
@@ -296,12 +349,20 @@
         xf = xg1[j].astype(jnp.float32)
         n_buf[:, j * cols:(j + 1) * cols] = (xf * inv_rms * gain_ref[:, j * cols:(j + 1) * cols]).astype(jnp.bfloat16)
     loads[2].wait()
+    loads[3].wait()
     nt = (((1,), (1,)), ((), ()))
-    gate = lax.dot_general(wg[...], n_buf[...], nt, preferred_element_type=jnp.float32)
-    loads[3].wait()
-    up = lax.dot_general(wu[...], n_buf[...], nt, preferred_element_type=jnp.float32)
-    mid_t = gate * (1.0 / (1.0 + jnp.exp(-gate))) * up
-    mid = mid_t.T.astype(jnp.bfloat16)
+    n_hid = wg.shape[0]
+    rows_per = n_hid // 2
+
+    def hidden_rows(r, carry):
+        at = pl.ds(pl.multiple_of(r * rows_per, 8), rows_per)
+        gate = lax.dot_general(wg[at, :], n_buf[...], nt, preferred_element_type=jnp.float32)
+        up = lax.dot_general(wu[at, :], n_buf[...], nt, preferred_element_type=jnp.float32)
+        mid_buf[at, :] = gate * (1.0 / (1.0 + jnp.exp(-gate))) * up
+        return carry
+
+    lax.fori_loop(0, 2, hidden_rows, 0)
+    mid = mid_buf[...].T.astype(jnp.bfloat16)
     loads[4].wait()
     sent += all_reduce(2, lambda p: jnp.dot(mid, wd[:, col_block(p)], preferred_element_type=jnp.float32),
                        xo1[...].astype(jnp.float32), ps2, pr2, xo2, xg2)
@@ -317,11 +378,11 @@
     d_model = w_o.shape[1]
     n_part = stats.shape[0]
     vmem = pl.BlockSpec(memory_space=pltpu.VMEM)
-    hbm = pl.BlockSpec(memory_space=pl.ANY)
+    hbm = pl.BlockSpec(memory_space=pltpu.HBM)
     return pl.pallas_call(
         functools.partial(tail_kernel, n_dev, n_part),
         out_shape=[jax.ShapeDtypeStruct((n_batch, d_model), jnp.bfloat16)] * 2,
-        in_specs=[hbm, vmem, vmem, hbm, hbm, hbm, hbm],
+        in_specs=[pl.BlockSpec(memory_space=pl.ANY), vmem, vmem, hbm, hbm, hbm, hbm],
         out_specs=[vmem, vmem],
         scratch_shapes=[
             pltpu.VMEM(w_o.shape, jnp.bfloat16),
@@ -332,6 +393,7 @@
             pltpu.VMEM((STAT_ROWS, n_batch, HEAD_DIM), jnp.float32),
             pltpu.VMEM((n_rows, w_o.shape[0]), jnp.float32),
             pltpu.VMEM((n_rows, d_model), jnp.bfloat16),
+            pltpu.VMEM((w_gate_t.shape[0], n_rows), jnp.float32),
             pltpu.VMEM((n_dev - 1, n_rows, cols), jnp.float32),
             pltpu.VMEM((n_dev - 1, n_rows, cols), jnp.float32),
             pltpu.VMEM((n_dev - 1, n_rows, cols), jnp.float32),
@@ -346,7 +408,7 @@
         ],
         compiler_params=pltpu.CompilerParams(collective_id=0, has_side_effects=True, vmem_limit_bytes=52 * 2 ** 20),
         name="tail",
-    )(stats, x_mine, gain, w_o, w_gate_t, w_up_t, w_down)
+    )(stats, x_mine, gain, *(pltpu.with_memory_space_constraint(w, pltpu.HBM) for w in (w_o, w_gate_t, w_up_t, w_down)))
 
 
 def solution(mesh):
@@ -372,21 +434,25 @@
         half = n_batch // 2
         wq, wk, wv = w_q[0], w_k[0], w_v[0]
 
-        y_parts = [(0, 1), (1, half), (half, n_batch)]
-        x_parts = [(half, half + 1), (half + 1, n_batch), (0, half)]
+        q1, q2 = n_batch // 8, n_batch // 4
+        y_parts = [(0, q1), (q1, q2), (q2, half), (half, n_batch)]
+        x_parts = [(half, half + q1), (half + q1, half + q2), (half + q2, n_batch), (0, half)]
+        from_y, from_x = {}, {}
+
+        def send_part(step, source):
+            y_part, x_part = y_parts[step], x_parts[step]
+            from_y[y_part] = swap(source[y_part[0]:y_part[1]], 4)
+            from_x[x_part] = swap(source[x_part[0]:x_part[1]], 2)
+
+        send_part(0, prompt)
         seq_pos = my_idx * blk + jnp.arange(blk)
         sel = (seq_pos[None, :] == (lengths - 1)[:, None]).astype(jnp.bfloat16)
-        from_y, from_x = {}, {}
-        from_y[y_parts[0]] = swap(prompt[0:1], 4)
-        from_x[x_parts[0]] = swap(prompt[half:half + 1], 2)
         last_x = jnp.einsum('bs,bsd->bd', sel, prompt, preferred_element_type=jnp.float32).astype(jnp.bfloat16)
         last_x = last_x + swap(last_x, 1)
-        rest, last_x = lax.optimization_barrier((prompt, last_x))
         last_x = (last_x + swap(last_x, 2)) + (swap(last_x, 4) + swap(last_x, 6))
-        for y_part, x_part in zip(y_parts[1:], x_parts[1:]):
-            from_y[y_part] = swap(rest[y_part[0]:y_part[1]], 4)
-            from_x[x_part] = swap(rest[x_part[0]:x_part[1]], 2)
-        core_all = swap(rest, 1)
+        for step in range(1, len(y_parts)):
+            send_part(step, prompt)
+        core_all = swap(prompt, 1)
         x_rows = jnp.concatenate([new_tok, last_x], axis=0)
         n_rows = rms_norm(x_rows, norm_attn[0])
         row_cos, row_sin = rotary_tables(jnp.stack([lengths, lengths - 1]))
@@ -412,8 +478,8 @@
         cache_shape = jax.ShapeDtypeStruct((n_batch, seq_len + 1, heads, HEAD_DIM), jnp.bfloat16)
         caches = (cache_shape, cache_shape, stats)
 
-        def run(streams, shards, batches, caches, new_rows=None):
-            return kv_call(streams, shards, batches, lengths, tabs, wk, wv, gain, q_diag, caches, new_rows)
+        def run(groups, per_group, shards, batches, caches, new_rows=None):
+            return kv_call(groups, per_group, shards, batches, lengths, tabs, wk, wv, gain, q_diag, caches, new_rows)
 
         def shard_of(bits):
             idx = my_idx
@@ -426,29 +492,23 @@
             out = lax.optimization_barrier((caches[2], *arrays))
             return (caches[0], caches[1], out[0]), out[1:]
 
-        s_own, s_core = my_idx, shard_of(1)
-        caches = run([(prompt, 0, half), (prompt, half, half)], [s_own] * 2, [0, half], caches,
-                     (k_new[:, None], v_new[:, None]))
-        caches, (core_all,) = after(caches, core_all)
-        caches = run([(core_all, 0, half), (core_all, half, half)], [s_core] * 2, [0, half], caches)
+        caches = run([[(arr, 0), (arr, half)] for arr in (prompt, core_all)], half,
+                     [[my_idx] * 2, [shard_of(1)] * 2], [[0, half]] * 2, caches, (k_new[:, None], v_new[:, None]))
         diag = {}
+        n_fwd = len(y_parts) - 1
         for step, (y_part, x_part) in enumerate(zip(y_parts, x_parts)):
-            n = y_part[1] - y_part[0]
             caches, (got_y, got_x) = after(caches, from_y[y_part], from_x[x_part])
             other_y, other_x = swap(got_y, 1), swap(got_x, 1)
-            if step < 2:
+            if step < n_fwd:
                 diag[step] = (swap(got_y, 2), swap(got_x, 4))
-            caches = run([(got_y, 0, n), (got_x, 0, n)], [shard_of(4), shard_of(2)], [y_part[0], x_part[0]], caches)
-            caches, (other_y, other_x) = after(caches, other_y, other_x)
-            caches = run([(other_y, 0, n), (other_x, 0, n)], [shard_of(5), shard_of(3)], [y_part[0], x_part[0]], caches)
-        for step in (1, 0):
+            caches = run([[(got_y, 0), (got_x, 0)], [(other_y, 0), (other_x, 0)]], y_part[1] - y_part[0],
+                         [[shard_of(4), shard_of(2)], [shard_of(5), shard_of(3)]], [[y_part[0], x_part[0]]] * 2, caches)
+        for step in reversed(range(n_fwd)):
             y_part, x_part = y_parts[step], x_parts[step]
-            n = y_part[1] - y_part[0]
             caches, (via_x, via_y) = after(caches, *diag[step])
             other_x, other_y = swap(via_x, 1), swap(via_y, 1)
-            caches = run([(via_x, 0, n), (via_y, 0, n)], [shard_of(6)] * 2, [y_part[0], x_part[0]], caches)
-            caches, (other_x, other_y) = after(caches, other_x, other_y)
-            caches = run([(other_x, 0, n), (other_y, 0, n)], [shard_of(7)] * 2, [y_part[0], x_part[0]], caches)
+            caches = run([[(via_x, 0), (via_y, 0)], [(other_x, 0), (other_y, 0)]], y_part[1] - y_part[0],
+                         [[shard_of(6)] * 2, [shard_of(7)] * 2], [[y_part[0], x_part[0]]] * 2, caches)
 
         k_cache, v_cache, stats = caches
         x_mine = lax.dynamic_slice_in_dim(x_rows, my_idx * (d_model // n_dev), d_model // n_dev, axis=1)

time: 392 us -> 392 us (level)
  waiting for transfers between devices: 68.6 us -> 117 us
  Pallas kernels: 245 us -> 204 us
  local copies, waits for them, and re-layouts: 40.2 us -> 30.6 us
    ppermute x25 -> x33, waiting for transfers between devices: 68.6 us -> 117 us  [swap(): return lax.ppermute(arr, 'model', [(i, i ^ bit) for i in range(n_dev)])]
    pallas_call x12 -> x8, Pallas kernels: 212 us -> 177 us  [kv_call(): pl.pallas_call(functools.partial(kv_kernel, n_in, n_groups, with_new), gr...]
    pallas_call x1, Pallas kernels: 32.6 us -> 26.6 us  [tail_call(): pl.pallas_call(functools.partial(tail_kernel, n_dev, n_part), out_shape=[...]
    unnamed x39 -> x37, local copies, waits for them, and re-layouts: 13.5 us -> 7.84 us
    slice x3, local copies, waits for them, and re-layouts: 13.2 us -> 8.52 us  [send_part(): from_x[x_part] = swap(source[x_part[0]:x_part[1]], 2)]
    ppermute x25 -> x33, starting transfers between devices: 20.5 us -> 23.3 us  [swap(): return lax.ppermute(arr, 'model', [(i, i ^ bit) for i in range(n_dev)])]
  transfers between devices with their start and end apart: 25 -> 33, of which waited for: 5 -> 18; matrix products, arithmetic and copies ran while one was open for 10% -> 10% of each run, Pallas kernels for 52% -> 42%
where the time goes in v2:
time: 392 us
  Pallas kernels  204 us (52%)
  waiting for transfers between devices  117 us (30%)
  local copies, waits for them, and re-layouts  30.6 us (8%)
  starting transfers between devices  23.3 us (6%)
  matrix products  12.1 us (3%)
  other arithmetic  4.05 us (1%)
    pallas_call x8, Pallas kernels, kv_call(): pl.pallas_call(functools.partial(kv_kernel, n_in, n_groups, with_new), gr...  177 us
    ppermute x33, waiting for transfers between devices, swap(): return lax.ppermute(arr, 'model', [(i, i ^ bit) for i in range(n_dev)])  117 us
    pallas_call x1, Pallas kernels, tail_call(): pl.pallas_call(functools.partial(tail_kernel, n_dev, n_part), out_shape=[...  26.6 us
    ppermute x33, starting transfers between devices, swap(): return lax.ppermute(arr, 'model', [(i, i ^ bit) for i in range(n_dev)])  23.3 us
    slice x3, local copies, waits for them, and re-layouts, send_part(): from_x[x_part] = swap(source[x_part[0]:x_part[1]], 2)  8.52 us
  transfers between devices with their start and end apart: 33, of which 18 were waited for; matrix products, arithmetic and copies ran while one was open for 10% of the time, Pallas kernels for 42%

profile of v2, /device:TPU:0, one launch (start us, length us, event | category | flops | bytes accessed | tf_op | source)
XLA Modules:
  0.0 391.5 jit_solution(10853159685081762623)
XLA Ops:
  0.6 0.9 collective-permute-start
  2.2 4.7 %fusion.16 = bf16[8,1,4096]{2,1,0:T(2,128)(2,1)S(1)} fusion(bf16[8,128,4096]{2,1,0:T(8,128)(2,1)} %refs_1_.1, pred[8,128,1]{1,0,2:T(8,128)(4,1)S(1)} %compare_bitcast_fusion), kind=kOutput, calls=%fused_computation.35 | convolution fusion | flops 8388608 | bytes 8455168 | tf_op jit(solution)/shard_map/bs,bsd->bd/dot_general | solution.py:450
  7.1 0.9 copy-done
  8.0 2.2 fusion.29
  10.2 2.5 collective-permute-start.10
  13.0 6.3 %copy.83 = bf16[512,4096]{1,0:T(8,128)(2,1)} copy(bf16[512,4096]{0,1:T(8,128)(2,1)} %bitcast.111) | data formatting | bytes 8388608 | tf_op jit(solution)/shard_map/dot_general | solution.py:459
  19.4 6.3 %copy.84 = bf16[512,4096]{1,0:T(8,128)(2,1)} copy(bf16[512,4096]{0,1:T(8,128)(2,1)} %bitcast.88) | data formatting | bytes 8388608 | tf_op jit(solution)/shard_map/dot_general | solution.py:461
  25.8 1.9 fusion.3
  28.4 1.5 collective-permute-start.4
  29.9 1.9 collective-permute-start.2
  32.0 7.9 %collective-permute-done.4 = bf16[8,4096]{1,0:T(8,128)(2,1)S(1)} collective-permute-done((bf16[8,4096]{1,0:T(8,128)(2,1)S(1)}, bf16[8,4096]{1,0:T(8,128)(2,1)S(1)}, u32[]{:S(2)}, u32[]{:S(2)}) %collective-permute-start.4) | collective-permute-done | bytes 65568 | tf_op jit(solution)/shard_map/ppermute | solution.py:426
  39.8 2.0 collective-permute-start.6
  41.8 1.5 collective-permute-start.5
  44.3 3.4 fusion.4
  48.0 3.4 fusion.6
  52.1 3.4 copy-done.1
  55.5 39.3 %kv_chunk.8 = (bf16[8,1025,4,128]{3,2,1,0:T(4,128)(2,1)}, bf16[8,1025,4,128]{3,2,1,0:T(4,128)(2,1)}, f32[9,8,3,8,128]{4,3,2,1,0:T(8,128)S(1)}) custom-call(s32[16]{0:T(128)S(1)} %concatenate.60.sc_ref, bf16[8,128,4096]{2,1,0:T(8,128)(2,1)S(1)} %copy-done.1, bf16[8,128,4096]{2,1,0:T(8,128)(2,1)S(1)} %copy-done.1, ...), custom_call_target="tpu_custom_call", output_to_operand_aliasing={{2}: (15, {})} | custom-call | flops 17179869184 | bytes 29360128 | tf_op jit(solution)/shard_map/kv_chunk/pallas_call | solution.py:238
  95.3 2.5 fusion.28
  98.5 0.9 collective-permute-done.8.refs_3_
  99.3 14.3 %kv_chunk.9 = (bf16[8,1025,4,128]{3,2,1,0:T(4,128)(2,1)}, bf16[8,1025,4,128]{3,2,1,0:T(4,128)(2,1)}, f32[9,8,3,8,128]{4,3,2,1,0:T(8,128)S(1)}) custom-call(s32[16]{0:T(128)S(1)} %concatenate.59.sc_ref, bf16[1,128,4096]{2,1,0:T(8,128)(2,1)} %collective-permute-done.5.refs_0_, ...), custom_call_target="tpu_custom_call", output_to_operand_aliasing={{0}: (13, {}), {1}: (14, {}), {2}: (15, {})} | custom-call | flops 4294967296 | bytes 13631488 | tf_op jit(solution)/shard_map/kv_chunk/pallas_call | solution.py:238
  114.2 3.8 fusion.27
  118.1 1.1 collective-permute-start.18
  119.2 1.0 copy-done.2
  120.2 1.5 collective-permute-start.17
  121.8 1.2 copy-done.3
  123.0 12.9 %kv_chunk.10 = (bf16[8,1025,4,128]{3,2,1,0:T(4,128)(2,1)}, bf16[8,1025,4,128]{3,2,1,0:T(4,128)(2,1)}, f32[9,8,3,8,128]{4,3,2,1,0:T(8,128)S(1)}) custom-call(s32[16]{0:T(128)S(1)} %concatenate.58.sc_ref, bf16[1,128,4096]{2,1,0:T(8,128)(2,1)} %collective-permute-done.9.refs_0_, ...), custom_call_target="tpu_custom_call", output_to_operand_aliasing={{0}: (13, {}), {1}: (14, {}), {2}: (15, {})} | custom-call | flops 4294967296 | bytes 13631488 | tf_op jit(solution)/shard_map/kv_chunk/pallas_call | solution.py:238
  135.9 10.7 %collective-permute-done.14.refs_1_ = bf16[2,128,4096]{2,1,0:T(8,128)(2,1)} collective-permute-done((bf16[2,128,4096]{2,1,0:T(8,128)(2,1)}, bf16[2,128,4096]{2,1,0:T(8,128)(2,1)}, u32[]{:S(2)}, u32[]{:S(2)}) %collective-permute-start.14) | collective-permute-done | bytes 2097184 | tf_op jit(solution)/shard_map/ppermute | solution.py:426
  147.9 3.9 collective-permute-done.15.refs_2_
  151.8 3.0 collective-permute-done.16.refs_3_
  154.8 22.2 %kv_chunk.11 = (bf16[8,1025,4,128]{3,2,1,0:T(4,128)(2,1)}, bf16[8,1025,4,128]{3,2,1,0:T(4,128)(2,1)}, f32[9,8,3,8,128]{4,3,2,1,0:T(8,128)S(1)}) custom-call(s32[16]{0:T(128)S(1)} %concatenate.57.sc_ref, bf16[2,128,4096]{2,1,0:T(8,128)(2,1)} %collective-permute-done.13.refs_0_, ...), custom_call_target="tpu_custom_call", output_to_operand_aliasing={{0}: (13, {}), {1}: (14, {}), {2}: (15, {})} | custom-call | flops 8589934592 | bytes 18874368 | tf_op jit(solution)/shard_map/kv_chunk/pallas_call | solution.py:238
  177.0 58.6 %collective-permute-done.18.refs_1_ = bf16[4,128,4096]{2,1,0:T(8,128)(2,1)} collective-permute-done((bf16[4,128,4096]{2,1,0:T(8,128)(2,1)}, bf16[4,128,4096]{2,1,0:T(8,128)(2,1)}, u32[]{:S(2)}, u32[]{:S(2)}) %collective-permute-start.18) | collective-permute-done | bytes 4194336 | tf_op jit(solution)/shard_map/ppermute | solution.py:426
  236.5 1.5 collective-permute-start.21
  238.5 4.9 %collective-permute-done.19.refs_2_ = bf16[4,128,4096]{2,1,0:T(8,128)(2,1)} collective-permute-done((bf16[4,128,4096]{2,1,0:T(8,128)(2,1)}, bf16[4,128,4096]{2,1,0:T(8,128)(2,1)}, u32[]{:S(2)}, u32[]{:S(2)}) %collective-permute-start.19) | collective-permute-done | bytes 4194336 | tf_op jit(solution)/shard_map/ppermute | solution.py:426
  243.5 6.0 %collective-permute-done.20.refs_3_ = bf16[4,128,4096]{2,1,0:T(8,128)(2,1)} collective-permute-done((bf16[4,128,4096]{2,1,0:T(8,128)(2,1)}, bf16[4,128,4096]{2,1,0:T(8,128)(2,1)}, u32[]{:S(2)}, u32[]{:S(2)}) %collective-permute-start.20) | collective-permute-done | bytes 4194336 | tf_op jit(solution)/shard_map/ppermute | solution.py:426
  249.5 39.6 %kv_chunk.12 = (bf16[8,1025,4,128]{3,2,1,0:T(4,128)(2,1)}, bf16[8,1025,4,128]{3,2,1,0:T(4,128)(2,1)}, f32[9,8,3,8,128]{4,3,2,1,0:T(8,128)S(1)}) custom-call(s32[16]{0:T(128)S(1)} %concatenate.56.sc_ref, bf16[4,128,4096]{2,1,0:T(8,128)(2,1)} %collective-permute-done.17.refs_0_, ...), custom_call_target="tpu_custom_call", output_to_operand_aliasing={{0}: (13, {}), {1}: (14, {}), {2}: (15, {})} | custom-call | flops 17179869184 | bytes 29360128 | tf_op jit(solution)/shard_map/kv_chunk/pallas_call | solution.py:238
  289.6 1.5 collective-permute-start.25
  291.7 1.9 collective-permute-done.23.refs_2_
  293.6 3.0 collective-permute-done.24.refs_3_
  296.6 22.2 %kv_chunk.13 = (bf16[8,1025,4,128]{3,2,1,0:T(4,128)(2,1)}, bf16[8,1025,4,128]{3,2,1,0:T(4,128)(2,1)}, f32[9,8,3,8,128]{4,3,2,1,0:T(8,128)S(1)}) custom-call(s32[16]{0:T(128)S(1)} %concatenate.55.sc_ref, bf16[2,128,4096]{2,1,0:T(8,128)(2,1)} %collective-permute-done.21.refs_0_, ...), custom_call_target="tpu_custom_call", output_to_operand_aliasing={{0}: (13, {}), {1}: (14, {}), {2}: (15, {})} | custom-call | flops 8589934592 | bytes 18874368 | tf_op jit(solution)/shard_map/kv_chunk/pallas_call | solution.py:238
  319.4 1.5 collective-permute-start.29
  321.9 1.5 collective-permute-done.28.refs_3_
  323.4 13.4 %kv_chunk.14 = (bf16[8,1025,4,128]{3,2,1,0:T(4,128)(2,1)}, bf16[8,1025,4,128]{3,2,1,0:T(4,128)(2,1)}, f32[9,8,3,8,128]{4,3,2,1,0:T(8,128)S(1)}) custom-call(s32[16]{0:T(128)S(1)} %concatenate.54.sc_ref, bf16[1,128,4096]{2,1,0:T(8,128)(2,1)} %collective-permute-done.25.refs_0_, ...), custom_call_target="tpu_custom_call", output_to_operand_aliasing={{0}: (13, {}), {1}: (14, {}), {2}: (15, {})} | custom-call | flops 4294967296 | bytes 13631488 | tf_op jit(solution)/shard_map/kv_chunk/pallas_call | solution.py:238
  336.7 8.1 %collective-permute-done.29.refs_0_ = bf16[1,128,4096]{2,1,0:T(8,128)(2,1)S(1)} collective-permute-done((bf16[1,128,4096]{2,1,0:T(8,128)(2,1)}, bf16[1,128,4096]{2,1,0:T(8,128)(2,1)S(1)}, u32[]{:S(2)}, u32[]{:S(2)}) %collective-permute-start.29) | collective-permute-done | bytes 1048608 | tf_op jit(solution)/shard_map/ppermute | solution.py:426
  344.8 1.3 collective-permute-done.30.refs_1_
  346.8 2.2 collective-permute-done.31.refs_2_
  348.9 1.5 collective-permute-done.32.refs_3_
  350.4 13.2 %kv_chunk.15 = (bf16[8,1025,4,128]{3,2,1,0:T(4,128)(2,1)}, bf16[8,1025,4,128]{3,2,1,0:T(4,128)(2,1)}, f32[9,8,3,8,128]{4,3,2,1,0:T(8,128)S(1)}) custom-call(s32[16]{0:T(128)S(1)} %concatenate.53.sc_ref, bf16[1,128,4096]{2,1,0:T(8,128)(2,1)S(1)} %collective-permute-done.29.refs_0_, ...), custom_call_target="tpu_custom_call", output_to_operand_aliasing={{0}: (13, {}), {1}: (14, {}), {2}: (15, {})} | custom-call | flops 4294967296 | bytes 13631488 | tf_op jit(solution)/shard_map/kv_chunk/pallas_call | solution.py:238
  363.7 26.6 %tail.1 = (bf16[8,4096]{1,0:T(8,128)(2,1)S(1)}, bf16[8,4096]{1,0:T(8,128)(2,1)S(1)}) custom-call(f32[9,8,3,8,128]{4,3,2,1,0:T(8,128)S(1)} %get-tuple-element.105.st_ref, bf16[16,512]{1,0:T(8,128)(2,1)S(1)} %fusion.12.xs_ref, f32[1,4096]{1,0:T(1,128)S(1)} %convert_element_type.115.gain_ref, bf16[512,4096]{1,0:T(8,128)(2,1)} %bitcast.110, ...), custom_call_target="tpu_custom_call" | custom-call | tf_op jit(solution)/shard_map/tail/pallas_call | solution.py:382
  (129 shorter events, 13.0 us)
Async XLA Ops:
  0.6 51.5 %collective-permute-start = (bf16[8,128,4096]{2,1,0:T(8,128)(2,1)}, bf16[8,128,4096]{2,1,0:T(8,128)(2,1)}, u32[]{:S(2)}, u32[]{:S(2)}) collective-permute-start(bf16[8,128,4096]{2,1,0:T(8,128)(2,1)} %refs_1_.1), channel_id=1, source_target_pairs={{0,1},{1,0},{2,3},{3,2},{4,5},{5,4},{6,7},{7,6}} | collective-permute-start | bytes 25165832 | tf_op jit(solution)/shard_map/ppermute | solution.py:426
  2.2 5.8 %copy-start = (bf16[8,128,4096]{2,1,0:T(8,128)(2,1)S(1)}, bf16[8,128,4096]{2,1,0:T(8,128)(2,1)}, u32[]{:S(2)}) copy-start(bf16[8,128,4096]{2,1,0:T(8,128)(2,1)} %refs_1_.1) | copy-start | bytes 25165828
  7.0 6.0 %copy-start.7 = (bf16[1,4096]{1,0:T(2,128)(2,1)S(1)}, bf16[1,4096]{1,0:T(2,128)(2,1)}, u32[]{:S(2)}) copy-start(bf16[1,4096]{1,0:T(2,128)(2,1)} %param.25) | copy-start | bytes 24580
  7.0 21.2 %collective-permute-start.1 = (bf16[8,4096]{1,0:T(8,128)(2,1)S(1)}, bf16[8,4096]{1,0:T(8,128)(2,1)S(1)}, u32[]{:S(2)}, u32[]{:S(2)}) collective-permute-start(bf16[8,4096]{1,0:T(8,128)(2,1)S(1)} %bitcast.114), channel_id=1, source_target_pairs={{0,1},{1,0},{2,3},{3,2},{4,5},{5,4},{6,7},{7,6}} | collective-permute-start | bytes 196616 | tf_op jit(solution)/shard_map/ppermute | solution.py:426
  10.2 103.5 %collective-permute-start.10 = (bf16[1,128,4096]{2,1,0:T(8,128)(2,1)}, bf16[1,128,4096]{2,1,0:T(8,128)(2,1)S(1)}, u32[]{:S(2)}, u32[]{:S(2)}) collective-permute-start(bf16[1,128,4096]{2,1,0:T(8,128)(2,1)} %get-tuple-element.116), channel_id=1, source_target_pairs={{0,2},{1,3},{2,0},{3,1},{4,6},{5,7},{6,4},{7,5}} | collective-permute-start | bytes 3145736 | tf_op jit(solution)/shard_map/ppermute | solution.py:426
  19.3 6.3 %copy-start.6 = (s32[8]{0:T(128)S(1)}, s32[8]{0:T(128)}, u32[]{:S(2)}) copy-start(s32[8]{0:T(128)} %param.23) | copy-start | bytes 100
  19.4 6.3 %copy-start.9 = (s32[4]{0:T(128)S(1)}, s32[4]{0:T(128)}, u32[]{:S(2)}) copy-start(s32[4]{0:T(128)} %constant.276.clone) | copy-start | bytes 52
  25.7 17.7 %copy-start.5 = (bf16[8,4096]{1,0:T(8,128)(2,1)S(1)}, bf16[8,4096]{1,0:T(8,128)(2,1)}, u32[]{:S(2)}) copy-start(bf16[8,4096]{1,0:T(8,128)(2,1)} %param.24) | copy-start | bytes 196612
  25.8 17.8 %copy-start.4 = (bf16[1,4096,512]{2,1,0:T(8,128)(2,1)S(1)}, bf16[1,4096,512]{2,1,0:T(8,128)(2,1)}, u32[]{:S(2)}) copy-start(bf16[1,4096,512]{2,1,0:T(8,128)(2,1)} %param.28) | copy-start | bytes 12582916
  28.4 11.4 %collective-permute-start.4 = (bf16[8,4096]{1,0:T(8,128)(2,1)S(1)}, bf16[8,4096]{1,0:T(8,128)(2,1)S(1)}, u32[]{:S(2)}, u32[]{:S(2)}) collective-permute-start(bf16[8,4096]{1,0:T(8,128)(2,1)S(1)} %fusion.35), channel_id=1, source_target_pairs={{0,6},{1,7},{2,4},{3,5},{4,2},{5,3},{6,0},{7,1}} | collective-permute-start | bytes 196616 | tf_op jit(solution)/shard_map/ppermute | solution.py:426
  29.9 9.9 %collective-permute-start.3 = (bf16[8,4096]{1,0:T(8,128)(2,1)S(1)}, bf16[8,4096]{1,0:T(8,128)(2,1)S(1)}, u32[]{:S(2)}, u32[]{:S(2)}) collective-permute-start(bf16[8,4096]{1,0:T(8,128)(2,1)S(1)} %fusion.35), channel_id=1, source_target_pairs={{0,4},{1,5},{2,6},{3,7},{4,0},{5,1},{6,2},{7,3}} | collective-permute-start | bytes 196616 | tf_op jit(solution)/shard_map/ppermute | solution.py:426
  29.9 11.9 %collective-permute-start.2 = (bf16[8,4096]{1,0:T(8,128)(2,1)S(1)}, bf16[8,4096]{1,0:T(8,128)(2,1)S(1)}, u32[]{:S(2)}, u32[]{:S(2)}) collective-permute-start(bf16[8,4096]{1,0:T(8,128)(2,1)S(1)} %fusion.35), channel_id=1, source_target_pairs={{0,2},{1,3},{2,0},{3,1},{4,6},{5,7},{6,4},{7,5}} | collective-permute-start | bytes 196616 | tf_op jit(solution)/shard_map/ppermute | solution.py:426
  39.8 73.9 %collective-permute-start.9 = (bf16[1,128,4096]{2,1,0:T(8,128)(2,1)}, bf16[1,128,4096]{2,1,0:T(8,128)(2,1)}, u32[]{:S(2)}, u32[]{:S(2)}) collective-permute-start(bf16[1,128,4096]{2,1,0:T(8,128)(2,1)} %get-tuple-element.117), channel_id=1, source_target_pairs={{0,4},{1,5},{2,6},{3,7},{4,0},{5,1},{6,2},{7,3}} | collective-permute-start | bytes 3145736 | tf_op jit(solution)/shard_map/ppermute | solution.py:426
  39.8 55.0 %collective-permute-start.6 = (bf16[1,128,4096]{2,1,0:T(8,128)(2,1)}, bf16[1,128,4096]{2,1,0:T(8,128)(2,1)}, u32[]{:S(2)}, u32[]{:S(2)}) collective-permute-start(bf16[1,128,4096]{2,1,0:T(8,128)(2,1)} %get-tuple-element.118), channel_id=1, source_target_pairs={{0,2},{1,3},{2,0},{3,1},{4,6},{5,7},{6,4},{7,5}} | collective-permute-start | bytes 3145736 | tf_op jit(solution)/shard_map/ppermute | solution.py:426
  41.8 53.0 %collective-permute-start.5 = (bf16[1,128,4096]{2,1,0:T(8,128)(2,1)}, bf16[1,128,4096]{2,1,0:T(8,128)(2,1)}, u32[]{:S(2)}, u32[]{:S(2)}) collective-permute-start(bf16[1,128,4096]{2,1,0:T(8,128)(2,1)} %get-tuple-element.119), channel_id=1, source_target_pairs={{0,4},{1,5},{2,6},{3,7},{4,0},{5,1},{6,2},{7,3}} | collective-permute-start | bytes 3145736 | tf_op jit(solution)/shard_map/ppermute | solution.py:426
  52.1 3.4 copy-start.1
  94.8 3.7 collective-permute-start.7
  94.8 4.5 %collective-permute-start.8 = (bf16[1,128,4096]{2,1,0:T(8,128)(2,1)}, bf16[1,128,4096]{2,1,0:T(8,128)(2,1)}, u32[]{:S(2)}, u32[]{:S(2)}) collective-permute-start(bf16[1,128,4096]{2,1,0:T(8,128)(2,1)} %collective-permute-done.6.refs_1_), channel_id=1, source_target_pairs={{0,1},{1,0},{2,3},{3,2},{4,5},{5,4},{6,7},{7,6}} | collective-permute-start | bytes 3145736 | tf_op jit(solution)/shard_map/ppermute | solution.py:426
  97.8 48.8 %collective-permute-start.14 = (bf16[2,128,4096]{2,1,0:T(8,128)(2,1)}, bf16[2,128,4096]{2,1,0:T(8,128)(2,1)}, u32[]{:S(2)}, u32[]{:S(2)}) collective-permute-start(bf16[2,128,4096]{2,1,0:T(8,128)(2,1)} %get-tuple-element.114), channel_id=1, source_target_pairs={{0,2},{1,3},{2,0},{3,1},{4,6},{5,7},{6,4},{7,5}} | collective-permute-start | bytes 6291464 | tf_op jit(solution)/shard_map/ppermute | solution.py:426
  98.5 48.8 %collective-permute-start.13 = (bf16[2,128,4096]{2,1,0:T(8,128)(2,1)}, bf16[2,128,4096]{2,1,0:T(8,128)(2,1)}, u32[]{:S(2)}, u32[]{:S(2)}) collective-permute-start(bf16[2,128,4096]{2,1,0:T(8,128)(2,1)} %get-tuple-element.115), channel_id=1, source_target_pairs={{0,4},{1,5},{2,6},{3,7},{4,0},{5,1},{6,2},{7,3}} | collective-permute-start | bytes 6291464 | tf_op jit(solution)/shard_map/ppermute | solution.py:426
  99.3 14.9 %slice-start = ((s8[8388608]{0:T(1024)(128)(4,1)}), s8[4194304]{0:T(1024)(128)(4,1)S(1)}, s32[]{:S(2)}) async-start(s8[8388608]{0:T(1024)(128)(4,1)} %bitcast.82), calls=%async_computation | async-start | bytes 8388608
  99.3 14.9 %slice-start.1 = ((s8[8388608]{0:T(1024)(128)(4,1)}), s8[4194304]{0:T(1024)(128)(4,1)S(1)}, s32[]{:S(2)}) async-start(s8[8388608]{0:T(1024)(128)(4,1)} %bitcast.82), calls=%async_computation.1 | async-start | bytes 8388608
  113.7 8.0 %copy-start.10 = (s32[4]{0:T(128)S(1)}, s32[4]{0:T(128)}, u32[]{:S(2)}) copy-start(s32[4]{0:T(128)} %constant.277.clone) | copy-start | bytes 52
  113.7 5.5 %collective-permute-start.11 = (bf16[1,128,4096]{2,1,0:T(8,128)(2,1)}, bf16[1,128,4096]{2,1,0:T(8,128)(2,1)S(1)}, u32[]{:S(2)}, u32[]{:S(2)}) collective-permute-start(bf16[1,128,4096]{2,1,0:T(8,128)(2,1)} %collective-permute-done.9.refs_0_), channel_id=1, source_target_pairs={{0,1},{1,0},{2,3},{3,2},{4,5},{5,4},{6,7},{7,6}} | collective-permute-start | bytes 3145736 | tf_op jit(solution)/shard_map/ppermute | solution.py:426
  113.9 7.9 %collective-permute-start.12 = (bf16[1,128,4096]{2,1,0:T(8,128)(2,1)S(1)}, bf16[1,128,4096]{2,1,0:T(8,128)(2,1)}, u32[]{:S(2)}, u32[]{:S(2)}) collective-permute-start(bf16[1,128,4096]{2,1,0:T(8,128)(2,1)S(1)} %collective-permute-done.10.refs_1_), channel_id=1, source_target_pairs={{0,1},{1,0},{2,3},{3,2},{4,5},{5,4},{6,7},{7,6}} | collective-permute-start | bytes 3145736 | tf_op jit(solution)/shard_map/ppermute | solution.py:426
  118.1 117.5 %collective-permute-start.18 = (bf16[4,128,4096]{2,1,0:T(8,128)(2,1)}, bf16[4,128,4096]{2,1,0:T(8,128)(2,1)}, u32[]{:S(2)}, u32[]{:S(2)}) collective-permute-start(bf16[4,128,4096]{2,1,0:T(8,128)(2,1)} %get-tuple-element.112), channel_id=1, source_target_pairs={{0,2},{1,3},{2,0},{3,1},{4,6},{5,7},{6,4},{7,5}} | collective-permute-start | bytes 12582920 | tf_op jit(solution)/shard_map/ppermute | solution.py:426
  119.2 1.0 copy-start.2
  120.2 115.8 %collective-permute-start.17 = (bf16[4,128,4096]{2,1,0:T(8,128)(2,1)}, bf16[4,128,4096]{2,1,0:T(8,128)(2,1)}, u32[]{:S(2)}, u32[]{:S(2)}) collective-permute-start(bf16[4,128,4096]{2,1,0:T(8,128)(2,1)} %get-tuple-element.113), channel_id=1, source_target_pairs={{0,4},{1,5},{2,6},{3,7},{4,0},{5,1},{6,2},{7,3}} | collective-permute-start | bytes 12582920 | tf_op jit(solution)/shard_map/ppermute | solution.py:426
  121.8 1.2 copy-start.3
  123.0 24.8 %copy-start.11 = (s32[4]{0:T(128)S(1)}, s32[4]{0:T(128)}, u32[]{:S(2)}) copy-start(s32[4]{0:T(128)} %constant.278.clone) | copy-start | bytes 52
  147.3 4.5 %collective-permute-start.15 = (bf16[2,128,4096]{2,1,0:T(8,128)(2,1)}, bf16[2,128,4096]{2,1,0:T(8,128)(2,1)}, u32[]{:S(2)}, u32[]{:S(2)}) collective-permute-start(bf16[2,128,4096]{2,1,0:T(8,128)(2,1)} %collective-permute-done.13.refs_0_), channel_id=1, source_target_pairs={{0,1},{1,0},{2,3},{3,2},{4,5},{5,4},{6,7},{7,6}} | collective-permute-start | bytes 6291464 | tf_op jit(solution)/shard_map/ppermute | solution.py:426
  147.3 7.5 %collective-permute-start.16 = (bf16[2,128,4096]{2,1,0:T(8,128)(2,1)}, bf16[2,128,4096]{2,1,0:T(8,128)(2,1)}, u32[]{:S(2)}, u32[]{:S(2)}) collective-permute-start(bf16[2,128,4096]{2,1,0:T(8,128)(2,1)} %collective-permute-done.14.refs_1_), channel_id=1, source_target_pairs={{0,1},{1,0},{2,3},{3,2},{4,5},{5,4},{6,7},{7,6}} | collective-permute-start | bytes 6291464 | tf_op jit(solution)/shard_map/ppermute | solution.py:426
  154.8 83.7 %copy-start.12 = (s32[4]{0:T(128)S(1)}, s32[4]{0:T(128)}, u32[]{:S(2)}) copy-start(s32[4]{0:T(128)} %constant.279.clone) | copy-start | bytes 52
  235.9 7.5 %collective-permute-start.19 = (bf16[4,128,4096]{2,1,0:T(8,128)(2,1)}, bf16[4,128,4096]{2,1,0:T(8,128)(2,1)}, u32[]{:S(2)}, u32[]{:S(2)}) collective-permute-start(bf16[4,128,4096]{2,1,0:T(8,128)(2,1)} %collective-permute-done.17.refs_0_), channel_id=1, source_target_pairs={{0,1},{1,0},{2,3},{3,2},{4,5},{5,4},{6,7},{7,6}} | collective-permute-start | bytes 12582920 | tf_op jit(solution)/shard_map/ppermute | solution.py:426
  236.0 13.5 %collective-permute-start.20 = (bf16[4,128,4096]{2,1,0:T(8,128)(2,1)}, bf16[4,128,4096]{2,1,0:T(8,128)(2,1)}, u32[]{:S(2)}, u32[]{:S(2)}) collective-permute-start(bf16[4,128,4096]{2,1,0:T(8,128)(2,1)} %collective-permute-done.18.refs_1_), channel_id=1, source_target_pairs={{0,1},{1,0},{2,3},{3,2},{4,5},{5,4},{6,7},{7,6}} | collective-permute-start | bytes 12582920 | tf_op jit(solution)/shard_map/ppermute | solution.py:426
  236.5 52.6 %collective-permute-start.21 = (bf16[2,128,4096]{2,1,0:T(8,128)(2,1)}, bf16[2,128,4096]{2,1,0:T(8,128)(2,1)}, u32[]{:S(2)}, u32[]{:S(2)}) collective-permute-start(bf16[2,128,4096]{2,1,0:T(8,128)(2,1)} %collective-permute-done.13.refs_0_), channel_id=1, source_target_pairs={{0,2},{1,3},{2,0},{3,1},{4,6},{5,7},{6,4},{7,5}} | collective-permute-start | bytes 6291464 | tf_op jit(solution)/shard_map/ppermute | solution.py:426
  237.9 51.1 %collective-permute-start.22 = (bf16[2,128,4096]{2,1,0:T(8,128)(2,1)}, bf16[2,128,4096]{2,1,0:T(8,128)(2,1)}, u32[]{:S(2)}, u32[]{:S(2)}) collective-permute-start(bf16[2,128,4096]{2,1,0:T(8,128)(2,1)} %collective-permute-done.14.refs_1_), channel_id=1, source_target_pairs={{0,4},{1,5},{2,6},{3,7},{4,0},{5,1},{6,2},{7,3}} | collective-permute-start | bytes 6291464 | tf_op jit(solution)/shard_map/ppermute | solution.py:426
  289.1 4.5 %collective-permute-start.23 = (bf16[2,128,4096]{2,1,0:T(8,128)(2,1)}, bf16[2,128,4096]{2,1,0:T(8,128)(2,1)}, u32[]{:S(2)}, u32[]{:S(2)}) collective-permute-start(bf16[2,128,4096]{2,1,0:T(8,128)(2,1)} %collective-permute-done.21.refs_0_), channel_id=1, source_target_pairs={{0,1},{1,0},{2,3},{3,2},{4,5},{5,4},{6,7},{7,6}} | collective-permute-start | bytes 6291464 | tf_op jit(solution)/shard_map/ppermute | solution.py:426
  289.2 7.4 %collective-permute-start.24 = (bf16[2,128,4096]{2,1,0:T(8,128)(2,1)}, bf16[2,128,4096]{2,1,0:T(8,128)(2,1)}, u32[]{:S(2)}, u32[]{:S(2)}) collective-permute-start(bf16[2,128,4096]{2,1,0:T(8,128)(2,1)} %collective-permute-done.22.refs_1_), channel_id=1, source_target_pairs={{0,1},{1,0},{2,3},{3,2},{4,5},{5,4},{6,7},{7,6}} | collective-permute-start | bytes 6291464 | tf_op jit(solution)/shard_map/ppermute | solution.py:426
  289.6 29.2 %collective-permute-start.25 = (bf16[1,128,4096]{2,1,0:T(8,128)(2,1)}, bf16[1,128,4096]{2,1,0:T(8,128)(2,1)}, u32[]{:S(2)}, u32[]{:S(2)}) collective-permute-start(bf16[1,128,4096]{2,1,0:T(8,128)(2,1)} %collective-permute-done.9.refs_0_), channel_id=1, source_target_pairs={{0,2},{1,3},{2,0},{3,1},{4,6},{5,7},{6,4},{7,5}} | collective-permute-start | bytes 3145736 | tf_op jit(solution)/shard_map/ppermute | solution.py:426
  291.1 27.7 %collective-permute-start.26 = (bf16[1,128,4096]{2,1,0:T(8,128)(2,1)S(1)}, bf16[1,128,4096]{2,1,0:T(8,128)(2,1)}, u32[]{:S(2)}, u32[]{:S(2)}) collective-permute-start(bf16[1,128,4096]{2,1,0:T(8,128)(2,1)S(1)} %collective-permute-done.10.refs_1_), channel_id=1, source_target_pairs={{0,4},{1,5},{2,6},{3,7},{4,0},{5,1},{6,2},{7,3}} | collective-permute-start | bytes 3145736 | tf_op jit(solution)/shard_map/ppermute | solution.py:426
  318.9 3.0 collective-permute-start.27
  319.0 4.4 %collective-permute-start.28 = (bf16[1,128,4096]{2,1,0:T(8,128)(2,1)}, bf16[1,128,4096]{2,1,0:T(8,128)(2,1)}, u32[]{:S(2)}, u32[]{:S(2)}) collective-permute-start(bf16[1,128,4096]{2,1,0:T(8,128)(2,1)} %collective-permute-done.26.refs_1_), channel_id=1, source_target_pairs={{0,1},{1,0},{2,3},{3,2},{4,5},{5,4},{6,7},{7,6}} | collective-permute-start | bytes 3145736 | tf_op jit(solution)/shard_map/ppermute | solution.py:426
  319.4 25.4 %collective-permute-start.29 = (bf16[1,128,4096]{2,1,0:T(8,128)(2,1)}, bf16[1,128,4096]{2,1,0:T(8,128)(2,1)S(1)}, u32[]{:S(2)}, u32[]{:S(2)}) collective-permute-start(bf16[1,128,4096]{2,1,0:T(8,128)(2,1)} %collective-permute-done.5.refs_0_), channel_id=1, source_target_pairs={{0,2},{1,3},{2,0},{3,1},{4,6},{5,7},{6,4},{7,5}} | collective-permute-start | bytes 3145736 | tf_op jit(solution)/shard_map/ppermute | solution.py:426
  320.9 25.2 %collective-permute-start.30 = (bf16[1,128,4096]{2,1,0:T(8,128)(2,1)}, bf16[1,128,4096]{2,1,0:T(8,128)(2,1)}, u32[]{:S(2)}, u32[]{:S(2)}) collective-permute-start(bf16[1,128,4096]{2,1,0:T(8,128)(2,1)} %collective-permute-done.6.refs_1_), channel_id=1, source_target_pairs={{0,4},{1,5},{2,6},{3,7},{4,0},{5,1},{6,2},{7,3}} | collective-permute-start | bytes 3145736 | tf_op jit(solution)/shard_map/ppermute | solution.py:426
  323.4 23.3 %copy-start.8 = (bf16[1,4096]{1,0:T(2,128)(2,1)S(1)}, bf16[1,4096]{1,0:T(2,128)(2,1)}, u32[]{:S(2)}) copy-start(bf16[1,4096]{1,0:T(2,128)(2,1)} %param.30) | copy-start | bytes 24580
  346.1 2.8 collective-permute-start.31
  346.1 4.3 %collective-permute-start.32 = (bf16[1,128,4096]{2,1,0:T(8,128)(2,1)}, bf16[1,128,4096]{2,1,0:T(8,128)(2,1)}, u32[]{:S(2)}, u32[]{:S(2)}) collective-permute-start(bf16[1,128,4096]{2,1,0:T(8,128)(2,1)} %collective-permute-done.30.refs_1_), channel_id=1, source_target_pairs={{0,1},{1,0},{2,3},{3,2},{4,5},{5,4},{6,7},{7,6}} | collective-permute-start | bytes 3145736 | tf_op jit(solution)/shard_map/ppermute | solution.py:426

commit v3 on v2

v3 whole, which is shorter than its diff:
```python
import functools

import jax
import jax.numpy as jnp
from jax import lax
from jax.experimental import pallas as pl
from jax.experimental.pallas import tpu as pltpu
from jax.sharding import PartitionSpec as P


HEAD_DIM = 128
NEG_BIG = -1e30
STAT_ROWS = 8
NORM_ROWS = 32
COL_TILE = 256
N_MASKS = 8
MESH = pl.DeviceIdType.MESH


def rotary_tables(positions):
    half_dim = HEAD_DIM // 2
    inv_freq = 10000.0 ** (-2.0 * jnp.arange(half_dim, dtype=jnp.float32) / HEAD_DIM)
    angles = positions.astype(jnp.float32)[..., None] * inv_freq
    cos_tab = jnp.cos(angles)
    sin_tab = jnp.sin(angles)
    return jnp.concatenate([cos_tab, cos_tab], axis=-1), jnp.concatenate([-sin_tab, sin_tab], axis=-1)


def load_kernel(*refs):
    n = len(refs) // 2
    sem = refs[-1]
    copies = [pltpu.make_async_copy(refs[i], refs[n + i], sem.at[i]) for i in range(n)]
    for copy in copies:
        copy.start()
    for copy in copies:
        copy.wait()


def keep_in_vmem(*arrays):
    return pl.pallas_call(
        load_kernel,
        out_shape=[pltpu.VMEM(arr.shape, arr.dtype) for arr in arrays],
        in_specs=[pl.BlockSpec(memory_space=pl.ANY)] * len(arrays),
        out_specs=[pl.BlockSpec(memory_space=pltpu.VMEM)] * len(arrays),
        scratch_shapes=[pltpu.SemaphoreType.DMA((len(arrays),))],
        compiler_params=pltpu.CompilerParams(vmem_limit_bytes=24 * 2 ** 20),
        name="keep",
    )(*(pltpu.with_memory_space_constraint(arr, pltpu.HBM) for arr in arrays))


def norm_kernel(outs_of, x_ref, gain_ref, *refs):
    n_out = len(refs) - 3
    out_refs = refs[:n_out]
    ss_buf, n_buf, sems = refs[n_out:]
    step = pl.program_id(0)
    blk, d_model = x_ref.shape[1:]
    lanes = [slice(c * HEAD_DIM, (c + 1) * HEAD_DIM) for c in range(d_model // HEAD_DIM)]

    def copies(at_step):
        return [pltpu.make_async_copy(n_buf.at[at_step % 2], out_refs[o].at[i], sems.at[at_step % 2, k])
                for k, (o, i) in enumerate(outs_of[at_step])]

    for at_step in range(2, len(outs_of)):
        @pl.when(step == at_step)
        def _():
            for copy in copies(at_step - 2):
                copy.wait()

    def square_rows(r, carry):
        rows = pl.ds(pl.multiple_of(r * NORM_ROWS, NORM_ROWS), NORM_ROWS)
        acc = [jnp.zeros((NORM_ROWS, HEAD_DIM), jnp.float32) for _ in range(2)]
        for c, lane in enumerate(lanes):
            xf = x_ref[0, rows, lane].astype(jnp.float32)
            acc[c % 2] += xf * xf
        ss_buf[rows, :] = acc[0] + acc[1]
        return carry

    lax.fori_loop(0, blk // NORM_ROWS, square_rows, 0)
    total = jnp.sum(ss_buf[...], axis=-1, keepdims=True)
    ss_buf[...] = jnp.broadcast_to(lax.rsqrt(total / d_model + 1e-5), (blk, HEAD_DIM))
    slot = lax.rem(step, 2)

    def norm_rows(r, carry):
        rows = pl.ds(pl.multiple_of(r * NORM_ROWS, NORM_ROWS), NORM_ROWS)
        inv_rms = ss_buf[rows, :]
        for lane in lanes:
            xf = x_ref[0, rows, lane].astype(jnp.float32)
            n_buf[slot, rows, lane] = (xf * inv_rms * gain_ref[:, lane]).astype(jnp.bfloat16)
        return carry

    lax.fori_loop(0, blk // NORM_ROWS, norm_rows, 0)
    for at_step in range(len(outs_of)):
        @pl.when(step == at_step)
        def _():
            for copy in copies(at_step):
                copy.start()
            if at_step == len(outs_of) - 1:
                for copy in copies(at_step):
                    copy.wait()
                if at_step >= 1:
                    for copy in copies(at_step - 1):
                        copy.wait()


def norm_call(x, gain, order, outs_of, sizes):
    blk, d_model = x.shape[1:]

    def prompt_of(g):
        idx = jnp.int32(order[-1])
        for k in range(len(order) - 1):
            idx = jnp.where(g == k, order[k], idx)
        return idx

    return pl.pallas_call(
        functools.partial(norm_kernel, outs_of),
        grid=(len(order),),
        in_specs=[pl.BlockSpec((1, blk, d_model), lambda g: (prompt_of(g), 0, 0)),
                  pl.BlockSpec((1, d_model), lambda g: (0, 0))],
        out_specs=[pl.BlockSpec(memory_space=pl.ANY)] * len(sizes),
        out_shape=[jax.ShapeDtypeStruct((size, blk, d_model), jnp.bfloat16) for size in sizes],
        scratch_shapes=[
            pltpu.VMEM((blk, HEAD_DIM), jnp.float32),
            pltpu.VMEM((2, blk, d_model), jnp.bfloat16),
            pltpu.SemaphoreType.DMA((2, max(len(o) for o in outs_of))),
        ],
        compiler_params=pltpu.CompilerParams(vmem_limit_bytes=24 * 2 ** 20),
        cost_estimate=pl.CostEstimate(flops=len(order) * blk * d_model * 8, bytes_accessed=len(order) * blk * d_model * 6, transcendentals=0),
        name="norm_rows",
    )(x, gain)


def rows_kernel(new_ref, last_ref, gain_ref, cos_ref, sin_ref, wq_hbm, wk, wv, q_ref, k_ref, v_ref, st_ref, wq, q_buf, sem):
    load = pltpu.make_async_copy(wq_hbm, wq, sem)
    load.start()
    n_batch = new_ref.shape[0]
    heads = wk.shape[1] // HEAD_DIM
    xf = jnp.concatenate([new_ref[...].astype(jnp.float32), last_ref[...].astype(jnp.float32)], axis=0)
    inv_rms = lax.rsqrt(jnp.mean(xf * xf, axis=-1, keepdims=True) + 1e-5)
    normed = (xf * inv_rms * gain_ref[...]).astype(jnp.bfloat16)
    k_all = jnp.dot(normed, wk[...], preferred_element_type=jnp.float32)[:n_batch]
    v_all = jnp.dot(normed, wv[...], preferred_element_type=jnp.float32)[:n_batch].astype(jnp.bfloat16)
    load.wait()
    q_all = jnp.dot(normed, wq[...], preferred_element_type=jnp.float32)
    q_buf[...] = jnp.zeros_like(q_buf)
    k_rot = []
    for h in range(heads):
        cols = slice(h * HEAD_DIM, (h + 1) * HEAD_DIM)
        qh = q_all[:, cols]
        qh = (qh * cos_ref[...] + pltpu.roll(qh, HEAD_DIM // 2, 1) * sin_ref[...]).astype(jnp.bfloat16).astype(jnp.float32)
        kh = k_all[:, cols]
        kh = (kh * cos_ref[:n_batch, :] + pltpu.roll(kh, HEAD_DIM // 2, 1) * sin_ref[:n_batch, :]).astype(jnp.bfloat16)
        k_rot.append(kh)
        score = jnp.sum(qh[:n_batch] * kh.astype(jnp.float32), axis=-1, keepdims=True) * (HEAD_DIM ** -0.5)
        zero = jnp.zeros((n_batch, HEAD_DIM), jnp.float32)
        for t in range(2):
            row = 2 * h + t
            q_buf[:, row, cols] = qh[t * n_batch:(t + 1) * n_batch]
            st_ref[0, :, row, :] = v_all[:, cols].astype(jnp.float32) if t == 0 else zero
            st_ref[1, :, row, :] = zero + score if t == 0 else zero + NEG_BIG
            st_ref[2, :, row, :] = zero + 1.0 if t == 0 else zero
    q_ref[...] = q_buf[...].astype(jnp.bfloat16)
    k_ref[...] = jnp.concatenate(k_rot, axis=1).reshape(n_batch, heads, HEAD_DIM)
    v_ref[...] = v_all.reshape(n_batch, heads, HEAD_DIM)


def rows_call(new_tok, last_x, gain, row_tabs, w_q, w_k, w_v):
    n_batch = new_tok.shape[0]
    width = w_q.shape[1]
    heads = width // HEAD_DIM
    vmem = pl.BlockSpec(memory_space=pltpu.VMEM)
    return pl.pallas_call(
        rows_kernel,
        out_shape=[
            jax.ShapeDtypeStruct((n_batch, STAT_ROWS, width), jnp.bfloat16),
            jax.ShapeDtypeStruct((n_batch, heads, HEAD_DIM), jnp.bfloat16),
            jax.ShapeDtypeStruct((n_batch, heads, HEAD_DIM), jnp.bfloat16),
            jax.ShapeDtypeStruct((3, n_batch, STAT_ROWS, HEAD_DIM), jnp.float32),
        ],
        in_specs=[vmem] * 5 + [pl.BlockSpec(memory_space=pl.ANY)] + [vmem] * 2,
        out_specs=[vmem] * 4,
        scratch_shapes=[
            pltpu.VMEM(w_q.shape, jnp.bfloat16),
            pltpu.VMEM((n_batch, STAT_ROWS, width), jnp.float32),
            pltpu.SemaphoreType.DMA,
        ],
        compiler_params=pltpu.CompilerParams(vmem_limit_bytes=24 * 2 ** 20),
        cost_estimate=pl.CostEstimate(flops=2 * 2 * n_batch * 3 * w_q.shape[0] * width, bytes_accessed=2 * w_q.size, transcendentals=0),
        name="query_rows",
    )(new_tok, last_x, gain, *row_tabs, pltpu.with_memory_space_constraint(w_q, pltpu.HBM), w_k, w_v)


def by_group(group, values):
    out = values[-1]
    for p in range(len(values) - 1):
        out = jnp.where(group == p, values[p], out)
    return out


def kv_kernel(n_in, masks, batches, firsts, with_new, sc_ref, *refs):
    n_groups = len(masks)
    n_arr = n_in * n_groups
    x_refs = refs[:n_arr]
    cos_refs = refs[n_arr:n_arr + n_in]
    sin_refs = refs[n_arr + n_in:n_arr + 2 * n_in]
    wk, wv, q_ref = refs[n_arr + 2 * n_in:n_arr + 2 * n_in + 3]
    rest = refs[n_arr + 2 * n_in + 3:]
    if with_new:
        new_refs = rest[:2]
        rest = rest[2:]
    else:
        rest = rest[3:]
    kc_ref, vc_ref, st_ref, x_buf, k_buf, v_buf, k_out, v_out, s_out, x_sem, sems, new_sem = rest
    step = pl.program_id(0)
    n_steps = pl.num_programs(0)
    slot = lax.rem(step, 2)
    per_group = n_steps // n_groups
    blk = x_buf.shape[2]
    width = wk.shape[1]
    heads = width // HEAD_DIM
    n_tok = n_in * blk

    def x_copies(at_step, which, group):
        local = at_step - group * per_group
        return [pltpu.make_async_copy(x_refs[group * n_in + i].at[firsts[group][i] + local],
                                      x_buf.at[which, i], x_sem.at[which, i]) for i in range(n_in)]

    def start_x(at_step, which):
        for group in range(n_groups):
            @pl.when(at_step // per_group == group)
            def _(group=group):
                for copy in x_copies(at_step, which, group):
                    copy.start()

    def place(i, at_step):
        group = at_step // per_group
        shard = sc_ref[by_group(group, [mask[i] for mask in masks])]
        return shard, by_group(group, [batch[i] for batch in batches]) + lax.rem(at_step, per_group)

    def out_copies(which, at_step):
        copies = []
        for i in range(n_in):
            shard, bat = place(i, at_step)
            rows = pl.ds(shard * blk, blk)
            copies.append(pltpu.make_async_copy(k_out.at[which, i], kc_ref.at[bat, rows], sems.at[which, i, 0]))
            copies.append(pltpu.make_async_copy(v_out.at[which, i], vc_ref.at[bat, rows], sems.at[which, i, 1]))
            copies.append(pltpu.make_async_copy(s_out.at[which, i], st_ref.at[shard, bat], sems.at[which, i, 2]))
        return copies

    def new_copies():
        return [pltpu.make_async_copy(src.at[pl.ds(b, 1)], dst.at[b, pl.ds(dst.shape[1] - 1, 1)], new_sem.at[idx, b])
                for idx, (src, dst) in enumerate(zip(new_refs, (kc_ref, vc_ref))) for b in range(src.shape[0])]

    @pl.when(step == 0)
    def _():
        start_x(step, slot)
        if with_new:
            for copy in new_copies():
                copy.start()

    @pl.when(step + 1 < n_steps)
    def _():
        start_x(step + 1, 1 - slot)

    @pl.when(step >= 2)
    def _():
        for copy in out_copies(slot, step - 2):
            copy.wait()

    for copy in x_copies(0, slot, 0):
        copy.wait()
    x_rows = x_buf.at[slot]

    def col_tile(c, carry):
        cols = pl.ds(pl.multiple_of(c * COL_TILE, COL_TILE), COL_TILE)
        normed = x_rows[...].reshape(n_tok, x_buf.shape[3])
        kf = jnp.dot(normed, wk[:, cols], preferred_element_type=jnp.float32)
        vf = jnp.dot(normed, wv[:, cols], preferred_element_type=jnp.float32)
        v_buf[:, cols] = vf.astype(jnp.bfloat16)
        parts = []
        for i in range(n_in):
            cos_tab = cos_refs[i][0]
            sin_tab = sin_refs[i][0]
            halves = []
            for h in range(COL_TILE // HEAD_DIM):
                kh = kf[i * blk:(i + 1) * blk, h * HEAD_DIM:(h + 1) * HEAD_DIM]
                halves.append(kh * cos_tab + pltpu.roll(kh, HEAD_DIM // 2, 1) * sin_tab)
            parts.append(jnp.concatenate(halves, axis=1))
        k_buf[:, cols] = jnp.concatenate(parts, axis=0).astype(jnp.bfloat16)
        return carry

    lax.fori_loop(0, width // COL_TILE, col_tile, 0)

    head_of_row = lax.broadcasted_iota(jnp.int32, (STAT_ROWS, HEAD_DIM), 0) // (STAT_ROWS // heads)
    probs = []
    for i in range(n_in):
        shard, bat = place(i, step)
        scores = lax.dot_general(q_ref[bat], k_buf[i * blk:(i + 1) * blk, :], (((1,), (1,)), ((), ())),
                                 preferred_element_type=jnp.float32) * (HEAD_DIM ** -0.5)
        pos = shard * blk + lax.broadcasted_iota(jnp.int32, scores.shape, 1)
        visible = pos < sc_ref[N_MASKS + bat]
        scores = jnp.where(visible, scores, NEG_BIG)
        blk_max = jnp.max(scores, axis=-1, keepdims=True)
        prob = jnp.where(visible, jnp.exp(scores - blk_max), 0.0)
        probs.append((blk_max, prob))
    stats = []
    for i, (blk_max, prob) in enumerate(probs):
        full = jnp.dot(prob.astype(jnp.bfloat16), v_buf[i * blk:(i + 1) * blk, :], preferred_element_type=jnp.float32)
        acc = jnp.zeros((STAT_ROWS, HEAD_DIM), jnp.float32)
        for h in range(heads):
            acc = jnp.where(head_of_row == h, full[:, h * HEAD_DIM:(h + 1) * HEAD_DIM], acc)
        stats.append((acc, blk_max, jnp.sum(prob, axis=-1, keepdims=True)))
    for i in range(n_in):
        k_out[slot, i] = k_buf[i * blk:(i + 1) * blk, :].reshape(blk, heads, HEAD_DIM)
        v_out[slot, i] = v_buf[i * blk:(i + 1) * blk, :].reshape(blk, heads, HEAD_DIM)
        for k, stat in enumerate(stats[i]):
            s_out[slot, i, k] = jnp.broadcast_to(stat, (STAT_ROWS, HEAD_DIM))

    for copy in out_copies(slot, step):
        copy.start()

    @pl.when(step == n_steps - 1)
    def _():
        for copy in out_copies(slot, step):
            copy.wait()
        if with_new:
            for copy in new_copies():
                copy.wait()

    @pl.when((step == n_steps - 1) & (n_steps >= 2))
    def _():
        for copy in out_copies(1 - slot, step - 1):
            copy.wait()


def kv_call(groups, per_group, masks, batches, scalars, tabs, w_k, w_v, q_diag, caches, new_rows=None):
    n_groups = len(groups)
    n_in = len(groups[0])
    n_steps = n_groups * per_group
    cos_tab, sin_tab = tabs
    blk, d_model = groups[0][0][0].shape[1:]
    width = w_k.shape[1]
    heads = width // HEAD_DIM
    any_spec = pl.BlockSpec(memory_space=pl.ANY)
    operands = [arr for group in groups for arr, _ in group]
    in_specs = [any_spec] * len(operands)
    for tab in (cos_tab, sin_tab):
        for i in range(n_in):
            in_specs.append(pl.BlockSpec((1, blk, HEAD_DIM), lambda g, sc, i=i: (
                sc[by_group(g // per_group, [mask[i] for mask in masks])], 0, 0)))
            operands.append(tab)
    in_specs += [pl.BlockSpec(memory_space=pltpu.VMEM)] * 2 + [pl.BlockSpec(q_diag.shape, lambda g, sc: (0, 0, 0))]
    operands += [w_k, w_v, q_diag]
    with_new = new_rows is not None
    if with_new:
        operands += new_rows
        in_specs += [any_spec] * 2
        aliases = {}
    else:
        operands += caches
        in_specs += [any_spec] * 3
        aliases = {len(operands) - 2: 0, len(operands) - 1: 1, len(operands): 2}
    tokens = n_in * blk
    n_batch = q_diag.shape[0]
    return pl.pallas_call(
        functools.partial(kv_kernel, n_in, masks, batches, [[first for _, first in group] for group in groups], with_new),
        grid_spec=pltpu.PrefetchScalarGridSpec(
            num_scalar_prefetch=1,
            grid=(n_steps,),
            in_specs=in_specs,
            out_specs=[any_spec] * 3,
            scratch_shapes=[
                pltpu.VMEM((2, n_in, blk, d_model), jnp.bfloat16),
                pltpu.VMEM((tokens, width), jnp.bfloat16),
                pltpu.VMEM((tokens, width), jnp.bfloat16),
                pltpu.VMEM((2, n_in, blk, heads, HEAD_DIM), jnp.bfloat16),
                pltpu.VMEM((2, n_in, blk, heads, HEAD_DIM), jnp.bfloat16),
                pltpu.VMEM((2, n_in, 3, STAT_ROWS, HEAD_DIM), jnp.float32),
                pltpu.SemaphoreType.DMA((2, n_in)),
                pltpu.SemaphoreType.DMA((2, n_in, 3)),
                pltpu.SemaphoreType.DMA((2, n_batch)),
            ],
        ),
        out_shape=[jax.ShapeDtypeStruct(c.shape, c.dtype) for c in caches],
        input_output_aliases=aliases,
        compiler_params=pltpu.CompilerParams(vmem_limit_bytes=20 * 2 ** 20),
        cost_estimate=pl.CostEstimate(flops=4 * n_steps * tokens * d_model * width, bytes_accessed=2 * n_steps * tokens * (d_model + 2 * width), transcendentals=0),
        name="kv_chunk",
    )(scalars, *operands)


def tail_kernel(n_dev, n_part, st_ref, self_ref, xs_ref, gain_ref, wo_hbm, wg_hbm, wu_hbm, wd_hbm, dec_ref, last_ref,
                wo, wg, wu, wd, stv, rows, a_buf, n_buf, mid_buf, ps1, pr1, ps2, pr2, xo1, xg1, xo2, xg2,
                w_sem, send_sem, recv_sem):
    me = lax.axis_index("model")
    n_batch = dec_ref.shape[0]
    n_rows = 2 * n_batch
    d_model = dec_ref.shape[1]
    cols = d_model // n_dev
    heads = STAT_ROWS // 2
    loads = [pltpu.make_async_copy(src, dst, w_sem.at[i]) for i, (src, dst) in enumerate(
        ((st_ref, stv), (wo_hbm, wo), (wg_hbm, wg), (wu_hbm, wu), (wd_hbm, wd)))]
    loads[0].start()
    loads[1].start()
    barrier = pltpu.get_barrier_semaphore()
    for k in range(1, n_dev):
        peer = lax.rem(me + k, n_dev)
        pl.semaphore_signal(barrier, inc=1, device_id={"model": peer}, device_id_type=MESH)

    def send(phase, k, src, dst):
        peer = lax.rem(me + k, n_dev)
        return pltpu.make_async_remote_copy(
            src_ref=src, dst_ref=dst, send_sem=send_sem.at[phase, k - 1], recv_sem=recv_sem.at[phase, k - 1],
            device_id={"model": peer}, device_id_type=MESH)

    loads[0].wait()
    for load in loads[2:]:
        load.start()
    for b in range(n_batch):
        top = self_ref[1, b]
        for j in range(n_part):
            top = jnp.maximum(top, stv[j, b, 1])
        scale = jnp.exp(self_ref[1, b] - top)
        den = scale * self_ref[2, b]
        num = scale * self_ref[0, b]
        for j in range(n_part):
            scale = jnp.exp(stv[j, b, 1] - top)
            den += scale * stv[j, b, 2]
            num += scale * stv[j, b, 0]
        rows[:, b, :] = num / den
    for h in range(heads):
        for t in range(2):
            a_buf[t * n_batch:(t + 1) * n_batch, h * HEAD_DIM:(h + 1) * HEAD_DIM] = rows[2 * h + t]
    att = a_buf[...].astype(jnp.bfloat16)

    def all_reduce(phase, partial, base, ps, pr, xo, xg):
        copies = []
        for k in range(1, n_dev):
            peer = lax.rem(me + k, n_dev)
            ps[k - 1] = partial(peer)
            copies.append(send(phase, k, ps.at[k - 1], pr.at[k - 1]))
            copies[-1].start()
        total = base + partial(me)
        for k in range(1, n_dev):
            copies[k - 1].wait_recv()
            total = total + pr[k - 1]
        xo[...] = total.astype(jnp.bfloat16)
        outs = []
        for k in range(1, n_dev):
            outs.append(send(phase + 1, k, xo, xg.at[me]))
            outs[-1].start()
        xg[me] = xo[...]
        for k in range(1, n_dev):
            outs[k - 1].wait_recv()
        return copies + outs

    def col_block(p):
        return pl.ds(pl.multiple_of(p * cols, cols), cols)

    loads[1].wait()
    pl.semaphore_wait(barrier, n_dev - 1)
    sent = all_reduce(0, lambda p: jnp.dot(att, wo[:, col_block(p)], preferred_element_type=jnp.float32),
                      xs_ref[...].astype(jnp.float32), ps1, pr1, xo1, xg1)
    sq = jnp.zeros((n_rows, 1), jnp.float32)
    for j in range(n_dev):
        xf = xg1[j].astype(jnp.float32)
        sq += jnp.sum(xf * xf, axis=-1, keepdims=True)
    inv_rms = lax.rsqrt(sq / d_model + 1e-5)
    for j in range(n_dev):
        xf = xg1[j].astype(jnp.float32)
        n_buf[:, j * cols:(j + 1) * cols] = (xf * inv_rms * gain_ref[:, j * cols:(j + 1) * cols]).astype(jnp.bfloat16)
    loads[2].wait()
    loads[3].wait()
    nt = (((1,), (1,)), ((), ()))
    n_hid = wg.shape[0]
    rows_per = n_hid // 2

    def hidden_rows(r, carry):
        at = pl.ds(pl.multiple_of(r * rows_per, 8), rows_per)
        gate = lax.dot_general(wg[at, :], n_buf[...], nt, preferred_element_type=jnp.float32)
        up = lax.dot_general(wu[at, :], n_buf[...], nt, preferred_element_type=jnp.float32)
        mid_buf[at, :] = gate * (1.0 / (1.0 + jnp.exp(-gate))) * up
        return carry

    lax.fori_loop(0, 2, hidden_rows, 0)
    mid = mid_buf[...].T.astype(jnp.bfloat16)
    loads[4].wait()
    sent += all_reduce(2, lambda p: jnp.dot(mid, wd[:, col_block(p)], preferred_element_type=jnp.float32),
                       xo1[...].astype(jnp.float32), ps2, pr2, xo2, xg2)
    for j in range(n_dev):
        dec_ref[:, j * cols:(j + 1) * cols] = xg2[j, :n_batch]
        last_ref[:, j * cols:(j + 1) * cols] = xg2[j, n_batch:]
    for copy in sent:
        copy.wait_send()


def tail_call(n_dev, stats, self_stat, x_mine, gain, w_o, w_gate_t, w_up_t, w_down, n_batch):
    n_rows, cols = x_mine.shape
    d_model = w_o.shape[1]
    n_part = stats.shape[0]
    vmem = pl.BlockSpec(memory_space=pltpu.VMEM)
    hbm = pl.BlockSpec(memory_space=pltpu.HBM)
    return pl.pallas_call(
        functools.partial(tail_kernel, n_dev, n_part),
        out_shape=[jax.ShapeDtypeStruct((n_batch, d_model), jnp.bfloat16)] * 2,
        in_specs=[pl.BlockSpec(memory_space=pl.ANY), vmem, vmem, vmem, hbm, hbm, hbm, hbm],
        out_specs=[vmem, vmem],
        scratch_shapes=[
            pltpu.VMEM(w_o.shape, jnp.bfloat16),
            pltpu.VMEM(w_gate_t.shape, jnp.bfloat16),
            pltpu.VMEM(w_up_t.shape, jnp.bfloat16),
            pltpu.VMEM(w_down.shape, jnp.bfloat16),
            pltpu.VMEM(stats.shape, jnp.float32),
            pltpu.VMEM((STAT_ROWS, n_batch, HEAD_DIM), jnp.float32),
            pltpu.VMEM((n_rows, w_o.shape[0]), jnp.float32),
            pltpu.VMEM((n_rows, d_model), jnp.bfloat16),
            pltpu.VMEM((w_gate_t.shape[0], n_rows), jnp.float32),
            pltpu.VMEM((n_dev - 1, n_rows, cols), jnp.float32),
            pltpu.VMEM((n_dev - 1, n_rows, cols), jnp.float32),
            pltpu.VMEM((n_dev - 1, n_rows, cols), jnp.float32),
            pltpu.VMEM((n_dev - 1, n_rows, cols), jnp.float32),
            pltpu.VMEM((n_rows, cols), jnp.bfloat16),
            pltpu.VMEM((n_dev, n_rows, cols), jnp.bfloat16),
            pltpu.VMEM((n_rows, cols), jnp.bfloat16),
            pltpu.VMEM((n_dev, n_rows, cols), jnp.bfloat16),
            pltpu.SemaphoreType.DMA((5,)),
            pltpu.SemaphoreType.DMA((4, n_dev - 1)),
            pltpu.SemaphoreType.DMA((4, n_dev - 1)),
        ],
        compiler_params=pltpu.CompilerParams(collective_id=0, has_side_effects=True, vmem_limit_bytes=52 * 2 ** 20),
        name="tail",
    )(stats, self_stat, x_mine, gain, *(pltpu.with_memory_space_constraint(w, pltpu.HBM) for w in (w_o, w_gate_t, w_up_t, w_down)))


def solution(mesh):
    n_dev = mesh.shape['model']
    seq_spec = P('replica', 'model', None)
    col_spec = P(None, None, 'model')
    row_spec = P(None, 'model', None)
    gain_spec = P(None, None)
    tok_spec = P('replica', None)
    cache_spec = P(None, 'replica', None, 'model', None)
    in_specs = (seq_spec, P('replica'), tok_spec, gain_spec, col_spec, col_spec, col_spec, row_spec, gain_spec, col_spec, col_spec, row_spec)
    out_specs = (tok_spec, tok_spec, cache_spec, cache_spec)

    def swap(arr, bit):
        return lax.ppermute(arr, 'model', [(i, i ^ bit) for i in range(n_dev)])

    def per_device(prompt, lengths, new_tok, norm_attn, w_q, w_k, w_v, w_o, norm_mlp, w_gate, w_up, w_down):
        my_idx = lax.axis_index('model')
        n_batch, blk, d_model = prompt.shape
        seq_len = blk * n_dev
        width = w_k.shape[2]
        heads = width // HEAD_DIM
        half = n_batch // 2
        wq = w_q[0]
        gain = norm_attn.astype(jnp.float32)

        q1, q2 = n_batch // 8, n_batch // 4
        bounds = [(0, q1), (q1, q2), (q2, half)]
        a_parts, b_parts = {}, {}
        first = [*range(q1), *range(half, half + q1)]
        a_parts[0], b_parts[0] = norm_call(prompt, gain, first, [[(k // q1, k % q1)] for k in range(2 * q1)], [q1, q1])
        from_y, from_x = {}, {}

        def send_part(step, along_y, along_x):
            from_y[step] = swap(along_y, 4)
            from_x[step] = swap(along_x, 2)

        send_part(0, a_parts[0], b_parts[0])
        seq_pos = my_idx * blk + jnp.arange(blk)
        sel = (seq_pos[None, :] == (lengths - 1)[:, None]).astype(jnp.bfloat16)
        last_x = jnp.einsum('bs,bsd->bd', sel, prompt, preferred_element_type=jnp.float32).astype(jnp.bfloat16)
        last_x = last_x + swap(last_x, 1)
        last_x = (last_x + swap(last_x, 2)) + (swap(last_x, 4) + swap(last_x, 6))
        order, outs_of = [], []
        for part in (1, 2, 0):
            lo, hi = bounds[part]
            for side in range(2):
                for k in range(lo, hi):
                    order.append(side * half + k)
                    outs_of.append([(4, side * half + k)] + ([(2 * part - 2 + side, k - lo)] if part else []))
        a_parts[1], b_parts[1], a_parts[2], b_parts[2], normed = norm_call(
            prompt, gain, order, outs_of, [q2 - q1, q2 - q1, half - q2, half - q2, n_batch])
        send_part(1, a_parts[1], b_parts[1])
        send_part(2, a_parts[2], b_parts[2])
        send_part(3, b_parts[2], a_parts[2])
        send_part(4, normed[half:half + q2], normed[:q2])
        core_all = swap(normed, 1)

        bits = jnp.arange(N_MASKS)
        scalars = jnp.concatenate([sum(((my_idx // bit + bits // bit) % 2) * bit for bit in (1, 2, 4)), lengths]).astype(jnp.int32)
        row_tabs = rotary_tables(jnp.concatenate([lengths, lengths - 1]))
        tabs = tuple(tab.reshape(n_dev, blk, HEAD_DIM) for tab in rotary_tables(jnp.arange(seq_len)))
        x_rows = jnp.concatenate([new_tok, last_x], axis=0)
        x_mine = lax.dynamic_slice_in_dim(x_rows, my_idx * (d_model // n_dev), d_model // n_dev, axis=1)
        wk, wv, last_x, scalars, row_tabs, tabs, x_mine, gain_mlp = lax.optimization_barrier(
            (w_k[0], w_v[0], last_x, scalars, row_tabs, tabs, x_mine, norm_mlp.astype(jnp.float32)))
        wk, wv = keep_in_vmem(wk, wv)
        q_diag, k_new, v_new, self_stat = rows_call(new_tok, last_x, gain, row_tabs, wq, wk, wv)
        cache_shape = jax.ShapeDtypeStruct((n_batch, seq_len + 1, heads, HEAD_DIM), jnp.bfloat16)
        caches = [cache_shape, cache_shape, jax.ShapeDtypeStruct((n_dev, n_batch, 3, STAT_ROWS, HEAD_DIM), jnp.float32)]

        def run(groups, per_group, masks, batches, caches, new_rows=None):
            return kv_call(groups, per_group, masks, batches, scalars, tabs, wk, wv, q_diag, caches, new_rows)

        def after(caches, *arrays):
            out = lax.optimization_barrier((caches[2], *arrays))
            return [caches[0], caches[1], out[0]], out[1:]

        caches = run([[(arr, 0), (arr, half)] for arr in (normed, core_all)], half,
                     [[0] * 2, [1] * 2], [[0, half]] * 2, caches, [k_new, v_new])
        diag = {}
        starts = [(lo, half + lo) for lo, _ in bounds] + [(half + q2, q2), (half, 0)]
        for step, start in enumerate(starts):
            caches, (got_y, got_x) = after(caches, from_y[step], from_x[step])
            other_y, other_x = swap(got_y, 1), swap(got_x, 1)
            if step < 3:
                diag[step] = (swap(got_y, 2), swap(got_x, 4))
            caches = run([[(got_y, 0), (got_x, 0)], [(other_y, 0), (other_x, 0)]], got_y.shape[0],
                         [[4, 2], [5, 3]], [list(start)] * 2, caches)
        for step in (2, 1, 0):
            caches, (via_x, via_y) = after(caches, *diag[step])
            other_x, other_y = swap(via_x, 1), swap(via_y, 1)
            caches = run([[(via_x, 0), (via_y, 0)], [(other_x, 0), (other_y, 0)]], via_x.shape[0],
                         [[6] * 2, [7] * 2], [list(starts[step])] * 2, caches)

        k_cache, v_cache, stats = caches
        dec_hidden, last_hidden = tail_call(n_dev, stats, self_stat, x_mine, gain_mlp, w_o[0],
                                            w_gate[0].T, w_up[0].T, w_down[0], n_batch)
        return dec_hidden, last_hidden, k_cache[None], v_cache[None]

    return jax.shard_map(per_device, mesh=mesh, in_specs=in_specs, out_specs=out_specs, check_vma=False)
```

time: 392 us -> 409 us (1.043)
  waiting for transfers between devices: 117 us -> 195 us
  Pallas kernels: 204 us -> 163 us
  local copies, waits for them, and re-layouts: 30.6 us -> 16.4 us
  matrix products: 12.1 us -> 4.59 us
    ppermute x33 -> x37, waiting for transfers between devices: 117 us -> 195 us  [swap(): return lax.ppermute(arr, 'model', [(i, i ^ bit) for i in range(n_dev)])]
    pallas_call x8 -> x13, Pallas kernels: 177 us -> 137 us  [the longest x9 121 us: kv_call(): pl.pallas_call(functools.partial(kv_kernel, n_in, masks, batches, [[first...]
    dot_general x2 -> x0, local copies, waits for them, and re-layouts: 12.7 us -> none  [the longest x1 6.34 us: per_device(): jnp.dot(n_rows[:n_batch], wk, preferred_element_type=jnp.float32)]
    dot_general x3 -> x0, matrix products: 7.38 us -> none  [the longest x1 3.37 us: per_device(): jnp.dot(n_rows, wq, preferred_element_type=jnp.float32)]
    slice x5 -> x1, local copies, waits for them, and re-layouts: 8.68 us -> 4.02 us  [per_device(): send_part(4, normed[half:half + q2], normed[:q2])]
    unnamed x37 -> x26, local copies, waits for them, and re-layouts: 7.84 us -> 12.3 us
    ppermute x33 -> x37, starting transfers between devices: 23.3 us -> 24.5 us  [swap(): return lax.ppermute(arr, 'model', [(i, i ^ bit) for i in range(n_dev)])]
  transfers between devices with their start and end apart: 33 -> 37, of which waited for: 18 -> 28; matrix products, arithmetic and copies ran while one was open for 10% -> 3% of each run, Pallas kernels for 42% -> 30%
where the time goes in v3:
time: 409 us; the launch traced here: 408 us
  waiting for transfers between devices  195 us (48%)
  Pallas kernels  163 us (40%)
  starting transfers between devices  24.5 us (6%)
  local copies, waits for them, and re-layouts  16.4 us (4%)
  matrix products  4.59 us (1%)
    ppermute x37, waiting for transfers between devices, swap(): return lax.ppermute(arr, 'model', [(i, i ^ bit) for i in range(n_dev)])  195 us
    pallas_call x9, Pallas kernels, kv_call(): pl.pallas_call(functools.partial(kv_kernel, n_in, masks, batches, [[first...  121 us
    pallas_call x1, Pallas kernels, tail_call(): pl.pallas_call(functools.partial(tail_kernel, n_dev, n_part), out_shape=[...  26.5 us
    ppermute x37, starting transfers between devices, swap(): return lax.ppermute(arr, 'model', [(i, i ^ bit) for i in range(n_dev)])  24.5 us
    unnamed x26, local copies, waits for them, and re-layouts  12.3 us
    pallas_call x2, Pallas kernels, norm_call(): pl.pallas_call(functools.partial(norm_kernel, outs_of), grid=(len(order),...  8.98 us
  transfers between devices with their start and end apart: 37, of which 28 were waited for; matrix products, arithmetic and copies ran while one was open for 3% of the time, Pallas kernels for 30%

profile of v3, /device:TPU:0, one launch (start us, length us, event | category | flops | bytes accessed | tf_op | source)
XLA Modules:
  0.0 408.3 jit_solution(10632099860119173258)
XLA Ops:
  1.4 3.4 copy-done
  4.8 7.3 %norm_rows.2 = (bf16[1,128,4096]{2,1,0:T(8,128)(2,1)S(1)}, bf16[1,128,4096]{2,1,0:T(8,128)(2,1)S(1)}, bf16[2,128,4096]{2,1,0:T(8,128)(2,1)S(1)}, bf16[2,128,4096]{2,1,0:T(8,128)(2,1)S(1)}, bf16[8,128,4096]{2,1,0:T(8,128)(2,1)}) custom-call(bf16[8,128,4096]{2,1,0:T(8,128)(2,1)S(1)} %copy-done, f32[1,4096]{1,0:T(1,128)S(1)} %convert_element_type.34.gain_ref), custom_call_target="tpu_custom_call" | custom-call | flops 33554432 | bytes 25165824 | tf_op jit(solution)/shard_map/norm_rows/pallas_call | solution.py:114
  16.4 4.6 %fusion.2 = bf16[8,1,4096]{2,1,0:T(2,128)(2,1)S(1)} fusion(bf16[8,128,4096]{2,1,0:T(8,128)(2,1)} %x_ref.3, pred[8,128,1]{1,0,2:T(8,128)(4,1)S(1)} %compare_bitcast_fusion), kind=kOutput, calls=%fused_computation.10 | convolution fusion | flops 8388608 | bytes 8455168 | tf_op jit(solution)/shard_map/bs,bsd->bd/dot_general | solution.py:572
  21.1 3.4 copy-done.1
  24.4 1.6 norm_rows.3
  27.1 3.0 collective-permute-start.5
  30.2 1.9 fusion
  34.2 1.5 collective-permute-start.2
  36.3 2.1 collective-permute-done.3
  39.6 16.8 %collective-permute-done.2 = bf16[8,4096]{1,0:T(8,128)(2,1)S(1)} collective-permute-done((bf16[8,4096]{1,0:T(8,128)(2,1)S(1)}, bf16[8,4096]{1,0:T(8,128)(2,1)S(1)}, u32[]{:S(2)}, u32[]{:S(2)}) %collective-permute-start.2) | collective-permute-done | bytes 65568 | tf_op jit(solution)/shard_map/ppermute | solution.py:546
  56.5 3.5 keep.1
  60.0 3.7 query_rows.1
  63.7 29.0 %kv_chunk.9 = (bf16[8,1025,4,128]{3,2,1,0:T(4,128)(2,1)}, bf16[8,1025,4,128]{3,2,1,0:T(4,128)(2,1)}, f32[8,8,3,8,128]{4,3,2,1,0:T(8,128)S(1)}) custom-call(s32[16]{0:T(128)S(1)} %get-tuple-element.80.sc_ref, bf16[8,128,4096]{2,1,0:T(8,128)(2,1)} %get-tuple-element.81.refs_0_.refs_1_, bf16[8,128,4096]{2,1,0:T(8,128)(2,1)} %get-tuple-element.81.refs_0_.refs_1_, ...), custom_call_target="tpu_custom_call" | custom-call | flops 17179869184 | bytes 20971520 | tf_op jit(solution)/shard_map/kv_chunk/pallas_call | solution.py:364
  93.3 1.7 collective-permute-start.9
  95.1 1.5 collective-permute-start.10
  97.4 8.1 %kv_chunk.10 = (bf16[8,1025,4,128]{3,2,1,0:T(4,128)(2,1)}, bf16[8,1025,4,128]{3,2,1,0:T(4,128)(2,1)}, f32[8,8,3,8,128]{4,3,2,1,0:T(8,128)S(1)}) custom-call(s32[16]{0:T(128)S(1)} %get-tuple-element.80.sc_ref, bf16[1,128,4096]{2,1,0:T(8,128)(2,1)S(1)} %collective-permute-done.5.refs_0_, ...), custom_call_target="tpu_custom_call", output_to_operand_aliasing={{0}: (12, {}), {1}: (13, {}), {2}: (14, {})} | custom-call | flops 4294967296 | bytes 5242880 | tf_op jit(solution)/shard_map/kv_chunk/pallas_call | solution.py:364
  105.5 13.8 %collective-permute-done.9.refs_0_ = bf16[1,128,4096]{2,1,0:T(8,128)(2,1)S(1)} collective-permute-done((bf16[1,128,4096]{2,1,0:T(8,128)(2,1)S(1)}, bf16[1,128,4096]{2,1,0:T(8,128)(2,1)S(1)}, u32[]{:S(2)}, u32[]{:S(2)}) %collective-permute-start.9) | collective-permute-done | bytes 1048608 | tf_op jit(solution)/shard_map/ppermute | solution.py:546
  119.4 1.7 collective-permute-done.10.refs_1_
  121.6 2.1 collective-permute-done.11.refs_2_
  123.8 1.5 collective-permute-done.12.refs_3_
  125.3 8.1 %kv_chunk.11 = (bf16[8,1025,4,128]{3,2,1,0:T(4,128)(2,1)}, bf16[8,1025,4,128]{3,2,1,0:T(4,128)(2,1)}, f32[8,8,3,8,128]{4,3,2,1,0:T(8,128)S(1)}) custom-call(s32[16]{0:T(128)S(1)} %get-tuple-element.80.sc_ref, bf16[1,128,4096]{2,1,0:T(8,128)(2,1)S(1)} %collective-permute-done.9.refs_0_, ...), custom_call_target="tpu_custom_call", output_to_operand_aliasing={{0}: (12, {}), {1}: (13, {}), {2}: (14, {})} | custom-call | flops 4294967296 | bytes 5242880 | tf_op jit(solution)/shard_map/kv_chunk/pallas_call | solution.py:364
  133.4 30.0 %collective-permute-done.13.refs_0_ = bf16[2,128,4096]{2,1,0:T(8,128)(2,1)S(1)} collective-permute-done((bf16[2,128,4096]{2,1,0:T(8,128)(2,1)S(1)}, bf16[2,128,4096]{2,1,0:T(8,128)(2,1)S(1)}, u32[]{:S(2)}, u32[]{:S(2)}) %collective-permute-start.13) | collective-permute-done | bytes 2097184 | tf_op jit(solution)/shard_map/ppermute | solution.py:546
  165.3 1.5 collective-permute-start.18
  167.3 1.7 collective-permute-done.15.refs_2_
  169.0 3.0 collective-permute-done.16.refs_3_
  172.0 15.0 %kv_chunk.12 = (bf16[8,1025,4,128]{3,2,1,0:T(4,128)(2,1)}, bf16[8,1025,4,128]{3,2,1,0:T(4,128)(2,1)}, f32[8,8,3,8,128]{4,3,2,1,0:T(8,128)S(1)}) custom-call(s32[16]{0:T(128)S(1)} %get-tuple-element.80.sc_ref, bf16[2,128,4096]{2,1,0:T(8,128)(2,1)S(1)} %collective-permute-done.13.refs_0_, ...), custom_call_target="tpu_custom_call", output_to_operand_aliasing={{0}: (12, {}), {1}: (13, {}), {2}: (14, {})} | custom-call | flops 8589934592 | bytes 10485760 | tf_op jit(solution)/shard_map/kv_chunk/pallas_call | solution.py:364
  187.0 25.9 %collective-permute-done.18.refs_1_ = bf16[2,128,4096]{2,1,0:T(8,128)(2,1)S(1)} collective-permute-done((bf16[2,128,4096]{2,1,0:T(8,128)(2,1)S(1)}, bf16[2,128,4096]{2,1,0:T(8,128)(2,1)S(1)}, u32[]{:S(2)}, u32[]{:S(2)}) %collective-permute-start.18) | collective-permute-done | bytes 2097184 | tf_op jit(solution)/shard_map/ppermute | solution.py:546
  214.6 4.0 fusion.14
  219.5 1.8 collective-permute-done.20.refs_3_
  221.3 14.8 %kv_chunk.13 = (bf16[8,1025,4,128]{3,2,1,0:T(4,128)(2,1)}, bf16[8,1025,4,128]{3,2,1,0:T(4,128)(2,1)}, f32[8,8,3,8,128]{4,3,2,1,0:T(8,128)S(1)}) custom-call(s32[16]{0:T(128)S(1)} %get-tuple-element.80.sc_ref, bf16[2,128,4096]{2,1,0:T(8,128)(2,1)S(1)} %collective-permute-done.17.refs_0_, ...), custom_call_target="tpu_custom_call", output_to_operand_aliasing={{0}: (12, {}), {1}: (13, {}), {2}: (14, {})} | custom-call | flops 8589934592 | bytes 10485760 | tf_op jit(solution)/shard_map/kv_chunk/pallas_call | solution.py:364
  236.0 30.3 %collective-permute-done.22.refs_1_ = bf16[2,128,4096]{2,1,0:T(8,128)(2,1)S(1)} collective-permute-done((bf16[2,128,4096]{2,1,0:T(8,128)(2,1)}, bf16[2,128,4096]{2,1,0:T(8,128)(2,1)S(1)}, u32[]{:S(2)}, u32[]{:S(2)}) %collective-permute-start.22) | collective-permute-done | bytes 2097184 | tf_op jit(solution)/shard_map/ppermute | solution.py:546
  266.9 1.5 collective-permute-start.25
  268.9 1.7 collective-permute-done.23.refs_2_
  270.6 3.0 collective-permute-done.24.refs_3_
  273.6 14.8 %kv_chunk.14 = (bf16[8,1025,4,128]{3,2,1,0:T(4,128)(2,1)}, bf16[8,1025,4,128]{3,2,1,0:T(4,128)(2,1)}, f32[8,8,3,8,128]{4,3,2,1,0:T(8,128)S(1)}) custom-call(s32[16]{0:T(128)S(1)} %get-tuple-element.80.sc_ref, bf16[2,128,4096]{2,1,0:T(8,128)(2,1)S(1)} %collective-permute-done.21.refs_0_, ...), custom_call_target="tpu_custom_call", output_to_operand_aliasing={{0}: (12, {}), {1}: (13, {}), {2}: (14, {})} | custom-call | flops 8589934592 | bytes 10485760 | tf_op jit(solution)/shard_map/kv_chunk/pallas_call | solution.py:364
  288.4 26.1 %collective-permute-done.25.refs_0_ = bf16[2,128,4096]{2,1,0:T(8,128)(2,1)S(1)} collective-permute-done((bf16[2,128,4096]{2,1,0:T(8,128)(2,1)S(1)}, bf16[2,128,4096]{2,1,0:T(8,128)(2,1)S(1)}, u32[]{:S(2)}, u32[]{:S(2)}) %collective-permute-start.25) | collective-permute-done | bytes 2097184 | tf_op jit(solution)/shard_map/ppermute | solution.py:546
  317.2 2.7 collective-permute-done.27.refs_2_
  319.8 3.0 collective-permute-done.28.refs_3_
  322.8 14.8 %kv_chunk.15 = (bf16[8,1025,4,128]{3,2,1,0:T(4,128)(2,1)}, bf16[8,1025,4,128]{3,2,1,0:T(4,128)(2,1)}, f32[8,8,3,8,128]{4,3,2,1,0:T(8,128)S(1)}) custom-call(s32[16]{0:T(128)S(1)} %get-tuple-element.80.sc_ref, bf16[2,128,4096]{2,1,0:T(8,128)(2,1)S(1)} %collective-permute-done.25.refs_0_, ...), custom_call_target="tpu_custom_call", output_to_operand_aliasing={{0}: (12, {}), {1}: (13, {}), {2}: (14, {})} | custom-call | flops 8589934592 | bytes 10485760 | tf_op jit(solution)/shard_map/kv_chunk/pallas_call | solution.py:364
  337.6 3.6 collective-permute-done.29.refs_0_
  342.0 1.5 collective-permute-start.33
  344.2 1.5 collective-permute-done.32.refs_3_
  345.7 8.1 %kv_chunk.16 = (bf16[8,1025,4,128]{3,2,1,0:T(4,128)(2,1)}, bf16[8,1025,4,128]{3,2,1,0:T(4,128)(2,1)}, f32[8,8,3,8,128]{4,3,2,1,0:T(8,128)S(1)}) custom-call(s32[16]{0:T(128)S(1)} %get-tuple-element.80.sc_ref, bf16[1,128,4096]{2,1,0:T(8,128)(2,1)S(1)} %collective-permute-done.29.refs_0_, ...), custom_call_target="tpu_custom_call", output_to_operand_aliasing={{0}: (12, {}), {1}: (13, {}), {2}: (14, {})} | custom-call | flops 4294967296 | bytes 5242880 | tf_op jit(solution)/shard_map/kv_chunk/pallas_call | solution.py:364
  353.8 13.3 %collective-permute-done.33.refs_0_ = bf16[1,128,4096]{2,1,0:T(8,128)(2,1)S(1)} collective-permute-done((bf16[1,128,4096]{2,1,0:T(8,128)(2,1)S(1)}, bf16[1,128,4096]{2,1,0:T(8,128)(2,1)S(1)}, u32[]{:S(2)}, u32[]{:S(2)}) %collective-permute-start.33) | collective-permute-done | bytes 1048608 | tf_op jit(solution)/shard_map/ppermute | solution.py:546
  368.8 2.1 collective-permute-done.35.refs_2_
  371.0 1.5 collective-permute-done.36.refs_3_
  372.5 8.1 %kv_chunk.17 = (bf16[8,1025,4,128]{3,2,1,0:T(4,128)(2,1)}, bf16[8,1025,4,128]{3,2,1,0:T(4,128)(2,1)}, f32[8,8,3,8,128]{4,3,2,1,0:T(8,128)S(1)}) custom-call(s32[16]{0:T(128)S(1)} %get-tuple-element.80.sc_ref, bf16[1,128,4096]{2,1,0:T(8,128)(2,1)S(1)} %collective-permute-done.33.refs_0_, ...), custom_call_target="tpu_custom_call", output_to_operand_aliasing={{0}: (12, {}), {1}: (13, {}), {2}: (14, {})} | custom-call | flops 4294967296 | bytes 5242880 | tf_op jit(solution)/shard_map/kv_chunk/pallas_call | solution.py:364
  380.6 26.5 %tail.1 = (bf16[8,4096]{1,0:T(8,128)(2,1)S(1)}, bf16[8,4096]{1,0:T(8,128)(2,1)S(1)}) custom-call(f32[8,8,3,8,128]{4,3,2,1,0:T(8,128)S(1)} %get-tuple-element.148.st_ref, f32[3,8,8,128]{3,2,1,0:T(8,128)S(1)} %get-tuple-element.149.self_ref, bf16[16,512]{1,0:T(8,128)(2,1)S(1)} %fusion.1.xs_ref, f32[1,4096]{1,0:T(1,128)S(1)} %convert_element_type.33.gain_ref, ...), custom_call_target="tpu_custom_call" | custom-call | tf_op jit(solution)/shard_map/tail/pallas_call | solution.py:502
  (85 shorter events, 25.1 us)
Async XLA Ops:
  0.6 15.6 %copy-start.11 = (s32[8]{0:T(128)S(1)}, s32[8]{0:T(128)}, u32[]{:S(2)}) copy-start(s32[8]{0:T(128)} %param.13) | copy-start | bytes 100
  1.4 3.4 copy-start
  12.1 1.3 copy-start.3
  14.4 1.0 copy-start.7
  15.4 48.3 %collective-permute-start.4 = (bf16[8,128,4096]{2,1,0:T(8,128)(2,1)}, bf16[8,128,4096]{2,1,0:T(8,128)(2,1)}, u32[]{:S(2)}, u32[]{:S(2)}) collective-permute-start(bf16[8,128,4096]{2,1,0:T(8,128)(2,1)} %get-tuple-element.81.refs_0_.refs_1_), channel_id=1, source_target_pairs={{0,1},{1,0},{2,3},{3,2},{4,5},{5,4},{6,7},{7,6}} | collective-permute-start | bytes 25165832 | tf_op jit(solution)/shard_map/ppermute | solution.py:546
  16.4 13.7 %copy-start.10 = (bf16[1,4096]{1,0:T(2,128)(2,1)S(1)}, bf16[1,4096]{1,0:T(2,128)(2,1)}, u32[]{:S(2)}) copy-start(bf16[1,4096]{1,0:T(2,128)(2,1)} %param.20) | copy-start | bytes 24580
  20.9 35.5 %copy-start.2 = (bf16[8,4096]{1,0:T(8,128)(2,1)S(1)}, bf16[8,4096]{1,0:T(8,128)(2,1)}, u32[]{:S(2)}) copy-start(bf16[8,4096]{1,0:T(8,128)(2,1)} %new_ref.1) | copy-start | bytes 196612
  21.0 11.6 %collective-permute-start = (bf16[8,4096]{1,0:T(8,128)(2,1)S(1)}, bf16[8,4096]{1,0:T(8,128)(2,1)S(1)}, u32[]{:S(2)}, u32[]{:S(2)}) collective-permute-start(bf16[8,4096]{1,0:T(8,128)(2,1)S(1)} %bitcast.30), channel_id=1, source_target_pairs={{0,1},{1,0},{2,3},{3,2},{4,5},{5,4},{6,7},{7,6}} | collective-permute-start | bytes 196616 | tf_op jit(solution)/shard_map/ppermute | solution.py:546
  21.1 3.4 copy-start.1
  26.1 1.0 copy-start.9
  27.1 65.7 %collective-permute-start.5 = (bf16[1,128,4096]{2,1,0:T(8,128)(2,1)}, bf16[1,128,4096]{2,1,0:T(8,128)(2,1)S(1)}, u32[]{:S(2)}, u32[]{:S(2)}) collective-permute-start(bf16[1,128,4096]{2,1,0:T(8,128)(2,1)} %get-tuple-element.95), channel_id=1, source_target_pairs={{0,4},{1,5},{2,6},{3,7},{4,0},{5,1},{6,2},{7,3}} | collective-permute-start | bytes 3145736 | tf_op jit(solution)/shard_map/ppermute | solution.py:546
  32.7 5.7 %collective-permute-start.3 = (bf16[8,4096]{1,0:T(8,128)(2,1)S(1)}, bf16[8,4096]{1,0:T(8,128)(2,1)S(1)}, u32[]{:S(2)}, u32[]{:S(2)}) collective-permute-start(bf16[8,4096]{1,0:T(8,128)(2,1)S(1)} %fusion.16), channel_id=1, source_target_pairs={{0,6},{1,7},{2,4},{3,5},{4,2},{5,3},{6,0},{7,1}} | collective-permute-start | bytes 196616 | tf_op jit(solution)/shard_map/ppermute | solution.py:546
  34.2 22.2 %collective-permute-start.2 = (bf16[8,4096]{1,0:T(8,128)(2,1)S(1)}, bf16[8,4096]{1,0:T(8,128)(2,1)S(1)}, u32[]{:S(2)}, u32[]{:S(2)}) collective-permute-start(bf16[8,4096]{1,0:T(8,128)(2,1)S(1)} %fusion.16), channel_id=1, source_target_pairs={{0,4},{1,5},{2,6},{3,7},{4,0},{5,1},{6,2},{7,3}} | collective-permute-start | bytes 196616 | tf_op jit(solution)/shard_map/ppermute | solution.py:546
  35.7 20.7 %collective-permute-start.1 = (bf16[8,4096]{1,0:T(8,128)(2,1)S(1)}, bf16[8,4096]{1,0:T(8,128)(2,1)S(1)}, u32[]{:S(2)}, u32[]{:S(2)}) collective-permute-start(bf16[8,4096]{1,0:T(8,128)(2,1)S(1)} %fusion.16), channel_id=1, source_target_pairs={{0,2},{1,3},{2,0},{3,1},{4,6},{5,7},{6,4},{7,5}} | collective-permute-start | bytes 196616 | tf_op jit(solution)/shard_map/ppermute | solution.py:546
  38.4 54.4 %collective-permute-start.6 = (bf16[1,128,4096]{2,1,0:T(8,128)(2,1)}, bf16[1,128,4096]{2,1,0:T(8,128)(2,1)S(1)}, u32[]{:S(2)}, u32[]{:S(2)}) collective-permute-start(bf16[1,128,4096]{2,1,0:T(8,128)(2,1)} %copy-done.9), channel_id=1, source_target_pairs={{0,2},{1,3},{2,0},{3,1},{4,6},{5,7},{6,4},{7,5}} | collective-permute-start | bytes 3145736 | tf_op jit(solution)/shard_map/ppermute | solution.py:546
  63.7 29.6 %copy-start.8 = (bf16[1,128,4096]{2,1,0:T(8,128)(2,1)S(1)}, bf16[1,128,4096]{2,1,0:T(8,128)(2,1)}, u32[]{:S(2)}) copy-start(bf16[1,128,4096]{2,1,0:T(8,128)(2,1)} %copy-done.7) | copy-start | bytes 3145732
  63.7 31.4 %copy-start.6 = (bf16[1,128,4096]{2,1,0:T(8,128)(2,1)S(1)}, bf16[1,128,4096]{2,1,0:T(8,128)(2,1)}, u32[]{:S(2)}) copy-start(bf16[1,128,4096]{2,1,0:T(8,128)(2,1)} %copy-done.5) | copy-start | bytes 3145732
  63.7 32.9 %copy-start.4 = (bf16[2,128,4096]{2,1,0:T(8,128)(2,1)S(1)}, bf16[2,128,4096]{2,1,0:T(8,128)(2,1)}, u32[]{:S(2)}) copy-start(bf16[2,128,4096]{2,1,0:T(8,128)(2,1)} %copy-done.3) | copy-start | bytes 6291460
  92.8 4.3 %collective-permute-start.7 = (bf16[1,128,4096]{2,1,0:T(8,128)(2,1)S(1)}, bf16[1,128,4096]{2,1,0:T(8,128)(2,1)S(1)}, u32[]{:S(2)}, u32[]{:S(2)}) collective-permute-start(bf16[1,128,4096]{2,1,0:T(8,128)(2,1)S(1)} %collective-permute-done.5.refs_0_), channel_id=1, source_target_pairs={{0,1},{1,0},{2,3},{3,2},{4,5},{5,4},{6,7},{7,6}} | collective-permute-start | bytes 3145736 | tf_op jit(solution)/shard_map/ppermute | solution.py:546
  92.8 4.6 %collective-permute-start.8 = (bf16[1,128,4096]{2,1,0:T(8,128)(2,1)S(1)}, bf16[1,128,4096]{2,1,0:T(8,128)(2,1)S(1)}, u32[]{:S(2)}, u32[]{:S(2)}) collective-permute-start(bf16[1,128,4096]{2,1,0:T(8,128)(2,1)S(1)} %collective-permute-done.6.refs_1_), channel_id=1, source_target_pairs={{0,1},{1,0},{2,3},{3,2},{4,5},{5,4},{6,7},{7,6}} | collective-permute-start | bytes 3145736 | tf_op jit(solution)/shard_map/ppermute | solution.py:546
  93.3 26.0 %collective-permute-start.9 = (bf16[1,128,4096]{2,1,0:T(8,128)(2,1)S(1)}, bf16[1,128,4096]{2,1,0:T(8,128)(2,1)S(1)}, u32[]{:S(2)}, u32[]{:S(2)}) collective-permute-start(bf16[1,128,4096]{2,1,0:T(8,128)(2,1)S(1)} %copy-done.8), channel_id=1, source_target_pairs={{0,4},{1,5},{2,6},{3,7},{4,0},{5,1},{6,2},{7,3}} | collective-permute-start | bytes 3145736 | tf_op jit(solution)/shard_map/ppermute | solution.py:546
  95.1 26.0 %collective-permute-start.10 = (bf16[1,128,4096]{2,1,0:T(8,128)(2,1)S(1)}, bf16[1,128,4096]{2,1,0:T(8,128)(2,1)S(1)}, u32[]{:S(2)}, u32[]{:S(2)}) collective-permute-start(bf16[1,128,4096]{2,1,0:T(8,128)(2,1)S(1)} %copy-done.6), channel_id=1, source_target_pairs={{0,2},{1,3},{2,0},{3,1},{4,6},{5,7},{6,4},{7,5}} | collective-permute-start | bytes 3145736 | tf_op jit(solution)/shard_map/ppermute | solution.py:546
  96.6 66.8 %collective-permute-start.13 = (bf16[2,128,4096]{2,1,0:T(8,128)(2,1)S(1)}, bf16[2,128,4096]{2,1,0:T(8,128)(2,1)S(1)}, u32[]{:S(2)}, u32[]{:S(2)}) collective-permute-start(bf16[2,128,4096]{2,1,0:T(8,128)(2,1)S(1)} %copy-done.4), channel_id=1, source_target_pairs={{0,4},{1,5},{2,6},{3,7},{4,0},{5,1},{6,2},{7,3}} | collective-permute-start | bytes 6291464 | tf_op jit(solution)/shard_map/ppermute | solution.py:546
  97.1 67.8 %collective-permute-start.14 = (bf16[2,128,4096]{2,1,0:T(8,128)(2,1)S(1)}, bf16[2,128,4096]{2,1,0:T(8,128)(2,1)S(1)}, u32[]{:S(2)}, u32[]{:S(2)}) collective-permute-start(bf16[2,128,4096]{2,1,0:T(8,128)(2,1)S(1)} %get-tuple-element.112), channel_id=1, source_target_pairs={{0,2},{1,3},{2,0},{3,1},{4,6},{5,7},{6,4},{7,5}} | collective-permute-start | bytes 6291464 | tf_op jit(solution)/shard_map/ppermute | solution.py:546
  121.1 2.7 collective-permute-start.11
  121.1 4.2 %collective-permute-start.12 = (bf16[1,128,4096]{2,1,0:T(8,128)(2,1)S(1)}, bf16[1,128,4096]{2,1,0:T(8,128)(2,1)S(1)}, u32[]{:S(2)}, u32[]{:S(2)}) collective-permute-start(bf16[1,128,4096]{2,1,0:T(8,128)(2,1)S(1)} %collective-permute-done.10.refs_1_), channel_id=1, source_target_pairs={{0,1},{1,0},{2,3},{3,2},{4,5},{5,4},{6,7},{7,6}} | collective-permute-start | bytes 3145736 | tf_op jit(solution)/shard_map/ppermute | solution.py:546
  164.8 4.2 %collective-permute-start.15 = (bf16[2,128,4096]{2,1,0:T(8,128)(2,1)S(1)}, bf16[2,128,4096]{2,1,0:T(8,128)(2,1)S(1)}, u32[]{:S(2)}, u32[]{:S(2)}) collective-permute-start(bf16[2,128,4096]{2,1,0:T(8,128)(2,1)S(1)} %collective-permute-done.13.refs_0_), channel_id=1, source_target_pairs={{0,1},{1,0},{2,3},{3,2},{4,5},{5,4},{6,7},{7,6}} | collective-permute-start | bytes 6291464 | tf_op jit(solution)/shard_map/ppermute | solution.py:546
  164.8 7.2 %collective-permute-start.16 = (bf16[2,128,4096]{2,1,0:T(8,128)(2,1)S(1)}, bf16[2,128,4096]{2,1,0:T(8,128)(2,1)S(1)}, u32[]{:S(2)}, u32[]{:S(2)}) collective-permute-start(bf16[2,128,4096]{2,1,0:T(8,128)(2,1)S(1)} %collective-permute-done.14.refs_1_), channel_id=1, source_target_pairs={{0,1},{1,0},{2,3},{3,2},{4,5},{5,4},{6,7},{7,6}} | collective-permute-start | bytes 6291464 | tf_op jit(solution)/shard_map/ppermute | solution.py:546
  165.3 47.5 %collective-permute-start.18 = (bf16[2,128,4096]{2,1,0:T(8,128)(2,1)S(1)}, bf16[2,128,4096]{2,1,0:T(8,128)(2,1)S(1)}, u32[]{:S(2)}, u32[]{:S(2)}) collective-permute-start(bf16[2,128,4096]{2,1,0:T(8,128)(2,1)S(1)} %copy-done.4), channel_id=1, source_target_pairs={{0,2},{1,3},{2,0},{3,1},{4,6},{5,7},{6,4},{7,5}} | collective-permute-start | bytes 6291464 | tf_op jit(solution)/shard_map/ppermute | solution.py:546
  166.8 47.3 %collective-permute-start.17 = (bf16[2,128,4096]{2,1,0:T(8,128)(2,1)S(1)}, bf16[2,128,4096]{2,1,0:T(8,128)(2,1)S(1)}, u32[]{:S(2)}, u32[]{:S(2)}) collective-permute-start(bf16[2,128,4096]{2,1,0:T(8,128)(2,1)S(1)} %get-tuple-element.112), channel_id=1, source_target_pairs={{0,4},{1,5},{2,6},{3,7},{4,0},{5,1},{6,2},{7,3}} | collective-permute-start | bytes 6291464 | tf_op jit(solution)/shard_map/ppermute | solution.py:546
  214.1 5.4 %collective-permute-start.19 = (bf16[2,128,4096]{2,1,0:T(8,128)(2,1)S(1)}, bf16[2,128,4096]{2,1,0:T(8,128)(2,1)S(1)}, u32[]{:S(2)}, u32[]{:S(2)}) collective-permute-start(bf16[2,128,4096]{2,1,0:T(8,128)(2,1)S(1)} %collective-permute-done.17.refs_0_), channel_id=1, source_target_pairs={{0,1},{1,0},{2,3},{3,2},{4,5},{5,4},{6,7},{7,6}} | collective-permute-start | bytes 6291464 | tf_op jit(solution)/shard_map/ppermute | solution.py:546
  214.1 7.2 %collective-permute-start.20 = (bf16[2,128,4096]{2,1,0:T(8,128)(2,1)S(1)}, bf16[2,128,4096]{2,1,0:T(8,128)(2,1)S(1)}, u32[]{:S(2)}, u32[]{:S(2)}) collective-permute-start(bf16[2,128,4096]{2,1,0:T(8,128)(2,1)S(1)} %collective-permute-done.18.refs_1_), channel_id=1, source_target_pairs={{0,1},{1,0},{2,3},{3,2},{4,5},{5,4},{6,7},{7,6}} | collective-permute-start | bytes 6291464 | tf_op jit(solution)/shard_map/ppermute | solution.py:546
  218.6 47.7 %collective-permute-start.22 = (bf16[2,128,4096]{2,1,0:T(8,128)(2,1)}, bf16[2,128,4096]{2,1,0:T(8,128)(2,1)S(1)}, u32[]{:S(2)}, u32[]{:S(2)}) collective-permute-start(bf16[2,128,4096]{2,1,0:T(8,128)(2,1)} %get-tuple-element.156), channel_id=1, source_target_pairs={{0,2},{1,3},{2,0},{3,1},{4,6},{5,7},{6,4},{7,5}} | collective-permute-start | bytes 6291464 | tf_op jit(solution)/shard_map/ppermute | solution.py:546
  219.2 47.3 %collective-permute-start.21 = (bf16[2,128,4096]{2,1,0:T(8,128)(2,1)S(1)}, bf16[2,128,4096]{2,1,0:T(8,128)(2,1)S(1)}, u32[]{:S(2)}, u32[]{:S(2)}) collective-permute-start(bf16[2,128,4096]{2,1,0:T(8,128)(2,1)S(1)} %get-tuple-element.157), channel_id=1, source_target_pairs={{0,4},{1,5},{2,6},{3,7},{4,0},{5,1},{6,2},{7,3}} | collective-permute-start | bytes 6291464 | tf_op jit(solution)/shard_map/ppermute | solution.py:546
  266.4 4.2 %collective-permute-start.23 = (bf16[2,128,4096]{2,1,0:T(8,128)(2,1)S(1)}, bf16[2,128,4096]{2,1,0:T(8,128)(2,1)S(1)}, u32[]{:S(2)}, u32[]{:S(2)}) collective-permute-start(bf16[2,128,4096]{2,1,0:T(8,128)(2,1)S(1)} %collective-permute-done.21.refs_0_), channel_id=1, source_target_pairs={{0,1},{1,0},{2,3},{3,2},{4,5},{5,4},{6,7},{7,6}} | collective-permute-start | bytes 6291464 | tf_op jit(solution)/shard_map/ppermute | solution.py:546
  266.4 7.2 %collective-permute-start.24 = (bf16[2,128,4096]{2,1,0:T(8,128)(2,1)S(1)}, bf16[2,128,4096]{2,1,0:T(8,128)(2,1)S(1)}, u32[]{:S(2)}, u32[]{:S(2)}) collective-permute-start(bf16[2,128,4096]{2,1,0:T(8,128)(2,1)S(1)} %collective-permute-done.22.refs_1_), channel_id=1, source_target_pairs={{0,1},{1,0},{2,3},{3,2},{4,5},{5,4},{6,7},{7,6}} | collective-permute-start | bytes 6291464 | tf_op jit(solution)/shard_map/ppermute | solution.py:546
  266.9 47.5 %collective-permute-start.25 = (bf16[2,128,4096]{2,1,0:T(8,128)(2,1)S(1)}, bf16[2,128,4096]{2,1,0:T(8,128)(2,1)S(1)}, u32[]{:S(2)}, u32[]{:S(2)}) collective-permute-start(bf16[2,128,4096]{2,1,0:T(8,128)(2,1)S(1)} %collective-permute-done.13.refs_0_), channel_id=1, source_target_pairs={{0,2},{1,3},{2,0},{3,1},{4,6},{5,7},{6,4},{7,5}} | collective-permute-start | bytes 6291464 | tf_op jit(solution)/shard_map/ppermute | solution.py:546
  268.4 47.3 %collective-permute-start.26 = (bf16[2,128,4096]{2,1,0:T(8,128)(2,1)S(1)}, bf16[2,128,4096]{2,1,0:T(8,128)(2,1)S(1)}, u32[]{:S(2)}, u32[]{:S(2)}) collective-permute-start(bf16[2,128,4096]{2,1,0:T(8,128)(2,1)S(1)} %collective-permute-done.14.refs_1_), channel_id=1, source_target_pairs={{0,4},{1,5},{2,6},{3,7},{4,0},{5,1},{6,2},{7,3}} | collective-permute-start | bytes 6291464 | tf_op jit(solution)/shard_map/ppermute | solution.py:546
  315.7 4.2 %collective-permute-start.27 = (bf16[2,128,4096]{2,1,0:T(8,128)(2,1)S(1)}, bf16[2,128,4096]{2,1,0:T(8,128)(2,1)S(1)}, u32[]{:S(2)}, u32[]{:S(2)}) collective-permute-start(bf16[2,128,4096]{2,1,0:T(8,128)(2,1)S(1)} %collective-permute-done.25.refs_0_), channel_id=1, source_target_pairs={{0,1},{1,0},{2,3},{3,2},{4,5},{5,4},{6,7},{7,6}} | collective-permute-start | bytes 6291464 | tf_op jit(solution)/shard_map/ppermute | solution.py:546
  315.7 7.2 %collective-permute-start.28 = (bf16[2,128,4096]{2,1,0:T(8,128)(2,1)S(1)}, bf16[2,128,4096]{2,1,0:T(8,128)(2,1)S(1)}, u32[]{:S(2)}, u32[]{:S(2)}) collective-permute-start(bf16[2,128,4096]{2,1,0:T(8,128)(2,1)S(1)} %collective-permute-done.26.refs_1_), channel_id=1, source_target_pairs={{0,1},{1,0},{2,3},{3,2},{4,5},{5,4},{6,7},{7,6}} | collective-permute-start | bytes 6291464 | tf_op jit(solution)/shard_map/ppermute | solution.py:546
  316.2 25.1 %collective-permute-start.29 = (bf16[1,128,4096]{2,1,0:T(8,128)(2,1)S(1)}, bf16[1,128,4096]{2,1,0:T(8,128)(2,1)S(1)}, u32[]{:S(2)}, u32[]{:S(2)}) collective-permute-start(bf16[1,128,4096]{2,1,0:T(8,128)(2,1)S(1)} %collective-permute-done.9.refs_0_), channel_id=1, source_target_pairs={{0,2},{1,3},{2,0},{3,1},{4,6},{5,7},{6,4},{7,5}} | collective-permute-start | bytes 3145736 | tf_op jit(solution)/shard_map/ppermute | solution.py:546
  316.7 24.8 %collective-permute-start.30 = (bf16[1,128,4096]{2,1,0:T(8,128)(2,1)S(1)}, bf16[1,128,4096]{2,1,0:T(8,128)(2,1)S(1)}, u32[]{:S(2)}, u32[]{:S(2)}) collective-permute-start(bf16[1,128,4096]{2,1,0:T(8,128)(2,1)S(1)} %collective-permute-done.10.refs_1_), channel_id=1, source_target_pairs={{0,4},{1,5},{2,6},{3,7},{4,0},{5,1},{6,2},{7,3}} | collective-permute-start | bytes 3145736 | tf_op jit(solution)/shard_map/ppermute | solution.py:546
  341.5 2.7 collective-permute-start.31
  341.5 4.2 %collective-permute-start.32 = (bf16[1,128,4096]{2,1,0:T(8,128)(2,1)S(1)}, bf16[1,128,4096]{2,1,0:T(8,128)(2,1)S(1)}, u32[]{:S(2)}, u32[]{:S(2)}) collective-permute-start(bf16[1,128,4096]{2,1,0:T(8,128)(2,1)S(1)} %collective-permute-done.30.refs_1_), channel_id=1, source_target_pairs={{0,1},{1,0},{2,3},{3,2},{4,5},{5,4},{6,7},{7,6}} | collective-permute-start | bytes 3145736 | tf_op jit(solution)/shard_map/ppermute | solution.py:546
  342.0 25.1 %collective-permute-start.33 = (bf16[1,128,4096]{2,1,0:T(8,128)(2,1)S(1)}, bf16[1,128,4096]{2,1,0:T(8,128)(2,1)S(1)}, u32[]{:S(2)}, u32[]{:S(2)}) collective-permute-start(bf16[1,128,4096]{2,1,0:T(8,128)(2,1)S(1)} %collective-permute-done.5.refs_0_), channel_id=1, source_target_pairs={{0,2},{1,3},{2,0},{3,1},{4,6},{5,7},{6,4},{7,5}} | collective-permute-start | bytes 3145736 | tf_op jit(solution)/shard_map/ppermute | solution.py:546
  343.5 24.8 %collective-permute-start.34 = (bf16[1,128,4096]{2,1,0:T(8,128)(2,1)S(1)}, bf16[1,128,4096]{2,1,0:T(8,128)(2,1)S(1)}, u32[]{:S(2)}, u32[]{:S(2)}) collective-permute-start(bf16[1,128,4096]{2,1,0:T(8,128)(2,1)S(1)} %collective-permute-done.6.refs_1_), channel_id=1, source_target_pairs={{0,4},{1,5},{2,6},{3,7},{4,0},{5,1},{6,2},{7,3}} | collective-permute-start | bytes 3145736 | tf_op jit(solution)/shard_map/ppermute | solution.py:546
  368.3 2.7 collective-permute-start.35
  368.3 4.2 %collective-permute-start.36 = (bf16[1,128,4096]{2,1,0:T(8,128)(2,1)S(1)}, bf16[1,128,4096]{2,1,0:T(8,128)(2,1)S(1)}, u32[]{:S(2)}, u32[]{:S(2)}) collective-permute-start(bf16[1,128,4096]{2,1,0:T(8,128)(2,1)S(1)} %collective-permute-done.34.refs_1_), channel_id=1, source_target_pairs={{0,1},{1,0},{2,3},{3,2},{4,5},{5,4},{6,7},{7,6}} | collective-permute-start | bytes 3145736 | tf_op jit(solution)/shard_map/ppermute | solution.py:546
  (1 other events, 1.0 us)

commit v4 on v3

--- a/solution.py
+++ b/solution.py
@@ -57,8 +57,8 @@
     lanes = [slice(c * HEAD_DIM, (c + 1) * HEAD_DIM) for c in range(d_model // HEAD_DIM)]
 
     def copies(at_step):
-        return [pltpu.make_async_copy(n_buf.at[at_step % 2], out_refs[o].at[i], sems.at[at_step % 2, k])
-                for k, (o, i) in enumerate(outs_of[at_step])]
+        return [pltpu.make_async_copy(n_buf.at[at_step % 2, pl.ds(lo, rows)], out_refs[o].at[i], sems.at[at_step % 2, k])
+                for k, (o, i, lo, rows) in enumerate(outs_of[at_step])]
 
     for at_step in range(2, len(outs_of)):
         @pl.when(step == at_step)
@@ -102,7 +102,7 @@
                         copy.wait()
 
 
-def norm_call(x, gain, order, outs_of, sizes):
+def norm_call(x, gain, order, outs_of, shapes):
     blk, d_model = x.shape[1:]
 
     def prompt_of(g):
@@ -116,8 +116,8 @@
         grid=(len(order),),
         in_specs=[pl.BlockSpec((1, blk, d_model), lambda g: (prompt_of(g), 0, 0)),
                   pl.BlockSpec((1, d_model), lambda g: (0, 0))],
-        out_specs=[pl.BlockSpec(memory_space=pl.ANY)] * len(sizes),
-        out_shape=[jax.ShapeDtypeStruct((size, blk, d_model), jnp.bfloat16) for size in sizes],
+        out_specs=[pl.BlockSpec(memory_space=pl.ANY)] * len(shapes),
+        out_shape=[jax.ShapeDtypeStruct((*shape, d_model), jnp.bfloat16) for shape in shapes],
         scratch_shapes=[
             pltpu.VMEM((blk, HEAD_DIM), jnp.float32),
             pltpu.VMEM((2, blk, d_model), jnp.bfloat16),
@@ -126,7 +126,7 @@
         compiler_params=pltpu.CompilerParams(vmem_limit_bytes=24 * 2 ** 20),
         cost_estimate=pl.CostEstimate(flops=len(order) * blk * d_model * 8, bytes_accessed=len(order) * blk * d_model * 6, transcendentals=0),
         name="norm_rows",
-    )(x, gain)
+    )(pltpu.with_memory_space_constraint(x, pltpu.HBM), gain)
 
 
 def rows_kernel(new_ref, last_ref, gain_ref, cos_ref, sin_ref, wq_hbm, wk, wv, q_ref, k_ref, v_ref, st_ref, wq, q_buf, sem):
@@ -196,14 +196,12 @@
     return out
 
 
-def kv_kernel(n_in, masks, batches, firsts, with_new, sc_ref, *refs):
+def kv_kernel(n_in, masks, batches, firsts, row0, stat_of, with_new, sc_ref, *refs):
     n_groups = len(masks)
     n_arr = n_in * n_groups
     x_refs = refs[:n_arr]
-    cos_refs = refs[n_arr:n_arr + n_in]
-    sin_refs = refs[n_arr + n_in:n_arr + 2 * n_in]
-    wk, wv, q_ref = refs[n_arr + 2 * n_in:n_arr + 2 * n_in + 3]
-    rest = refs[n_arr + 2 * n_in + 3:]
+    cos_ref, sin_ref, wk, wv, q_ref = refs[n_arr:n_arr + 5]
+    rest = refs[n_arr + 5:]
     if with_new:
         new_refs = rest[:2]
         rest = rest[2:]
@@ -215,6 +213,7 @@
     slot = lax.rem(step, 2)
     per_group = n_steps // n_groups
     blk = x_buf.shape[2]
+    shard_rows = cos_ref.shape[1]
     width = wk.shape[1]
     heads = width // HEAD_DIM
     n_tok = n_in * blk
@@ -233,17 +232,17 @@
 
     def place(i, at_step):
         group = at_step // per_group
-        shard = sc_ref[by_group(group, [mask[i] for mask in masks])]
-        return shard, by_group(group, [batch[i] for batch in batches]) + lax.rem(at_step, per_group)
+        mask = by_group(group, [m[i] for m in masks])
+        return sc_ref[mask], by_group(group, [b[i] for b in batches]) + lax.rem(at_step, per_group), mask
 
     def out_copies(which, at_step):
         copies = []
         for i in range(n_in):
-            shard, bat = place(i, at_step)
-            rows = pl.ds(shard * blk, blk)
+            shard, bat, mask = place(i, at_step)
+            rows = pl.ds(shard * shard_rows + row0, blk)
             copies.append(pltpu.make_async_copy(k_out.at[which, i], kc_ref.at[bat, rows], sems.at[which, i, 0]))
             copies.append(pltpu.make_async_copy(v_out.at[which, i], vc_ref.at[bat, rows], sems.at[which, i, 1]))
-            copies.append(pltpu.make_async_copy(s_out.at[which, i], st_ref.at[shard, bat], sems.at[which, i, 2]))
+            copies.append(pltpu.make_async_copy(s_out.at[which, i], st_ref.at[mask + stat_of, bat], sems.at[which, i, 2]))
         return copies
 
     def new_copies():
@@ -278,8 +277,9 @@
         v_buf[:, cols] = vf.astype(jnp.bfloat16)
         parts = []
         for i in range(n_in):
-            cos_tab = cos_refs[i][0]
-            sin_tab = sin_refs[i][0]
+            shard = place(i, step)[0]
+            cos_tab = cos_ref[shard, row0:row0 + blk]
+            sin_tab = sin_ref[shard, row0:row0 + blk]
             halves = []
             for h in range(COL_TILE // HEAD_DIM):
                 kh = kf[i * blk:(i + 1) * blk, h * HEAD_DIM:(h + 1) * HEAD_DIM]
@@ -293,10 +293,10 @@
     head_of_row = lax.broadcasted_iota(jnp.int32, (STAT_ROWS, HEAD_DIM), 0) // (STAT_ROWS // heads)
     probs = []
     for i in range(n_in):
-        shard, bat = place(i, step)
+        shard, bat, _ = place(i, step)
         scores = lax.dot_general(q_ref[bat], k_buf[i * blk:(i + 1) * blk, :], (((1,), (1,)), ((), ())),
                                  preferred_element_type=jnp.float32) * (HEAD_DIM ** -0.5)
-        pos = shard * blk + lax.broadcasted_iota(jnp.int32, scores.shape, 1)
+        pos = shard * shard_rows + row0 + lax.broadcasted_iota(jnp.int32, scores.shape, 1)
         visible = pos < sc_ref[N_MASKS + bat]
         scores = jnp.where(visible, scores, NEG_BIG)
         blk_max = jnp.max(scores, axis=-1, keepdims=True)
@@ -332,7 +332,7 @@
             copy.wait()
 
 
-def kv_call(groups, per_group, masks, batches, scalars, tabs, w_k, w_v, q_diag, caches, new_rows=None):
+def kv_call(groups, per_group, masks, batches, scalars, tabs, w_k, w_v, q_diag, caches, new_rows=None, row0=0, stat_of=0):
     n_groups = len(groups)
     n_in = len(groups[0])
     n_steps = n_groups * per_group
@@ -342,14 +342,8 @@
     heads = width // HEAD_DIM
     any_spec = pl.BlockSpec(memory_space=pl.ANY)
     operands = [arr for group in groups for arr, _ in group]
-    in_specs = [any_spec] * len(operands)
-    for tab in (cos_tab, sin_tab):
-        for i in range(n_in):
-            in_specs.append(pl.BlockSpec((1, blk, HEAD_DIM), lambda g, sc, i=i: (
-                sc[by_group(g // per_group, [mask[i] for mask in masks])], 0, 0)))
-            operands.append(tab)
-    in_specs += [pl.BlockSpec(memory_space=pltpu.VMEM)] * 2 + [pl.BlockSpec(q_diag.shape, lambda g, sc: (0, 0, 0))]
-    operands += [w_k, w_v, q_diag]
+    in_specs = [any_spec] * len(operands) + [pl.BlockSpec(memory_space=pltpu.VMEM)] * 5
+    operands += [cos_tab, sin_tab, w_k, w_v, q_diag]
     with_new = new_rows is not None
     if with_new:
         operands += new_rows
@@ -362,7 +356,7 @@
     tokens = n_in * blk
     n_batch = q_diag.shape[0]
     return pl.pallas_call(
-        functools.partial(kv_kernel, n_in, masks, batches, [[first for _, first in group] for group in groups], with_new),
+        functools.partial(kv_kernel, n_in, masks, batches, [[first for _, first in group] for group in groups], row0, stat_of, with_new),
         grid_spec=pltpu.PrefetchScalarGridSpec(
             num_scalar_prefetch=1,
             grid=(n_steps,),
@@ -388,7 +382,7 @@
     )(scalars, *operands)
 
 
-def tail_kernel(n_dev, n_part, st_ref, self_ref, xs_ref, gain_ref, wo_hbm, wg_hbm, wu_hbm, wd_hbm, dec_ref, last_ref,
+def tail_kernel(n_dev, parts_of, st_ref, self_ref, xs_ref, gain_ref, wo_hbm, wg_hbm, wu_hbm, wd_hbm, dec_ref, last_ref,
                 wo, wg, wu, wd, stv, rows, a_buf, n_buf, mid_buf, ps1, pr1, ps2, pr2, xo1, xg1, xo2, xg2,
                 w_sem, send_sem, recv_sem):
     me = lax.axis_index("model")
@@ -402,27 +396,30 @@
     loads[0].start()
     loads[1].start()
     barrier = pltpu.get_barrier_semaphore()
-    for k in range(1, n_dev):
-        peer = lax.rem(me + k, n_dev)
-        pl.semaphore_signal(barrier, inc=1, device_id={"model": peer}, device_id_type=MESH)
-
-    def send(phase, k, src, dst):
-        peer = lax.rem(me + k, n_dev)
+
+    def peer_of(mask):
+        return sum(lax.rem(me // bit + mask // bit, 2) * bit for bit in (1, 2, 4))
+
+    far_first = sorted(range(1, n_dev), key=lambda mask: (-(mask & 2) - (mask & 4) // 2, mask))
+    for mask in far_first:
+        pl.semaphore_signal(barrier, inc=1, device_id={"model": peer_of(mask)}, device_id_type=MESH)
+
+    def send(phase, mask, src, dst):
         return pltpu.make_async_remote_copy(
-            src_ref=src, dst_ref=dst, send_sem=send_sem.at[phase, k - 1], recv_sem=recv_sem.at[phase, k - 1],
-            device_id={"model": peer}, device_id_type=MESH)
+            src_ref=src, dst_ref=dst, send_sem=send_sem.at[phase, mask - 1], recv_sem=recv_sem.at[phase, mask - 1],
+            device_id={"model": peer_of(mask)}, device_id_type=MESH)
 
     loads[0].wait()
     for load in loads[2:]:
         load.start()
     for b in range(n_batch):
         top = self_ref[1, b]
-        for j in range(n_part):
+        for j in range(parts_of[b]):
             top = jnp.maximum(top, stv[j, b, 1])
         scale = jnp.exp(self_ref[1, b] - top)
         den = scale * self_ref[2, b]
         num = scale * self_ref[0, b]
-        for j in range(n_part):
+        for j in range(parts_of[b]):
             scale = jnp.exp(stv[j, b, 1] - top)
             den += scale * stv[j, b, 2]
             num += scale * stv[j, b, 0]
@@ -434,23 +431,22 @@
 
     def all_reduce(phase, partial, base, ps, pr, xo, xg):
         copies = []
-        for k in range(1, n_dev):
-            peer = lax.rem(me + k, n_dev)
-            ps[k - 1] = partial(peer)
-            copies.append(send(phase, k, ps.at[k - 1], pr.at[k - 1]))
+        for mask in far_first:
+            ps[mask - 1] = partial(peer_of(mask))
+            copies.append(send(phase, mask, ps.at[mask - 1], pr.at[mask - 1]))
             copies[-1].start()
         total = base + partial(me)
-        for k in range(1, n_dev):
-            copies[k - 1].wait_recv()
-            total = total + pr[k - 1]
+        for copy, mask in zip(reversed(copies), reversed(far_first)):
+            copy.wait_recv()
+            total = total + pr[mask - 1]
         xo[...] = total.astype(jnp.bfloat16)
         outs = []
-        for k in range(1, n_dev):
-            outs.append(send(phase + 1, k, xo, xg.at[me]))
+        for mask in far_first:
+            outs.append(send(phase + 1, mask, xo, xg.at[me]))
             outs[-1].start()
         xg[me] = xo[...]
-        for k in range(1, n_dev):
-            outs[k - 1].wait_recv()
+        for out in outs:
+            out.wait_recv()
         return copies + outs
 
     def col_block(p):
@@ -493,14 +489,13 @@
         copy.wait_send()
 
 
-def tail_call(n_dev, stats, self_stat, x_mine, gain, w_o, w_gate_t, w_up_t, w_down, n_batch):
+def tail_call(n_dev, parts_of, stats, self_stat, x_mine, gain, w_o, w_gate_t, w_up_t, w_down, n_batch):
     n_rows, cols = x_mine.shape
     d_model = w_o.shape[1]
-    n_part = stats.shape[0]
     vmem = pl.BlockSpec(memory_space=pltpu.VMEM)
     hbm = pl.BlockSpec(memory_space=pltpu.HBM)
     return pl.pallas_call(
-        functools.partial(tail_kernel, n_dev, n_part),
+        functools.partial(tail_kernel, n_dev, parts_of),
         out_shape=[jax.ShapeDtypeStruct((n_batch, d_model), jnp.bfloat16)] * 2,
         in_specs=[pl.BlockSpec(memory_space=pl.ANY), vmem, vmem, vmem, hbm, hbm, hbm, hbm],
         out_specs=[vmem, vmem],
@@ -555,36 +550,36 @@
         wq = w_q[0]
         gain = norm_attn.astype(jnp.float32)
 
-        q1, q2 = n_batch // 8, n_batch // 4
-        bounds = [(0, q1), (q1, q2), (q2, half)]
+        q1, q2, rows_h = n_batch // 8, n_batch // 4, blk // 2
         a_parts, b_parts = {}, {}
-        first = [*range(q1), *range(half, half + q1)]
-        a_parts[0], b_parts[0] = norm_call(prompt, gain, first, [[(k // q1, k % q1)] for k in range(2 * q1)], [q1, q1])
+        order = [side * half + k for k in range(q1) for side in range(2)]
+        outs_of = [[(2 * h + side, k, h * rows_h, rows_h) for h in range(2)] for k in range(q1) for side in range(2)]
+        a_parts["0a"], b_parts["0a"], a_parts["0b"], b_parts["0b"] = norm_call(prompt, gain, order, outs_of, [(q1, rows_h)] * 4)
         from_y, from_x = {}, {}
 
         def send_part(step, along_y, along_x):
             from_y[step] = swap(along_y, 4)
             from_x[step] = swap(along_x, 2)
 
-        send_part(0, a_parts[0], b_parts[0])
+        send_part("0a", a_parts["0a"], b_parts["0a"])
+        send_part("0b", a_parts["0b"], b_parts["0b"])
+        order, outs_of = [], []
+        for part, (lo, hi) in ((1, (q1, q2)), (2, (q2, half)), (0, (0, q1))):
+            for k in range(lo, hi):
+                for side in range(2):
+                    order.append(side * half + k)
+                    outs_of.append([(4, side * half + k, 0, blk)] + ([(2 * part - 2 + side, k - lo, 0, blk)] if part else []))
+        a_parts["1"], b_parts["1"], a_parts["2"], b_parts["2"], normed = norm_call(
+            prompt, gain, order, outs_of, [(q2 - q1, blk)] * 2 + [(half - q2, blk)] * 2 + [(n_batch, blk)])
+        send_part("1", a_parts["1"], b_parts["1"])
         seq_pos = my_idx * blk + jnp.arange(blk)
         sel = (seq_pos[None, :] == (lengths - 1)[:, None]).astype(jnp.bfloat16)
         last_x = jnp.einsum('bs,bsd->bd', sel, prompt, preferred_element_type=jnp.float32).astype(jnp.bfloat16)
         last_x = last_x + swap(last_x, 1)
         last_x = (last_x + swap(last_x, 2)) + (swap(last_x, 4) + swap(last_x, 6))
-        order, outs_of = [], []
-        for part in (1, 2, 0):
-            lo, hi = bounds[part]
-            for side in range(2):
-                for k in range(lo, hi):
-                    order.append(side * half + k)
-                    outs_of.append([(4, side * half + k)] + ([(2 * part - 2 + side, k - lo)] if part else []))
-        a_parts[1], b_parts[1], a_parts[2], b_parts[2], normed = norm_call(
-            prompt, gain, order, outs_of, [q2 - q1, q2 - q1, half - q2, half - q2, n_batch])
-        send_part(1, a_parts[1], b_parts[1])
-        send_part(2, a_parts[2], b_parts[2])
-        send_part(3, b_parts[2], a_parts[2])
-        send_part(4, normed[half:half + q2], normed[:q2])
+        send_part("2", a_parts["2"], b_parts["2"])
+        send_part("3", b_parts["2"], a_parts["2"])
+        send_part("4", normed[half:half + q2], normed[:q2])
         core_all = swap(normed, 1)
 
         bits = jnp.arange(N_MASKS)
@@ -598,34 +593,45 @@
         wk, wv = keep_in_vmem(wk, wv)
         q_diag, k_new, v_new, self_stat = rows_call(new_tok, last_x, gain, row_tabs, wq, wk, wv)
         cache_shape = jax.ShapeDtypeStruct((n_batch, seq_len + 1, heads, HEAD_DIM), jnp.bfloat16)
-        caches = [cache_shape, cache_shape, jax.ShapeDtypeStruct((n_dev, n_batch, 3, STAT_ROWS, HEAD_DIM), jnp.float32)]
-
-        def run(groups, per_group, masks, batches, caches, new_rows=None):
-            return kv_call(groups, per_group, masks, batches, scalars, tabs, wk, wv, q_diag, caches, new_rows)
+        caches = [cache_shape, cache_shape, jax.ShapeDtypeStruct((2 * n_dev - 2, n_batch, 3, STAT_ROWS, HEAD_DIM), jnp.float32)]
+
+        def run(groups, per_group, masks, batches, caches, **kw):
+            return kv_call(groups, per_group, masks, batches, scalars, tabs, wk, wv, q_diag, caches, **kw)
+
+        def half_rows(step):
+            return {"row0": rows_h * (step == "0b"), "stat_of": (n_dev - 2) * (step == "0b")}
 
         def after(caches, *arrays):
             out = lax.optimization_barrier((caches[2], *arrays))
             return [caches[0], caches[1], out[0]], out[1:]
 
         caches = run([[(arr, 0), (arr, half)] for arr in (normed, core_all)], half,
-                     [[0] * 2, [1] * 2], [[0, half]] * 2, caches, [k_new, v_new])
+                     [[0] * 2, [1] * 2], [[0, half]] * 2, caches, new_rows=[k_new, v_new])
         diag = {}
-        starts = [(lo, half + lo) for lo, _ in bounds] + [(half + q2, q2), (half, 0)]
-        for step, start in enumerate(starts):
+        starts = {"0a": (0, half), "0b": (0, half), "1": (q1, half + q1), "2": (q2, half + q2), "3": (half + q2, q2), "4": (half, 0)}
+        for step, start in starts.items():
             caches, (got_y, got_x) = after(caches, from_y[step], from_x[step])
             other_y, other_x = swap(got_y, 1), swap(got_x, 1)
-            if step < 3:
+            if step not in "34":
                 diag[step] = (swap(got_y, 2), swap(got_x, 4))
-            caches = run([[(got_y, 0), (got_x, 0)], [(other_y, 0), (other_x, 0)]], got_y.shape[0],
-                         [[4, 2], [5, 3]], [list(start)] * 2, caches)
-        for step in (2, 1, 0):
+            streams = [[(got_y, 0), (got_x, 0)], [(other_y, 0), (other_x, 0)]]
+            if step in ("0a", "0b"):
+                caches = run([streams[0] + streams[1]], q1, [[4, 2, 5, 3]], [[*start, *start]], caches, **half_rows(step))
+            else:
+                caches = run(streams, got_y.shape[0], [[4, 2], [5, 3]], [list(start)] * 2, caches)
+        for step in ("2", "1", "0a", "0b"):
             caches, (via_x, via_y) = after(caches, *diag[step])
             other_x, other_y = swap(via_x, 1), swap(via_y, 1)
-            caches = run([[(via_x, 0), (via_y, 0)], [(other_x, 0), (other_y, 0)]], via_x.shape[0],
-                         [[6] * 2, [7] * 2], [list(starts[step])] * 2, caches)
+            start = starts[step]
+            streams = [[(via_x, 0), (via_y, 0)], [(other_x, 0), (other_y, 0)]]
+            if step in ("0a", "0b"):
+                caches = run([streams[0] + streams[1]], q1, [[6, 6, 7, 7]], [[*start, *start]], caches, **half_rows(step))
+            else:
+                caches = run(streams, via_x.shape[0], [[6] * 2, [7] * 2], [list(start)] * 2, caches)
 
         k_cache, v_cache, stats = caches
-        dec_hidden, last_hidden = tail_call(n_dev, stats, self_stat, x_mine, gain_mlp, w_o[0],
+        parts_of = [2 * n_dev - 2 if b % half < q1 else n_dev for b in range(n_batch)]
+        dec_hidden, last_hidden = tail_call(n_dev, parts_of, stats, self_stat, x_mine, gain_mlp, w_o[0],
                                             w_gate[0].T, w_up[0].T, w_down[0], n_batch)
         return dec_hidden, last_hidden, k_cache[None], v_cache[None]
 

time: 409 us -> 408 us (level)
  waiting for transfers between devices: 195 us -> 181 us
  starting transfers between devices: 24.5 us -> 36.8 us
  Pallas kernels: 163 us -> 172 us
  local copies, waits for them, and re-layouts: 16.4 us -> 8.85 us
    ppermute x37 -> x45, waiting for transfers between devices: 195 us -> 181 us  [swap(): return lax.ppermute(arr, 'model', [(i, i ^ bit) for i in range(n_dev)])]
    ppermute x37 -> x45, starting transfers between devices: 24.5 us -> 36.8 us  [swap(): return lax.ppermute(arr, 'model', [(i, i ^ bit) for i in range(n_dev)])]
    unnamed x26 -> x28, local copies, waits for them, and re-layouts: 12.3 us -> 6.17 us
    pallas_call x2, Pallas kernels: 8.98 us -> 13.4 us  [norm_call(): pl.pallas_call(functools.partial(norm_kernel, outs_of), grid=(len(order),...]
    pallas_call x9 -> x11, Pallas kernels: 121 us -> 124 us  [kv_call(): pl.pallas_call(functools.partial(kv_kernel, n_in, masks, batches, [[first...]
  transfers between devices with their start and end apart: 37 -> 45, of which waited for: 28 -> 32; matrix products, arithmetic and copies ran while one was open for 3% -> 2% of each run, Pallas kernels for 30% -> 32%
where the time goes in v4:
time: 408 us; the launch traced here: 407 us
  waiting for transfers between devices  181 us (44%)
  Pallas kernels  172 us (42%)
  starting transfers between devices  36.8 us (9%)
  local copies, waits for them, and re-layouts  8.85 us (2%)
  matrix products  4.57 us (1%)
    ppermute x45, waiting for transfers between devices, swap(): return lax.ppermute(arr, 'model', [(i, i ^ bit) for i in range(n_dev)])  181 us
    pallas_call x11, Pallas kernels, kv_call(): pl.pallas_call(functools.partial(kv_kernel, n_in, masks, batches, [[first...  124 us
    ppermute x45, starting transfers between devices, swap(): return lax.ppermute(arr, 'model', [(i, i ^ bit) for i in range(n_dev)])  36.8 us
    pallas_call x1, Pallas kernels, tail_call(): pl.pallas_call(functools.partial(tail_kernel, n_dev, parts_of), out_shape...  27.3 us
    pallas_call x2, Pallas kernels, norm_call(): pl.pallas_call(functools.partial(norm_kernel, outs_of), grid=(len(order),...  13.4 us
  transfers between devices with their start and end apart: 45, of which 32 were waited for; matrix products, arithmetic and copies ran while one was open for 2% of the time, Pallas kernels for 32%

profile of v4, /device:TPU:0, one launch (start us, length us, event | category | flops | bytes accessed | tf_op | source)
XLA Modules:
  0.0 407.4 jit_solution(11016144174195867142)
XLA Ops:
  1.4 10.7 %norm_rows.2 = (bf16[1,128,4096]{2,1,0:T(8,128)(2,1)S(1)}, bf16[1,128,4096]{2,1,0:T(8,128)(2,1)S(1)}, bf16[2,128,4096]{2,1,0:T(8,128)(2,1)S(1)}, bf16[2,128,4096]{2,1,0:T(8,128)(2,1)S(1)}, bf16[8,128,4096]{2,1,0:T(8,128)(2,1)}) custom-call(bf16[8,128,4096]{2,1,0:T(8,128)(2,1)} %x_ref.3, f32[1,4096]{1,0:T(1,128)S(1)} %convert_element_type.34.gain_ref), custom_call_target="tpu_custom_call" | custom-call | flops 33554432 | bytes 25165824 | tf_op jit(solution)/shard_map/norm_rows/pallas_call | solution.py:114
  16.3 4.6 %fusion.2 = bf16[8,1,4096]{2,1,0:T(2,128)(2,1)S(1)} fusion(bf16[8,128,4096]{2,1,0:T(8,128)(2,1)} %x_ref.3, pred[8,128,1]{1,0,2:T(8,128)(4,1)S(1)} %compare_bitcast_fusion), kind=kOutput, calls=%fused_computation.10 | convolution fusion | flops 8388608 | bytes 8455168 | tf_op jit(solution)/shard_map/bs,bsd->bd/dot_general | solution.py:577
  21.0 2.7 norm_rows.3
  25.3 3.0 collective-permute-start.5
  28.4 1.9 fusion
  31.0 2.2 collective-permute-start.3
  34.5 1.6 collective-permute-done.3
  36.2 1.8 collective-permute-start.6
  37.9 5.5 %collective-permute-done.2 = bf16[8,4096]{1,0:T(8,128)(2,1)S(1)} collective-permute-done((bf16[8,4096]{1,0:T(8,128)(2,1)S(1)}, bf16[8,4096]{1,0:T(8,128)(2,1)S(1)}, u32[]{:S(2)}, u32[]{:S(2)}) %collective-permute-start.2) | collective-permute-done | bytes 65568 | tf_op jit(solution)/shard_map/ppermute | solution.py:541
  43.5 3.5 keep.1
  47.0 3.7 query_rows.1
  50.7 28.5 %kv_chunk.11 = (bf16[8,1025,4,128]{3,2,1,0:T(4,128)(2,1)}, bf16[8,1025,4,128]{3,2,1,0:T(4,128)(2,1)}, f32[14,8,3,8,128]{4,3,2,1,0:T(8,128)S(1)}) custom-call(s32[16]{0:T(128)S(1)} %get-tuple-element.94.sc_ref, bf16[8,128,4096]{2,1,0:T(8,128)(2,1)} %get-tuple-element.95.refs_0_.refs_1_, bf16[8,128,4096]{2,1,0:T(8,128)(2,1)} %get-tuple-element.95.refs_0_.refs_1_, ...), custom_call_target="tpu_custom_call" | custom-call | flops 17179869184 | bytes 20971520 | tf_op jit(solution)/shard_map/kv_chunk/pallas_call | solution.py:358
  79.7 1.8 collective-permute-start.9
  83.0 4.9 %kv_chunk.12 = (bf16[8,1025,4,128]{3,2,1,0:T(4,128)(2,1)}, bf16[8,1025,4,128]{3,2,1,0:T(4,128)(2,1)}, f32[14,8,3,8,128]{4,3,2,1,0:T(8,128)S(1)}) custom-call(s32[16]{0:T(128)S(1)} %get-tuple-element.94.sc_ref, bf16[1,64,4096]{2,1,0:T(8,128)(2,1)S(1)} %collective-permute-done.5.refs_0_, ...), custom_call_target="tpu_custom_call", output_to_operand_aliasing={{0}: (10, {}), {1}: (11, {}), {2}: (12, {})} | custom-call | flops 2147483648 | bytes 2621440 | tf_op jit(solution)/shard_map/kv_chunk/pallas_call | solution.py:358
  87.9 5.7 %collective-permute-done.9.refs_0_ = bf16[1,64,4096]{2,1,0:T(8,128)(2,1)S(1)} collective-permute-done((bf16[1,64,4096]{2,1,0:T(8,128)(2,1)S(1)}, bf16[1,64,4096]{2,1,0:T(8,128)(2,1)S(1)}, u32[]{:S(2)}, u32[]{:S(2)}) %collective-permute-start.9) | collective-permute-done | bytes 524320 | tf_op jit(solution)/shard_map/ppermute | solution.py:541
  95.4 1.7 collective-permute-start.14
  97.1 1.5 collective-permute-start.17
  99.1 4.9 %kv_chunk.13 = (bf16[8,1025,4,128]{3,2,1,0:T(4,128)(2,1)}, bf16[8,1025,4,128]{3,2,1,0:T(4,128)(2,1)}, f32[14,8,3,8,128]{4,3,2,1,0:T(8,128)S(1)}) custom-call(s32[16]{0:T(128)S(1)} %get-tuple-element.94.sc_ref, bf16[1,64,4096]{2,1,0:T(8,128)(2,1)S(1)} %collective-permute-done.9.refs_0_, ...), custom_call_target="tpu_custom_call", output_to_operand_aliasing={{0}: (10, {}), {1}: (11, {}), {2}: (12, {})} | custom-call | flops 2147483648 | bytes 2621440 | tf_op jit(solution)/shard_map/kv_chunk/pallas_call | solution.py:358
  104.1 17.0 %collective-permute-done.13.refs_0_ = bf16[1,128,4096]{2,1,0:T(8,128)(2,1)S(1)} collective-permute-done((bf16[1,128,4096]{2,1,0:T(8,128)(2,1)S(1)}, bf16[1,128,4096]{2,1,0:T(8,128)(2,1)S(1)}, u32[]{:S(2)}, u32[]{:S(2)}) %collective-permute-start.13) | collective-permute-done | bytes 1048608 | tf_op jit(solution)/shard_map/ppermute | solution.py:541
  121.9 2.1 collective-permute-done.15.refs_2_
  125.6 8.3 %kv_chunk.14 = (bf16[8,1025,4,128]{3,2,1,0:T(4,128)(2,1)}, bf16[8,1025,4,128]{3,2,1,0:T(4,128)(2,1)}, f32[14,8,3,8,128]{4,3,2,1,0:T(8,128)S(1)}) custom-call(s32[16]{0:T(128)S(1)} %get-tuple-element.94.sc_ref, bf16[1,128,4096]{2,1,0:T(8,128)(2,1)S(1)} %collective-permute-done.13.refs_0_, ...), custom_call_target="tpu_custom_call", output_to_operand_aliasing={{0}: (10, {}), {1}: (11, {}), {2}: (12, {})} | custom-call | flops 4294967296 | bytes 5242880 | tf_op jit(solution)/shard_map/kv_chunk/pallas_call | solution.py:358
  133.9 31.7 %collective-permute-done.17.refs_0_ = bf16[2,128,4096]{2,1,0:T(8,128)(2,1)S(1)} collective-permute-done((bf16[2,128,4096]{2,1,0:T(8,128)(2,1)S(1)}, bf16[2,128,4096]{2,1,0:T(8,128)(2,1)S(1)}, u32[]{:S(2)}, u32[]{:S(2)}) %collective-permute-start.17) | collective-permute-done | bytes 2097184 | tf_op jit(solution)/shard_map/ppermute | solution.py:541
  166.1 1.7 collective-permute-start.22
  169.8 3.0 collective-permute-done.20.refs_3_
  172.8 14.7 %kv_chunk.15 = (bf16[8,1025,4,128]{3,2,1,0:T(4,128)(2,1)}, bf16[8,1025,4,128]{3,2,1,0:T(4,128)(2,1)}, f32[14,8,3,8,128]{4,3,2,1,0:T(8,128)S(1)}) custom-call(s32[16]{0:T(128)S(1)} %get-tuple-element.94.sc_ref, bf16[2,128,4096]{2,1,0:T(8,128)(2,1)S(1)} %collective-permute-done.17.refs_0_, ...), custom_call_target="tpu_custom_call", output_to_operand_aliasing={{0}: (10, {}), {1}: (11, {}), {2}: (12, {})} | custom-call | flops 8589934592 | bytes 10485760 | tf_op jit(solution)/shard_map/kv_chunk/pallas_call | solution.py:358
  187.5 26.1 %collective-permute-done.22.refs_1_ = bf16[2,128,4096]{2,1,0:T(8,128)(2,1)S(1)} collective-permute-done((bf16[2,128,4096]{2,1,0:T(8,128)(2,1)S(1)}, bf16[2,128,4096]{2,1,0:T(8,128)(2,1)S(1)}, u32[]{:S(2)}, u32[]{:S(2)}) %collective-permute-start.22) | collective-permute-done | bytes 2097184 | tf_op jit(solution)/shard_map/ppermute | solution.py:541
  215.6 2.6 fusion.14
  218.5 1.7 collective-permute-start.25
  220.3 2.0 collective-permute-done.24.refs_3_
  222.2 14.7 %kv_chunk.16 = (bf16[8,1025,4,128]{3,2,1,0:T(4,128)(2,1)}, bf16[8,1025,4,128]{3,2,1,0:T(4,128)(2,1)}, f32[14,8,3,8,128]{4,3,2,1,0:T(8,128)S(1)}) custom-call(s32[16]{0:T(128)S(1)} %get-tuple-element.94.sc_ref, bf16[2,128,4096]{2,1,0:T(8,128)(2,1)S(1)} %collective-permute-done.21.refs_0_, ...), custom_call_target="tpu_custom_call", output_to_operand_aliasing={{0}: (10, {}), {1}: (11, {}), {2}: (12, {})} | custom-call | flops 8589934592 | bytes 10485760 | tf_op jit(solution)/shard_map/kv_chunk/pallas_call | solution.py:358
  237.0 28.8 %collective-permute-done.26.refs_1_ = bf16[2,128,4096]{2,1,0:T(8,128)(2,1)S(1)} collective-permute-done((bf16[2,128,4096]{2,1,0:T(8,128)(2,1)S(1)}, bf16[2,128,4096]{2,1,0:T(8,128)(2,1)S(1)}, u32[]{:S(2)}, u32[]{:S(2)}) %collective-permute-start.26) | collective-permute-done | bytes 2097184 | tf_op jit(solution)/shard_map/ppermute | solution.py:541
  266.3 1.7 collective-permute-start.29
  270.0 3.0 collective-permute-done.28.refs_3_
  273.0 14.7 %kv_chunk.17 = (bf16[8,1025,4,128]{3,2,1,0:T(4,128)(2,1)}, bf16[8,1025,4,128]{3,2,1,0:T(4,128)(2,1)}, f32[14,8,3,8,128]{4,3,2,1,0:T(8,128)S(1)}) custom-call(s32[16]{0:T(128)S(1)} %get-tuple-element.94.sc_ref, bf16[2,128,4096]{2,1,0:T(8,128)(2,1)S(1)} %collective-permute-done.25.refs_0_, ...), custom_call_target="tpu_custom_call", output_to_operand_aliasing={{0}: (10, {}), {1}: (11, {}), {2}: (12, {})} | custom-call | flops 8589934592 | bytes 10485760 | tf_op jit(solution)/shard_map/kv_chunk/pallas_call | solution.py:358
  287.7 26.1 %collective-permute-done.29.refs_0_ = bf16[2,128,4096]{2,1,0:T(8,128)(2,1)S(1)} collective-permute-done((bf16[2,128,4096]{2,1,0:T(8,128)(2,1)S(1)}, bf16[2,128,4096]{2,1,0:T(8,128)(2,1)S(1)}, u32[]{:S(2)}, u32[]{:S(2)}) %collective-permute-start.29) | collective-permute-done | bytes 2097184 | tf_op jit(solution)/shard_map/ppermute | solution.py:541
  316.1 1.7 collective-permute-start.34
  317.8 1.6 collective-permute-done.31.refs_2_
  319.4 3.0 collective-permute-done.32.refs_3_
  322.4 14.7 %kv_chunk.18 = (bf16[8,1025,4,128]{3,2,1,0:T(4,128)(2,1)}, bf16[8,1025,4,128]{3,2,1,0:T(4,128)(2,1)}, f32[14,8,3,8,128]{4,3,2,1,0:T(8,128)S(1)}) custom-call(s32[16]{0:T(128)S(1)} %get-tuple-element.94.sc_ref, bf16[2,128,4096]{2,1,0:T(8,128)(2,1)S(1)} %collective-permute-done.29.refs_0_, ...), custom_call_target="tpu_custom_call", output_to_operand_aliasing={{0}: (10, {}), {1}: (11, {}), {2}: (12, {})} | custom-call | flops 8589934592 | bytes 10485760 | tf_op jit(solution)/shard_map/kv_chunk/pallas_call | solution.py:358
  337.1 3.7 collective-permute-done.33.refs_0_
  341.4 1.7 collective-permute-start.37
  345.1 8.1 %kv_chunk.19 = (bf16[8,1025,4,128]{3,2,1,0:T(4,128)(2,1)}, bf16[8,1025,4,128]{3,2,1,0:T(4,128)(2,1)}, f32[14,8,3,8,128]{4,3,2,1,0:T(8,128)S(1)}) custom-call(s32[16]{0:T(128)S(1)} %get-tuple-element.94.sc_ref, bf16[1,128,4096]{2,1,0:T(8,128)(2,1)S(1)} %collective-permute-done.33.refs_0_, ...), custom_call_target="tpu_custom_call", output_to_operand_aliasing={{0}: (10, {}), {1}: (11, {}), {2}: (12, {})} | custom-call | flops 4294967296 | bytes 5242880 | tf_op jit(solution)/shard_map/kv_chunk/pallas_call | solution.py:358
  353.2 2.1 collective-permute-done.37.refs_0_
  357.5 1.7 collective-permute-start.42
  359.3 4.9 %kv_chunk.20 = (bf16[8,1025,4,128]{3,2,1,0:T(4,128)(2,1)}, bf16[8,1025,4,128]{3,2,1,0:T(4,128)(2,1)}, f32[14,8,3,8,128]{4,3,2,1,0:T(8,128)S(1)}) custom-call(s32[16]{0:T(128)S(1)} %get-tuple-element.94.sc_ref, bf16[1,64,4096]{2,1,0:T(8,128)(2,1)S(1)} %collective-permute-done.37.refs_0_, ...), custom_call_target="tpu_custom_call", output_to_operand_aliasing={{0}: (10, {}), {1}: (11, {}), {2}: (12, {})} | custom-call | flops 2147483648 | bytes 2621440 | tf_op jit(solution)/shard_map/kv_chunk/pallas_call | solution.py:358
  364.2 6.7 %collective-permute-done.41.refs_0_ = bf16[1,64,4096]{2,1,0:T(8,128)(2,1)S(1)} collective-permute-done((bf16[1,64,4096]{2,1,0:T(8,128)(2,1)S(1)}, bf16[1,64,4096]{2,1,0:T(8,128)(2,1)S(1)}, u32[]{:S(2)}, u32[]{:S(2)}) %collective-permute-start.41) | collective-permute-done | bytes 524320 | tf_op jit(solution)/shard_map/ppermute | solution.py:541
  373.7 5.1 %kv_chunk.21 = (bf16[8,1025,4,128]{3,2,1,0:T(4,128)(2,1)}, bf16[8,1025,4,128]{3,2,1,0:T(4,128)(2,1)}, f32[14,8,3,8,128]{4,3,2,1,0:T(8,128)S(1)}) custom-call(s32[16]{0:T(128)S(1)} %get-tuple-element.94.sc_ref, bf16[1,64,4096]{2,1,0:T(8,128)(2,1)S(1)} %collective-permute-done.41.refs_0_, ...), custom_call_target="tpu_custom_call", output_to_operand_aliasing={{0}: (10, {}), {1}: (11, {}), {2}: (12, {})} | custom-call | flops 2147483648 | bytes 2621440 | tf_op jit(solution)/shard_map/kv_chunk/pallas_call | solution.py:358
  378.8 27.3 %tail.1 = (bf16[8,4096]{1,0:T(8,128)(2,1)S(1)}, bf16[8,4096]{1,0:T(8,128)(2,1)S(1)}) custom-call(f32[14,8,3,8,128]{4,3,2,1,0:T(8,128)S(1)} %get-tuple-element.176.st_ref, f32[3,8,8,128]{3,2,1,0:T(8,128)S(1)} %get-tuple-element.177.self_ref, bf16[16,512]{1,0:T(8,128)(2,1)S(1)} %fusion.1.xs_ref, f32[1,4096]{1,0:T(1,128)S(1)} %convert_element_type.33.gain_ref, ...), custom_call_target="tpu_custom_call" | custom-call | tf_op jit(solution)/shard_map/tail/pallas_call | solution.py:497
  (105 shorter events, 33.8 us)
Async XLA Ops:
  1.4 14.8 %copy-start.12 = (s32[8]{0:T(128)S(1)}, s32[8]{0:T(128)}, u32[]{:S(2)}) copy-start(s32[8]{0:T(128)} %param.13) | copy-start | bytes 100
  15.3 35.3 %collective-permute-start.4 = (bf16[8,128,4096]{2,1,0:T(8,128)(2,1)}, bf16[8,128,4096]{2,1,0:T(8,128)(2,1)}, u32[]{:S(2)}, u32[]{:S(2)}) collective-permute-start(bf16[8,128,4096]{2,1,0:T(8,128)(2,1)} %get-tuple-element.95.refs_0_.refs_1_), channel_id=1, source_target_pairs={{0,1},{1,0},{2,3},{3,2},{4,5},{5,4},{6,7},{7,6}} | collective-permute-start | bytes 25165832 | tf_op jit(solution)/shard_map/ppermute | solution.py:541
  20.9 9.9 %collective-permute-start = (bf16[8,4096]{1,0:T(8,128)(2,1)S(1)}, bf16[8,4096]{1,0:T(8,128)(2,1)S(1)}, u32[]{:S(2)}, u32[]{:S(2)}) collective-permute-start(bf16[8,4096]{1,0:T(8,128)(2,1)S(1)} %bitcast.30), channel_id=1, source_target_pairs={{0,1},{1,0},{2,3},{3,2},{4,5},{5,4},{6,7},{7,6}} | collective-permute-start | bytes 196616 | tf_op jit(solution)/shard_map/ppermute | solution.py:541
  25.3 18.1 %copy-start = (bf16[8,4096]{1,0:T(8,128)(2,1)S(1)}, bf16[8,4096]{1,0:T(8,128)(2,1)}, u32[]{:S(2)}) copy-start(bf16[8,4096]{1,0:T(8,128)(2,1)} %new_ref.1) | copy-start | bytes 196612
  25.3 53.9 %collective-permute-start.5 = (bf16[1,64,4096]{2,1,0:T(8,128)(2,1)}, bf16[1,64,4096]{2,1,0:T(8,128)(2,1)S(1)}, u32[]{:S(2)}, u32[]{:S(2)}) collective-permute-start(bf16[1,64,4096]{2,1,0:T(8,128)(2,1)} %get-tuple-element.109), channel_id=1, source_target_pairs={{0,4},{1,5},{2,6},{3,7},{4,0},{5,1},{6,2},{7,3}} | collective-permute-start | bytes 1572872 | tf_op jit(solution)/shard_map/ppermute | solution.py:541
  31.0 5.2 %collective-permute-start.3 = (bf16[8,4096]{1,0:T(8,128)(2,1)S(1)}, bf16[8,4096]{1,0:T(8,128)(2,1)S(1)}, u32[]{:S(2)}, u32[]{:S(2)}) collective-permute-start(bf16[8,4096]{1,0:T(8,128)(2,1)S(1)} %fusion.16), channel_id=1, source_target_pairs={{0,6},{1,7},{2,4},{3,5},{4,2},{5,3},{6,0},{7,1}} | collective-permute-start | bytes 196616 | tf_op jit(solution)/shard_map/ppermute | solution.py:541
  33.2 10.2 %collective-permute-start.2 = (bf16[8,4096]{1,0:T(8,128)(2,1)S(1)}, bf16[8,4096]{1,0:T(8,128)(2,1)S(1)}, u32[]{:S(2)}, u32[]{:S(2)}) collective-permute-start(bf16[8,4096]{1,0:T(8,128)(2,1)S(1)} %fusion.16), channel_id=1, source_target_pairs={{0,4},{1,5},{2,6},{3,7},{4,0},{5,1},{6,2},{7,3}} | collective-permute-start | bytes 196616 | tf_op jit(solution)/shard_map/ppermute | solution.py:541
  33.9 9.5 %collective-permute-start.1 = (bf16[8,4096]{1,0:T(8,128)(2,1)S(1)}, bf16[8,4096]{1,0:T(8,128)(2,1)S(1)}, u32[]{:S(2)}, u32[]{:S(2)}) collective-permute-start(bf16[8,4096]{1,0:T(8,128)(2,1)S(1)} %fusion.16), channel_id=1, source_target_pairs={{0,2},{1,3},{2,0},{3,1},{4,6},{5,7},{6,4},{7,5}} | collective-permute-start | bytes 196616 | tf_op jit(solution)/shard_map/ppermute | solution.py:541
  36.2 43.0 %collective-permute-start.6 = (bf16[1,64,4096]{2,1,0:T(8,128)(2,1)S(1)}, bf16[1,64,4096]{2,1,0:T(8,128)(2,1)S(1)}, u32[]{:S(2)}, u32[]{:S(2)}) collective-permute-start(bf16[1,64,4096]{2,1,0:T(8,128)(2,1)S(1)} %copy-done.10), channel_id=1, source_target_pairs={{0,2},{1,3},{2,0},{3,1},{4,6},{5,7},{6,4},{7,5}} | collective-permute-start | bytes 1572872 | tf_op jit(solution)/shard_map/ppermute | solution.py:541
  50.7 29.0 %copy-start.8 = (bf16[1,64,4096]{2,1,0:T(8,128)(2,1)S(1)}, bf16[1,64,4096]{2,1,0:T(8,128)(2,1)}, u32[]{:S(2)}) copy-start(bf16[1,64,4096]{2,1,0:T(8,128)(2,1)} %copy-done.7) | copy-start | bytes 1572868
  79.2 3.8 collective-permute-start.7
  79.2 3.7 collective-permute-start.8
  79.7 13.9 %collective-permute-start.9 = (bf16[1,64,4096]{2,1,0:T(8,128)(2,1)S(1)}, bf16[1,64,4096]{2,1,0:T(8,128)(2,1)S(1)}, u32[]{:S(2)}, u32[]{:S(2)}) collective-permute-start(bf16[1,64,4096]{2,1,0:T(8,128)(2,1)S(1)} %copy-done.8), channel_id=1, source_target_pairs={{0,4},{1,5},{2,6},{3,7},{4,0},{5,1},{6,2},{7,3}} | collective-permute-start | bytes 1572872 | tf_op jit(solution)/shard_map/ppermute | solution.py:541
  81.5 13.6 %collective-permute-start.10 = (bf16[1,64,4096]{2,1,0:T(8,128)(2,1)S(1)}, bf16[1,64,4096]{2,1,0:T(8,128)(2,1)S(1)}, u32[]{:S(2)}, u32[]{:S(2)}) collective-permute-start(bf16[1,64,4096]{2,1,0:T(8,128)(2,1)S(1)} %get-tuple-element.118), channel_id=1, source_target_pairs={{0,2},{1,3},{2,0},{3,1},{4,6},{5,7},{6,4},{7,5}} | collective-permute-start | bytes 1572872 | tf_op jit(solution)/shard_map/ppermute | solution.py:541
  95.0 3.5 collective-permute-start.11
  95.1 26.0 %collective-permute-start.13 = (bf16[1,128,4096]{2,1,0:T(8,128)(2,1)S(1)}, bf16[1,128,4096]{2,1,0:T(8,128)(2,1)S(1)}, u32[]{:S(2)}, u32[]{:S(2)}) collective-permute-start(bf16[1,128,4096]{2,1,0:T(8,128)(2,1)S(1)} %copy-done.6), channel_id=1, source_target_pairs={{0,4},{1,5},{2,6},{3,7},{4,0},{5,1},{6,2},{7,3}} | collective-permute-start | bytes 3145736 | tf_op jit(solution)/shard_map/ppermute | solution.py:541
  95.4 26.0 %collective-permute-start.14 = (bf16[1,128,4096]{2,1,0:T(8,128)(2,1)S(1)}, bf16[1,128,4096]{2,1,0:T(8,128)(2,1)S(1)}, u32[]{:S(2)}, u32[]{:S(2)}) collective-permute-start(bf16[1,128,4096]{2,1,0:T(8,128)(2,1)S(1)} %copy-done.4), channel_id=1, source_target_pairs={{0,2},{1,3},{2,0},{3,1},{4,6},{5,7},{6,4},{7,5}} | collective-permute-start | bytes 3145736 | tf_op jit(solution)/shard_map/ppermute | solution.py:541
  97.1 2.1 collective-permute-start.12
  97.1 68.5 %collective-permute-start.17 = (bf16[2,128,4096]{2,1,0:T(8,128)(2,1)S(1)}, bf16[2,128,4096]{2,1,0:T(8,128)(2,1)S(1)}, u32[]{:S(2)}, u32[]{:S(2)}) collective-permute-start(bf16[2,128,4096]{2,1,0:T(8,128)(2,1)S(1)} %copy-done.2), channel_id=1, source_target_pairs={{0,4},{1,5},{2,6},{3,7},{4,0},{5,1},{6,2},{7,3}} | collective-permute-start | bytes 6291464 | tf_op jit(solution)/shard_map/ppermute | solution.py:541
  98.6 67.0 %collective-permute-start.18 = (bf16[2,128,4096]{2,1,0:T(8,128)(2,1)S(1)}, bf16[2,128,4096]{2,1,0:T(8,128)(2,1)S(1)}, u32[]{:S(2)}, u32[]{:S(2)}) collective-permute-start(bf16[2,128,4096]{2,1,0:T(8,128)(2,1)S(1)} %get-tuple-element.134), channel_id=1, source_target_pairs={{0,2},{1,3},{2,0},{3,1},{4,6},{5,7},{6,4},{7,5}} | collective-permute-start | bytes 6291464 | tf_op jit(solution)/shard_map/ppermute | solution.py:541
  121.4 2.7 collective-permute-start.15
  121.4 4.2 %collective-permute-start.16 = (bf16[1,128,4096]{2,1,0:T(8,128)(2,1)S(1)}, bf16[1,128,4096]{2,1,0:T(8,128)(2,1)S(1)}, u32[]{:S(2)}, u32[]{:S(2)}) collective-permute-start(bf16[1,128,4096]{2,1,0:T(8,128)(2,1)S(1)} %collective-permute-done.14.refs_1_), channel_id=1, source_target_pairs={{0,1},{1,0},{2,3},{3,2},{4,5},{5,4},{6,7},{7,6}} | collective-permute-start | bytes 3145736 | tf_op jit(solution)/shard_map/ppermute | solution.py:541
  165.6 4.2 %collective-permute-start.19 = (bf16[2,128,4096]{2,1,0:T(8,128)(2,1)S(1)}, bf16[2,128,4096]{2,1,0:T(8,128)(2,1)S(1)}, u32[]{:S(2)}, u32[]{:S(2)}) collective-permute-start(bf16[2,128,4096]{2,1,0:T(8,128)(2,1)S(1)} %collective-permute-done.17.refs_0_), channel_id=1, source_target_pairs={{0,1},{1,0},{2,3},{3,2},{4,5},{5,4},{6,7},{7,6}} | collective-permute-start | bytes 6291464 | tf_op jit(solution)/shard_map/ppermute | solution.py:541
  165.6 7.2 %collective-permute-start.20 = (bf16[2,128,4096]{2,1,0:T(8,128)(2,1)S(1)}, bf16[2,128,4096]{2,1,0:T(8,128)(2,1)S(1)}, u32[]{:S(2)}, u32[]{:S(2)}) collective-permute-start(bf16[2,128,4096]{2,1,0:T(8,128)(2,1)S(1)} %collective-permute-done.18.refs_1_), channel_id=1, source_target_pairs={{0,1},{1,0},{2,3},{3,2},{4,5},{5,4},{6,7},{7,6}} | collective-permute-start | bytes 6291464 | tf_op jit(solution)/shard_map/ppermute | solution.py:541
  166.1 47.5 %collective-permute-start.22 = (bf16[2,128,4096]{2,1,0:T(8,128)(2,1)S(1)}, bf16[2,128,4096]{2,1,0:T(8,128)(2,1)S(1)}, u32[]{:S(2)}, u32[]{:S(2)}) collective-permute-start(bf16[2,128,4096]{2,1,0:T(8,128)(2,1)S(1)} %copy-done.2), channel_id=1, source_target_pairs={{0,2},{1,3},{2,0},{3,1},{4,6},{5,7},{6,4},{7,5}} | collective-permute-start | bytes 6291464 | tf_op jit(solution)/shard_map/ppermute | solution.py:541
  167.8 47.3 %collective-permute-start.21 = (bf16[2,128,4096]{2,1,0:T(8,128)(2,1)S(1)}, bf16[2,128,4096]{2,1,0:T(8,128)(2,1)S(1)}, u32[]{:S(2)}, u32[]{:S(2)}) collective-permute-start(bf16[2,128,4096]{2,1,0:T(8,128)(2,1)S(1)} %get-tuple-element.134), channel_id=1, source_target_pairs={{0,4},{1,5},{2,6},{3,7},{4,0},{5,1},{6,2},{7,3}} | collective-permute-start | bytes 6291464 | tf_op jit(solution)/shard_map/ppermute | solution.py:541
  215.1 5.2 %collective-permute-start.23 = (bf16[2,128,4096]{2,1,0:T(8,128)(2,1)S(1)}, bf16[2,128,4096]{2,1,0:T(8,128)(2,1)S(1)}, u32[]{:S(2)}, u32[]{:S(2)}) collective-permute-start(bf16[2,128,4096]{2,1,0:T(8,128)(2,1)S(1)} %collective-permute-done.21.refs_0_), channel_id=1, source_target_pairs={{0,1},{1,0},{2,3},{3,2},{4,5},{5,4},{6,7},{7,6}} | collective-permute-start | bytes 6291464 | tf_op jit(solution)/shard_map/ppermute | solution.py:541
  215.1 7.2 %collective-permute-start.24 = (bf16[2,128,4096]{2,1,0:T(8,128)(2,1)S(1)}, bf16[2,128,4096]{2,1,0:T(8,128)(2,1)S(1)}, u32[]{:S(2)}, u32[]{:S(2)}) collective-permute-start(bf16[2,128,4096]{2,1,0:T(8,128)(2,1)S(1)} %collective-permute-done.22.refs_1_), channel_id=1, source_target_pairs={{0,1},{1,0},{2,3},{3,2},{4,5},{5,4},{6,7},{7,6}} | collective-permute-start | bytes 6291464 | tf_op jit(solution)/shard_map/ppermute | solution.py:541
  218.2 47.6 %collective-permute-start.26 = (bf16[2,128,4096]{2,1,0:T(8,128)(2,1)S(1)}, bf16[2,128,4096]{2,1,0:T(8,128)(2,1)S(1)}, u32[]{:S(2)}, u32[]{:S(2)}) collective-permute-start(bf16[2,128,4096]{2,1,0:T(8,128)(2,1)S(1)} %get-tuple-element.184), channel_id=1, source_target_pairs={{0,2},{1,3},{2,0},{3,1},{4,6},{5,7},{6,4},{7,5}} | collective-permute-start | bytes 6291464 | tf_op jit(solution)/shard_map/ppermute | solution.py:541
  218.5 47.3 %collective-permute-start.25 = (bf16[2,128,4096]{2,1,0:T(8,128)(2,1)S(1)}, bf16[2,128,4096]{2,1,0:T(8,128)(2,1)S(1)}, u32[]{:S(2)}, u32[]{:S(2)}) collective-permute-start(bf16[2,128,4096]{2,1,0:T(8,128)(2,1)S(1)} %get-tuple-element.185), channel_id=1, source_target_pairs={{0,4},{1,5},{2,6},{3,7},{4,0},{5,1},{6,2},{7,3}} | collective-permute-start | bytes 6291464 | tf_op jit(solution)/shard_map/ppermute | solution.py:541
  265.8 4.2 %collective-permute-start.27 = (bf16[2,128,4096]{2,1,0:T(8,128)(2,1)S(1)}, bf16[2,128,4096]{2,1,0:T(8,128)(2,1)S(1)}, u32[]{:S(2)}, u32[]{:S(2)}) collective-permute-start(bf16[2,128,4096]{2,1,0:T(8,128)(2,1)S(1)} %collective-permute-done.25.refs_0_), channel_id=1, source_target_pairs={{0,1},{1,0},{2,3},{3,2},{4,5},{5,4},{6,7},{7,6}} | collective-permute-start | bytes 6291464 | tf_op jit(solution)/shard_map/ppermute | solution.py:541
  265.8 7.2 %collective-permute-start.28 = (bf16[2,128,4096]{2,1,0:T(8,128)(2,1)S(1)}, bf16[2,128,4096]{2,1,0:T(8,128)(2,1)S(1)}, u32[]{:S(2)}, u32[]{:S(2)}) collective-permute-start(bf16[2,128,4096]{2,1,0:T(8,128)(2,1)S(1)} %collective-permute-done.26.refs_1_), channel_id=1, source_target_pairs={{0,1},{1,0},{2,3},{3,2},{4,5},{5,4},{6,7},{7,6}} | collective-permute-start | bytes 6291464 | tf_op jit(solution)/shard_map/ppermute | solution.py:541
  266.3 47.5 %collective-permute-start.29 = (bf16[2,128,4096]{2,1,0:T(8,128)(2,1)S(1)}, bf16[2,128,4096]{2,1,0:T(8,128)(2,1)S(1)}, u32[]{:S(2)}, u32[]{:S(2)}) collective-permute-start(bf16[2,128,4096]{2,1,0:T(8,128)(2,1)S(1)} %collective-permute-done.17.refs_0_), channel_id=1, source_target_pairs={{0,2},{1,3},{2,0},{3,1},{4,6},{5,7},{6,4},{7,5}} | collective-permute-start | bytes 6291464 | tf_op jit(solution)/shard_map/ppermute | solution.py:541
  268.0 47.3 %collective-permute-start.30 = (bf16[2,128,4096]{2,1,0:T(8,128)(2,1)S(1)}, bf16[2,128,4096]{2,1,0:T(8,128)(2,1)S(1)}, u32[]{:S(2)}, u32[]{:S(2)}) collective-permute-start(bf16[2,128,4096]{2,1,0:T(8,128)(2,1)S(1)} %collective-permute-done.18.refs_1_), channel_id=1, source_target_pairs={{0,4},{1,5},{2,6},{3,7},{4,0},{5,1},{6,2},{7,3}} | collective-permute-start | bytes 6291464 | tf_op jit(solution)/shard_map/ppermute | solution.py:541
  315.3 4.2 %collective-permute-start.31 = (bf16[2,128,4096]{2,1,0:T(8,128)(2,1)S(1)}, bf16[2,128,4096]{2,1,0:T(8,128)(2,1)S(1)}, u32[]{:S(2)}, u32[]{:S(2)}) collective-permute-start(bf16[2,128,4096]{2,1,0:T(8,128)(2,1)S(1)} %collective-permute-done.29.refs_0_), channel_id=1, source_target_pairs={{0,1},{1,0},{2,3},{3,2},{4,5},{5,4},{6,7},{7,6}} | collective-permute-start | bytes 6291464 | tf_op jit(solution)/shard_map/ppermute | solution.py:541
  315.3 7.2 %collective-permute-start.32 = (bf16[2,128,4096]{2,1,0:T(8,128)(2,1)S(1)}, bf16[2,128,4096]{2,1,0:T(8,128)(2,1)S(1)}, u32[]{:S(2)}, u32[]{:S(2)}) collective-permute-start(bf16[2,128,4096]{2,1,0:T(8,128)(2,1)S(1)} %collective-permute-done.30.refs_1_), channel_id=1, source_target_pairs={{0,1},{1,0},{2,3},{3,2},{4,5},{5,4},{6,7},{7,6}} | collective-permute-start | bytes 6291464 | tf_op jit(solution)/shard_map/ppermute | solution.py:541
  315.8 25.1 %collective-permute-start.33 = (bf16[1,128,4096]{2,1,0:T(8,128)(2,1)S(1)}, bf16[1,128,4096]{2,1,0:T(8,128)(2,1)S(1)}, u32[]{:S(2)}, u32[]{:S(2)}) collective-permute-start(bf16[1,128,4096]{2,1,0:T(8,128)(2,1)S(1)} %collective-permute-done.13.refs_0_), channel_id=1, source_target_pairs={{0,2},{1,3},{2,0},{3,1},{4,6},{5,7},{6,4},{7,5}} | collective-permute-start | bytes 3145736 | tf_op jit(solution)/shard_map/ppermute | solution.py:541
  316.1 24.8 %collective-permute-start.34 = (bf16[1,128,4096]{2,1,0:T(8,128)(2,1)S(1)}, bf16[1,128,4096]{2,1,0:T(8,128)(2,1)S(1)}, u32[]{:S(2)}, u32[]{:S(2)}) collective-permute-start(bf16[1,128,4096]{2,1,0:T(8,128)(2,1)S(1)} %collective-permute-done.14.refs_1_), channel_id=1, source_target_pairs={{0,4},{1,5},{2,6},{3,7},{4,0},{5,1},{6,2},{7,3}} | collective-permute-start | bytes 3145736 | tf_op jit(solution)/shard_map/ppermute | solution.py:541
  340.9 3.7 collective-permute-start.35
  340.9 4.2 %collective-permute-start.36 = (bf16[1,128,4096]{2,1,0:T(8,128)(2,1)S(1)}, bf16[1,128,4096]{2,1,0:T(8,128)(2,1)S(1)}, u32[]{:S(2)}, u32[]{:S(2)}) collective-permute-start(bf16[1,128,4096]{2,1,0:T(8,128)(2,1)S(1)} %collective-permute-done.34.refs_1_), channel_id=1, source_target_pairs={{0,1},{1,0},{2,3},{3,2},{4,5},{5,4},{6,7},{7,6}} | collective-permute-start | bytes 3145736 | tf_op jit(solution)/shard_map/ppermute | solution.py:541
  341.4 13.8 %collective-permute-start.37 = (bf16[1,64,4096]{2,1,0:T(8,128)(2,1)S(1)}, bf16[1,64,4096]{2,1,0:T(8,128)(2,1)S(1)}, u32[]{:S(2)}, u32[]{:S(2)}) collective-permute-start(bf16[1,64,4096]{2,1,0:T(8,128)(2,1)S(1)} %collective-permute-done.5.refs_0_), channel_id=1, source_target_pairs={{0,2},{1,3},{2,0},{3,1},{4,6},{5,7},{6,4},{7,5}} | collective-permute-start | bytes 1572872 | tf_op jit(solution)/shard_map/ppermute | solution.py:541
  343.1 13.6 %collective-permute-start.38 = (bf16[1,64,4096]{2,1,0:T(8,128)(2,1)S(1)}, bf16[1,64,4096]{2,1,0:T(8,128)(2,1)S(1)}, u32[]{:S(2)}, u32[]{:S(2)}) collective-permute-start(bf16[1,64,4096]{2,1,0:T(8,128)(2,1)S(1)} %collective-permute-done.6.refs_1_), channel_id=1, source_target_pairs={{0,4},{1,5},{2,6},{3,7},{4,0},{5,1},{6,2},{7,3}} | collective-permute-start | bytes 1572872 | tf_op jit(solution)/shard_map/ppermute | solution.py:541
  356.6 2.6 collective-permute-start.39
  356.6 2.7 collective-permute-start.40
  357.2 13.8 %collective-permute-start.41 = (bf16[1,64,4096]{2,1,0:T(8,128)(2,1)S(1)}, bf16[1,64,4096]{2,1,0:T(8,128)(2,1)S(1)}, u32[]{:S(2)}, u32[]{:S(2)}) collective-permute-start(bf16[1,64,4096]{2,1,0:T(8,128)(2,1)S(1)} %collective-permute-done.9.refs_0_), channel_id=1, source_target_pairs={{0,2},{1,3},{2,0},{3,1},{4,6},{5,7},{6,4},{7,5}} | collective-permute-start | bytes 1572872 | tf_op jit(solution)/shard_map/ppermute | solution.py:541
  357.5 13.6 %collective-permute-start.42 = (bf16[1,64,4096]{2,1,0:T(8,128)(2,1)S(1)}, bf16[1,64,4096]{2,1,0:T(8,128)(2,1)S(1)}, u32[]{:S(2)}, u32[]{:S(2)}) collective-permute-start(bf16[1,64,4096]{2,1,0:T(8,128)(2,1)S(1)} %collective-permute-done.10.refs_1_), channel_id=1, source_target_pairs={{0,4},{1,5},{2,6},{3,7},{4,0},{5,1},{6,2},{7,3}} | collective-permute-start | bytes 1572872 | tf_op jit(solution)/shard_map/ppermute | solution.py:541
  371.0 1.9 collective-permute-start.43
  371.0 2.7 collective-permute-start.44
  (10 other events, 58.7 us)

commit v5 on v4

--- a/solution.py
+++ b/solution.py
@@ -48,6 +48,25 @@
     )(*(pltpu.with_memory_space_constraint(arr, pltpu.HBM) for arr in arrays))
 
 
+def turn_kernel(w_ref, out_ref):
+    out_ref[...] = w_ref[...].T
+
+
+def turn_call(w_t):
+    n, d = w_t.shape
+    cols = 512
+    return pl.pallas_call(
+        turn_kernel,
+        grid=(d // cols,),
+        in_specs=[pl.BlockSpec((n, cols), lambda g: (0, g))],
+        out_specs=pl.BlockSpec((cols, n), lambda g: (g, 0)),
+        out_shape=jax.ShapeDtypeStruct((d, n), w_t.dtype),
+        compiler_params=pltpu.CompilerParams(vmem_limit_bytes=12 * 2 ** 20),
+        cost_estimate=pl.CostEstimate(flops=2 * d * n * 128, bytes_accessed=4 * d * n, transcendentals=0),
+        name="turn",
+    )(pltpu.with_memory_space_constraint(w_t, pltpu.HBM))
+
+
 def norm_kernel(outs_of, x_ref, gain_ref, *refs):
     n_out = len(refs) - 3
     out_refs = refs[:n_out]
@@ -85,7 +104,7 @@
         inv_rms = ss_buf[rows, :]
         for lane in lanes:
             xf = x_ref[0, rows, lane].astype(jnp.float32)
-            n_buf[slot, rows, lane] = (xf * inv_rms * gain_ref[:, lane]).astype(jnp.bfloat16)
+            n_buf[slot, rows, lane] = (xf * inv_rms * gain_ref[:, lane].astype(jnp.float32)).astype(jnp.bfloat16)
         return carry
 
     lax.fori_loop(0, blk // NORM_ROWS, norm_rows, 0)
@@ -102,8 +121,9 @@
                         copy.wait()
 
 
-def norm_call(x, gain, order, outs_of, shapes):
-    blk, d_model = x.shape[1:]
+def norm_call(x, gain, order, outs_of, shapes, blk=None, row_block=0):
+    d_model = x.shape[2]
+    blk = blk or x.shape[1]
 
     def prompt_of(g):
         idx = jnp.int32(order[-1])
@@ -114,7 +134,7 @@
     return pl.pallas_call(
         functools.partial(norm_kernel, outs_of),
         grid=(len(order),),
-        in_specs=[pl.BlockSpec((1, blk, d_model), lambda g: (prompt_of(g), 0, 0)),
+        in_specs=[pl.BlockSpec((1, blk, d_model), lambda g: (prompt_of(g), row_block, 0)),
                   pl.BlockSpec((1, d_model), lambda g: (0, 0))],
         out_specs=[pl.BlockSpec(memory_space=pl.ANY)] * len(shapes),
         out_shape=[jax.ShapeDtypeStruct((*shape, d_model), jnp.bfloat16) for shape in shapes],
@@ -136,7 +156,7 @@
     heads = wk.shape[1] // HEAD_DIM
     xf = jnp.concatenate([new_ref[...].astype(jnp.float32), last_ref[...].astype(jnp.float32)], axis=0)
     inv_rms = lax.rsqrt(jnp.mean(xf * xf, axis=-1, keepdims=True) + 1e-5)
-    normed = (xf * inv_rms * gain_ref[...]).astype(jnp.bfloat16)
+    normed = (xf * inv_rms * gain_ref[...].astype(jnp.float32)).astype(jnp.bfloat16)
     k_all = jnp.dot(normed, wk[...], preferred_element_type=jnp.float32)[:n_batch]
     v_all = jnp.dot(normed, wv[...], preferred_element_type=jnp.float32)[:n_batch].astype(jnp.bfloat16)
     load.wait()
@@ -207,7 +227,7 @@
         rest = rest[2:]
     else:
         rest = rest[3:]
-    kc_ref, vc_ref, st_ref, x_buf, k_buf, v_buf, k_out, v_out, s_out, x_sem, sems, new_sem = rest
+    kc_ref, vc_ref, st_ref, x_buf, k_buf, v_buf, k_out, v_out, s_out, x_sem, sems, s_sem, new_sem = rest
     step = pl.program_id(0)
     n_steps = pl.num_programs(0)
     slot = lax.rem(step, 2)
@@ -238,11 +258,10 @@
     def out_copies(which, at_step):
         copies = []
         for i in range(n_in):
-            shard, bat, mask = place(i, at_step)
+            shard, bat, _ = place(i, at_step)
             rows = pl.ds(shard * shard_rows + row0, blk)
             copies.append(pltpu.make_async_copy(k_out.at[which, i], kc_ref.at[bat, rows], sems.at[which, i, 0]))
             copies.append(pltpu.make_async_copy(v_out.at[which, i], vc_ref.at[bat, rows], sems.at[which, i, 1]))
-            copies.append(pltpu.make_async_copy(s_out.at[which, i], st_ref.at[mask + stat_of, bat], sems.at[which, i, 2]))
         return copies
 
     def new_copies():
@@ -290,6 +309,12 @@
 
     lax.fori_loop(0, width // COL_TILE, col_tile, 0)
 
+    for i in range(n_in):
+        k_out[slot, i] = k_buf[i * blk:(i + 1) * blk, :].reshape(blk, heads, HEAD_DIM)
+        v_out[slot, i] = v_buf[i * blk:(i + 1) * blk, :].reshape(blk, heads, HEAD_DIM)
+    for copy in out_copies(slot, step):
+        copy.start()
+
     head_of_row = lax.broadcasted_iota(jnp.int32, (STAT_ROWS, HEAD_DIM), 0) // (STAT_ROWS // heads)
     probs = []
     for i in range(n_in):
@@ -302,21 +327,21 @@
         blk_max = jnp.max(scores, axis=-1, keepdims=True)
         prob = jnp.where(visible, jnp.exp(scores - blk_max), 0.0)
         probs.append((blk_max, prob))
-    stats = []
     for i, (blk_max, prob) in enumerate(probs):
         full = jnp.dot(prob.astype(jnp.bfloat16), v_buf[i * blk:(i + 1) * blk, :], preferred_element_type=jnp.float32)
         acc = jnp.zeros((STAT_ROWS, HEAD_DIM), jnp.float32)
         for h in range(heads):
             acc = jnp.where(head_of_row == h, full[:, h * HEAD_DIM:(h + 1) * HEAD_DIM], acc)
-        stats.append((acc, blk_max, jnp.sum(prob, axis=-1, keepdims=True)))
+        s_out[i, 0] = acc
+        s_out[i, 1] = jnp.broadcast_to(blk_max, (STAT_ROWS, HEAD_DIM))
+        s_out[i, 2] = jnp.broadcast_to(jnp.sum(prob, axis=-1, keepdims=True), (STAT_ROWS, HEAD_DIM))
+    stat_copies = []
     for i in range(n_in):
-        k_out[slot, i] = k_buf[i * blk:(i + 1) * blk, :].reshape(blk, heads, HEAD_DIM)
-        v_out[slot, i] = v_buf[i * blk:(i + 1) * blk, :].reshape(blk, heads, HEAD_DIM)
-        for k, stat in enumerate(stats[i]):
-            s_out[slot, i, k] = jnp.broadcast_to(stat, (STAT_ROWS, HEAD_DIM))
-
-    for copy in out_copies(slot, step):
-        copy.start()
+        _, bat, mask = place(i, step)
+        stat_copies.append(pltpu.make_async_copy(s_out.at[i], st_ref.at[mask + stat_of, bat], s_sem.at[i]))
+        stat_copies[-1].start()
+    for copy in stat_copies:
+        copy.wait()
 
     @pl.when(step == n_steps - 1)
     def _():
@@ -350,7 +375,7 @@
         in_specs += [any_spec] * 2
         aliases = {}
     else:
-        operands += caches
+        operands += [*caches[:2], pltpu.with_memory_space_constraint(caches[2], pltpu.VMEM)]
         in_specs += [any_spec] * 3
         aliases = {len(operands) - 2: 0, len(operands) - 1: 1, len(operands): 2}
     tokens = n_in * blk
@@ -368,13 +393,14 @@
                 pltpu.VMEM((tokens, width), jnp.bfloat16),
                 pltpu.VMEM((2, n_in, blk, heads, HEAD_DIM), jnp.bfloat16),
                 pltpu.VMEM((2, n_in, blk, heads, HEAD_DIM), jnp.bfloat16),
-                pltpu.VMEM((2, n_in, 3, STAT_ROWS, HEAD_DIM), jnp.float32),
+                pltpu.VMEM((n_in, 3, STAT_ROWS, HEAD_DIM), jnp.float32),
                 pltpu.SemaphoreType.DMA((2, n_in)),
-                pltpu.SemaphoreType.DMA((2, n_in, 3)),
+                pltpu.SemaphoreType.DMA((2, n_in, 2)),
+                pltpu.SemaphoreType.DMA((n_in,)),
                 pltpu.SemaphoreType.DMA((2, n_batch)),
             ],
         ),
-        out_shape=[jax.ShapeDtypeStruct(c.shape, c.dtype) for c in caches],
+        out_shape=[*(jax.ShapeDtypeStruct(c.shape, c.dtype) for c in caches[:2]), pltpu.VMEM(caches[2].shape, caches[2].dtype)],
         input_output_aliases=aliases,
         compiler_params=pltpu.CompilerParams(vmem_limit_bytes=20 * 2 ** 20),
         cost_estimate=pl.CostEstimate(flops=4 * n_steps * tokens * d_model * width, bytes_accessed=2 * n_steps * tokens * (d_model + 2 * width), transcendentals=0),
@@ -382,26 +408,24 @@
     )(scalars, *operands)
 
 
-def tail_kernel(n_dev, parts_of, st_ref, self_ref, xs_ref, gain_ref, wo_hbm, wg_hbm, wu_hbm, wd_hbm, dec_ref, last_ref,
-                wo, wg, wu, wd, stv, rows, a_buf, n_buf, mid_buf, ps1, pr1, ps2, pr2, xo1, xg1, xo2, xg2,
-                w_sem, send_sem, recv_sem):
+def tail_kernel(n_dev, parts_of, stv, self_ref, xs_ref, gain_ref, wo, wg_hbm, wu_hbm, wd_hbm, out_ref,
+                wg, wu, wd, rows, a_buf, n_buf, ps1, pr1, ps2, pr2, xo1, xg1, xo2, xg2, w_sem, send_sem, recv_sem):
     me = lax.axis_index("model")
-    n_batch = dec_ref.shape[0]
+    n_batch = out_ref.shape[1]
     n_rows = 2 * n_batch
-    d_model = dec_ref.shape[1]
+    d_model = out_ref.shape[2]
     cols = d_model // n_dev
     heads = STAT_ROWS // 2
-    loads = [pltpu.make_async_copy(src, dst, w_sem.at[i]) for i, (src, dst) in enumerate(
-        ((st_ref, stv), (wo_hbm, wo), (wg_hbm, wg), (wu_hbm, wu), (wd_hbm, wd)))]
-    loads[0].start()
-    loads[1].start()
+    loads = [pltpu.make_async_copy(src, dst, w_sem.at[i]) for i, (src, dst) in enumerate(((wg_hbm, wg), (wu_hbm, wu), (wd_hbm, wd)))]
+    for load in loads:
+        load.start()
     barrier = pltpu.get_barrier_semaphore()
 
     def peer_of(mask):
         return sum(lax.rem(me // bit + mask // bit, 2) * bit for bit in (1, 2, 4))
 
-    far_first = sorted(range(1, n_dev), key=lambda mask: (-(mask & 2) - (mask & 4) // 2, mask))
-    for mask in far_first:
+    far_first = ((6, 7), (2, 3, 4, 5), (1,))
+    for mask in sum(far_first, ()):
         pl.semaphore_signal(barrier, inc=1, device_id={"model": peer_of(mask)}, device_id_type=MESH)
 
     def send(phase, mask, src, dst):
@@ -409,9 +433,6 @@
             src_ref=src, dst_ref=dst, send_sem=send_sem.at[phase, mask - 1], recv_sem=recv_sem.at[phase, mask - 1],
             device_id={"model": peer_of(mask)}, device_id_type=MESH)
 
-    loads[0].wait()
-    for load in loads[2:]:
-        load.start()
     for b in range(n_batch):
         top = self_ref[1, b]
         for j in range(parts_of[b]):
@@ -429,101 +450,93 @@
             a_buf[t * n_batch:(t + 1) * n_batch, h * HEAD_DIM:(h + 1) * HEAD_DIM] = rows[2 * h + t]
     att = a_buf[...].astype(jnp.bfloat16)
 
-    def all_reduce(phase, partial, base, ps, pr, xo, xg):
-        copies = []
-        for mask in far_first:
-            ps[mask - 1] = partial(peer_of(mask))
-            copies.append(send(phase, mask, ps.at[mask - 1], pr.at[mask - 1]))
-            copies[-1].start()
-        total = base + partial(me)
-        for copy, mask in zip(reversed(copies), reversed(far_first)):
+    def exchange(phase, base, copies, pr, xo, xg):
+        total = base
+        for copy, mask in reversed(copies):
             copy.wait_recv()
             total = total + pr[mask - 1]
         xo[...] = total.astype(jnp.bfloat16)
         outs = []
-        for mask in far_first:
+        for mask in sum(far_first, ()):
             outs.append(send(phase + 1, mask, xo, xg.at[me]))
             outs[-1].start()
         xg[me] = xo[...]
         for out in outs:
             out.wait_recv()
-        return copies + outs
+        return [copy for copy, _ in copies] + outs
 
     def col_block(p):
         return pl.ds(pl.multiple_of(p * cols, cols), cols)
 
-    loads[1].wait()
+    part = jnp.dot(att, wo[...], preferred_element_type=jnp.float32)
+    for j in range(n_dev):
+        ps1[j] = part[:, j * cols:(j + 1) * cols]
     pl.semaphore_wait(barrier, n_dev - 1)
-    sent = all_reduce(0, lambda p: jnp.dot(att, wo[:, col_block(p)], preferred_element_type=jnp.float32),
-                      xs_ref[...].astype(jnp.float32), ps1, pr1, xo1, xg1)
+    copies = []
+    for mask in sum(far_first, ()):
+        copies.append((send(0, mask, ps1.at[peer_of(mask)], pr1.at[mask - 1]), mask))
+        copies[-1][0].start()
+    sent = exchange(0, xs_ref[...].astype(jnp.float32) + ps1[me], copies, pr1, xo1, xg1)
     sq = jnp.zeros((n_rows, 1), jnp.float32)
     for j in range(n_dev):
         xf = xg1[j].astype(jnp.float32)
         sq += jnp.sum(xf * xf, axis=-1, keepdims=True)
     inv_rms = lax.rsqrt(sq / d_model + 1e-5)
     for j in range(n_dev):
-        xf = xg1[j].astype(jnp.float32)
-        n_buf[:, j * cols:(j + 1) * cols] = (xf * inv_rms * gain_ref[:, j * cols:(j + 1) * cols]).astype(jnp.bfloat16)
+        at = slice(j * cols, (j + 1) * cols)
+        n_buf[:, at] = (xg1[j].astype(jnp.float32) * inv_rms * gain_ref[:, at].astype(jnp.float32)).astype(jnp.bfloat16)
+    loads[0].wait()
+    loads[1].wait()
+    gate = jnp.dot(n_buf[...], wg[...], preferred_element_type=jnp.float32)
+    up = jnp.dot(n_buf[...], wu[...], preferred_element_type=jnp.float32)
+    mid = (gate * (1.0 / (1.0 + jnp.exp(-gate))) * up).astype(jnp.bfloat16)
     loads[2].wait()
-    loads[3].wait()
-    nt = (((1,), (1,)), ((), ()))
-    n_hid = wg.shape[0]
-    rows_per = n_hid // 2
-
-    def hidden_rows(r, carry):
-        at = pl.ds(pl.multiple_of(r * rows_per, 8), rows_per)
-        gate = lax.dot_general(wg[at, :], n_buf[...], nt, preferred_element_type=jnp.float32)
-        up = lax.dot_general(wu[at, :], n_buf[...], nt, preferred_element_type=jnp.float32)
-        mid_buf[at, :] = gate * (1.0 / (1.0 + jnp.exp(-gate))) * up
-        return carry
-
-    lax.fori_loop(0, 2, hidden_rows, 0)
-    mid = mid_buf[...].T.astype(jnp.bfloat16)
-    loads[4].wait()
-    sent += all_reduce(2, lambda p: jnp.dot(mid, wd[:, col_block(p)], preferred_element_type=jnp.float32),
-                       xo1[...].astype(jnp.float32), ps2, pr2, xo2, xg2)
+    copies = []
+    for group in far_first:
+        for mask in group:
+            ps2[mask] = jnp.dot(mid, wd[:, col_block(peer_of(mask))], preferred_element_type=jnp.float32)
+        if group == far_first[-1]:
+            ps2[0] = jnp.dot(mid, wd[:, col_block(me)], preferred_element_type=jnp.float32)
+        for mask in group:
+            copies.append((send(2, mask, ps2.at[mask], pr2.at[mask - 1]), mask))
+            copies[-1][0].start()
+    sent += exchange(2, xo1[...].astype(jnp.float32) + ps2[0], copies, pr2, xo2, xg2)
     for j in range(n_dev):
-        dec_ref[:, j * cols:(j + 1) * cols] = xg2[j, :n_batch]
-        last_ref[:, j * cols:(j + 1) * cols] = xg2[j, n_batch:]
+        at = slice(j * cols, (j + 1) * cols)
+        out_ref[0, :, at] = xg2[j, :n_batch]
+        out_ref[1, :, at] = xg2[j, n_batch:]
     for copy in sent:
         copy.wait_send()
 
 
-def tail_call(n_dev, parts_of, stats, self_stat, x_mine, gain, w_o, w_gate_t, w_up_t, w_down, n_batch):
+def tail_call(n_dev, parts_of, stats, self_stat, x_mine, gain, w_o, w_gate, w_up, w_down, n_batch):
     n_rows, cols = x_mine.shape
     d_model = w_o.shape[1]
     vmem = pl.BlockSpec(memory_space=pltpu.VMEM)
-    hbm = pl.BlockSpec(memory_space=pltpu.HBM)
+    any_spec = pl.BlockSpec(memory_space=pl.ANY)
+    exchanged = [pltpu.VMEM((n_dev, n_rows, cols), jnp.float32), pltpu.VMEM((n_dev - 1, n_rows, cols), jnp.float32)]
+    summed = [pltpu.VMEM((n_rows, cols), jnp.bfloat16), pltpu.VMEM((n_dev, n_rows, cols), jnp.bfloat16)]
     return pl.pallas_call(
         functools.partial(tail_kernel, n_dev, parts_of),
-        out_shape=[jax.ShapeDtypeStruct((n_batch, d_model), jnp.bfloat16)] * 2,
-        in_specs=[pl.BlockSpec(memory_space=pl.ANY), vmem, vmem, vmem, hbm, hbm, hbm, hbm],
-        out_specs=[vmem, vmem],
+        out_shape=jax.ShapeDtypeStruct((2, n_batch, d_model), jnp.bfloat16),
+        in_specs=[vmem] * 5 + [any_spec] * 3,
+        out_specs=vmem,
         scratch_shapes=[
-            pltpu.VMEM(w_o.shape, jnp.bfloat16),
-            pltpu.VMEM(w_gate_t.shape, jnp.bfloat16),
-            pltpu.VMEM(w_up_t.shape, jnp.bfloat16),
+            pltpu.VMEM(w_gate.shape, jnp.bfloat16),
+            pltpu.VMEM(w_up.shape, jnp.bfloat16),
             pltpu.VMEM(w_down.shape, jnp.bfloat16),
-            pltpu.VMEM(stats.shape, jnp.float32),
             pltpu.VMEM((STAT_ROWS, n_batch, HEAD_DIM), jnp.float32),
             pltpu.VMEM((n_rows, w_o.shape[0]), jnp.float32),
             pltpu.VMEM((n_rows, d_model), jnp.bfloat16),
-            pltpu.VMEM((w_gate_t.shape[0], n_rows), jnp.float32),
-            pltpu.VMEM((n_dev - 1, n_rows, cols), jnp.float32),
-            pltpu.VMEM((n_dev - 1, n_rows, cols), jnp.float32),
-            pltpu.VMEM((n_dev - 1, n_rows, cols), jnp.float32),
-            pltpu.VMEM((n_dev - 1, n_rows, cols), jnp.float32),
-            pltpu.VMEM((n_rows, cols), jnp.bfloat16),
-            pltpu.VMEM((n_dev, n_rows, cols), jnp.bfloat16),
-            pltpu.VMEM((n_rows, cols), jnp.bfloat16),
-            pltpu.VMEM((n_dev, n_rows, cols), jnp.bfloat16),
-            pltpu.SemaphoreType.DMA((5,)),
+            *exchanged, *exchanged, *summed, *summed,
+            pltpu.SemaphoreType.DMA((3,)),
             pltpu.SemaphoreType.DMA((4, n_dev - 1)),
             pltpu.SemaphoreType.DMA((4, n_dev - 1)),
         ],
-        compiler_params=pltpu.CompilerParams(collective_id=0, has_side_effects=True, vmem_limit_bytes=52 * 2 ** 20),
+        compiler_params=pltpu.CompilerParams(collective_id=0, has_side_effects=True, vmem_limit_bytes=46 * 2 ** 20),
         name="tail",
-    )(stats, self_stat, x_mine, gain, *(pltpu.with_memory_space_constraint(w, pltpu.HBM) for w in (w_o, w_gate_t, w_up_t, w_down)))
+    )(pltpu.with_memory_space_constraint(stats, pltpu.VMEM), self_stat, x_mine, gain, w_o,
+      *(pltpu.with_memory_space_constraint(w, pltpu.HBM) for w in (w_gate, w_up, w_down)))
 
 
 def solution(mesh):
@@ -548,13 +561,14 @@
         heads = width // HEAD_DIM
         half = n_batch // 2
         wq = w_q[0]
-        gain = norm_attn.astype(jnp.float32)
+        gain = norm_attn
 
         q1, q2, rows_h = n_batch // 8, n_batch // 4, blk // 2
         a_parts, b_parts = {}, {}
         order = [side * half + k for k in range(q1) for side in range(2)]
-        outs_of = [[(2 * h + side, k, h * rows_h, rows_h) for h in range(2)] for k in range(q1) for side in range(2)]
-        a_parts["0a"], b_parts["0a"], a_parts["0b"], b_parts["0b"] = norm_call(prompt, gain, order, outs_of, [(q1, rows_h)] * 4)
+        outs_of = [[(side, k, 0, rows_h)] for k in range(q1) for side in range(2)]
+        for h, name in enumerate(("0a", "0b")):
+            a_parts[name], b_parts[name] = norm_call(prompt, gain, order, outs_of, [(q1, rows_h)] * 2, rows_h, h)
         from_y, from_x = {}, {}
 
         def send_part(step, along_y, along_x):
@@ -588,9 +602,9 @@
         tabs = tuple(tab.reshape(n_dev, blk, HEAD_DIM) for tab in rotary_tables(jnp.arange(seq_len)))
         x_rows = jnp.concatenate([new_tok, last_x], axis=0)
         x_mine = lax.dynamic_slice_in_dim(x_rows, my_idx * (d_model // n_dev), d_model // n_dev, axis=1)
-        wk, wv, last_x, scalars, row_tabs, tabs, x_mine, gain_mlp = lax.optimization_barrier(
-            (w_k[0], w_v[0], last_x, scalars, row_tabs, tabs, x_mine, norm_mlp.astype(jnp.float32)))
-        wk, wv = keep_in_vmem(wk, wv)
+        wk, wv, wo, last_x, scalars, row_tabs, tabs, x_mine = lax.optimization_barrier(
+            (w_k[0], w_v[0], w_o[0], last_x, scalars, row_tabs, tabs, x_mine))
+        wk, wv, wo = keep_in_vmem(wk, wv, wo)
         q_diag, k_new, v_new, self_stat = rows_call(new_tok, last_x, gain, row_tabs, wq, wk, wv)
         cache_shape = jax.ShapeDtypeStruct((n_batch, seq_len + 1, heads, HEAD_DIM), jnp.bfloat16)
         caches = [cache_shape, cache_shape, jax.ShapeDtypeStruct((2 * n_dev - 2, n_batch, 3, STAT_ROWS, HEAD_DIM), jnp.float32)]
@@ -607,7 +621,7 @@
 
         caches = run([[(arr, 0), (arr, half)] for arr in (normed, core_all)], half,
                      [[0] * 2, [1] * 2], [[0, half]] * 2, caches, new_rows=[k_new, v_new])
-        diag = {}
+        diag, turned = {}, {}
         starts = {"0a": (0, half), "0b": (0, half), "1": (q1, half + q1), "2": (q2, half + q2), "3": (half + q2, q2), "4": (half, 0)}
         for step, start in starts.items():
             caches, (got_y, got_x) = after(caches, from_y[step], from_x[step])
@@ -619,6 +633,10 @@
                 caches = run([streams[0] + streams[1]], q1, [[4, 2, 5, 3]], [[*start, *start]], caches, **half_rows(step))
             else:
                 caches = run(streams, got_y.shape[0], [[4, 2], [5, 3]], [list(start)] * 2, caches)
+            if step in "34":
+                caches, (w_t,) = after(caches, (w_gate if step == "3" else w_up)[0].T)
+                turned[step] = turn_call(w_t)
+                caches, (turned[step],) = after(caches, turned[step])
         for step in ("2", "1", "0a", "0b"):
             caches, (via_x, via_y) = after(caches, *diag[step])
             other_x, other_y = swap(via_x, 1), swap(via_y, 1)
@@ -631,8 +649,7 @@
 
         k_cache, v_cache, stats = caches
         parts_of = [2 * n_dev - 2 if b % half < q1 else n_dev for b in range(n_batch)]
-        dec_hidden, last_hidden = tail_call(n_dev, parts_of, stats, self_stat, x_mine, gain_mlp, w_o[0],
-                                            w_gate[0].T, w_up[0].T, w_down[0], n_batch)
-        return dec_hidden, last_hidden, k_cache[None], v_cache[None]
+        both = tail_call(n_dev, parts_of, stats, self_stat, x_mine, norm_mlp, wo, turned["3"], turned["4"], w_down[0], n_batch)
+        return both[0], both[1], k_cache[None], v_cache[None]
 
     return jax.shard_map(per_device, mesh=mesh, in_specs=in_specs, out_specs=out_specs, check_vma=False)

time: 408 us -> 407 us (level)
  waiting for transfers between devices: 181 us -> 156 us
  Pallas kernels: 172 us -> 185 us
  local copies, waits for them, and re-layouts: 8.85 us -> 18 us
    ppermute x45, waiting for transfers between devices: 181 us -> 156 us  [swap(): return lax.ppermute(arr, 'model', [(i, i ^ bit) for i in range(n_dev)])]
    pallas_call x0 -> x2, Pallas kernels: none -> 15.8 us  [turn_call(): pl.pallas_call(turn_kernel, grid=(d // cols,), in_specs=[pl.BlockSpec((n,...]
    unnamed x28 -> x26, local copies, waits for them, and re-layouts: 6.17 us -> 12.6 us
    pallas_call x2 -> x3, Pallas kernels: 13.4 us -> 15 us  [norm_call(): pl.pallas_call(functools.partial(norm_kernel, outs_of), grid=(len(order),...]
  transfers between devices with their start and end apart: 45 -> 45, of which waited for: 32 -> 31; matrix products, arithmetic and copies ran while one was open for 2% -> 3% of each run, Pallas kernels for 32% -> 36%
where the time goes in v5:
time: 407 us; the launch traced here: 406 us
  Pallas kernels  185 us (45%)
  waiting for transfers between devices  156 us (38%)
  starting transfers between devices  37.5 us (9%)
  local copies, waits for them, and re-layouts  18 us (4%)
  matrix products  4.59 us (1%)
    ppermute x45, waiting for transfers between devices, swap(): return lax.ppermute(arr, 'model', [(i, i ^ bit) for i in range(n_dev)])  156 us
    pallas_call x11, Pallas kernels, kv_call(): pl.pallas_call(functools.partial(kv_kernel, n_in, masks, batches, [[first...  123 us
    ppermute x45, starting transfers between devices, swap(): return lax.ppermute(arr, 'model', [(i, i ^ bit) for i in range(n_dev)])  37.5 us
    pallas_call x1, Pallas kernels, tail_call(): pl.pallas_call(functools.partial(tail_kernel, n_dev, parts_of), out_shape...  23.3 us
    pallas_call x2, Pallas kernels, turn_call(): pl.pallas_call(turn_kernel, grid=(d // cols,), in_specs=[pl.BlockSpec((n,...  15.8 us
    pallas_call x3, Pallas kernels, norm_call(): pl.pallas_call(functools.partial(norm_kernel, outs_of), grid=(len(order),...  15 us
    unnamed x26, local copies, waits for them, and re-layouts  12.6 us
  transfers between devices with their start and end apart: 45, of which 31 were waited for; matrix products, arithmetic and copies ran while one was open for 3% of the time, Pallas kernels for 36%

profile of v5, /device:TPU:0, one launch (start us, length us, event | category | flops | bytes accessed | tf_op | source)
XLA Modules:
  0.0 405.8 jit_solution(18141543508754295608)
XLA Ops:
  1.4 10.8 %norm_rows.3 = (bf16[1,128,4096]{2,1,0:T(8,128)(2,1)S(1)}, bf16[1,128,4096]{2,1,0:T(8,128)(2,1)S(1)}, bf16[2,128,4096]{2,1,0:T(8,128)(2,1)S(1)}, bf16[2,128,4096]{2,1,0:T(8,128)(2,1)S(1)}, bf16[8,128,4096]{2,1,0:T(8,128)(2,1)}) custom-call(bf16[8,128,4096]{2,1,0:T(8,128)(2,1)} %x_ref.5, bf16[1,4096]{1,0:T(2,128)(2,1)S(1)} %copy-done.2), custom_call_target="tpu_custom_call" | custom-call | flops 33554432 | bytes 25165824 | tf_op jit(solution)/shard_map/norm_rows/pallas_call | solution.py:134
  15.8 4.6 %fusion.2 = bf16[8,1,4096]{2,1,0:T(2,128)(2,1)S(1)} fusion(bf16[8,128,4096]{2,1,0:T(8,128)(2,1)} %x_ref.5, pred[8,128,1]{1,0,2:T(8,128)(4,1)S(1)} %compare_bitcast_fusion), kind=kOutput, calls=%fused_computation.12 | convolution fusion | flops 8388608 | bytes 8455168 | tf_op jit(solution)/shard_map/bs,bsd->bd/dot_general | solution.py:591
  20.5 2.3 norm_rows.4
  23.6 3.0 collective-permute-start.5
  26.7 1.9 fusion
  30.1 3.6 collective-permute-start.3
  34.4 1.8 collective-permute-done.3
  36.2 1.8 collective-permute-start.6
  37.9 3.8 collective-permute-done.2
  41.8 4.7 %keep.1 = (bf16[4096,512]{1,0:T(8,128)(2,1)S(1)}, bf16[4096,512]{1,0:T(8,128)(2,1)S(1)}, bf16[512,4096]{1,0:T(8,128)(2,1)S(1)}) custom-call(bf16[4096,512]{1,0:T(8,128)(2,1)} %bitcast.30, bf16[4096,512]{1,0:T(8,128)(2,1)} %bitcast.31, bf16[512,4096]{1,0:T(8,128)(2,1)} %bitcast.32), custom_call_target="tpu_custom_call" | custom-call | tf_op jit(solution)/shard_map/keep/pallas_call | solution.py:40
  46.5 3.1 query_rows.1
  49.6 28.4 %kv_chunk.11 = (bf16[8,1025,4,128]{3,2,1,0:T(4,128)(2,1)}, bf16[8,1025,4,128]{3,2,1,0:T(4,128)(2,1)}, f32[14,8,3,8,128]{4,3,2,1,0:T(8,128)S(1)}) custom-call(s32[16]{0:T(128)S(1)} %get-tuple-element.101.sc_ref, bf16[8,128,4096]{2,1,0:T(8,128)(2,1)} %get-tuple-element.102.refs_0_.refs_1_, bf16[8,128,4096]{2,1,0:T(8,128)(2,1)} %get-tuple-element.102.refs_0_.refs_1_, ...), custom_call_target="tpu_custom_call" | custom-call | flops 17179869184 | bytes 20971520 | tf_op jit(solution)/shard_map/kv_chunk/pallas_call | solution.py:383
  78.6 1.9 norm_rows.5
  80.5 1.8 collective-permute-start.9
  83.7 4.9 %kv_chunk.12 = (bf16[8,1025,4,128]{3,2,1,0:T(4,128)(2,1)}, bf16[8,1025,4,128]{3,2,1,0:T(4,128)(2,1)}, f32[14,8,3,8,128]{4,3,2,1,0:T(8,128)S(1)}) custom-call(s32[16]{0:T(128)S(1)} %get-tuple-element.101.sc_ref, bf16[1,64,4096]{2,1,0:T(8,128)(2,1)S(1)} %collective-permute-done.5.refs_0_, ...), custom_call_target="tpu_custom_call", output_to_operand_aliasing={{0}: (10, {}), {1}: (11, {}), {2}: (12, {})} | custom-call | flops 2147483648 | bytes 2621440 | tf_op jit(solution)/shard_map/kv_chunk/pallas_call | solution.py:383
  88.6 5.7 %collective-permute-done.9.refs_0_ = bf16[1,64,4096]{2,1,0:T(8,128)(2,1)S(1)} collective-permute-done((bf16[1,64,4096]{2,1,0:T(8,128)(2,1)S(1)}, bf16[1,64,4096]{2,1,0:T(8,128)(2,1)S(1)}, u32[]{:S(2)}, u32[]{:S(2)}) %collective-permute-start.9) | collective-permute-done | bytes 524320 | tf_op jit(solution)/shard_map/ppermute | solution.py:554
  96.1 1.7 collective-permute-start.14
  99.9 4.9 %kv_chunk.13 = (bf16[8,1025,4,128]{3,2,1,0:T(4,128)(2,1)}, bf16[8,1025,4,128]{3,2,1,0:T(4,128)(2,1)}, f32[14,8,3,8,128]{4,3,2,1,0:T(8,128)S(1)}) custom-call(s32[16]{0:T(128)S(1)} %get-tuple-element.101.sc_ref, bf16[1,64,4096]{2,1,0:T(8,128)(2,1)S(1)} %collective-permute-done.9.refs_0_, ...), custom_call_target="tpu_custom_call", output_to_operand_aliasing={{0}: (10, {}), {1}: (11, {}), {2}: (12, {})} | custom-call | flops 2147483648 | bytes 2621440 | tf_op jit(solution)/shard_map/kv_chunk/pallas_call | solution.py:383
  104.8 17.1 %collective-permute-done.13.refs_0_ = bf16[1,128,4096]{2,1,0:T(8,128)(2,1)S(1)} collective-permute-done((bf16[1,128,4096]{2,1,0:T(8,128)(2,1)S(1)}, bf16[1,128,4096]{2,1,0:T(8,128)(2,1)S(1)}, u32[]{:S(2)}, u32[]{:S(2)}) %collective-permute-start.13) | collective-permute-done | bytes 1048608 | tf_op jit(solution)/shard_map/ppermute | solution.py:554
  122.7 2.1 collective-permute-done.15.refs_2_
  126.3 8.3 %kv_chunk.14 = (bf16[8,1025,4,128]{3,2,1,0:T(4,128)(2,1)}, bf16[8,1025,4,128]{3,2,1,0:T(4,128)(2,1)}, f32[14,8,3,8,128]{4,3,2,1,0:T(8,128)S(1)}) custom-call(s32[16]{0:T(128)S(1)} %get-tuple-element.101.sc_ref, bf16[1,128,4096]{2,1,0:T(8,128)(2,1)S(1)} %collective-permute-done.13.refs_0_, ...), custom_call_target="tpu_custom_call", output_to_operand_aliasing={{0}: (10, {}), {1}: (11, {}), {2}: (12, {})} | custom-call | flops 4294967296 | bytes 5242880 | tf_op jit(solution)/shard_map/kv_chunk/pallas_call | solution.py:383
  134.6 31.7 %collective-permute-done.17.refs_0_ = bf16[2,128,4096]{2,1,0:T(8,128)(2,1)S(1)} collective-permute-done((bf16[2,128,4096]{2,1,0:T(8,128)(2,1)S(1)}, bf16[2,128,4096]{2,1,0:T(8,128)(2,1)S(1)}, u32[]{:S(2)}, u32[]{:S(2)}) %collective-permute-start.17) | collective-permute-done | bytes 2097184 | tf_op jit(solution)/shard_map/ppermute | solution.py:554
  166.9 1.7 collective-permute-start.22
  170.5 3.0 collective-permute-done.20.refs_3_
  173.5 14.7 %kv_chunk.15 = (bf16[8,1025,4,128]{3,2,1,0:T(4,128)(2,1)}, bf16[8,1025,4,128]{3,2,1,0:T(4,128)(2,1)}, f32[14,8,3,8,128]{4,3,2,1,0:T(8,128)S(1)}) custom-call(s32[16]{0:T(128)S(1)} %get-tuple-element.101.sc_ref, bf16[2,128,4096]{2,1,0:T(8,128)(2,1)S(1)} %collective-permute-done.17.refs_0_, ...), custom_call_target="tpu_custom_call", output_to_operand_aliasing={{0}: (10, {}), {1}: (11, {}), {2}: (12, {})} | custom-call | flops 8589934592 | bytes 10485760 | tf_op jit(solution)/shard_map/kv_chunk/pallas_call | solution.py:383
  188.3 26.2 %collective-permute-done.22.refs_1_ = bf16[2,128,4096]{2,1,0:T(8,128)(2,1)S(1)} collective-permute-done((bf16[2,128,4096]{2,1,0:T(8,128)(2,1)S(1)}, bf16[2,128,4096]{2,1,0:T(8,128)(2,1)S(1)}, u32[]{:S(2)}, u32[]{:S(2)}) %collective-permute-start.22) | collective-permute-done | bytes 2097184 | tf_op jit(solution)/shard_map/ppermute | solution.py:554
  216.3 4.7 %fusion.14 = (bf16[2,128,4096]{2,1,0:T(8,128)(2,1)}, bf16[2,128,4096]{2,1,0:T(8,128)(2,1)}) fusion(bf16[8,128,4096]{2,1,0:T(8,128)(2,1)} %get-tuple-element.102.refs_0_.refs_1_), kind=kLoop, calls=%fused_computation.51 | loop fusion | bytes 8388608 | tf_op jit(solution)/shard_map/slice | solution.py:596
  221.3 1.7 collective-permute-start.25
  223.1 14.7 %kv_chunk.16 = (bf16[8,1025,4,128]{3,2,1,0:T(4,128)(2,1)}, bf16[8,1025,4,128]{3,2,1,0:T(4,128)(2,1)}, f32[14,8,3,8,128]{4,3,2,1,0:T(8,128)S(1)}) custom-call(s32[16]{0:T(128)S(1)} %get-tuple-element.101.sc_ref, bf16[2,128,4096]{2,1,0:T(8,128)(2,1)S(1)} %collective-permute-done.21.refs_0_, ...), custom_call_target="tpu_custom_call", output_to_operand_aliasing={{0}: (10, {}), {1}: (11, {}), {2}: (12, {})} | custom-call | flops 8589934592 | bytes 10485760 | tf_op jit(solution)/shard_map/kv_chunk/pallas_call | solution.py:383
  237.8 7.9 %turn.2.wg_hbm = bf16[4096,1376]{1,0:T(8,128)(2,1)S(1)} custom-call(bf16[1376,4096]{1,0:T(8,128)(2,1)} %bitcast.27), custom_call_target="tpu_custom_call" | custom-call | flops 1442840576 | bytes 22544384 | tf_op jit(solution)/shard_map/turn/pallas_call | solution.py:58
  245.7 4.2 %copy-done = bf16[4096,1376]{1,0:T(8,128)(2,1)} copy-done((bf16[4096,1376]{1,0:T(8,128)(2,1)}, bf16[4096,1376]{1,0:T(8,128)(2,1)S(1)}, u32[]{:S(2)}) %copy-start) | copy-done | bytes 11272216
  249.9 18.8 %collective-permute-done.26.refs_1_ = bf16[2,128,4096]{2,1,0:T(8,128)(2,1)S(1)} collective-permute-done((bf16[2,128,4096]{2,1,0:T(8,128)(2,1)}, bf16[2,128,4096]{2,1,0:T(8,128)(2,1)S(1)}, u32[]{:S(2)}, u32[]{:S(2)}) %collective-permute-start.26) | collective-permute-done | bytes 2097184 | tf_op jit(solution)/shard_map/ppermute | solution.py:554
  273.0 3.0 collective-permute-done.28.refs_3_
  276.0 14.7 %kv_chunk.17 = (bf16[8,1025,4,128]{3,2,1,0:T(4,128)(2,1)}, bf16[8,1025,4,128]{3,2,1,0:T(4,128)(2,1)}, f32[14,8,3,8,128]{4,3,2,1,0:T(8,128)S(1)}) custom-call(s32[16]{0:T(128)S(1)} %get-tuple-element.101.sc_ref, bf16[2,128,4096]{2,1,0:T(8,128)(2,1)S(1)} %collective-permute-done.25.refs_0_, ...), custom_call_target="tpu_custom_call", output_to_operand_aliasing={{0}: (10, {}), {1}: (11, {}), {2}: (12, {})} | custom-call | flops 8589934592 | bytes 10485760 | tf_op jit(solution)/shard_map/kv_chunk/pallas_call | solution.py:383
  290.7 7.9 %turn.3.wu_hbm = bf16[4096,1376]{1,0:T(8,128)(2,1)S(1)} custom-call(bf16[1376,4096]{1,0:T(8,128)(2,1)} %bitcast.28), custom_call_target="tpu_custom_call" | custom-call | flops 1442840576 | bytes 22544384 | tf_op jit(solution)/shard_map/turn/pallas_call | solution.py:58
  298.6 4.2 %copy-done.1 = bf16[4096,1376]{1,0:T(8,128)(2,1)} copy-done((bf16[4096,1376]{1,0:T(8,128)(2,1)}, bf16[4096,1376]{1,0:T(8,128)(2,1)S(1)}, u32[]{:S(2)}) %copy-start.1) | copy-done | bytes 11272216
  302.8 14.1 %collective-permute-done.29.refs_0_ = bf16[2,128,4096]{2,1,0:T(8,128)(2,1)S(1)} collective-permute-done((bf16[2,128,4096]{2,1,0:T(8,128)(2,1)S(1)}, bf16[2,128,4096]{2,1,0:T(8,128)(2,1)S(1)}, u32[]{:S(2)}, u32[]{:S(2)}) %collective-permute-start.29) | collective-permute-done | bytes 2097184 | tf_op jit(solution)/shard_map/ppermute | solution.py:554
  319.1 1.7 collective-permute-start.34
  322.4 3.0 collective-permute-done.32.refs_3_
  325.4 14.7 %kv_chunk.18 = (bf16[8,1025,4,128]{3,2,1,0:T(4,128)(2,1)}, bf16[8,1025,4,128]{3,2,1,0:T(4,128)(2,1)}, f32[14,8,3,8,128]{4,3,2,1,0:T(8,128)S(1)}) custom-call(s32[16]{0:T(128)S(1)} %get-tuple-element.101.sc_ref, bf16[2,128,4096]{2,1,0:T(8,128)(2,1)S(1)} %collective-permute-done.29.refs_0_, ...), custom_call_target="tpu_custom_call", output_to_operand_aliasing={{0}: (10, {}), {1}: (11, {}), {2}: (12, {})} | custom-call | flops 8589934592 | bytes 10485760 | tf_op jit(solution)/shard_map/kv_chunk/pallas_call | solution.py:383
  340.1 3.7 collective-permute-done.33.refs_0_
  348.1 8.1 %kv_chunk.19 = (bf16[8,1025,4,128]{3,2,1,0:T(4,128)(2,1)}, bf16[8,1025,4,128]{3,2,1,0:T(4,128)(2,1)}, f32[14,8,3,8,128]{4,3,2,1,0:T(8,128)S(1)}) custom-call(s32[16]{0:T(128)S(1)} %get-tuple-element.101.sc_ref, bf16[1,128,4096]{2,1,0:T(8,128)(2,1)S(1)} %collective-permute-done.33.refs_0_, ...), custom_call_target="tpu_custom_call", output_to_operand_aliasing={{0}: (10, {}), {1}: (11, {}), {2}: (12, {})} | custom-call | flops 4294967296 | bytes 5242880 | tf_op jit(solution)/shard_map/kv_chunk/pallas_call | solution.py:383
  356.2 2.1 collective-permute-done.37.refs_0_
  360.5 1.7 collective-permute-start.42
  362.3 4.9 %kv_chunk.20 = (bf16[8,1025,4,128]{3,2,1,0:T(4,128)(2,1)}, bf16[8,1025,4,128]{3,2,1,0:T(4,128)(2,1)}, f32[14,8,3,8,128]{4,3,2,1,0:T(8,128)S(1)}) custom-call(s32[16]{0:T(128)S(1)} %get-tuple-element.101.sc_ref, bf16[1,64,4096]{2,1,0:T(8,128)(2,1)S(1)} %collective-permute-done.37.refs_0_, ...), custom_call_target="tpu_custom_call", output_to_operand_aliasing={{0}: (10, {}), {1}: (11, {}), {2}: (12, {})} | custom-call | flops 2147483648 | bytes 2621440 | tf_op jit(solution)/shard_map/kv_chunk/pallas_call | solution.py:383
  367.2 6.8 %collective-permute-done.41.refs_0_ = bf16[1,64,4096]{2,1,0:T(8,128)(2,1)S(1)} collective-permute-done((bf16[1,64,4096]{2,1,0:T(8,128)(2,1)S(1)}, bf16[1,64,4096]{2,1,0:T(8,128)(2,1)S(1)}, u32[]{:S(2)}, u32[]{:S(2)}) %collective-permute-start.41) | collective-permute-done | bytes 524320 | tf_op jit(solution)/shard_map/ppermute | solution.py:554
  376.7 5.1 %kv_chunk.21 = (bf16[8,1025,4,128]{3,2,1,0:T(4,128)(2,1)}, bf16[8,1025,4,128]{3,2,1,0:T(4,128)(2,1)}, f32[14,8,3,8,128]{4,3,2,1,0:T(8,128)S(1)}) custom-call(s32[16]{0:T(128)S(1)} %get-tuple-element.101.sc_ref, bf16[1,64,4096]{2,1,0:T(8,128)(2,1)S(1)} %collective-permute-done.41.refs_0_, ...), custom_call_target="tpu_custom_call", output_to_operand_aliasing={{0}: (10, {}), {1}: (11, {}), {2}: (12, {})} | custom-call | flops 2147483648 | bytes 2621440 | tf_op jit(solution)/shard_map/kv_chunk/pallas_call | solution.py:383
  381.8 23.3 %tail.1 = bf16[2,8,4096]{2,1,0:T(8,128)(2,1)S(1)} custom-call(f32[14,8,3,8,128]{4,3,2,1,0:T(8,128)S(1)} %get-tuple-element.190.stv, f32[3,8,8,128]{3,2,1,0:T(8,128)S(1)} %get-tuple-element.191.self_ref, bf16[16,512]{1,0:T(8,128)(2,1)S(1)} %fusion.1.xs_ref, bf16[1,4096]{1,0:T(2,128)(2,1)S(1)} %copy-done.5, bf16[512,4096]{1,0:T(8,128)(2,1)S(1)} %get-tuple-element.193.wo, ...), custom_call_target="tpu_custom_call" | custom-call | tf_op jit(solution)/shard_map/tail/pallas_call | solution.py:519
  (105 shorter events, 38.5 us)
Async XLA Ops:
  1.4 14.4 %copy-start.12 = (s32[8]{0:T(128)S(1)}, s32[8]{0:T(128)}, u32[]{:S(2)}) copy-start(s32[8]{0:T(128)} %param.13) | copy-start | bytes 100
  14.9 34.7 %collective-permute-start.4 = (bf16[8,128,4096]{2,1,0:T(8,128)(2,1)}, bf16[8,128,4096]{2,1,0:T(8,128)(2,1)}, u32[]{:S(2)}, u32[]{:S(2)}) collective-permute-start(bf16[8,128,4096]{2,1,0:T(8,128)(2,1)} %get-tuple-element.102.refs_0_.refs_1_), channel_id=1, source_target_pairs={{0,1},{1,0},{2,3},{3,2},{4,5},{5,4},{6,7},{7,6}} | collective-permute-start | bytes 25165832 | tf_op jit(solution)/shard_map/ppermute | solution.py:554
  20.5 8.6 %collective-permute-start = (bf16[8,4096]{1,0:T(8,128)(2,1)S(1)}, bf16[8,4096]{1,0:T(8,128)(2,1)}, u32[]{:S(2)}, u32[]{:S(2)}) collective-permute-start(bf16[8,4096]{1,0:T(8,128)(2,1)S(1)} %bitcast.34), channel_id=1, source_target_pairs={{0,1},{1,0},{2,3},{3,2},{4,5},{5,4},{6,7},{7,6}} | collective-permute-start | bytes 196616 | tf_op jit(solution)/shard_map/ppermute | solution.py:554
  23.6 18.1 %copy-start.4 = (bf16[8,4096]{1,0:T(8,128)(2,1)S(1)}, bf16[8,4096]{1,0:T(8,128)(2,1)}, u32[]{:S(2)}) copy-start(bf16[8,4096]{1,0:T(8,128)(2,1)} %new_ref.1) | copy-start | bytes 196612
  23.6 54.4 %collective-permute-start.5 = (bf16[1,64,4096]{2,1,0:T(8,128)(2,1)}, bf16[1,64,4096]{2,1,0:T(8,128)(2,1)S(1)}, u32[]{:S(2)}, u32[]{:S(2)}) collective-permute-start(bf16[1,64,4096]{2,1,0:T(8,128)(2,1)} %get-tuple-element.117), channel_id=1, source_target_pairs={{0,4},{1,5},{2,6},{3,7},{4,0},{5,1},{6,2},{7,3}} | collective-permute-start | bytes 1572872 | tf_op jit(solution)/shard_map/ppermute | solution.py:554
  30.1 6.1 %collective-permute-start.3 = (bf16[8,4096]{1,0:T(8,128)(2,1)S(1)}, bf16[8,4096]{1,0:T(8,128)(2,1)S(1)}, u32[]{:S(2)}, u32[]{:S(2)}) collective-permute-start(bf16[8,4096]{1,0:T(8,128)(2,1)S(1)} %fusion.16), channel_id=1, source_target_pairs={{0,6},{1,7},{2,4},{3,5},{4,2},{5,3},{6,0},{7,1}} | collective-permute-start | bytes 196616 | tf_op jit(solution)/shard_map/ppermute | solution.py:554
  33.7 8.0 %collective-permute-start.2 = (bf16[8,4096]{1,0:T(8,128)(2,1)S(1)}, bf16[8,4096]{1,0:T(8,128)(2,1)S(1)}, u32[]{:S(2)}, u32[]{:S(2)}) collective-permute-start(bf16[8,4096]{1,0:T(8,128)(2,1)S(1)} %fusion.16), channel_id=1, source_target_pairs={{0,4},{1,5},{2,6},{3,7},{4,0},{5,1},{6,2},{7,3}} | collective-permute-start | bytes 196616 | tf_op jit(solution)/shard_map/ppermute | solution.py:554
  34.2 7.5 %collective-permute-start.1 = (bf16[8,4096]{1,0:T(8,128)(2,1)S(1)}, bf16[8,4096]{1,0:T(8,128)(2,1)S(1)}, u32[]{:S(2)}, u32[]{:S(2)}) collective-permute-start(bf16[8,4096]{1,0:T(8,128)(2,1)S(1)} %fusion.16), channel_id=1, source_target_pairs={{0,2},{1,3},{2,0},{3,1},{4,6},{5,7},{6,4},{7,5}} | collective-permute-start | bytes 196616 | tf_op jit(solution)/shard_map/ppermute | solution.py:554
  36.2 41.8 %collective-permute-start.6 = (bf16[1,64,4096]{2,1,0:T(8,128)(2,1)S(1)}, bf16[1,64,4096]{2,1,0:T(8,128)(2,1)S(1)}, u32[]{:S(2)}, u32[]{:S(2)}) collective-permute-start(bf16[1,64,4096]{2,1,0:T(8,128)(2,1)S(1)} %copy-done.11), channel_id=1, source_target_pairs={{0,2},{1,3},{2,0},{3,1},{4,6},{5,7},{6,4},{7,5}} | collective-permute-start | bytes 1572872 | tf_op jit(solution)/shard_map/ppermute | solution.py:554
  78.0 5.7 %collective-permute-start.7 = (bf16[1,64,4096]{2,1,0:T(8,128)(2,1)S(1)}, bf16[1,64,4096]{2,1,0:T(8,128)(2,1)S(1)}, u32[]{:S(2)}, u32[]{:S(2)}) collective-permute-start(bf16[1,64,4096]{2,1,0:T(8,128)(2,1)S(1)} %collective-permute-done.5.refs_0_), channel_id=1, source_target_pairs={{0,1},{1,0},{2,3},{3,2},{4,5},{5,4},{6,7},{7,6}} | collective-permute-start | bytes 1572872 | tf_op jit(solution)/shard_map/ppermute | solution.py:554
  78.1 5.7 %collective-permute-start.8 = (bf16[1,64,4096]{2,1,0:T(8,128)(2,1)S(1)}, bf16[1,64,4096]{2,1,0:T(8,128)(2,1)S(1)}, u32[]{:S(2)}, u32[]{:S(2)}) collective-permute-start(bf16[1,64,4096]{2,1,0:T(8,128)(2,1)S(1)} %collective-permute-done.6.refs_1_), channel_id=1, source_target_pairs={{0,1},{1,0},{2,3},{3,2},{4,5},{5,4},{6,7},{7,6}} | collective-permute-start | bytes 1572872 | tf_op jit(solution)/shard_map/ppermute | solution.py:554
  80.5 13.9 %collective-permute-start.9 = (bf16[1,64,4096]{2,1,0:T(8,128)(2,1)S(1)}, bf16[1,64,4096]{2,1,0:T(8,128)(2,1)S(1)}, u32[]{:S(2)}, u32[]{:S(2)}) collective-permute-start(bf16[1,64,4096]{2,1,0:T(8,128)(2,1)S(1)} %get-tuple-element.125), channel_id=1, source_target_pairs={{0,4},{1,5},{2,6},{3,7},{4,0},{5,1},{6,2},{7,3}} | collective-permute-start | bytes 1572872 | tf_op jit(solution)/shard_map/ppermute | solution.py:554
  82.2 13.6 %collective-permute-start.10 = (bf16[1,64,4096]{2,1,0:T(8,128)(2,1)S(1)}, bf16[1,64,4096]{2,1,0:T(8,128)(2,1)S(1)}, u32[]{:S(2)}, u32[]{:S(2)}) collective-permute-start(bf16[1,64,4096]{2,1,0:T(8,128)(2,1)S(1)} %get-tuple-element.126), channel_id=1, source_target_pairs={{0,2},{1,3},{2,0},{3,1},{4,6},{5,7},{6,4},{7,5}} | collective-permute-start | bytes 1572872 | tf_op jit(solution)/shard_map/ppermute | solution.py:554
  83.7 15.6 %copy-start.7 = (bf16[2,128,4096]{2,1,0:T(8,128)(2,1)S(1)}, bf16[2,128,4096]{2,1,0:T(8,128)(2,1)}, u32[]{:S(2)}) copy-start(bf16[2,128,4096]{2,1,0:T(8,128)(2,1)} %copy-done.6) | copy-start | bytes 6291460
  95.8 3.5 collective-permute-start.11
  95.8 26.0 %collective-permute-start.13 = (bf16[1,128,4096]{2,1,0:T(8,128)(2,1)S(1)}, bf16[1,128,4096]{2,1,0:T(8,128)(2,1)S(1)}, u32[]{:S(2)}, u32[]{:S(2)}) collective-permute-start(bf16[1,128,4096]{2,1,0:T(8,128)(2,1)S(1)} %get-tuple-element.133), channel_id=1, source_target_pairs={{0,4},{1,5},{2,6},{3,7},{4,0},{5,1},{6,2},{7,3}} | collective-permute-start | bytes 3145736 | tf_op jit(solution)/shard_map/ppermute | solution.py:554
  96.1 26.0 %collective-permute-start.14 = (bf16[1,128,4096]{2,1,0:T(8,128)(2,1)S(1)}, bf16[1,128,4096]{2,1,0:T(8,128)(2,1)S(1)}, u32[]{:S(2)}, u32[]{:S(2)}) collective-permute-start(bf16[1,128,4096]{2,1,0:T(8,128)(2,1)S(1)} %get-tuple-element.134), channel_id=1, source_target_pairs={{0,2},{1,3},{2,0},{3,1},{4,6},{5,7},{6,4},{7,5}} | collective-permute-start | bytes 3145736 | tf_op jit(solution)/shard_map/ppermute | solution.py:554
  97.8 2.1 collective-permute-start.12
  97.8 68.5 %collective-permute-start.17 = (bf16[2,128,4096]{2,1,0:T(8,128)(2,1)S(1)}, bf16[2,128,4096]{2,1,0:T(8,128)(2,1)S(1)}, u32[]{:S(2)}, u32[]{:S(2)}) collective-permute-start(bf16[2,128,4096]{2,1,0:T(8,128)(2,1)S(1)} %copy-done.9), channel_id=1, source_target_pairs={{0,4},{1,5},{2,6},{3,7},{4,0},{5,1},{6,2},{7,3}} | collective-permute-start | bytes 6291464 | tf_op jit(solution)/shard_map/ppermute | solution.py:554
  99.3 67.0 %collective-permute-start.18 = (bf16[2,128,4096]{2,1,0:T(8,128)(2,1)S(1)}, bf16[2,128,4096]{2,1,0:T(8,128)(2,1)S(1)}, u32[]{:S(2)}, u32[]{:S(2)}) collective-permute-start(bf16[2,128,4096]{2,1,0:T(8,128)(2,1)S(1)} %copy-done.7), channel_id=1, source_target_pairs={{0,2},{1,3},{2,0},{3,1},{4,6},{5,7},{6,4},{7,5}} | collective-permute-start | bytes 6291464 | tf_op jit(solution)/shard_map/ppermute | solution.py:554
  122.2 2.7 collective-permute-start.15
  122.2 4.2 %collective-permute-start.16 = (bf16[1,128,4096]{2,1,0:T(8,128)(2,1)S(1)}, bf16[1,128,4096]{2,1,0:T(8,128)(2,1)S(1)}, u32[]{:S(2)}, u32[]{:S(2)}) collective-permute-start(bf16[1,128,4096]{2,1,0:T(8,128)(2,1)S(1)} %collective-permute-done.14.refs_1_), channel_id=1, source_target_pairs={{0,1},{1,0},{2,3},{3,2},{4,5},{5,4},{6,7},{7,6}} | collective-permute-start | bytes 3145736 | tf_op jit(solution)/shard_map/ppermute | solution.py:554
  166.4 4.2 %collective-permute-start.19 = (bf16[2,128,4096]{2,1,0:T(8,128)(2,1)S(1)}, bf16[2,128,4096]{2,1,0:T(8,128)(2,1)S(1)}, u32[]{:S(2)}, u32[]{:S(2)}) collective-permute-start(bf16[2,128,4096]{2,1,0:T(8,128)(2,1)S(1)} %collective-permute-done.17.refs_0_), channel_id=1, source_target_pairs={{0,1},{1,0},{2,3},{3,2},{4,5},{5,4},{6,7},{7,6}} | collective-permute-start | bytes 6291464 | tf_op jit(solution)/shard_map/ppermute | solution.py:554
  166.4 7.2 %collective-permute-start.20 = (bf16[2,128,4096]{2,1,0:T(8,128)(2,1)S(1)}, bf16[2,128,4096]{2,1,0:T(8,128)(2,1)S(1)}, u32[]{:S(2)}, u32[]{:S(2)}) collective-permute-start(bf16[2,128,4096]{2,1,0:T(8,128)(2,1)S(1)} %collective-permute-done.18.refs_1_), channel_id=1, source_target_pairs={{0,1},{1,0},{2,3},{3,2},{4,5},{5,4},{6,7},{7,6}} | collective-permute-start | bytes 6291464 | tf_op jit(solution)/shard_map/ppermute | solution.py:554
  166.9 47.5 %collective-permute-start.22 = (bf16[2,128,4096]{2,1,0:T(8,128)(2,1)S(1)}, bf16[2,128,4096]{2,1,0:T(8,128)(2,1)S(1)}, u32[]{:S(2)}, u32[]{:S(2)}) collective-permute-start(bf16[2,128,4096]{2,1,0:T(8,128)(2,1)S(1)} %copy-done.9), channel_id=1, source_target_pairs={{0,2},{1,3},{2,0},{3,1},{4,6},{5,7},{6,4},{7,5}} | collective-permute-start | bytes 6291464 | tf_op jit(solution)/shard_map/ppermute | solution.py:554
  168.6 47.3 %collective-permute-start.21 = (bf16[2,128,4096]{2,1,0:T(8,128)(2,1)S(1)}, bf16[2,128,4096]{2,1,0:T(8,128)(2,1)S(1)}, u32[]{:S(2)}, u32[]{:S(2)}) collective-permute-start(bf16[2,128,4096]{2,1,0:T(8,128)(2,1)S(1)} %copy-done.7), channel_id=1, source_target_pairs={{0,4},{1,5},{2,6},{3,7},{4,0},{5,1},{6,2},{7,3}} | collective-permute-start | bytes 6291464 | tf_op jit(solution)/shard_map/ppermute | solution.py:554
  215.8 7.2 %collective-permute-start.23 = (bf16[2,128,4096]{2,1,0:T(8,128)(2,1)S(1)}, bf16[2,128,4096]{2,1,0:T(8,128)(2,1)S(1)}, u32[]{:S(2)}, u32[]{:S(2)}) collective-permute-start(bf16[2,128,4096]{2,1,0:T(8,128)(2,1)S(1)} %collective-permute-done.21.refs_0_), channel_id=1, source_target_pairs={{0,1},{1,0},{2,3},{3,2},{4,5},{5,4},{6,7},{7,6}} | collective-permute-start | bytes 6291464 | tf_op jit(solution)/shard_map/ppermute | solution.py:554
  215.8 7.2 %collective-permute-start.24 = (bf16[2,128,4096]{2,1,0:T(8,128)(2,1)S(1)}, bf16[2,128,4096]{2,1,0:T(8,128)(2,1)S(1)}, u32[]{:S(2)}, u32[]{:S(2)}) collective-permute-start(bf16[2,128,4096]{2,1,0:T(8,128)(2,1)S(1)} %collective-permute-done.22.refs_1_), channel_id=1, source_target_pairs={{0,1},{1,0},{2,3},{3,2},{4,5},{5,4},{6,7},{7,6}} | collective-permute-start | bytes 6291464 | tf_op jit(solution)/shard_map/ppermute | solution.py:554
  221.0 47.7 %collective-permute-start.26 = (bf16[2,128,4096]{2,1,0:T(8,128)(2,1)}, bf16[2,128,4096]{2,1,0:T(8,128)(2,1)S(1)}, u32[]{:S(2)}, u32[]{:S(2)}) collective-permute-start(bf16[2,128,4096]{2,1,0:T(8,128)(2,1)} %get-tuple-element.198), channel_id=1, source_target_pairs={{0,2},{1,3},{2,0},{3,1},{4,6},{5,7},{6,4},{7,5}} | collective-permute-start | bytes 6291464 | tf_op jit(solution)/shard_map/ppermute | solution.py:554
  221.3 47.5 %collective-permute-start.25 = (bf16[2,128,4096]{2,1,0:T(8,128)(2,1)}, bf16[2,128,4096]{2,1,0:T(8,128)(2,1)S(1)}, u32[]{:S(2)}, u32[]{:S(2)}) collective-permute-start(bf16[2,128,4096]{2,1,0:T(8,128)(2,1)} %get-tuple-element.199), channel_id=1, source_target_pairs={{0,4},{1,5},{2,6},{3,7},{4,0},{5,1},{6,2},{7,3}} | collective-permute-start | bytes 6291464 | tf_op jit(solution)/shard_map/ppermute | solution.py:554
  268.8 4.2 %collective-permute-start.27 = (bf16[2,128,4096]{2,1,0:T(8,128)(2,1)S(1)}, bf16[2,128,4096]{2,1,0:T(8,128)(2,1)S(1)}, u32[]{:S(2)}, u32[]{:S(2)}) collective-permute-start(bf16[2,128,4096]{2,1,0:T(8,128)(2,1)S(1)} %collective-permute-done.25.refs_0_), channel_id=1, source_target_pairs={{0,1},{1,0},{2,3},{3,2},{4,5},{5,4},{6,7},{7,6}} | collective-permute-start | bytes 6291464 | tf_op jit(solution)/shard_map/ppermute | solution.py:554
  268.8 7.2 %collective-permute-start.28 = (bf16[2,128,4096]{2,1,0:T(8,128)(2,1)S(1)}, bf16[2,128,4096]{2,1,0:T(8,128)(2,1)S(1)}, u32[]{:S(2)}, u32[]{:S(2)}) collective-permute-start(bf16[2,128,4096]{2,1,0:T(8,128)(2,1)S(1)} %collective-permute-done.26.refs_1_), channel_id=1, source_target_pairs={{0,1},{1,0},{2,3},{3,2},{4,5},{5,4},{6,7},{7,6}} | collective-permute-start | bytes 6291464 | tf_op jit(solution)/shard_map/ppermute | solution.py:554
  269.3 47.5 %collective-permute-start.29 = (bf16[2,128,4096]{2,1,0:T(8,128)(2,1)S(1)}, bf16[2,128,4096]{2,1,0:T(8,128)(2,1)S(1)}, u32[]{:S(2)}, u32[]{:S(2)}) collective-permute-start(bf16[2,128,4096]{2,1,0:T(8,128)(2,1)S(1)} %collective-permute-done.17.refs_0_), channel_id=1, source_target_pairs={{0,2},{1,3},{2,0},{3,1},{4,6},{5,7},{6,4},{7,5}} | collective-permute-start | bytes 6291464 | tf_op jit(solution)/shard_map/ppermute | solution.py:554
  271.0 47.3 %collective-permute-start.30 = (bf16[2,128,4096]{2,1,0:T(8,128)(2,1)S(1)}, bf16[2,128,4096]{2,1,0:T(8,128)(2,1)S(1)}, u32[]{:S(2)}, u32[]{:S(2)}) collective-permute-start(bf16[2,128,4096]{2,1,0:T(8,128)(2,1)S(1)} %collective-permute-done.18.refs_1_), channel_id=1, source_target_pairs={{0,4},{1,5},{2,6},{3,7},{4,0},{5,1},{6,2},{7,3}} | collective-permute-start | bytes 6291464 | tf_op jit(solution)/shard_map/ppermute | solution.py:554
  318.2 4.2 %collective-permute-start.31 = (bf16[2,128,4096]{2,1,0:T(8,128)(2,1)S(1)}, bf16[2,128,4096]{2,1,0:T(8,128)(2,1)S(1)}, u32[]{:S(2)}, u32[]{:S(2)}) collective-permute-start(bf16[2,128,4096]{2,1,0:T(8,128)(2,1)S(1)} %collective-permute-done.29.refs_0_), channel_id=1, source_target_pairs={{0,1},{1,0},{2,3},{3,2},{4,5},{5,4},{6,7},{7,6}} | collective-permute-start | bytes 6291464 | tf_op jit(solution)/shard_map/ppermute | solution.py:554
  318.2 7.2 %collective-permute-start.32 = (bf16[2,128,4096]{2,1,0:T(8,128)(2,1)S(1)}, bf16[2,128,4096]{2,1,0:T(8,128)(2,1)S(1)}, u32[]{:S(2)}, u32[]{:S(2)}) collective-permute-start(bf16[2,128,4096]{2,1,0:T(8,128)(2,1)S(1)} %collective-permute-done.30.refs_1_), channel_id=1, source_target_pairs={{0,1},{1,0},{2,3},{3,2},{4,5},{5,4},{6,7},{7,6}} | collective-permute-start | bytes 6291464 | tf_op jit(solution)/shard_map/ppermute | solution.py:554
  318.8 25.1 %collective-permute-start.33 = (bf16[1,128,4096]{2,1,0:T(8,128)(2,1)S(1)}, bf16[1,128,4096]{2,1,0:T(8,128)(2,1)S(1)}, u32[]{:S(2)}, u32[]{:S(2)}) collective-permute-start(bf16[1,128,4096]{2,1,0:T(8,128)(2,1)S(1)} %collective-permute-done.13.refs_0_), channel_id=1, source_target_pairs={{0,2},{1,3},{2,0},{3,1},{4,6},{5,7},{6,4},{7,5}} | collective-permute-start | bytes 3145736 | tf_op jit(solution)/shard_map/ppermute | solution.py:554
  319.1 24.8 %collective-permute-start.34 = (bf16[1,128,4096]{2,1,0:T(8,128)(2,1)S(1)}, bf16[1,128,4096]{2,1,0:T(8,128)(2,1)S(1)}, u32[]{:S(2)}, u32[]{:S(2)}) collective-permute-start(bf16[1,128,4096]{2,1,0:T(8,128)(2,1)S(1)} %collective-permute-done.14.refs_1_), channel_id=1, source_target_pairs={{0,4},{1,5},{2,6},{3,7},{4,0},{5,1},{6,2},{7,3}} | collective-permute-start | bytes 3145736 | tf_op jit(solution)/shard_map/ppermute | solution.py:554
  343.9 3.7 collective-permute-start.35
  343.9 4.2 %collective-permute-start.36 = (bf16[1,128,4096]{2,1,0:T(8,128)(2,1)S(1)}, bf16[1,128,4096]{2,1,0:T(8,128)(2,1)S(1)}, u32[]{:S(2)}, u32[]{:S(2)}) collective-permute-start(bf16[1,128,4096]{2,1,0:T(8,128)(2,1)S(1)} %collective-permute-done.34.refs_1_), channel_id=1, source_target_pairs={{0,1},{1,0},{2,3},{3,2},{4,5},{5,4},{6,7},{7,6}} | collective-permute-start | bytes 3145736 | tf_op jit(solution)/shard_map/ppermute | solution.py:554
  344.4 13.8 %collective-permute-start.37 = (bf16[1,64,4096]{2,1,0:T(8,128)(2,1)S(1)}, bf16[1,64,4096]{2,1,0:T(8,128)(2,1)S(1)}, u32[]{:S(2)}, u32[]{:S(2)}) collective-permute-start(bf16[1,64,4096]{2,1,0:T(8,128)(2,1)S(1)} %collective-permute-done.5.refs_0_), channel_id=1, source_target_pairs={{0,2},{1,3},{2,0},{3,1},{4,6},{5,7},{6,4},{7,5}} | collective-permute-start | bytes 1572872 | tf_op jit(solution)/shard_map/ppermute | solution.py:554
  346.1 13.6 %collective-permute-start.38 = (bf16[1,64,4096]{2,1,0:T(8,128)(2,1)S(1)}, bf16[1,64,4096]{2,1,0:T(8,128)(2,1)S(1)}, u32[]{:S(2)}, u32[]{:S(2)}) collective-permute-start(bf16[1,64,4096]{2,1,0:T(8,128)(2,1)S(1)} %collective-permute-done.6.refs_1_), channel_id=1, source_target_pairs={{0,4},{1,5},{2,6},{3,7},{4,0},{5,1},{6,2},{7,3}} | collective-permute-start | bytes 1572872 | tf_op jit(solution)/shard_map/ppermute | solution.py:554
  359.6 2.6 collective-permute-start.39
  359.6 2.7 collective-permute-start.40
  360.1 13.8 %collective-permute-start.41 = (bf16[1,64,4096]{2,1,0:T(8,128)(2,1)S(1)}, bf16[1,64,4096]{2,1,0:T(8,128)(2,1)S(1)}, u32[]{:S(2)}, u32[]{:S(2)}) collective-permute-start(bf16[1,64,4096]{2,1,0:T(8,128)(2,1)S(1)} %collective-permute-done.9.refs_0_), channel_id=1, source_target_pairs={{0,2},{1,3},{2,0},{3,1},{4,6},{5,7},{6,4},{7,5}} | collective-permute-start | bytes 1572872 | tf_op jit(solution)/shard_map/ppermute | solution.py:554
  360.5 13.6 %collective-permute-start.42 = (bf16[1,64,4096]{2,1,0:T(8,128)(2,1)S(1)}, bf16[1,64,4096]{2,1,0:T(8,128)(2,1)S(1)}, u32[]{:S(2)}, u32[]{:S(2)}) collective-permute-start(bf16[1,64,4096]{2,1,0:T(8,128)(2,1)S(1)} %collective-permute-done.10.refs_1_), channel_id=1, source_target_pairs={{0,4},{1,5},{2,6},{3,7},{4,0},{5,1},{6,2},{7,3}} | collective-permute-start | bytes 1572872 | tf_op jit(solution)/shard_map/ppermute | solution.py:554
  374.1 1.9 collective-permute-start.43
  374.1 2.7 collective-permute-start.44
  (10 other events, 46.1 us)

commit v6 on v0

v6 whole, which is shorter than its diff:
```python
import jax
import jax.numpy as jnp
from jax import lax
from jax.sharding import PartitionSpec as P

HEAD_DIM = 128
NEG_BIG = -1e30


def rms_norm(hidden, gain_vec):
    hid_f32 = hidden.astype(jnp.float32)
    inv_rms = lax.rsqrt(jnp.mean(hid_f32 * hid_f32, axis=-1, keepdims=True) + 1e-5)
    return (hid_f32 * inv_rms * gain_vec.astype(jnp.float32)).astype(jnp.bfloat16)


def rotary(heads_f32, positions):
    half_dim = HEAD_DIM // 2
    inv_freq = 10000.0 ** (-2.0 * jnp.arange(half_dim, dtype=jnp.float32) / HEAD_DIM)
    angles = positions.astype(jnp.float32)[..., None] * inv_freq
    cos_tab = jnp.cos(angles)[..., None, :]
    sin_tab = jnp.sin(angles)[..., None, :]
    lo_half = heads_f32[..., :half_dim]
    hi_half = heads_f32[..., half_dim:]
    return jnp.concatenate([lo_half * cos_tab - hi_half * sin_tab, hi_half * cos_tab + lo_half * sin_tab], axis=-1)


def attend(queries, keys, values, visible):
    scores = jnp.einsum('bqhd,bkhd->bhqk', queries, keys, preferred_element_type=jnp.float32) * (HEAD_DIM ** -0.5)
    scores = jnp.where(visible[:, None], scores, NEG_BIG)
    top = jnp.max(scores, axis=-1, keepdims=True)
    prob = jnp.exp(scores - top)
    total = jnp.sum(prob, axis=-1)
    out = jnp.einsum('bhqk,bkhd->bqhd', prob.astype(jnp.bfloat16), values, preferred_element_type=jnp.float32)
    return (out / jnp.moveaxis(total, 1, 2)[..., None]).reshape(*queries.shape[:2], -1).astype(jnp.bfloat16)


def solution(mesh):
    n_dev = mesh.shape['model']
    seq_spec = P('replica', 'model', None)
    col_spec = P(None, None, 'model')
    row_spec = P(None, 'model', None)
    gain_spec = P(None, None)
    tok_spec = P('replica', None)
    cache_spec = P(None, 'replica', None, 'model', None)
    in_specs = (seq_spec, P('replica'), tok_spec, gain_spec, col_spec, col_spec, col_spec, row_spec, gain_spec, col_spec, col_spec, row_spec)
    out_specs = (tok_spec, tok_spec, cache_spec, cache_spec)
    fours = [[0, 1, 2, 3], [4, 5, 6, 7]]
    across = [(i, i ^ 4) for i in range(n_dev)]

    def dot(a, b):
        return jnp.dot(a, b, preferred_element_type=jnp.float32)

    def per_device(prompt, lengths, new_tok, norm_attn, w_q, w_k, w_v, w_o, norm_mlp, w_gate, w_up, w_down):
        my_idx = lax.axis_index('model')
        n_batch, blk, d_model = prompt.shape
        n_tok = n_batch * blk
        seq_len = blk * n_dev
        heads = w_k.shape[2] // HEAD_DIM
        wq, wk, wv = w_q[0], w_k[0], w_v[0]
        key_pos = jnp.arange(seq_len)

        normed = lax.all_gather(rms_norm(prompt, norm_attn[0]), 'model', axis=0)
        rows = normed.reshape(n_dev * n_tok, d_model)
        pos = key_pos.reshape(n_dev, 1, blk)

        def project(w):
            return dot(rows, w).reshape(n_dev, n_batch, blk, heads, HEAD_DIM)

        def in_order(x):
            return jnp.moveaxis(x, 0, 1).reshape(n_batch, seq_len, heads, HEAD_DIM)

        q_all = in_order(rotary(project(wq), pos).astype(jnp.bfloat16))
        k_all = in_order(rotary(project(wk), pos).astype(jnp.bfloat16))
        v_all = in_order(project(wv).astype(jnp.bfloat16))
        outs = []
        for i in range(n_dev):
            seen = (i + 1) * blk
            q_pos = i * blk + jnp.arange(blk)
            visible = (key_pos[None, None, :seen] <= q_pos[None, :, None]) & (key_pos[None, None, :seen] < lengths[:, None, None])
            outs.append(attend(q_all[:, i * blk:seen], k_all[:, :seen], v_all[:, :seen], visible))
        heads_out = jnp.stack(outs)
        mine = lax.all_to_all(heads_out, 'model', split_axis=0, concat_axis=0)
        att = jnp.moveaxis(mine.reshape(n_dev, n_tok, -1), 0, 1).reshape(n_tok, -1)

        wo_full = lax.all_gather(w_o[0], 'model', axis=0, tiled=True)
        hidden = (prompt.astype(jnp.float32) + dot(att, wo_full).reshape(n_batch, blk, d_model)).astype(jnp.bfloat16)
        near = rms_norm(hidden, norm_mlp[0]).reshape(n_tok, d_model)
        pair = jnp.concatenate([near, lax.ppermute(near, 'model', across)], axis=0)
        wg, wu = (lax.all_gather(w[0], 'model', axis=1, tiled=True, axis_index_groups=fours) for w in (w_gate, w_up))
        wd = lax.all_gather(w_down[0], 'model', axis=0, tiled=True, axis_index_groups=fours)
        mid = (jax.nn.silu(dot(pair, wg)) * dot(pair, wu)).astype(jnp.bfloat16)
        other = lax.ppermute(dot(mid[n_tok:], wd), 'model', across)
        total = dot(mid[:n_tok], wd) + other
        hidden = (hidden.astype(jnp.float32) + total.reshape(n_batch, blk, d_model)).astype(jnp.bfloat16)
        seq_pos = my_idx * blk + jnp.arange(blk)
        last_sel = (seq_pos[None, :] == (lengths - 1)[:, None]).astype(jnp.bfloat16)
        last_hidden = lax.psum(jnp.einsum('bs,bsd->bd', last_sel, hidden, preferred_element_type=jnp.float32), 'model').astype(jnp.bfloat16)

        tok_norm = rms_norm(new_tok, norm_attn[0])
        q_new = rotary(dot(tok_norm, wq).reshape(n_batch, heads, HEAD_DIM), lengths).astype(jnp.bfloat16)
        k_new = rotary(dot(tok_norm, wk).reshape(n_batch, heads, HEAD_DIM), lengths).astype(jnp.bfloat16)
        v_new = dot(tok_norm, wv).astype(jnp.bfloat16).reshape(n_batch, heads, HEAD_DIM)
        k_cache = jnp.concatenate([k_all, k_new[:, None]], axis=1)
        v_cache = jnp.concatenate([v_all, v_new[:, None]], axis=1)
        cache_pos = jnp.arange(seq_len + 1)
        visible = (cache_pos[None, :] < lengths[:, None]) | (cache_pos[None, :] == seq_len)
        tok_attn = attend(q_new[:, None], k_cache, v_cache, visible[:, None])[:, 0]
        dec_hidden = (new_tok.astype(jnp.float32) + lax.psum(dot(tok_attn, w_o[0]), 'model')).astype(jnp.bfloat16)
        tok_norm = rms_norm(dec_hidden, norm_mlp[0])
        tok_mid = (jax.nn.silu(dot(tok_norm, w_gate[0])) * dot(tok_norm, w_up[0])).astype(jnp.bfloat16)
        dec_hidden = (dec_hidden.astype(jnp.float32) + lax.psum(dot(tok_mid, w_down[0]), 'model')).astype(jnp.bfloat16)
        return dec_hidden, last_hidden, k_cache[None], v_cache[None]

    return jax.shard_map(per_device, mesh=mesh, in_specs=in_specs, out_specs=out_specs, check_vma=False)
```

time: 2700 us -> 1890 us (0.70)
  waiting for transfers between devices: 1720 us -> 864 us
  matrix products: 575 us -> 678 us
  local copies, waits for them, and re-layouts: 243 us -> 160 us
    all_gather x9 -> x5, waiting for transfers between devices: 1700 us -> 265 us  [the longest x1 265 us: per_device(): normed = lax.all_gather(rms_norm(prompt, norm_attn[0]), 'model', axis=0)]
    ppermute x0 -> x2, waiting for transfers between devices: none -> 404 us  [the longest x1 226 us: per_device(): other = lax.ppermute(dot(mid[n_tok:], wd), 'model', across)]
    all_to_all x0 -> x1, waiting for transfers between devices: none -> 158 us  [per_device(): mine = lax.all_to_all(heads_out, 'model', split_axis=0, concat_axis=0)]
    dot_general x17 -> x32, matrix products: 565 us -> 670 us  [the longest x14 545 us: dot(): return jnp.dot(a, b, preferred_element_type=jnp.float32)]
    dot_general x4, local copies, waits for them, and re-layouts: 95.4 us -> 33.7 us  [dot(): return jnp.dot(a, b, preferred_element_type=jnp.float32)]
    dynamic_slice x3 -> x0, local copies, waits for them, and re-layouts: 43.9 us -> none  [the longest x2 22.8 us: step_fn(): lax.dynamic_index_in_dim(val_blocks, blk_idx, axis=0, keepdims=False)]
    concatenate x5 -> x2, other arithmetic: 39.9 us -> 0.16 us  [rotary(): jnp.concatenate([lo_half * cos_tab - hi_half * sin_tab, hi_half * cos_tab...]
    transpose x0 -> x3, local copies, waits for them, and re-layouts: none -> 34.3 us  [the longest x2 22.7 us: in_order(): return jnp.moveaxis(x, 0, 1).reshape(n_batch, seq_len, heads, HEAD_DIM)]
  transfers between devices with their start and end apart: 11 -> 10, of which waited for: 10 -> 5; matrix products, arithmetic and copies ran while one was open for 34% -> 44% of each run, Pallas kernels for 0% -> 0%
where the time goes in v6:
time: 1890 us; the launch traced here: 1880 us
  waiting for transfers between devices  864 us (46%)
  matrix products  678 us (36%)
  local copies, waits for them, and re-layouts  160 us (8%)
  other arithmetic  133 us (7%)
  blocking collectives  25.8 us (1%)
    dot_general x14, matrix products, dot(): return jnp.dot(a, b, preferred_element_type=jnp.float32)  545 us
    all_gather x1, waiting for transfers between devices, per_device(): normed = lax.all_gather(rms_norm(prompt, norm_attn[0]), 'model', axis=0)  265 us
    ppermute x1, waiting for transfers between devices, per_device(): other = lax.ppermute(dot(mid[n_tok:], wd), 'model', across)  226 us
    ppermute x1, waiting for transfers between devices, per_device(): pair = jnp.concatenate([near, lax.ppermute(near, 'model', across)], axis=0)  179 us
    all_to_all x1, waiting for transfers between devices, per_device(): mine = lax.all_to_all(heads_out, 'model', split_axis=0, concat_axis=0)  158 us
    dot_general x9, matrix products, attend(): jnp.einsum('bhqk,bkhd->bqhd', prob.astype(jnp.bfloat16), values, preferre...  71.8 us
    unnamed x77, local copies, waits for them, and re-layouts  65.1 us
    dot_general x9, matrix products, attend(): jnp.einsum('bqhd,bkhd->bhqk', queries, keys, preferred_element_type=jnp.f...  53.8 us
  transfers between devices with their start and end apart: 10, of which 5 were waited for; matrix products, arithmetic and copies ran while one was open for 44% of the time, Pallas kernels for 0%

profile of v6, /device:TPU:0, one launch (start us, length us, event | category | flops | bytes accessed | tf_op | source)
XLA Modules:
  0.0 1881.5 jit_solution(4697501980693009592)
XLA Ops:
  13.1 10.5 fusion.13
  26.6 6.9 dot_general.121
  33.5 7.0 dot_general.124
  40.6 6.4 copy.129
  59.2 264.6 %all-gather.11.cloned.1.call-done = bf16[64,128,4096]{2,1,0:T(8,128)(2,1)} async-done(((bf16[8,128,4096]{2,1,0:T(8,128)(2,1)}), bf16[64,128,4096]{2,1,0:T(8,128)(2,1)}) %all-gather.11.cloned.1.call-update) | async-done | bytes 67108880 | tf_op jit(solution)/shard_map/all_gather | solution.py:62
  323.8 42.3 %fusion.104 = f32[8,8,128,4,128]{2,4,3,1,0:T(8,128)} fusion(bf16[8,8,128,4096,1]{3,2,4,1,0:T(8,128)(2,1)} %bitcast.3, bf16[4,128,4096,1,1]{1,0,2,4,3:T(4,128)(2,1)} %bitcast.246), kind=kOutput, calls=%fused_computation.119 | convolution fusion | flops 34359738368 | bytes 88080384 | tf_op jit(solution)/shard_map/dot_general | solution.py:51
  366.1 42.3 %fusion.108 = f32[8,8,128,4,128]{2,4,3,1,0:T(8,128)} fusion(bf16[8,8,128,4096,1]{3,2,4,1,0:T(8,128)(2,1)} %bitcast.3, bf16[4,128,4096,1,1]{1,0,2,4,3:T(4,128)(2,1)S(1)} %bitcast.245), kind=kOutput, calls=%fused_computation.123 | convolution fusion | flops 34359738368 | bytes 88080384 | tf_op jit(solution)/shard_map/dot_general | solution.py:51
  408.4 19.9 %subtract_convert_fusion = (bf16[8,8,128,4,64]{2,4,3,1,0:T(8,128)(2,1)}, bf16[8,8,128,4,64]{2,4,3,1,0:T(8,128)(2,1)}, bf16[8,8,128,4,64]{2,4,3,1,0:T(8,128)(2,1)}, bf16[8,8,128,4,64]{2,4,3,1,0:T(8,128)(2,1)}) fusion(f32[8,8,128,4,128]{2,4,3,1,0:T(8,128)} %fusion.104, f32[8,128,64]{1,2,0:T(8,128)S(1)} %copy-done.16, f32[8,128,64]{1,2,0:T(8,128)S(1)} %copy-done.15, ...), kind=kLoop, calls=%fused_computation.65 | loop fusion | flops 33554432 | bytes 50855936 | tf_op jit(solution)/shard_map/convert.4
  428.3 11.8 maximum_bitcast_fusion
  440.1 11.4 copy.91
  451.5 11.4 copy.97
  462.8 42.0 %convert_bitcast_fusion = bf16[8,8,128,4,128]{4,2,3,0,1:T(8,128)(2,1)} fusion(bf16[8,8,128,4096,1]{3,2,4,1,0:T(8,128)(2,1)} %bitcast.3, bf16[4,128,4096,1,1]{2,1,0,4,3:T(8,128)(2,1)} %bitcast.244), kind=kOutput, calls=%fused_computation.68 | convolution fusion | flops 34363932672 | bytes 79691776 | tf_op jit(solution)/shard_map/dot_general | solution.py:51
  504.9 10.6 copy.87
  515.5 12.8 fusion.19
  528.3 11.6 fusion.20
  539.9 8.1 fusion.21
  548.0 11.6 fusion.141
  559.6 7.7 fusion.31
  567.3 11.1 fusion.142
  578.4 7.5 fusion.33
  585.9 6.8 fusion.36
  592.7 12.0 fusion.143
  604.7 5.2 fusion.38
  617.0 10.6 fusion.144
  637.2 9.0 fusion.145
  651.6 5.6 fusion.146
  703.6 157.7 %all-to-all-done = bf16[8,8,128,512]{3,2,1,0:T(8,128)(2,1)} async-done(((bf16[8,8,128,512]{3,2,1,0:T(8,128)(2,1)}), bf16[8,8,128,512]{3,2,1,0:T(8,128)(2,1)}, u32[]{:S(2)}, u32[]{:S(2)}) %all-to-all-start) | async-done | bytes 8388640 | tf_op jit(solution)/shard_map/all_to_all | solution.py:82
  861.2 11.5 copy.114
  872.7 13.5 dot_general.150
  886.2 42.9 %fusion.15 = (f32[8,128]{1,0:T(8,128)S(1)}, bf16[8,128,4096]{2,1,0:T(8,128)(2,1)}) fusion(bf16[8,128,4096]{2,1,0:T(8,128)(2,1)} %dot_general.150, bf16[1,4096,4096]{2,1,0:T(8,128)(2,1)} %all-gather.13.cloned.1.call-done, bf16[8,128,4096]{2,1,0:T(8,128)(2,1)} %param.12), kind=kOutput, calls=%fused_computation.22 | convolution fusion | flops 34384904192 | bytes 58724352 | tf_op jit(solution)/shard_map/dot_general | solution.py:51
  929.2 10.5 fusion.17
  940.2 178.6 %collective-permute-done = bf16[1024,4096]{1,0:T(8,128)(2,1)S(1)} collective-permute-done((bf16[1024,4096]{1,0:T(8,128)(2,1)}, bf16[1024,4096]{1,0:T(8,128)(2,1)S(1)}, u32[]{:S(2)}, u32[]{:S(2)}) %collective-permute-start) | collective-permute-done | bytes 8388640 | tf_op jit(solution)/shard_map/ppermute | solution.py:88
  1122.2 10.6 pad_maximum_fusion.14
  1132.8 115.9 %fusion.7 = f32[2048,5504]{1,0:T(8,128)} fusion(bf16[1,4096,5504]{1,2,0:T(8,128)(2,1)} %all-gather.15.cloned.1.call-done, bf16[1024,4096]{1,0:T(8,128)(2,1)} %copy-done.6, bf16[1024,4096]{1,0:T(8,128)(2,1)} %bitcast.231), kind=kOutput, calls=%fused_computation.7 | convolution fusion | flops 92375351296 | bytes 106954752 | tf_op jit(solution)/shard_map/dot_general | solution.py:51
  1248.7 116.3 %multiply_convert_fusion = bf16[2048,5504]{1,0:T(8,128)(2,1)} fusion(f32[2048,5504]{1,0:T(8,128)} %fusion.7, bf16[1,4096,5504]{1,2,0:T(8,128)(2,1)} %all-gather.17.cloned.1.call-done, bf16[2048,4096]{1,0:T(8,128)(2,1)} %pad_maximum_fusion.14), kind=kOutput, calls=%fused_computation.9 | convolution fusion | flops 92409430016 | bytes 129499136 | tf_op jit(solution)/shard_map/dot_general | solution.py:51
  1365.0 57.8 %fusion.1 = f32[1024,4096]{1,0:T(8,128)} fusion(bf16[1,5504,4096]{2,1,0:T(8,128)(2,1)} %all-gather.19.cloned.1.call-done, bf16[2048,5504]{1,0:T(8,128)(2,1)} %multiply_convert_fusion), kind=kOutput, calls=%fused_computation.1 | convolution fusion | flops 46170898432 | bytes 73138176 | tf_op jit(solution)/shard_map/dot_general | solution.py:51
  1431.6 5.7 fusion.79
  1444.1 7.3 fusion.78
  1451.4 34.9 %all-reduce.4.cloned.1.call-done = f32[8,4096]{1,0:T(8,128)} async-done(((f32[8,4096]{1,0:T(8,128)}), f32[8,4096]{1,0:T(8,128)}) %all-reduce.4.cloned.1.call-update) | async-done | bytes 131088 | tf_op jit(solution)/shard_map/psum | solution.py:108
  1487.4 7.2 fusion.29
  1494.6 13.2 fusion.25
  1507.8 7.3 fusion.80
  1515.1 22.4 %copy.115 = bf16[1,8,1025,4,128]{4,3,2,1,0:T(4,128)(2,1)} copy(bf16[1,8,1025,4,128]{4,2,3,1,0:T(8,128)(2,1)} %fusion.78) | data formatting | bytes 16793600
  1537.5 19.5 %copy.116 = bf16[1,8,1025,4,128]{4,3,2,1,0:T(4,128)(2,1)} copy(bf16[1,8,1025,4,128]{4,2,3,1,0:T(8,128)(2,1)S(1)} %copy-done) | data formatting | bytes 16793600
  1558.7 225.8 %collective-permute-done.1 = f32[1024,4096]{1,0:T(8,128)} collective-permute-done((f32[1024,4096]{1,0:T(8,128)}, f32[1024,4096]{1,0:T(8,128)}, u32[]{:S(2)}, u32[]{:S(2)}) %collective-permute-start.1) | collective-permute-done | bytes 16777248 | tf_op jit(solution)/shard_map/ppermute | solution.py:92
  1784.5 56.8 %fusion.51 = f32[1024,4096]{1,0:T(8,128)} fusion(f32[1024,4096]{1,0:T(8,128)} %collective-permute-done.1, bf16[1,5504,4096]{2,1,0:T(8,128)(2,1)} %all-gather.19.cloned.1.call-done, bf16[2048,5504]{1,0:T(8,128)(2,1)} %multiply_convert_fusion), kind=kOutput, calls=%fused_computation.72 | convolution fusion | flops 46175092736 | bytes 89915392 | tf_op jit(solution)/shard_map/dot_general | solution.py:51
  1841.3 7.2 fusion.41
  1848.6 25.8 %all-reduce.7 = bf16[8,4096]{1,0:T(8,128)(2,1)} all-reduce(f32[8,4096]{1,0:T(8,128)S(1)} %bitcast.255), channel_id=1, replica_groups=mesh['replica'=1,'model'=8] {'model'}, use_global_device_ids=true, to_apply=%region_24.25 | all-reduce | flops 32768 | bytes 196608 | tf_op jit(solution)/shard_map/psum | solution.py:97
  (196 shorter events, 111.5 us)
Async XLA Ops:
  7.2 316.6 %all-gather.11.cloned.1.call-start = ((), (), s32[]{:S(2)}) async-start(), calls=%async_computation.3 | async-start | bytes 75497472 | tf_op jit(solution)/shard_map/all_gather | solution.py:62
  7.9 5.1 copy-start.19
  23.6 862.6 %all-gather.13.cloned.1.call-start = ((), (), s32[]{:S(2)}) async-start(), calls=%async_computation.4 | async-start | bytes 37748736 | tf_op jit(solution)/shard_map/all_gather | solution.py:85
  24.4 1108.4 %all-gather.15.cloned.1.call-start = ((), (), s32[]{:S(2)}) async-start(), calls=%async_computation.5 | async-start | bytes 56360960 | tf_op jit(solution)/shard_map/all_gather | solution.py:89
  25.1 1223.6 %all-gather.17.cloned.1.call-start = ((), (), s32[]{:S(2)}) async-start(), calls=%async_computation.6 | async-start | bytes 56360960 | tf_op jit(solution)/shard_map/all_gather | solution.py:89
  25.7 0.7 copy-start.23
  25.7 1339.3 %all-gather.19.cloned.1.call-start = ((), (), s32[]{:S(2)}) async-start(), calls=%async_computation.7 | async-start | bytes 56360960 | tf_op jit(solution)/shard_map/all_gather | solution.py:90
  26.3 22.0 %copy-start.26 = (f32[64]{0:T(128)}, f32[64]{0:T(128)S(1)}, u32[]{:S(2)}) copy-start(f32[64]{0:T(128)S(1)} %multiply_power_fusion) | copy-start | bytes 772
  323.8 42.3 %copy-start.7 = (bf16[4,128,4096]{1,0,2:T(4,128)(2,1)S(1)}, bf16[4,128,4096]{1,0,2:T(4,128)(2,1)}, u32[]{:S(2)}) copy-start(bf16[4,128,4096]{1,0,2:T(4,128)(2,1)} %dot_general.124) | copy-start | bytes 12582916
  366.1 42.3 %copy-start.15 = (f32[8,128,64]{1,2,0:T(8,128)S(1)}, f32[8,128,64]{1,2,0:T(8,128)}, u32[]{:S(2)}) copy-start(f32[8,128,64]{1,2,0:T(8,128)} %get-tuple-element.36) | copy-start | bytes 786436
  366.1 42.3 %copy-start.16 = (f32[8,128,64]{1,2,0:T(8,128)S(1)}, f32[8,128,64]{1,2,0:T(8,128)}, u32[]{:S(2)}) copy-start(f32[8,128,64]{1,2,0:T(8,128)} %get-tuple-element.37) | copy-start | bytes 786436
  504.9 10.6 copy-start.4
  515.5 12.8 copy-start.9
  559.6 18.8 slice-start
  567.3 11.1 slice-start.1
  567.3 11.1 copy-start.10
  592.7 12.0 copy-start.11
  609.9 4.0 copy-start.3
  617.0 10.6 copy-start.12
  631.4 3.4 copy-start.5
  634.8 11.4 slice-start.2
  637.2 9.0 slice-start.3
  637.2 9.0 copy-start.14
  651.6 5.6 copy-start.17
  665.1 12.6 copy-start.18
  686.0 9.1 copy-start.8
  699.5 4.0 copy-start.25
  699.5 161.7 %all-to-all-start = ((bf16[8,8,128,512]{3,2,1,0:T(8,128)(2,1)}), bf16[8,8,128,512]{3,2,1,0:T(8,128)(2,1)}, u32[]{:S(2)}, u32[]{:S(2)}) async-start(bf16[8,8,128,512]{3,2,1,0:T(8,128)(2,1)} %constant_dynamic-update-slice_fusion), calls=%async_computation | async-start | bytes 16777216 | tf_op jit(solution)/shard_map/all_to_all | solution.py:82
  703.3 783.0 %all-reduce.4.cloned.1.call-start = ((), (), s32[]{:S(2)}) async-start(), calls=%async_computation.1 | async-start | bytes 262144 | tf_op jit(solution)/shard_map/psum | solution.py:108
  703.5 225.6 %copy-start.21 = (f32[1,4096]{1,0:T(1,128)}, f32[1,4096]{1,0:T(1,128)S(1)}, u32[]{:S(2)}) copy-start(f32[1,4096]{1,0:T(1,128)S(1)} %mul.446) | copy-start | bytes 49156
  939.7 179.2 %collective-permute-start = (bf16[1024,4096]{1,0:T(8,128)(2,1)}, bf16[1024,4096]{1,0:T(8,128)(2,1)S(1)}, u32[]{:S(2)}, u32[]{:S(2)}) collective-permute-start(bf16[1024,4096]{1,0:T(8,128)(2,1)} %bitcast.229), channel_id=1, source_target_pairs={{0,4},{1,5},{2,6},{3,7},{4,0},{5,1},{6,2},{7,3}} | collective-permute-start | bytes 25165832 | tf_op jit(solution)/shard_map/ppermute | solution.py:88
  1118.8 3.3 copy-start.6
  1365.0 59.2 %copy-start.13 = (bf16[8,4096]{1,0:T(8,128)(2,1)S(1)}, bf16[8,4096]{1,0:T(8,128)(2,1)}, u32[]{:S(2)}) copy-start(bf16[8,4096]{1,0:T(8,128)(2,1)} %param.14) | copy-start | bytes 196612
  1365.0 59.4 %copy-start.24 = (s32[8]{0:T(128)S(1)}, s32[8]{0:T(128)}, u32[]{:S(2)}) copy-start(s32[8]{0:T(128)} %param.13) | copy-start | bytes 100
  1365.0 59.4 %copy-start.27 = (f32[64]{0:T(128)S(1)}, f32[64]{0:T(128)}, u32[]{:S(2)}) copy-start(f32[64]{0:T(128)} %copy-done.26) | copy-start | bytes 772
  1365.0 59.5 %copy-start.20 = (f32[1,4096]{1,0:T(1,128)S(1)}, f32[1,4096]{1,0:T(1,128)}, u32[]{:S(2)}) copy-start(f32[1,4096]{1,0:T(1,128)} %copy-done.19) | copy-start | bytes 49156
  1422.8 361.6 %collective-permute-start.1 = (f32[1024,4096]{1,0:T(8,128)}, f32[1024,4096]{1,0:T(8,128)}, u32[]{:S(2)}, u32[]{:S(2)}) collective-permute-start(f32[1024,4096]{1,0:T(8,128)} %fusion.1), channel_id=1, source_target_pairs={{0,4},{1,5},{2,6},{3,7},{4,0},{5,1},{6,2},{7,3}} | collective-permute-start | bytes 50331656 | tf_op jit(solution)/shard_map/ppermute | solution.py:92
  1424.2 6.4 copy-start.1
  1437.6 4.9 copy-start.2
  1443.8 43.6 %copy-start.22 = (f32[1,4096]{1,0:T(1,128)S(1)}, f32[1,4096]{1,0:T(1,128)}, u32[]{:S(2)}) copy-start(f32[1,4096]{1,0:T(1,128)} %copy-done.21) | copy-start | bytes 49156
  1443.8 113.2 %all-reduce.6.cloned.1.call-start = ((), (), s32[]{:S(2)}) async-start(), calls=%async_computation.2 | async-start | bytes 262144 | tf_op jit(solution)/shard_map/psum | solution.py:111
  1515.1 22.4 %copy-start = (bf16[1,8,1025,4,128]{4,2,3,1,0:T(8,128)(2,1)S(1)}, bf16[1,8,1025,4,128]{4,2,3,1,0:T(8,128)(2,1)}, u32[]{:S(2)}) copy-start(bf16[1,8,1025,4,128]{4,2,3,1,0:T(8,128)(2,1)} %fusion.80) | copy-start | bytes 25190404
  1557.0 284.2 %slice-start.4 = ((s8[8388608]{0:T(1024)(128)(4,1)}), s8[4194304]{0:T(1024)(128)(4,1)S(1)}, s32[]{:S(2)}) async-start(s8[8388608]{0:T(1024)(128)(4,1)} %bitcast.227), calls=%async_computation.12 | async-start | bytes 8388608
  1558.7 282.5 %slice-start.5 = ((s8[8388608]{0:T(1024)(128)(4,1)}), s8[4194304]{0:T(1024)(128)(4,1)S(1)}, s32[]{:S(2)}) async-start(s8[8388608]{0:T(1024)(128)(4,1)} %bitcast.227), calls=%async_computation.13 | async-start | bytes 8388608
Sparse Core Ops, SparseCore 0:
  23.7 300.0 all-gather.10
  325.6 155.2 all-gather.12
  482.4 304.1 all-gather.14
  788.0 291.2 all-gather.16
  1080.7 265.4 all-gather.18
  1443.9 42.3 all-reduce.3
  1508.0 41.8 all-reduce.5

commit v7 on v5

--- a/solution.py
+++ b/solution.py
@@ -119,6 +119,53 @@
                 if at_step >= 1:
                     for copy in copies(at_step - 1):
                         copy.wait()
+
+
+def first_kernel(places, rows, x_hbm, gain_hbm, *refs):
+    n = len(places)
+    out_refs = refs[:n]
+    x_buf, gain_ref, sem = refs[n:]
+    d_model = x_hbm.shape[2]
+    loads = [pltpu.make_async_copy(x_hbm.at[bat, pl.ds(row0, rows)], x_buf.at[i], sem.at[i]) for i, (bat, row0) in enumerate(places)]
+    loads.append(pltpu.make_async_copy(gain_hbm, gain_ref, sem.at[n]))
+    for load in loads:
+        load.start()
+    loads[n].wait()
+    lanes = [slice(c * HEAD_DIM, (c + 1) * HEAD_DIM) for c in range(d_model // HEAD_DIM)]
+    for i in range(n):
+        loads[i].wait()
+
+        def norm_rows(r, carry):
+            at = pl.ds(pl.multiple_of(r * NORM_ROWS, NORM_ROWS), NORM_ROWS)
+            acc = [jnp.zeros((NORM_ROWS, HEAD_DIM), jnp.float32) for _ in range(2)]
+            for c, lane in enumerate(lanes):
+                xf = x_buf[i, at, lane].astype(jnp.float32)
+                acc[c % 2] += xf * xf
+            inv_rms = lax.rsqrt(jnp.sum(acc[0] + acc[1], axis=-1, keepdims=True) / d_model + 1e-5)
+            for lane in lanes:
+                xf = x_buf[i, at, lane].astype(jnp.float32)
+                out_refs[i][0, at, lane] = (xf * inv_rms * gain_ref[:, lane].astype(jnp.float32)).astype(jnp.bfloat16)
+            return carry
+
+        lax.fori_loop(0, rows // NORM_ROWS, norm_rows, 0)
+
+
+def first_call(x, gain, places, rows):
+    d_model = x.shape[2]
+    return pl.pallas_call(
+        functools.partial(first_kernel, places, rows),
+        out_shape=[pltpu.VMEM((1, rows, d_model), jnp.bfloat16)] * len(places),
+        in_specs=[pl.BlockSpec(memory_space=pl.ANY)] * 2,
+        out_specs=[pl.BlockSpec(memory_space=pltpu.VMEM)] * len(places),
+        scratch_shapes=[
+            pltpu.VMEM((len(places), rows, d_model), jnp.bfloat16),
+            pltpu.VMEM(gain.shape, gain.dtype),
+            pltpu.SemaphoreType.DMA((len(places) + 1,)),
+        ],
+        compiler_params=pltpu.CompilerParams(vmem_limit_bytes=8 * 2 ** 20),
+        cost_estimate=pl.CostEstimate(flops=len(places) * rows * d_model * 8, bytes_accessed=len(places) * rows * d_model * 4, transcendentals=0),
+        name="first_rows",
+    )(*(pltpu.with_memory_space_constraint(a, pltpu.HBM) for a in (x, gain)))
 
 
 def norm_call(x, gain, order, outs_of, shapes, blk=None, row_block=0):
@@ -456,11 +503,11 @@
             copy.wait_recv()
             total = total + pr[mask - 1]
         xo[...] = total.astype(jnp.bfloat16)
+        xg[me] = xo[...]
         outs = []
         for mask in sum(far_first, ()):
             outs.append(send(phase + 1, mask, xo, xg.at[me]))
             outs[-1].start()
-        xg[me] = xo[...]
         for out in outs:
             out.wait_recv()
         return [copy for copy, _ in copies] + outs
@@ -563,12 +610,10 @@
         wq = w_q[0]
         gain = norm_attn
 
-        q1, q2, rows_h = n_batch // 8, n_batch // 4, blk // 2
+        q1, q2, rows_h = 1, n_batch // 4, blk // 2
         a_parts, b_parts = {}, {}
-        order = [side * half + k for k in range(q1) for side in range(2)]
-        outs_of = [[(side, k, 0, rows_h)] for k in range(q1) for side in range(2)]
         for h, name in enumerate(("0a", "0b")):
-            a_parts[name], b_parts[name] = norm_call(prompt, gain, order, outs_of, [(q1, rows_h)] * 2, rows_h, h)
+            a_parts[name], b_parts[name] = first_call(prompt, norm_attn, [(0, h * rows_h), (half, h * rows_h)], rows_h)
         from_y, from_x = {}, {}
 
         def send_part(step, along_y, along_x):
@@ -589,8 +634,12 @@
         seq_pos = my_idx * blk + jnp.arange(blk)
         sel = (seq_pos[None, :] == (lengths - 1)[:, None]).astype(jnp.bfloat16)
         last_x = jnp.einsum('bs,bsd->bd', sel, prompt, preferred_element_type=jnp.float32).astype(jnp.bfloat16)
+        core, cols_h = my_idx % 2, d_model // 2
         last_x = last_x + swap(last_x, 1)
+        last_x = lax.dynamic_slice_in_dim(last_x, core * cols_h, cols_h, axis=1)
         last_x = (last_x + swap(last_x, 2)) + (swap(last_x, 4) + swap(last_x, 6))
+        other_x = swap(last_x, 1)
+        last_x = jnp.where(core == 0, jnp.concatenate([last_x, other_x], axis=1), jnp.concatenate([other_x, last_x], axis=1))
         send_part("2", a_parts["2"], b_parts["2"])
         send_part("3", b_parts["2"], a_parts["2"])
         send_part("4", normed[half:half + q2], normed[:q2])

time: 407 us -> 409 us (level)
    pallas_call x3 -> x1, Pallas kernels: 15 us -> 10.8 us  [norm_call(): pl.pallas_call(functools.partial(norm_kernel, outs_of), grid=(len(order),...]
    ppermute x45 -> x46, waiting for transfers between devices: 156 us -> 160 us  [swap(): return lax.ppermute(arr, 'model', [(i, i ^ bit) for i in range(n_dev)])]
    ppermute x45 -> x46, starting transfers between devices: 37.5 us -> 36.1 us  [swap(): return lax.ppermute(arr, 'model', [(i, i ^ bit) for i in range(n_dev)])]
    unnamed x26 -> x28, local copies, waits for them, and re-layouts: 12.6 us -> 13.6 us
  transfers between devices with their start and end apart: 45 -> 46, of which waited for: 31 -> 32; matrix products, arithmetic and copies ran while one was open for 3% -> 3% of each run, Pallas kernels for 36% -> 36%
where the time goes in v7:
time: 409 us; the launch traced here: 408 us
  Pallas kernels  185 us (45%)
  waiting for transfers between devices  160 us (39%)
  starting transfers between devices  36.1 us (9%)
  local copies, waits for them, and re-layouts  19 us (5%)
  matrix products  4.57 us (1%)
    ppermute x46, waiting for transfers between devices, swap(): return lax.ppermute(arr, 'model', [(i, i ^ bit) for i in range(n_dev)])  160 us
    pallas_call x11, Pallas kernels, kv_call(): pl.pallas_call(functools.partial(kv_kernel, n_in, masks, batches, [[first...  123 us
    ppermute x46, starting transfers between devices, swap(): return lax.ppermute(arr, 'model', [(i, i ^ bit) for i in range(n_dev)])  36.1 us
    pallas_call x1, Pallas kernels, tail_call(): pl.pallas_call(functools.partial(tail_kernel, n_dev, parts_of), out_shape...  22.8 us
    pallas_call x2, Pallas kernels, turn_call(): pl.pallas_call(turn_kernel, grid=(d // cols,), in_specs=[pl.BlockSpec((n,...  15.8 us
    unnamed x28, local copies, waits for them, and re-layouts  13.6 us
    pallas_call x1, Pallas kernels, norm_call(): pl.pallas_call(functools.partial(norm_kernel, outs_of), grid=(len(order),...  10.8 us
  transfers between devices with their start and end apart: 46, of which 32 were waited for; matrix products, arithmetic and copies ran while one was open for 3% of the time, Pallas kernels for 36%

profile of v7, /device:TPU:0, one launch (start us, length us, event | category | flops | bytes accessed | tf_op | source)
XLA Modules:
  0.0 407.8 jit_solution(11238323741666316257)
XLA Ops:
  1.4 10.8 %norm_rows.1 = (bf16[1,128,4096]{2,1,0:T(8,128)(2,1)S(1)}, bf16[1,128,4096]{2,1,0:T(8,128)(2,1)S(1)}, bf16[2,128,4096]{2,1,0:T(8,128)(2,1)S(1)}, bf16[2,128,4096]{2,1,0:T(8,128)(2,1)S(1)}, bf16[8,128,4096]{2,1,0:T(8,128)(2,1)}) custom-call(bf16[8,128,4096]{2,1,0:T(8,128)(2,1)} %x_hbm.3, bf16[1,4096]{1,0:T(2,128)(2,1)S(1)} %copy-done.2), custom_call_target="tpu_custom_call" | custom-call | flops 33554432 | bytes 25165824 | tf_op jit(solution)/shard_map/norm_rows/pallas_call | solution.py:181
  16.8 4.6 %fusion.2 = bf16[8,1,4096]{2,1,0:T(2,128)(2,1)S(1)} fusion(bf16[8,128,4096]{2,1,0:T(8,128)(2,1)} %x_hbm.3, pred[8,128,1]{1,0,2:T(8,128)(4,1)S(1)} %compare_bitcast_fusion), kind=kOutput, calls=%fused_computation.14 | convolution fusion | flops 8388608 | bytes 8455168 | tf_op jit(solution)/shard_map/bs,bsd->bd/dot_general | solution.py:636
  21.5 2.4 first_rows.2
  24.7 3.0 collective-permute-start.6
  27.9 1.9 fusion
  30.2 2.6 collective-permute-start.2
  34.3 7.0 %collective-permute-done.2 = bf16[8,2048]{1,0:T(8,128)(2,1)S(1)} collective-permute-done((bf16[8,2048]{1,0:T(8,128)(2,1)S(1)}, bf16[8,2048]{1,0:T(8,128)(2,1)S(1)}, u32[]{:S(2)}, u32[]{:S(2)}) %collective-permute-start.2) | collective-permute-done | bytes 32800 | tf_op jit(solution)/shard_map/ppermute | solution.py:601
  41.4 1.7 collective-permute-start.7
  44.4 4.7 %keep.1 = (bf16[4096,512]{1,0:T(8,128)(2,1)S(1)}, bf16[4096,512]{1,0:T(8,128)(2,1)S(1)}, bf16[512,4096]{1,0:T(8,128)(2,1)S(1)}) custom-call(bf16[4096,512]{1,0:T(8,128)(2,1)} %bitcast.28, bf16[4096,512]{1,0:T(8,128)(2,1)} %bitcast.29, bf16[512,4096]{1,0:T(8,128)(2,1)} %bitcast.30), custom_call_target="tpu_custom_call" | custom-call | tf_op jit(solution)/shard_map/keep/pallas_call | solution.py:40
  49.1 3.1 query_rows.1
  52.2 28.4 %kv_chunk.11 = (bf16[8,1025,4,128]{3,2,1,0:T(4,128)(2,1)}, bf16[8,1025,4,128]{3,2,1,0:T(4,128)(2,1)}, f32[14,8,3,8,128]{4,3,2,1,0:T(8,128)S(1)}) custom-call(s32[16]{0:T(128)S(1)} %get-tuple-element.101.sc_ref, bf16[8,128,4096]{2,1,0:T(8,128)(2,1)} %get-tuple-element.102.refs_0_.refs_1_, bf16[8,128,4096]{2,1,0:T(8,128)(2,1)} %get-tuple-element.102.refs_0_.refs_1_, ...), custom_call_target="tpu_custom_call" | custom-call | flops 17179869184 | bytes 20971520 | tf_op jit(solution)/shard_map/kv_chunk/pallas_call | solution.py:430
  81.2 1.7 first_rows.3
  85.0 4.9 %kv_chunk.12 = (bf16[8,1025,4,128]{3,2,1,0:T(4,128)(2,1)}, bf16[8,1025,4,128]{3,2,1,0:T(4,128)(2,1)}, f32[14,8,3,8,128]{4,3,2,1,0:T(8,128)S(1)}) custom-call(s32[16]{0:T(128)S(1)} %get-tuple-element.101.sc_ref, bf16[1,64,4096]{2,1,0:T(8,128)(2,1)S(1)} %collective-permute-done.6.refs_0_, ...), custom_call_target="tpu_custom_call", output_to_operand_aliasing={{0}: (10, {}), {1}: (11, {}), {2}: (12, {})} | custom-call | flops 2147483648 | bytes 2621440 | tf_op jit(solution)/shard_map/kv_chunk/pallas_call | solution.py:430
  89.9 7.0 %collective-permute-done.10.refs_0_ = bf16[1,64,4096]{2,1,0:T(8,128)(2,1)S(1)} collective-permute-done((bf16[1,64,4096]{2,1,0:T(8,128)(2,1)S(1)}, bf16[1,64,4096]{2,1,0:T(8,128)(2,1)S(1)}, u32[]{:S(2)}, u32[]{:S(2)}) %collective-permute-start.10) | collective-permute-done | bytes 524320 | tf_op jit(solution)/shard_map/ppermute | solution.py:601
  99.1 1.7 collective-permute-start.18
  102.3 4.9 %kv_chunk.13 = (bf16[8,1025,4,128]{3,2,1,0:T(4,128)(2,1)}, bf16[8,1025,4,128]{3,2,1,0:T(4,128)(2,1)}, f32[14,8,3,8,128]{4,3,2,1,0:T(8,128)S(1)}) custom-call(s32[16]{0:T(128)S(1)} %get-tuple-element.101.sc_ref, bf16[1,64,4096]{2,1,0:T(8,128)(2,1)S(1)} %collective-permute-done.10.refs_0_, ...), custom_call_target="tpu_custom_call", output_to_operand_aliasing={{0}: (10, {}), {1}: (11, {}), {2}: (12, {})} | custom-call | flops 2147483648 | bytes 2621440 | tf_op jit(solution)/shard_map/kv_chunk/pallas_call | solution.py:430
  107.1 17.1 %collective-permute-done.14.refs_0_ = bf16[1,128,4096]{2,1,0:T(8,128)(2,1)S(1)} collective-permute-done((bf16[1,128,4096]{2,1,0:T(8,128)(2,1)S(1)}, bf16[1,128,4096]{2,1,0:T(8,128)(2,1)S(1)}, u32[]{:S(2)}, u32[]{:S(2)}) %collective-permute-start.14) | collective-permute-done | bytes 1048608 | tf_op jit(solution)/shard_map/ppermute | solution.py:601
  125.3 2.1 collective-permute-done.16.refs_2_
  128.9 8.3 %kv_chunk.14 = (bf16[8,1025,4,128]{3,2,1,0:T(4,128)(2,1)}, bf16[8,1025,4,128]{3,2,1,0:T(4,128)(2,1)}, f32[14,8,3,8,128]{4,3,2,1,0:T(8,128)S(1)}) custom-call(s32[16]{0:T(128)S(1)} %get-tuple-element.101.sc_ref, bf16[1,128,4096]{2,1,0:T(8,128)(2,1)S(1)} %collective-permute-done.14.refs_0_, ...), custom_call_target="tpu_custom_call", output_to_operand_aliasing={{0}: (10, {}), {1}: (11, {}), {2}: (12, {})} | custom-call | flops 4294967296 | bytes 5242880 | tf_op jit(solution)/shard_map/kv_chunk/pallas_call | solution.py:430
  137.2 31.5 %collective-permute-done.18.refs_0_ = bf16[2,128,4096]{2,1,0:T(8,128)(2,1)S(1)} collective-permute-done((bf16[2,128,4096]{2,1,0:T(8,128)(2,1)S(1)}, bf16[2,128,4096]{2,1,0:T(8,128)(2,1)S(1)}, u32[]{:S(2)}, u32[]{:S(2)}) %collective-permute-start.18) | collective-permute-done | bytes 2097184 | tf_op jit(solution)/shard_map/ppermute | solution.py:601
  169.8 1.7 collective-permute-start.22
  173.1 3.0 collective-permute-done.21.refs_3_
  176.1 14.7 %kv_chunk.15 = (bf16[8,1025,4,128]{3,2,1,0:T(4,128)(2,1)}, bf16[8,1025,4,128]{3,2,1,0:T(4,128)(2,1)}, f32[14,8,3,8,128]{4,3,2,1,0:T(8,128)S(1)}) custom-call(s32[16]{0:T(128)S(1)} %get-tuple-element.101.sc_ref, bf16[2,128,4096]{2,1,0:T(8,128)(2,1)S(1)} %collective-permute-done.18.refs_0_, ...), custom_call_target="tpu_custom_call", output_to_operand_aliasing={{0}: (10, {}), {1}: (11, {}), {2}: (12, {})} | custom-call | flops 8589934592 | bytes 10485760 | tf_op jit(solution)/shard_map/kv_chunk/pallas_call | solution.py:430
  190.8 26.2 %collective-permute-done.23.refs_1_ = bf16[2,128,4096]{2,1,0:T(8,128)(2,1)S(1)} collective-permute-done((bf16[2,128,4096]{2,1,0:T(8,128)(2,1)S(1)}, bf16[2,128,4096]{2,1,0:T(8,128)(2,1)S(1)}, u32[]{:S(2)}, u32[]{:S(2)}) %collective-permute-start.23) | collective-permute-done | bytes 2097184 | tf_op jit(solution)/shard_map/ppermute | solution.py:601
  217.6 4.6 %fusion.14 = (bf16[2,128,4096]{2,1,0:T(8,128)(2,1)}, bf16[2,128,4096]{2,1,0:T(8,128)(2,1)}) fusion(bf16[8,128,4096]{2,1,0:T(8,128)(2,1)} %get-tuple-element.102.refs_0_.refs_1_), kind=kLoop, calls=%fused_computation.53 | loop fusion | bytes 8388608 | tf_op jit(solution)/shard_map/slice | solution.py:645
  222.2 1.7 collective-permute-start.27
  225.4 14.7 %kv_chunk.16 = (bf16[8,1025,4,128]{3,2,1,0:T(4,128)(2,1)}, bf16[8,1025,4,128]{3,2,1,0:T(4,128)(2,1)}, f32[14,8,3,8,128]{4,3,2,1,0:T(8,128)S(1)}) custom-call(s32[16]{0:T(128)S(1)} %get-tuple-element.101.sc_ref, bf16[2,128,4096]{2,1,0:T(8,128)(2,1)S(1)} %collective-permute-done.22.refs_0_, ...), custom_call_target="tpu_custom_call", output_to_operand_aliasing={{0}: (10, {}), {1}: (11, {}), {2}: (12, {})} | custom-call | flops 8589934592 | bytes 10485760 | tf_op jit(solution)/shard_map/kv_chunk/pallas_call | solution.py:430
  240.1 7.9 %turn.2.wg_hbm = bf16[4096,1376]{1,0:T(8,128)(2,1)S(1)} custom-call(bf16[1376,4096]{1,0:T(8,128)(2,1)} %bitcast.25), custom_call_target="tpu_custom_call" | custom-call | flops 1442840576 | bytes 22544384 | tf_op jit(solution)/shard_map/turn/pallas_call | solution.py:58
  248.0 4.2 %copy-done = bf16[4096,1376]{1,0:T(8,128)(2,1)} copy-done((bf16[4096,1376]{1,0:T(8,128)(2,1)}, bf16[4096,1376]{1,0:T(8,128)(2,1)S(1)}, u32[]{:S(2)}) %copy-start) | copy-done | bytes 11272216
  252.2 17.7 %collective-permute-done.27.refs_1_ = bf16[2,128,4096]{2,1,0:T(8,128)(2,1)S(1)} collective-permute-done((bf16[2,128,4096]{2,1,0:T(8,128)(2,1)}, bf16[2,128,4096]{2,1,0:T(8,128)(2,1)S(1)}, u32[]{:S(2)}, u32[]{:S(2)}) %collective-permute-start.27) | collective-permute-done | bytes 2097184 | tf_op jit(solution)/shard_map/ppermute | solution.py:601
  272.2 1.7 collective-permute-start.31
  275.5 3.0 collective-permute-done.29.refs_3_
  278.5 14.7 %kv_chunk.17 = (bf16[8,1025,4,128]{3,2,1,0:T(4,128)(2,1)}, bf16[8,1025,4,128]{3,2,1,0:T(4,128)(2,1)}, f32[14,8,3,8,128]{4,3,2,1,0:T(8,128)S(1)}) custom-call(s32[16]{0:T(128)S(1)} %get-tuple-element.101.sc_ref, bf16[2,128,4096]{2,1,0:T(8,128)(2,1)S(1)} %collective-permute-done.26.refs_0_, ...), custom_call_target="tpu_custom_call", output_to_operand_aliasing={{0}: (10, {}), {1}: (11, {}), {2}: (12, {})} | custom-call | flops 8589934592 | bytes 10485760 | tf_op jit(solution)/shard_map/kv_chunk/pallas_call | solution.py:430
  293.2 7.9 %turn.3.wu_hbm = bf16[4096,1376]{1,0:T(8,128)(2,1)S(1)} custom-call(bf16[1376,4096]{1,0:T(8,128)(2,1)} %bitcast.26), custom_call_target="tpu_custom_call" | custom-call | flops 1442840576 | bytes 22544384 | tf_op jit(solution)/shard_map/turn/pallas_call | solution.py:58
  301.1 4.2 %copy-done.1 = bf16[4096,1376]{1,0:T(8,128)(2,1)} copy-done((bf16[4096,1376]{1,0:T(8,128)(2,1)}, bf16[4096,1376]{1,0:T(8,128)(2,1)S(1)}, u32[]{:S(2)}) %copy-start.1) | copy-done | bytes 11272216
  305.3 14.1 %collective-permute-done.30.refs_0_ = bf16[2,128,4096]{2,1,0:T(8,128)(2,1)S(1)} collective-permute-done((bf16[2,128,4096]{2,1,0:T(8,128)(2,1)S(1)}, bf16[2,128,4096]{2,1,0:T(8,128)(2,1)S(1)}, u32[]{:S(2)}, u32[]{:S(2)}) %collective-permute-start.30) | collective-permute-done | bytes 2097184 | tf_op jit(solution)/shard_map/ppermute | solution.py:601
  320.0 1.7 collective-permute-start.34
  323.6 3.0 collective-permute-done.33.refs_3_
  326.6 14.7 %kv_chunk.18 = (bf16[8,1025,4,128]{3,2,1,0:T(4,128)(2,1)}, bf16[8,1025,4,128]{3,2,1,0:T(4,128)(2,1)}, f32[14,8,3,8,128]{4,3,2,1,0:T(8,128)S(1)}) custom-call(s32[16]{0:T(128)S(1)} %get-tuple-element.101.sc_ref, bf16[2,128,4096]{2,1,0:T(8,128)(2,1)S(1)} %collective-permute-done.30.refs_0_, ...), custom_call_target="tpu_custom_call", output_to_operand_aliasing={{0}: (10, {}), {1}: (11, {}), {2}: (12, {})} | custom-call | flops 8589934592 | bytes 10485760 | tf_op jit(solution)/shard_map/kv_chunk/pallas_call | solution.py:430
  341.3 3.7 collective-permute-done.34.refs_0_
  347.3 1.7 collective-permute-start.39
  350.6 8.1 %kv_chunk.19 = (bf16[8,1025,4,128]{3,2,1,0:T(4,128)(2,1)}, bf16[8,1025,4,128]{3,2,1,0:T(4,128)(2,1)}, f32[14,8,3,8,128]{4,3,2,1,0:T(8,128)S(1)}) custom-call(s32[16]{0:T(128)S(1)} %get-tuple-element.101.sc_ref, bf16[1,128,4096]{2,1,0:T(8,128)(2,1)S(1)} %collective-permute-done.34.refs_0_, ...), custom_call_target="tpu_custom_call", output_to_operand_aliasing={{0}: (10, {}), {1}: (11, {}), {2}: (12, {})} | custom-call | flops 4294967296 | bytes 5242880 | tf_op jit(solution)/shard_map/kv_chunk/pallas_call | solution.py:430
  358.7 2.1 collective-permute-done.38.refs_0_
  361.4 1.7 collective-permute-start.42
  364.6 4.9 %kv_chunk.20 = (bf16[8,1025,4,128]{3,2,1,0:T(4,128)(2,1)}, bf16[8,1025,4,128]{3,2,1,0:T(4,128)(2,1)}, f32[14,8,3,8,128]{4,3,2,1,0:T(8,128)S(1)}) custom-call(s32[16]{0:T(128)S(1)} %get-tuple-element.101.sc_ref, bf16[1,64,4096]{2,1,0:T(8,128)(2,1)S(1)} %collective-permute-done.38.refs_0_, ...), custom_call_target="tpu_custom_call", output_to_operand_aliasing={{0}: (10, {}), {1}: (11, {}), {2}: (12, {})} | custom-call | flops 2147483648 | bytes 2621440 | tf_op jit(solution)/shard_map/kv_chunk/pallas_call | solution.py:430
  369.5 5.7 %collective-permute-done.42.refs_0_ = bf16[1,64,4096]{2,1,0:T(8,128)(2,1)S(1)} collective-permute-done((bf16[1,64,4096]{2,1,0:T(8,128)(2,1)S(1)}, bf16[1,64,4096]{2,1,0:T(8,128)(2,1)S(1)}, u32[]{:S(2)}, u32[]{:S(2)}) %collective-permute-start.42) | collective-permute-done | bytes 524320 | tf_op jit(solution)/shard_map/ppermute | solution.py:601
  379.3 5.1 %kv_chunk.21 = (bf16[8,1025,4,128]{3,2,1,0:T(4,128)(2,1)}, bf16[8,1025,4,128]{3,2,1,0:T(4,128)(2,1)}, f32[14,8,3,8,128]{4,3,2,1,0:T(8,128)S(1)}) custom-call(s32[16]{0:T(128)S(1)} %get-tuple-element.101.sc_ref, bf16[1,64,4096]{2,1,0:T(8,128)(2,1)S(1)} %collective-permute-done.42.refs_0_, ...), custom_call_target="tpu_custom_call", output_to_operand_aliasing={{0}: (10, {}), {1}: (11, {}), {2}: (12, {})} | custom-call | flops 2147483648 | bytes 2621440 | tf_op jit(solution)/shard_map/kv_chunk/pallas_call | solution.py:430
  384.4 22.8 %tail.1 = bf16[2,8,4096]{2,1,0:T(8,128)(2,1)S(1)} custom-call(f32[14,8,3,8,128]{4,3,2,1,0:T(8,128)S(1)} %get-tuple-element.190.stv, f32[3,8,8,128]{3,2,1,0:T(8,128)S(1)} %get-tuple-element.191.self_ref, bf16[16,512]{1,0:T(8,128)(2,1)S(1)} %fusion.1.xs_ref, bf16[1,4096]{1,0:T(2,128)(2,1)S(1)} %copy-done.5, bf16[512,4096]{1,0:T(8,128)(2,1)S(1)} %get-tuple-element.193.wo, ...), custom_call_target="tpu_custom_call" | custom-call | tf_op jit(solution)/shard_map/tail/pallas_call | solution.py:566
  (110 shorter events, 40.2 us)
Async XLA Ops:
  15.9 36.3 %collective-permute-start.5 = (bf16[8,128,4096]{2,1,0:T(8,128)(2,1)}, bf16[8,128,4096]{2,1,0:T(8,128)(2,1)}, u32[]{:S(2)}, u32[]{:S(2)}) collective-permute-start(bf16[8,128,4096]{2,1,0:T(8,128)(2,1)} %get-tuple-element.102.refs_0_.refs_1_), channel_id=1, source_target_pairs={{0,1},{1,0},{2,3},{3,2},{4,5},{5,4},{6,7},{7,6}} | collective-permute-start | bytes 25165832 | tf_op jit(solution)/shard_map/ppermute | solution.py:601
  21.5 8.7 %collective-permute-start = (bf16[8,4096]{1,0:T(8,128)(2,1)S(1)}, bf16[8,4096]{1,0:T(8,128)(2,1)S(1)}, u32[]{:S(2)}, u32[]{:S(2)}) collective-permute-start(bf16[8,4096]{1,0:T(8,128)(2,1)S(1)} %bitcast.32), channel_id=1, source_target_pairs={{0,1},{1,0},{2,3},{3,2},{4,5},{5,4},{6,7},{7,6}} | collective-permute-start | bytes 196616 | tf_op jit(solution)/shard_map/ppermute | solution.py:601
  24.7 19.7 %copy-start.4 = (bf16[8,4096]{1,0:T(8,128)(2,1)S(1)}, bf16[8,4096]{1,0:T(8,128)(2,1)}, u32[]{:S(2)}) copy-start(bf16[8,4096]{1,0:T(8,128)(2,1)} %new_ref.1) | copy-start | bytes 196612
  24.7 56.0 %collective-permute-start.6 = (bf16[1,64,4096]{2,1,0:T(8,128)(2,1)}, bf16[1,64,4096]{2,1,0:T(8,128)(2,1)S(1)}, u32[]{:S(2)}, u32[]{:S(2)}) collective-permute-start(bf16[1,64,4096]{2,1,0:T(8,128)(2,1)} %get-tuple-element.117), channel_id=1, source_target_pairs={{0,4},{1,5},{2,6},{3,7},{4,0},{5,1},{6,2},{7,3}} | collective-permute-start | bytes 1572872 | tf_op jit(solution)/shard_map/ppermute | solution.py:601
  30.2 11.2 %collective-permute-start.2 = (bf16[8,2048]{1,0:T(8,128)(2,1)S(1)}, bf16[8,2048]{1,0:T(8,128)(2,1)S(1)}, u32[]{:S(2)}, u32[]{:S(2)}) collective-permute-start(bf16[8,2048]{1,0:T(8,128)(2,1)S(1)} %dynamic-slice_add_fusion), channel_id=1, source_target_pairs={{0,4},{1,5},{2,6},{3,7},{4,0},{5,1},{6,2},{7,3}} | collective-permute-start | bytes 98312 | tf_op jit(solution)/shard_map/ppermute | solution.py:601
  32.8 10.3 %collective-permute-start.1 = (bf16[8,2048]{1,0:T(8,128)(2,1)S(1)}, bf16[8,2048]{1,0:T(8,128)(2,1)S(1)}, u32[]{:S(2)}, u32[]{:S(2)}) collective-permute-start(bf16[8,2048]{1,0:T(8,128)(2,1)S(1)} %dynamic-slice_add_fusion), channel_id=1, source_target_pairs={{0,2},{1,3},{2,0},{3,1},{4,6},{5,7},{6,4},{7,5}} | collective-permute-start | bytes 98312 | tf_op jit(solution)/shard_map/ppermute | solution.py:601
  34.3 8.8 %collective-permute-start.3 = (bf16[8,2048]{1,0:T(8,128)(2,1)S(1)}, bf16[8,2048]{1,0:T(8,128)(2,1)S(1)}, u32[]{:S(2)}, u32[]{:S(2)}) collective-permute-start(bf16[8,2048]{1,0:T(8,128)(2,1)S(1)} %dynamic-slice_add_fusion), channel_id=1, source_target_pairs={{0,6},{1,7},{2,4},{3,5},{4,2},{5,3},{6,0},{7,1}} | collective-permute-start | bytes 98312 | tf_op jit(solution)/shard_map/ppermute | solution.py:601
  41.4 39.3 %collective-permute-start.7 = (bf16[1,64,4096]{2,1,0:T(8,128)(2,1)}, bf16[1,64,4096]{2,1,0:T(8,128)(2,1)S(1)}, u32[]{:S(2)}, u32[]{:S(2)}) collective-permute-start(bf16[1,64,4096]{2,1,0:T(8,128)(2,1)} %copy-done.12), channel_id=1, source_target_pairs={{0,2},{1,3},{2,0},{3,1},{4,6},{5,7},{6,4},{7,5}} | collective-permute-start | bytes 1572872 | tf_op jit(solution)/shard_map/ppermute | solution.py:601
  43.1 1.2 collective-permute-start.4
  80.7 4.3 %collective-permute-start.8 = (bf16[1,64,4096]{2,1,0:T(8,128)(2,1)S(1)}, bf16[1,64,4096]{2,1,0:T(8,128)(2,1)S(1)}, u32[]{:S(2)}, u32[]{:S(2)}) collective-permute-start(bf16[1,64,4096]{2,1,0:T(8,128)(2,1)S(1)} %collective-permute-done.6.refs_0_), channel_id=1, source_target_pairs={{0,1},{1,0},{2,3},{3,2},{4,5},{5,4},{6,7},{7,6}} | collective-permute-start | bytes 1572872 | tf_op jit(solution)/shard_map/ppermute | solution.py:601
  80.9 4.1 %collective-permute-start.9 = (bf16[1,64,4096]{2,1,0:T(8,128)(2,1)S(1)}, bf16[1,64,4096]{2,1,0:T(8,128)(2,1)S(1)}, u32[]{:S(2)}, u32[]{:S(2)}) collective-permute-start(bf16[1,64,4096]{2,1,0:T(8,128)(2,1)S(1)} %collective-permute-done.7.refs_1_), channel_id=1, source_target_pairs={{0,1},{1,0},{2,3},{3,2},{4,5},{5,4},{6,7},{7,6}} | collective-permute-start | bytes 1572872 | tf_op jit(solution)/shard_map/ppermute | solution.py:601
  82.9 14.0 %collective-permute-start.10 = (bf16[1,64,4096]{2,1,0:T(8,128)(2,1)S(1)}, bf16[1,64,4096]{2,1,0:T(8,128)(2,1)S(1)}, u32[]{:S(2)}, u32[]{:S(2)}) collective-permute-start(bf16[1,64,4096]{2,1,0:T(8,128)(2,1)S(1)} %get-tuple-element.125), channel_id=1, source_target_pairs={{0,4},{1,5},{2,6},{3,7},{4,0},{5,1},{6,2},{7,3}} | collective-permute-start | bytes 1572872 | tf_op jit(solution)/shard_map/ppermute | solution.py:601
  84.5 13.7 %collective-permute-start.11 = (bf16[1,64,4096]{2,1,0:T(8,128)(2,1)S(1)}, bf16[1,64,4096]{2,1,0:T(8,128)(2,1)S(1)}, u32[]{:S(2)}, u32[]{:S(2)}) collective-permute-start(bf16[1,64,4096]{2,1,0:T(8,128)(2,1)S(1)} %get-tuple-element.126), channel_id=1, source_target_pairs={{0,2},{1,3},{2,0},{3,1},{4,6},{5,7},{6,4},{7,5}} | collective-permute-start | bytes 1572872 | tf_op jit(solution)/shard_map/ppermute | solution.py:601
  85.0 15.7 %copy-start.7 = (bf16[2,128,4096]{2,1,0:T(8,128)(2,1)S(1)}, bf16[2,128,4096]{2,1,0:T(8,128)(2,1)}, u32[]{:S(2)}) copy-start(bf16[2,128,4096]{2,1,0:T(8,128)(2,1)} %copy-done.6) | copy-start | bytes 6291460
  98.2 2.6 collective-permute-start.12
  98.2 26.0 %collective-permute-start.14 = (bf16[1,128,4096]{2,1,0:T(8,128)(2,1)S(1)}, bf16[1,128,4096]{2,1,0:T(8,128)(2,1)S(1)}, u32[]{:S(2)}, u32[]{:S(2)}) collective-permute-start(bf16[1,128,4096]{2,1,0:T(8,128)(2,1)S(1)} %copy-done.11), channel_id=1, source_target_pairs={{0,4},{1,5},{2,6},{3,7},{4,0},{5,1},{6,2},{7,3}} | collective-permute-start | bytes 3145736 | tf_op jit(solution)/shard_map/ppermute | solution.py:601
  98.7 26.0 %collective-permute-start.15 = (bf16[1,128,4096]{2,1,0:T(8,128)(2,1)S(1)}, bf16[1,128,4096]{2,1,0:T(8,128)(2,1)S(1)}, u32[]{:S(2)}, u32[]{:S(2)}) collective-permute-start(bf16[1,128,4096]{2,1,0:T(8,128)(2,1)S(1)} %get-tuple-element.134), channel_id=1, source_target_pairs={{0,2},{1,3},{2,0},{3,1},{4,6},{5,7},{6,4},{7,5}} | collective-permute-start | bytes 3145736 | tf_op jit(solution)/shard_map/ppermute | solution.py:601
  99.1 3.2 collective-permute-start.13
  99.1 69.6 %collective-permute-start.18 = (bf16[2,128,4096]{2,1,0:T(8,128)(2,1)S(1)}, bf16[2,128,4096]{2,1,0:T(8,128)(2,1)S(1)}, u32[]{:S(2)}, u32[]{:S(2)}) collective-permute-start(bf16[2,128,4096]{2,1,0:T(8,128)(2,1)S(1)} %copy-done.9), channel_id=1, source_target_pairs={{0,4},{1,5},{2,6},{3,7},{4,0},{5,1},{6,2},{7,3}} | collective-permute-start | bytes 6291464 | tf_op jit(solution)/shard_map/ppermute | solution.py:601
  100.8 68.2 %collective-permute-start.19 = (bf16[2,128,4096]{2,1,0:T(8,128)(2,1)S(1)}, bf16[2,128,4096]{2,1,0:T(8,128)(2,1)S(1)}, u32[]{:S(2)}, u32[]{:S(2)}) collective-permute-start(bf16[2,128,4096]{2,1,0:T(8,128)(2,1)S(1)} %copy-done.7), channel_id=1, source_target_pairs={{0,2},{1,3},{2,0},{3,1},{4,6},{5,7},{6,4},{7,5}} | collective-permute-start | bytes 6291464 | tf_op jit(solution)/shard_map/ppermute | solution.py:601
  124.7 2.7 collective-permute-start.16
  124.8 4.2 %collective-permute-start.17 = (bf16[1,128,4096]{2,1,0:T(8,128)(2,1)S(1)}, bf16[1,128,4096]{2,1,0:T(8,128)(2,1)S(1)}, u32[]{:S(2)}, u32[]{:S(2)}) collective-permute-start(bf16[1,128,4096]{2,1,0:T(8,128)(2,1)S(1)} %collective-permute-done.15.refs_1_), channel_id=1, source_target_pairs={{0,1},{1,0},{2,3},{3,2},{4,5},{5,4},{6,7},{7,6}} | collective-permute-start | bytes 3145736 | tf_op jit(solution)/shard_map/ppermute | solution.py:601
  168.9 4.2 %collective-permute-start.20 = (bf16[2,128,4096]{2,1,0:T(8,128)(2,1)S(1)}, bf16[2,128,4096]{2,1,0:T(8,128)(2,1)S(1)}, u32[]{:S(2)}, u32[]{:S(2)}) collective-permute-start(bf16[2,128,4096]{2,1,0:T(8,128)(2,1)S(1)} %collective-permute-done.18.refs_0_), channel_id=1, source_target_pairs={{0,1},{1,0},{2,3},{3,2},{4,5},{5,4},{6,7},{7,6}} | collective-permute-start | bytes 6291464 | tf_op jit(solution)/shard_map/ppermute | solution.py:601
  169.0 7.2 %collective-permute-start.21 = (bf16[2,128,4096]{2,1,0:T(8,128)(2,1)S(1)}, bf16[2,128,4096]{2,1,0:T(8,128)(2,1)S(1)}, u32[]{:S(2)}, u32[]{:S(2)}) collective-permute-start(bf16[2,128,4096]{2,1,0:T(8,128)(2,1)S(1)} %collective-permute-done.19.refs_1_), channel_id=1, source_target_pairs={{0,1},{1,0},{2,3},{3,2},{4,5},{5,4},{6,7},{7,6}} | collective-permute-start | bytes 6291464 | tf_op jit(solution)/shard_map/ppermute | solution.py:601
  169.5 47.5 %collective-permute-start.23 = (bf16[2,128,4096]{2,1,0:T(8,128)(2,1)S(1)}, bf16[2,128,4096]{2,1,0:T(8,128)(2,1)S(1)}, u32[]{:S(2)}, u32[]{:S(2)}) collective-permute-start(bf16[2,128,4096]{2,1,0:T(8,128)(2,1)S(1)} %copy-done.9), channel_id=1, source_target_pairs={{0,2},{1,3},{2,0},{3,1},{4,6},{5,7},{6,4},{7,5}} | collective-permute-start | bytes 6291464 | tf_op jit(solution)/shard_map/ppermute | solution.py:601
  169.8 47.3 %collective-permute-start.22 = (bf16[2,128,4096]{2,1,0:T(8,128)(2,1)S(1)}, bf16[2,128,4096]{2,1,0:T(8,128)(2,1)S(1)}, u32[]{:S(2)}, u32[]{:S(2)}) collective-permute-start(bf16[2,128,4096]{2,1,0:T(8,128)(2,1)S(1)} %copy-done.7), channel_id=1, source_target_pairs={{0,4},{1,5},{2,6},{3,7},{4,0},{5,1},{6,2},{7,3}} | collective-permute-start | bytes 6291464 | tf_op jit(solution)/shard_map/ppermute | solution.py:601
  217.1 8.4 %collective-permute-start.24 = (bf16[2,128,4096]{2,1,0:T(8,128)(2,1)S(1)}, bf16[2,128,4096]{2,1,0:T(8,128)(2,1)S(1)}, u32[]{:S(2)}, u32[]{:S(2)}) collective-permute-start(bf16[2,128,4096]{2,1,0:T(8,128)(2,1)S(1)} %collective-permute-done.22.refs_0_), channel_id=1, source_target_pairs={{0,1},{1,0},{2,3},{3,2},{4,5},{5,4},{6,7},{7,6}} | collective-permute-start | bytes 6291464 | tf_op jit(solution)/shard_map/ppermute | solution.py:601
  217.1 8.4 %collective-permute-start.25 = (bf16[2,128,4096]{2,1,0:T(8,128)(2,1)S(1)}, bf16[2,128,4096]{2,1,0:T(8,128)(2,1)S(1)}, u32[]{:S(2)}, u32[]{:S(2)}) collective-permute-start(bf16[2,128,4096]{2,1,0:T(8,128)(2,1)S(1)} %collective-permute-done.23.refs_1_), channel_id=1, source_target_pairs={{0,1},{1,0},{2,3},{3,2},{4,5},{5,4},{6,7},{7,6}} | collective-permute-start | bytes 6291464 | tf_op jit(solution)/shard_map/ppermute | solution.py:601
  222.2 47.7 %collective-permute-start.27 = (bf16[2,128,4096]{2,1,0:T(8,128)(2,1)}, bf16[2,128,4096]{2,1,0:T(8,128)(2,1)S(1)}, u32[]{:S(2)}, u32[]{:S(2)}) collective-permute-start(bf16[2,128,4096]{2,1,0:T(8,128)(2,1)} %get-tuple-element.198), channel_id=1, source_target_pairs={{0,2},{1,3},{2,0},{3,1},{4,6},{5,7},{6,4},{7,5}} | collective-permute-start | bytes 6291464 | tf_op jit(solution)/shard_map/ppermute | solution.py:601
  223.9 47.5 %collective-permute-start.26 = (bf16[2,128,4096]{2,1,0:T(8,128)(2,1)}, bf16[2,128,4096]{2,1,0:T(8,128)(2,1)S(1)}, u32[]{:S(2)}, u32[]{:S(2)}) collective-permute-start(bf16[2,128,4096]{2,1,0:T(8,128)(2,1)} %get-tuple-element.199), channel_id=1, source_target_pairs={{0,4},{1,5},{2,6},{3,7},{4,0},{5,1},{6,2},{7,3}} | collective-permute-start | bytes 6291464 | tf_op jit(solution)/shard_map/ppermute | solution.py:601
  271.4 4.2 %collective-permute-start.28 = (bf16[2,128,4096]{2,1,0:T(8,128)(2,1)S(1)}, bf16[2,128,4096]{2,1,0:T(8,128)(2,1)S(1)}, u32[]{:S(2)}, u32[]{:S(2)}) collective-permute-start(bf16[2,128,4096]{2,1,0:T(8,128)(2,1)S(1)} %collective-permute-done.26.refs_0_), channel_id=1, source_target_pairs={{0,1},{1,0},{2,3},{3,2},{4,5},{5,4},{6,7},{7,6}} | collective-permute-start | bytes 6291464 | tf_op jit(solution)/shard_map/ppermute | solution.py:601
  271.4 7.2 %collective-permute-start.29 = (bf16[2,128,4096]{2,1,0:T(8,128)(2,1)S(1)}, bf16[2,128,4096]{2,1,0:T(8,128)(2,1)S(1)}, u32[]{:S(2)}, u32[]{:S(2)}) collective-permute-start(bf16[2,128,4096]{2,1,0:T(8,128)(2,1)S(1)} %collective-permute-done.27.refs_1_), channel_id=1, source_target_pairs={{0,1},{1,0},{2,3},{3,2},{4,5},{5,4},{6,7},{7,6}} | collective-permute-start | bytes 6291464 | tf_op jit(solution)/shard_map/ppermute | solution.py:601
  271.9 47.5 %collective-permute-start.30 = (bf16[2,128,4096]{2,1,0:T(8,128)(2,1)S(1)}, bf16[2,128,4096]{2,1,0:T(8,128)(2,1)S(1)}, u32[]{:S(2)}, u32[]{:S(2)}) collective-permute-start(bf16[2,128,4096]{2,1,0:T(8,128)(2,1)S(1)} %collective-permute-done.18.refs_0_), channel_id=1, source_target_pairs={{0,2},{1,3},{2,0},{3,1},{4,6},{5,7},{6,4},{7,5}} | collective-permute-start | bytes 6291464 | tf_op jit(solution)/shard_map/ppermute | solution.py:601
  272.2 47.3 %collective-permute-start.31 = (bf16[2,128,4096]{2,1,0:T(8,128)(2,1)S(1)}, bf16[2,128,4096]{2,1,0:T(8,128)(2,1)S(1)}, u32[]{:S(2)}, u32[]{:S(2)}) collective-permute-start(bf16[2,128,4096]{2,1,0:T(8,128)(2,1)S(1)} %collective-permute-done.19.refs_1_), channel_id=1, source_target_pairs={{0,4},{1,5},{2,6},{3,7},{4,0},{5,1},{6,2},{7,3}} | collective-permute-start | bytes 6291464 | tf_op jit(solution)/shard_map/ppermute | solution.py:601
  319.5 4.2 %collective-permute-start.32 = (bf16[2,128,4096]{2,1,0:T(8,128)(2,1)S(1)}, bf16[2,128,4096]{2,1,0:T(8,128)(2,1)S(1)}, u32[]{:S(2)}, u32[]{:S(2)}) collective-permute-start(bf16[2,128,4096]{2,1,0:T(8,128)(2,1)S(1)} %collective-permute-done.30.refs_0_), channel_id=1, source_target_pairs={{0,1},{1,0},{2,3},{3,2},{4,5},{5,4},{6,7},{7,6}} | collective-permute-start | bytes 6291464 | tf_op jit(solution)/shard_map/ppermute | solution.py:601
  319.5 7.2 %collective-permute-start.33 = (bf16[2,128,4096]{2,1,0:T(8,128)(2,1)S(1)}, bf16[2,128,4096]{2,1,0:T(8,128)(2,1)S(1)}, u32[]{:S(2)}, u32[]{:S(2)}) collective-permute-start(bf16[2,128,4096]{2,1,0:T(8,128)(2,1)S(1)} %collective-permute-done.31.refs_1_), channel_id=1, source_target_pairs={{0,1},{1,0},{2,3},{3,2},{4,5},{5,4},{6,7},{7,6}} | collective-permute-start | bytes 6291464 | tf_op jit(solution)/shard_map/ppermute | solution.py:601
  320.0 25.1 %collective-permute-start.34 = (bf16[1,128,4096]{2,1,0:T(8,128)(2,1)S(1)}, bf16[1,128,4096]{2,1,0:T(8,128)(2,1)S(1)}, u32[]{:S(2)}, u32[]{:S(2)}) collective-permute-start(bf16[1,128,4096]{2,1,0:T(8,128)(2,1)S(1)} %collective-permute-done.14.refs_0_), channel_id=1, source_target_pairs={{0,2},{1,3},{2,0},{3,1},{4,6},{5,7},{6,4},{7,5}} | collective-permute-start | bytes 3145736 | tf_op jit(solution)/shard_map/ppermute | solution.py:601
  321.7 24.8 %collective-permute-start.35 = (bf16[1,128,4096]{2,1,0:T(8,128)(2,1)S(1)}, bf16[1,128,4096]{2,1,0:T(8,128)(2,1)S(1)}, u32[]{:S(2)}, u32[]{:S(2)}) collective-permute-start(bf16[1,128,4096]{2,1,0:T(8,128)(2,1)S(1)} %collective-permute-done.15.refs_1_), channel_id=1, source_target_pairs={{0,4},{1,5},{2,6},{3,7},{4,0},{5,1},{6,2},{7,3}} | collective-permute-start | bytes 3145736 | tf_op jit(solution)/shard_map/ppermute | solution.py:601
  346.5 2.7 collective-permute-start.36
  346.5 4.2 %collective-permute-start.37 = (bf16[1,128,4096]{2,1,0:T(8,128)(2,1)S(1)}, bf16[1,128,4096]{2,1,0:T(8,128)(2,1)S(1)}, u32[]{:S(2)}, u32[]{:S(2)}) collective-permute-start(bf16[1,128,4096]{2,1,0:T(8,128)(2,1)S(1)} %collective-permute-done.35.refs_1_), channel_id=1, source_target_pairs={{0,1},{1,0},{2,3},{3,2},{4,5},{5,4},{6,7},{7,6}} | collective-permute-start | bytes 3145736 | tf_op jit(solution)/shard_map/ppermute | solution.py:601
  347.0 13.8 %collective-permute-start.38 = (bf16[1,64,4096]{2,1,0:T(8,128)(2,1)S(1)}, bf16[1,64,4096]{2,1,0:T(8,128)(2,1)S(1)}, u32[]{:S(2)}, u32[]{:S(2)}) collective-permute-start(bf16[1,64,4096]{2,1,0:T(8,128)(2,1)S(1)} %collective-permute-done.6.refs_0_), channel_id=1, source_target_pairs={{0,2},{1,3},{2,0},{3,1},{4,6},{5,7},{6,4},{7,5}} | collective-permute-start | bytes 1572872 | tf_op jit(solution)/shard_map/ppermute | solution.py:601
  347.3 13.6 %collective-permute-start.39 = (bf16[1,64,4096]{2,1,0:T(8,128)(2,1)S(1)}, bf16[1,64,4096]{2,1,0:T(8,128)(2,1)S(1)}, u32[]{:S(2)}, u32[]{:S(2)}) collective-permute-start(bf16[1,64,4096]{2,1,0:T(8,128)(2,1)S(1)} %collective-permute-done.7.refs_1_), channel_id=1, source_target_pairs={{0,4},{1,5},{2,6},{3,7},{4,0},{5,1},{6,2},{7,3}} | collective-permute-start | bytes 1572872 | tf_op jit(solution)/shard_map/ppermute | solution.py:601
  360.9 3.7 collective-permute-start.40
  360.9 3.7 collective-permute-start.41
  361.4 13.8 %collective-permute-start.42 = (bf16[1,64,4096]{2,1,0:T(8,128)(2,1)S(1)}, bf16[1,64,4096]{2,1,0:T(8,128)(2,1)S(1)}, u32[]{:S(2)}, u32[]{:S(2)}) collective-permute-start(bf16[1,64,4096]{2,1,0:T(8,128)(2,1)S(1)} %collective-permute-done.10.refs_0_), channel_id=1, source_target_pairs={{0,2},{1,3},{2,0},{3,1},{4,6},{5,7},{6,4},{7,5}} | collective-permute-start | bytes 1572872 | tf_op jit(solution)/shard_map/ppermute | solution.py:601
  363.1 13.6 %collective-permute-start.43 = (bf16[1,64,4096]{2,1,0:T(8,128)(2,1)S(1)}, bf16[1,64,4096]{2,1,0:T(8,128)(2,1)S(1)}, u32[]{:S(2)}, u32[]{:S(2)}) collective-permute-start(bf16[1,64,4096]{2,1,0:T(8,128)(2,1)S(1)} %collective-permute-done.11.refs_1_), channel_id=1, source_target_pairs={{0,4},{1,5},{2,6},{3,7},{4,0},{5,1},{6,2},{7,3}} | collective-permute-start | bytes 1572872 | tf_op jit(solution)/shard_map/ppermute | solution.py:601
  376.6 1.9 collective-permute-start.44
  376.6 2.7 collective-permute-start.45
  (12 other events, 66.0 us)

commit v8 on v7

--- a/solution.py
+++ b/solution.py
@@ -13,7 +13,6 @@
 STAT_ROWS = 8
 NORM_ROWS = 32
 COL_TILE = 256
-N_MASKS = 8
 MESH = pl.DeviceIdType.MESH
 
 
@@ -256,28 +255,36 @@
     )(new_tok, last_x, gain, *row_tabs, pltpu.with_memory_space_constraint(w_q, pltpu.HBM), w_k, w_v)
 
 
+def when(condition):
+    if isinstance(condition, bool):
+        return lambda body: body() if condition else None
+    return pl.when(condition)
+
+
 def by_group(group, values):
+    if isinstance(group, int):
+        return values[group]
     out = values[-1]
     for p in range(len(values) - 1):
         out = jnp.where(group == p, values[p], out)
     return out
 
 
-def kv_kernel(n_in, masks, batches, firsts, row0, stat_of, with_new, sc_ref, *refs):
+def kv_kernel(n_in, n_steps, masks, batches, firsts, row0, stat_of, with_new, *refs):
     n_groups = len(masks)
     n_arr = n_in * n_groups
     x_refs = refs[:n_arr]
-    cos_ref, sin_ref, wk, wv, q_ref = refs[n_arr:n_arr + 5]
-    rest = refs[n_arr + 5:]
+    cos_ref, sin_ref, len_ref, wk, wv, q_ref = refs[n_arr:n_arr + 6]
+    rest = refs[n_arr + 6:]
     if with_new:
         new_refs = rest[:2]
         rest = rest[2:]
     else:
         rest = rest[3:]
-    kc_ref, vc_ref, st_ref, x_buf, k_buf, v_buf, k_out, v_out, s_out, x_sem, sems, s_sem, new_sem = rest
-    step = pl.program_id(0)
-    n_steps = pl.num_programs(0)
-    slot = lax.rem(step, 2)
+    kc_ref, vc_ref, st_ref, x_buf, k_buf, v_buf, k_out, v_out, s_out, x_sem, sems, s_sem = rest[:12]
+    me = lax.axis_index("model")
+    step = pl.program_id(0) if n_steps > 1 else 0
+    slot = lax.rem(step, 2) if n_steps > 1 else 0
     per_group = n_steps // n_groups
     blk = x_buf.shape[2]
     shard_rows = cos_ref.shape[1]
@@ -292,7 +299,7 @@
 
     def start_x(at_step, which):
         for group in range(n_groups):
-            @pl.when(at_step // per_group == group)
+            @when(at_step // per_group == group)
             def _(group=group):
                 for copy in x_copies(at_step, which, group):
                     copy.start()
@@ -300,7 +307,8 @@
     def place(i, at_step):
         group = at_step // per_group
         mask = by_group(group, [m[i] for m in masks])
-        return sc_ref[mask], by_group(group, [b[i] for b in batches]) + lax.rem(at_step, per_group), mask
+        shard = sum(lax.rem(me // bit + mask // bit, 2) * bit for bit in (1, 2, 4))
+        return shard, by_group(group, [b[i] for b in batches]) + at_step % per_group, mask
 
     def out_copies(which, at_step):
         copies = []
@@ -312,21 +320,21 @@
         return copies
 
     def new_copies():
-        return [pltpu.make_async_copy(src.at[pl.ds(b, 1)], dst.at[b, pl.ds(dst.shape[1] - 1, 1)], new_sem.at[idx, b])
+        return [pltpu.make_async_copy(src.at[pl.ds(b, 1)], dst.at[b, pl.ds(dst.shape[1] - 1, 1)], rest[12].at[idx, b])
                 for idx, (src, dst) in enumerate(zip(new_refs, (kc_ref, vc_ref))) for b in range(src.shape[0])]
 
-    @pl.when(step == 0)
+    @when(step == 0)
     def _():
         start_x(step, slot)
         if with_new:
             for copy in new_copies():
                 copy.start()
 
-    @pl.when(step + 1 < n_steps)
+    @when(step + 1 < n_steps)
     def _():
         start_x(step + 1, 1 - slot)
 
-    @pl.when(step >= 2)
+    @when(step >= 2)
     def _():
         for copy in out_copies(slot, step - 2):
             copy.wait()
@@ -336,7 +344,7 @@
     x_rows = x_buf.at[slot]
 
     def col_tile(c, carry):
-        cols = pl.ds(pl.multiple_of(c * COL_TILE, COL_TILE), COL_TILE)
+        cols = pl.ds(pl.multiple_of(c * COL_TILE, COL_TILE), COL_TILE) if n_steps > 1 else slice(c * COL_TILE, (c + 1) * COL_TILE)
         normed = x_rows[...].reshape(n_tok, x_buf.shape[3])
         kf = jnp.dot(normed, wk[:, cols], preferred_element_type=jnp.float32)
         vf = jnp.dot(normed, wv[:, cols], preferred_element_type=jnp.float32)
@@ -354,7 +362,11 @@
         k_buf[:, cols] = jnp.concatenate(parts, axis=0).astype(jnp.bfloat16)
         return carry
 
-    lax.fori_loop(0, width // COL_TILE, col_tile, 0)
+    if n_steps > 1:
+        lax.fori_loop(0, width // COL_TILE, col_tile, 0)
+    else:
+        for c in range(width // COL_TILE):
+            col_tile(c, 0)
 
     for i in range(n_in):
         k_out[slot, i] = k_buf[i * blk:(i + 1) * blk, :].reshape(blk, heads, HEAD_DIM)
@@ -369,7 +381,7 @@
         scores = lax.dot_general(q_ref[bat], k_buf[i * blk:(i + 1) * blk, :], (((1,), (1,)), ((), ())),
                                  preferred_element_type=jnp.float32) * (HEAD_DIM ** -0.5)
         pos = shard * shard_rows + row0 + lax.broadcasted_iota(jnp.int32, scores.shape, 1)
-        visible = pos < sc_ref[N_MASKS + bat]
+        visible = pos < len_ref[pl.ds(bat, 1), :blk]
         scores = jnp.where(visible, scores, NEG_BIG)
         blk_max = jnp.max(scores, axis=-1, keepdims=True)
         prob = jnp.where(visible, jnp.exp(scores - blk_max), 0.0)
@@ -390,21 +402,19 @@
     for copy in stat_copies:
         copy.wait()
 
-    @pl.when(step == n_steps - 1)
+    @when(step == n_steps - 1)
     def _():
         for copy in out_copies(slot, step):
             copy.wait()
         if with_new:
             for copy in new_copies():
                 copy.wait()
-
-    @pl.when((step == n_steps - 1) & (n_steps >= 2))
-    def _():
-        for copy in out_copies(1 - slot, step - 1):
-            copy.wait()
-
-
-def kv_call(groups, per_group, masks, batches, scalars, tabs, w_k, w_v, q_diag, caches, new_rows=None, row0=0, stat_of=0):
+        if n_steps > 1:
+            for copy in out_copies(1 - slot, step - 1):
+                copy.wait()
+
+
+def kv_call(groups, per_group, masks, batches, lengths, tabs, w_k, w_v, q_diag, caches, new_rows=None, row0=0, stat_of=0):
     n_groups = len(groups)
     n_in = len(groups[0])
     n_steps = n_groups * per_group
@@ -414,8 +424,8 @@
     heads = width // HEAD_DIM
     any_spec = pl.BlockSpec(memory_space=pl.ANY)
     operands = [arr for group in groups for arr, _ in group]
-    in_specs = [any_spec] * len(operands) + [pl.BlockSpec(memory_space=pltpu.VMEM)] * 5
-    operands += [cos_tab, sin_tab, w_k, w_v, q_diag]
+    in_specs = [any_spec] * len(operands) + [pl.BlockSpec(memory_space=pltpu.VMEM)] * 6
+    operands += [cos_tab, sin_tab, lengths, w_k, w_v, q_diag]
     with_new = new_rows is not None
     if with_new:
         operands += new_rows
@@ -424,35 +434,32 @@
     else:
         operands += [*caches[:2], pltpu.with_memory_space_constraint(caches[2], pltpu.VMEM)]
         in_specs += [any_spec] * 3
-        aliases = {len(operands) - 2: 0, len(operands) - 1: 1, len(operands): 2}
+        aliases = {len(operands) - 3: 0, len(operands) - 2: 1, len(operands) - 1: 2}
     tokens = n_in * blk
     n_batch = q_diag.shape[0]
+    slots = min(n_steps, 2)
     return pl.pallas_call(
-        functools.partial(kv_kernel, n_in, masks, batches, [[first for _, first in group] for group in groups], row0, stat_of, with_new),
-        grid_spec=pltpu.PrefetchScalarGridSpec(
-            num_scalar_prefetch=1,
-            grid=(n_steps,),
-            in_specs=in_specs,
-            out_specs=[any_spec] * 3,
-            scratch_shapes=[
-                pltpu.VMEM((2, n_in, blk, d_model), jnp.bfloat16),
-                pltpu.VMEM((tokens, width), jnp.bfloat16),
-                pltpu.VMEM((tokens, width), jnp.bfloat16),
-                pltpu.VMEM((2, n_in, blk, heads, HEAD_DIM), jnp.bfloat16),
-                pltpu.VMEM((2, n_in, blk, heads, HEAD_DIM), jnp.bfloat16),
-                pltpu.VMEM((n_in, 3, STAT_ROWS, HEAD_DIM), jnp.float32),
-                pltpu.SemaphoreType.DMA((2, n_in)),
-                pltpu.SemaphoreType.DMA((2, n_in, 2)),
-                pltpu.SemaphoreType.DMA((n_in,)),
-                pltpu.SemaphoreType.DMA((2, n_batch)),
-            ],
-        ),
+        functools.partial(kv_kernel, n_in, n_steps, masks, batches, [[first for _, first in group] for group in groups], row0, stat_of, with_new),
+        grid=(n_steps,) if n_steps > 1 else (),
+        in_specs=in_specs,
+        out_specs=[any_spec] * 3,
+        scratch_shapes=[
+            pltpu.VMEM((slots, n_in, blk, d_model), jnp.bfloat16),
+            pltpu.VMEM((tokens, width), jnp.bfloat16),
+            pltpu.VMEM((tokens, width), jnp.bfloat16),
+            pltpu.VMEM((slots, n_in, blk, heads, HEAD_DIM), jnp.bfloat16),
+            pltpu.VMEM((slots, n_in, blk, heads, HEAD_DIM), jnp.bfloat16),
+            pltpu.VMEM((n_in, 3, STAT_ROWS, HEAD_DIM), jnp.float32),
+            pltpu.SemaphoreType.DMA((slots, n_in)),
+            pltpu.SemaphoreType.DMA((slots, n_in, 2)),
+            pltpu.SemaphoreType.DMA((n_in,)),
+        ] + [pltpu.SemaphoreType.DMA((2, n_batch))] * with_new,
         out_shape=[*(jax.ShapeDtypeStruct(c.shape, c.dtype) for c in caches[:2]), pltpu.VMEM(caches[2].shape, caches[2].dtype)],
         input_output_aliases=aliases,
         compiler_params=pltpu.CompilerParams(vmem_limit_bytes=20 * 2 ** 20),
         cost_estimate=pl.CostEstimate(flops=4 * n_steps * tokens * d_model * width, bytes_accessed=2 * n_steps * tokens * (d_model + 2 * width), transcendentals=0),
         name="kv_chunk",
-    )(scalars, *operands)
+    )(*operands)
 
 
 def tail_kernel(n_dev, parts_of, stv, self_ref, xs_ref, gain_ref, wo, wg_hbm, wu_hbm, wd_hbm, out_ref,
@@ -645,21 +652,20 @@
         send_part("4", normed[half:half + q2], normed[:q2])
         core_all = swap(normed, 1)
 
-        bits = jnp.arange(N_MASKS)
-        scalars = jnp.concatenate([sum(((my_idx // bit + bits // bit) % 2) * bit for bit in (1, 2, 4)), lengths]).astype(jnp.int32)
+        len_rows = jnp.broadcast_to(lengths.astype(jnp.int32)[:, None], (n_batch, HEAD_DIM))
         row_tabs = rotary_tables(jnp.concatenate([lengths, lengths - 1]))
         tabs = tuple(tab.reshape(n_dev, blk, HEAD_DIM) for tab in rotary_tables(jnp.arange(seq_len)))
         x_rows = jnp.concatenate([new_tok, last_x], axis=0)
         x_mine = lax.dynamic_slice_in_dim(x_rows, my_idx * (d_model // n_dev), d_model // n_dev, axis=1)
-        wk, wv, wo, last_x, scalars, row_tabs, tabs, x_mine = lax.optimization_barrier(
-            (w_k[0], w_v[0], w_o[0], last_x, scalars, row_tabs, tabs, x_mine))
+        wk, wv, wo, last_x, len_rows, row_tabs, tabs, x_mine = lax.optimization_barrier(
+            (w_k[0], w_v[0], w_o[0], last_x, len_rows, row_tabs, tabs, x_mine))
         wk, wv, wo = keep_in_vmem(wk, wv, wo)
         q_diag, k_new, v_new, self_stat = rows_call(new_tok, last_x, gain, row_tabs, wq, wk, wv)
         cache_shape = jax.ShapeDtypeStruct((n_batch, seq_len + 1, heads, HEAD_DIM), jnp.bfloat16)
         caches = [cache_shape, cache_shape, jax.ShapeDtypeStruct((2 * n_dev - 2, n_batch, 3, STAT_ROWS, HEAD_DIM), jnp.float32)]
 
         def run(groups, per_group, masks, batches, caches, **kw):
-            return kv_call(groups, per_group, masks, batches, scalars, tabs, wk, wv, q_diag, caches, **kw)
+            return kv_call(groups, per_group, masks, batches, len_rows, tabs, wk, wv, q_diag, caches, **kw)
 
         def half_rows(step):
             return {"row0": rows_h * (step == "0b"), "stat_of": (n_dev - 2) * (step == "0b")}
@@ -676,7 +682,9 @@
             caches, (got_y, got_x) = after(caches, from_y[step], from_x[step])
             other_y, other_x = swap(got_y, 1), swap(got_x, 1)
             if step not in "34":
-                diag[step] = (swap(got_y, 2), swap(got_x, 4))
+                via_x = swap(got_y, 2)
+                via_y = swap(got_x, 4)
+                diag[step] = (via_x, via_y)
             streams = [[(got_y, 0), (got_x, 0)], [(other_y, 0), (other_x, 0)]]
             if step in ("0a", "0b"):
                 caches = run([streams[0] + streams[1]], q1, [[4, 2, 5, 3]], [[*start, *start]], caches, **half_rows(step))
@@ -687,8 +695,10 @@
                 turned[step] = turn_call(w_t)
                 caches, (turned[step],) = after(caches, turned[step])
         for step in ("2", "1", "0a", "0b"):
-            caches, (via_x, via_y) = after(caches, *diag[step])
-            other_x, other_y = swap(via_x, 1), swap(via_y, 1)
+            caches, (via_y,) = after(caches, diag[step][1])
+            caches, (via_x,) = after(caches, diag[step][0])
+            other_y = swap(via_y, 1)
+            other_x = swap(via_x, 1)
             start = starts[step]
             streams = [[(via_x, 0), (via_y, 0)], [(other_x, 0), (other_y, 0)]]
             if step in ("0a", "0b"):

time: 409 us -> 407 us (level)
  Pallas kernels: 185 us -> 174 us
  waiting for transfers between devices: 160 us -> 171 us
  starting transfers between devices: 36.1 us -> 30.9 us
    ppermute x46, waiting for transfers between devices: 160 us -> 171 us  [swap(): return lax.ppermute(arr, 'model', [(i, i ^ bit) for i in range(n_dev)])]
    pallas_call x11, Pallas kernels: 123 us -> 113 us  [kv_call(): pl.pallas_call(functools.partial(kv_kernel, n_in, n_steps, masks, batches...]
    ppermute x46, starting transfers between devices: 36.1 us -> 30.9 us  [swap(): return lax.ppermute(arr, 'model', [(i, i ^ bit) for i in range(n_dev)])]
  transfers between devices with their start and end apart: 46 -> 46, of which waited for: 32 -> 34; matrix products, arithmetic and copies ran while one was open for 3% -> 4% of each run, Pallas kernels for 36% -> 34%
where the time goes in v8:
time: 407 us; the launch traced here: 406 us
  Pallas kernels  174 us (43%)
  waiting for transfers between devices  171 us (42%)
  starting transfers between devices  30.9 us (8%)
  local copies, waits for them, and re-layouts  19.1 us (5%)
  other arithmetic  5.18 us (1%)
  matrix products  4.57 us (1%)
    ppermute x46, waiting for transfers between devices, swap(): return lax.ppermute(arr, 'model', [(i, i ^ bit) for i in range(n_dev)])  171 us
    pallas_call x11, Pallas kernels, kv_call(): pl.pallas_call(functools.partial(kv_kernel, n_in, n_steps, masks, batches...  113 us
    ppermute x46, starting transfers between devices, swap(): return lax.ppermute(arr, 'model', [(i, i ^ bit) for i in range(n_dev)])  30.9 us
    pallas_call x1, Pallas kernels, tail_call(): pl.pallas_call(functools.partial(tail_kernel, n_dev, parts_of), out_shape...  22.8 us
    pallas_call x2, Pallas kernels, turn_call(): pl.pallas_call(turn_kernel, grid=(d // cols,), in_specs=[pl.BlockSpec((n,...  15.8 us
    unnamed x28, local copies, waits for them, and re-layouts  13.6 us
    pallas_call x1, Pallas kernels, norm_call(): pl.pallas_call(functools.partial(norm_kernel, outs_of), grid=(len(order),...  10.8 us
  transfers between devices with their start and end apart: 46, of which 34 were waited for; matrix products, arithmetic and copies ran while one was open for 4% of the time, Pallas kernels for 34%

profile of v8, /device:TPU:0, one launch (start us, length us, event | category | flops | bytes accessed | tf_op | source)
XLA Modules:
  0.0 406.1 jit_solution(14812649329483351255)
XLA Ops:
  1.4 10.8 %norm_rows.1 = (bf16[1,128,4096]{2,1,0:T(8,128)(2,1)S(1)}, bf16[1,128,4096]{2,1,0:T(8,128)(2,1)S(1)}, bf16[2,128,4096]{2,1,0:T(8,128)(2,1)S(1)}, bf16[2,128,4096]{2,1,0:T(8,128)(2,1)S(1)}, bf16[8,128,4096]{2,1,0:T(8,128)(2,1)}) custom-call(bf16[8,128,4096]{2,1,0:T(8,128)(2,1)} %x_hbm.3, bf16[1,4096]{1,0:T(2,128)(2,1)S(1)} %copy-done.2), custom_call_target="tpu_custom_call" | custom-call | flops 33554432 | bytes 25165824 | tf_op jit(solution)/shard_map/norm_rows/pallas_call | solution.py:180
  16.8 4.6 %fusion.2 = bf16[8,1,4096]{2,1,0:T(2,128)(2,1)S(1)} fusion(bf16[8,128,4096]{2,1,0:T(8,128)(2,1)} %x_hbm.3, pred[8,128,1]{1,0,2:T(8,128)(4,1)S(1)} %compare_bitcast_fusion), kind=kOutput, calls=%fused_computation.14 | convolution fusion | flops 8388608 | bytes 8455168 | tf_op jit(solution)/shard_map/bs,bsd->bd/dot_general | solution.py:643
  21.5 2.4 first_rows.2
  24.7 3.0 collective-permute-start.6
  27.8 3.0 fusion
  31.0 1.8 collective-permute-start.3
  34.5 1.7 pad_maximum_fusion
  36.2 5.2 %collective-permute-done.3 = bf16[8,2048]{1,0:T(8,128)(2,1)S(1)} collective-permute-done((bf16[8,2048]{1,0:T(8,128)(2,1)S(1)}, bf16[8,2048]{1,0:T(8,128)(2,1)S(1)}, u32[]{:S(2)}, u32[]{:S(2)}) %collective-permute-start.3) | collective-permute-done | bytes 32800 | tf_op jit(solution)/shard_map/ppermute | solution.py:608
  41.4 1.7 collective-permute-start.7
  44.5 4.7 %keep.1 = (bf16[4096,512]{1,0:T(8,128)(2,1)S(1)}, bf16[4096,512]{1,0:T(8,128)(2,1)S(1)}, bf16[512,4096]{1,0:T(8,128)(2,1)S(1)}) custom-call(bf16[4096,512]{1,0:T(8,128)(2,1)} %bitcast.28, bf16[4096,512]{1,0:T(8,128)(2,1)} %bitcast.29, bf16[512,4096]{1,0:T(8,128)(2,1)} %bitcast.30), custom_call_target="tpu_custom_call" | custom-call | tf_op jit(solution)/shard_map/keep/pallas_call | solution.py:39
  49.2 3.1 query_rows.1
  52.3 27.9 %kv_chunk.11 = (bf16[8,1025,4,128]{3,2,1,0:T(4,128)(2,1)}, bf16[8,1025,4,128]{3,2,1,0:T(4,128)(2,1)}, f32[14,8,3,8,128]{4,3,2,1,0:T(8,128)S(1)}) custom-call(bf16[8,128,4096]{2,1,0:T(8,128)(2,1)} %get-tuple-element.105.refs_0_.refs_1_, bf16[8,128,4096]{2,1,0:T(8,128)(2,1)} %get-tuple-element.105.refs_0_.refs_1_, ...), custom_call_target="tpu_custom_call" | custom-call | flops 17179869184 | bytes 20971520 | tf_op jit(solution)/shard_map/kv_chunk/pallas_call | solution.py:441
  80.8 1.7 first_rows.3
  84.6 3.6 kv_chunk.12
  88.1 8.3 %collective-permute-done.10.refs_0_ = bf16[1,64,4096]{2,1,0:T(8,128)(2,1)S(1)} collective-permute-done((bf16[1,64,4096]{2,1,0:T(8,128)(2,1)S(1)}, bf16[1,64,4096]{2,1,0:T(8,128)(2,1)S(1)}, u32[]{:S(2)}, u32[]{:S(2)}) %collective-permute-start.10) | collective-permute-done | bytes 524320 | tf_op jit(solution)/shard_map/ppermute | solution.py:608
  98.6 1.7 collective-permute-start.18
  101.8 3.5 kv_chunk.13
  105.3 18.4 %collective-permute-done.14.refs_0_ = bf16[1,128,4096]{2,1,0:T(8,128)(2,1)S(1)} collective-permute-done((bf16[1,128,4096]{2,1,0:T(8,128)(2,1)S(1)}, bf16[1,128,4096]{2,1,0:T(8,128)(2,1)S(1)}, u32[]{:S(2)}, u32[]{:S(2)}) %collective-permute-start.14) | collective-permute-done | bytes 1048608 | tf_op jit(solution)/shard_map/ppermute | solution.py:608
  124.8 2.1 collective-permute-done.16.refs_2_
  128.4 7.4 %kv_chunk.14 = (bf16[8,1025,4,128]{3,2,1,0:T(4,128)(2,1)}, bf16[8,1025,4,128]{3,2,1,0:T(4,128)(2,1)}, f32[14,8,3,8,128]{4,3,2,1,0:T(8,128)S(1)}) custom-call(bf16[1,128,4096]{2,1,0:T(8,128)(2,1)S(1)} %collective-permute-done.14.refs_0_, ...), custom_call_target="tpu_custom_call", output_to_operand_aliasing={{0}: (10, {}), {1}: (11, {}), {2}: (12, {})} | custom-call | flops 4294967296 | bytes 5242880 | tf_op jit(solution)/shard_map/kv_chunk/pallas_call | solution.py:441
  135.8 32.4 %collective-permute-done.18.refs_0_ = bf16[2,128,4096]{2,1,0:T(8,128)(2,1)S(1)} collective-permute-done((bf16[2,128,4096]{2,1,0:T(8,128)(2,1)S(1)}, bf16[2,128,4096]{2,1,0:T(8,128)(2,1)S(1)}, u32[]{:S(2)}, u32[]{:S(2)}) %collective-permute-start.18) | collective-permute-done | bytes 2097184 | tf_op jit(solution)/shard_map/ppermute | solution.py:608
  169.3 1.7 collective-permute-start.22
  171.0 1.6 collective-permute-done.20.refs_2_
  172.6 3.0 collective-permute-done.21.refs_3_
  175.6 14.0 %kv_chunk.15 = (bf16[8,1025,4,128]{3,2,1,0:T(4,128)(2,1)}, bf16[8,1025,4,128]{3,2,1,0:T(4,128)(2,1)}, f32[14,8,3,8,128]{4,3,2,1,0:T(8,128)S(1)}) custom-call(bf16[2,128,4096]{2,1,0:T(8,128)(2,1)S(1)} %collective-permute-done.18.refs_0_, ...), custom_call_target="tpu_custom_call", output_to_operand_aliasing={{0}: (10, {}), {1}: (11, {}), {2}: (12, {})} | custom-call | flops 8589934592 | bytes 10485760 | tf_op jit(solution)/shard_map/kv_chunk/pallas_call | solution.py:441
  189.6 26.9 %collective-permute-done.23.refs_1_ = bf16[2,128,4096]{2,1,0:T(8,128)(2,1)S(1)} collective-permute-done((bf16[2,128,4096]{2,1,0:T(8,128)(2,1)S(1)}, bf16[2,128,4096]{2,1,0:T(8,128)(2,1)S(1)}, u32[]{:S(2)}, u32[]{:S(2)}) %collective-permute-start.23) | collective-permute-done | bytes 2097184 | tf_op jit(solution)/shard_map/ppermute | solution.py:608
  217.1 4.7 %fusion.5 = (bf16[2,128,4096]{2,1,0:T(8,128)(2,1)}, bf16[2,128,4096]{2,1,0:T(8,128)(2,1)}) fusion(bf16[8,128,4096]{2,1,0:T(8,128)(2,1)} %get-tuple-element.105.refs_0_.refs_1_), kind=kLoop, calls=%fused_computation.27 | loop fusion | bytes 8388608 | tf_op jit(solution)/shard_map/slice | solution.py:652
  221.7 1.7 collective-permute-start.27
  225.0 14.0 %kv_chunk.16 = (bf16[8,1025,4,128]{3,2,1,0:T(4,128)(2,1)}, bf16[8,1025,4,128]{3,2,1,0:T(4,128)(2,1)}, f32[14,8,3,8,128]{4,3,2,1,0:T(8,128)S(1)}) custom-call(bf16[2,128,4096]{2,1,0:T(8,128)(2,1)S(1)} %collective-permute-done.22.refs_0_, ...), custom_call_target="tpu_custom_call", output_to_operand_aliasing={{0}: (10, {}), {1}: (11, {}), {2}: (12, {})} | custom-call | flops 8589934592 | bytes 10485760 | tf_op jit(solution)/shard_map/kv_chunk/pallas_call | solution.py:441
  239.0 7.9 %turn.2.wg_hbm = bf16[4096,1376]{1,0:T(8,128)(2,1)S(1)} custom-call(bf16[1376,4096]{1,0:T(8,128)(2,1)} %bitcast.25), custom_call_target="tpu_custom_call" | custom-call | flops 1442840576 | bytes 22544384 | tf_op jit(solution)/shard_map/turn/pallas_call | solution.py:57
  246.9 4.2 %copy-done = bf16[4096,1376]{1,0:T(8,128)(2,1)} copy-done((bf16[4096,1376]{1,0:T(8,128)(2,1)}, bf16[4096,1376]{1,0:T(8,128)(2,1)S(1)}, u32[]{:S(2)}) %copy-start) | copy-done | bytes 11272216
  251.1 18.4 %collective-permute-done.27.refs_1_ = bf16[2,128,4096]{2,1,0:T(8,128)(2,1)S(1)} collective-permute-done((bf16[2,128,4096]{2,1,0:T(8,128)(2,1)}, bf16[2,128,4096]{2,1,0:T(8,128)(2,1)S(1)}, u32[]{:S(2)}, u32[]{:S(2)}) %collective-permute-start.27) | collective-permute-done | bytes 2097184 | tf_op jit(solution)/shard_map/ppermute | solution.py:608
  273.5 1.6 collective-permute-done.28.refs_2_
  275.1 3.0 collective-permute-done.29.refs_3_
  278.1 14.0 %kv_chunk.17 = (bf16[8,1025,4,128]{3,2,1,0:T(4,128)(2,1)}, bf16[8,1025,4,128]{3,2,1,0:T(4,128)(2,1)}, f32[14,8,3,8,128]{4,3,2,1,0:T(8,128)S(1)}) custom-call(bf16[2,128,4096]{2,1,0:T(8,128)(2,1)S(1)} %collective-permute-done.26.refs_0_, ...), custom_call_target="tpu_custom_call", output_to_operand_aliasing={{0}: (10, {}), {1}: (11, {}), {2}: (12, {})} | custom-call | flops 8589934592 | bytes 10485760 | tf_op jit(solution)/shard_map/kv_chunk/pallas_call | solution.py:441
  292.1 7.9 %turn.3.wu_hbm = bf16[4096,1376]{1,0:T(8,128)(2,1)S(1)} custom-call(bf16[1376,4096]{1,0:T(8,128)(2,1)} %bitcast.26), custom_call_target="tpu_custom_call" | custom-call | flops 1442840576 | bytes 22544384 | tf_op jit(solution)/shard_map/turn/pallas_call | solution.py:57
  300.0 4.2 %copy-done.1 = bf16[4096,1376]{1,0:T(8,128)(2,1)} copy-done((bf16[4096,1376]{1,0:T(8,128)(2,1)}, bf16[4096,1376]{1,0:T(8,128)(2,1)S(1)}, u32[]{:S(2)}) %copy-start.1) | copy-done | bytes 11272216
  304.2 14.8 %collective-permute-done.30.refs_1_ = bf16[2,128,4096]{2,1,0:T(8,128)(2,1)S(1)} collective-permute-done((bf16[2,128,4096]{2,1,0:T(8,128)(2,1)S(1)}, bf16[2,128,4096]{2,1,0:T(8,128)(2,1)S(1)}, u32[]{:S(2)}, u32[]{:S(2)}) %collective-permute-start.30) | collective-permute-done | bytes 2097184 | tf_op jit(solution)/shard_map/ppermute | solution.py:608
  321.6 2.8 collective-permute-done.32.refs_2_
  324.3 3.0 collective-permute-done.33.refs_3_
  327.3 14.0 %kv_chunk.18 = (bf16[8,1025,4,128]{3,2,1,0:T(4,128)(2,1)}, bf16[8,1025,4,128]{3,2,1,0:T(4,128)(2,1)}, f32[14,8,3,8,128]{4,3,2,1,0:T(8,128)S(1)}) custom-call(bf16[2,128,4096]{2,1,0:T(8,128)(2,1)S(1)} %collective-permute-done.31.refs_0_, ...), custom_call_target="tpu_custom_call", output_to_operand_aliasing={{0}: (10, {}), {1}: (11, {}), {2}: (12, {})} | custom-call | flops 8589934592 | bytes 10485760 | tf_op jit(solution)/shard_map/kv_chunk/pallas_call | solution.py:441
  341.3 4.4 %collective-permute-done.34.refs_1_ = bf16[1,128,4096]{2,1,0:T(8,128)(2,1)S(1)} collective-permute-done((bf16[1,128,4096]{2,1,0:T(8,128)(2,1)S(1)}, bf16[1,128,4096]{2,1,0:T(8,128)(2,1)S(1)}, u32[]{:S(2)}, u32[]{:S(2)}) %collective-permute-start.34) | collective-permute-done | bytes 1048608 | tf_op jit(solution)/shard_map/ppermute | solution.py:608
  350.2 7.4 %kv_chunk.19 = (bf16[8,1025,4,128]{3,2,1,0:T(4,128)(2,1)}, bf16[8,1025,4,128]{3,2,1,0:T(4,128)(2,1)}, f32[14,8,3,8,128]{4,3,2,1,0:T(8,128)S(1)}) custom-call(bf16[1,128,4096]{2,1,0:T(8,128)(2,1)S(1)} %collective-permute-done.35.refs_0_, ...), custom_call_target="tpu_custom_call", output_to_operand_aliasing={{0}: (10, {}), {1}: (11, {}), {2}: (12, {})} | custom-call | flops 4294967296 | bytes 5242880 | tf_op jit(solution)/shard_map/kv_chunk/pallas_call | solution.py:441
  357.5 2.8 collective-permute-done.38.refs_1_
  364.2 3.6 kv_chunk.20
  367.8 8.1 %collective-permute-done.42.refs_1_ = bf16[1,64,4096]{2,1,0:T(8,128)(2,1)S(1)} collective-permute-done((bf16[1,64,4096]{2,1,0:T(8,128)(2,1)S(1)}, bf16[1,64,4096]{2,1,0:T(8,128)(2,1)S(1)}, u32[]{:S(2)}, u32[]{:S(2)}) %collective-permute-start.42) | collective-permute-done | bytes 524320 | tf_op jit(solution)/shard_map/ppermute | solution.py:608
  378.8 3.8 kv_chunk.21
  382.6 22.8 %tail.1 = bf16[2,8,4096]{2,1,0:T(8,128)(2,1)S(1)} custom-call(f32[14,8,3,8,128]{4,3,2,1,0:T(8,128)S(1)} %get-tuple-element.198.stv, f32[3,8,8,128]{3,2,1,0:T(8,128)S(1)} %get-tuple-element.199.self_ref, bf16[16,512]{1,0:T(8,128)(2,1)S(1)} %fusion.1.xs_ref, bf16[1,4096]{1,0:T(2,128)(2,1)S(1)} %copy-done.5, bf16[512,4096]{1,0:T(8,128)(2,1)S(1)} %get-tuple-element.201.wo, ...), custom_call_target="tpu_custom_call" | custom-call | tf_op jit(solution)/shard_map/tail/pallas_call | solution.py:573
  (110 shorter events, 39.8 us)
Async XLA Ops:
  15.9 36.4 %collective-permute-start = (bf16[8,128,4096]{2,1,0:T(8,128)(2,1)}, bf16[8,128,4096]{2,1,0:T(8,128)(2,1)}, u32[]{:S(2)}, u32[]{:S(2)}) collective-permute-start(bf16[8,128,4096]{2,1,0:T(8,128)(2,1)} %get-tuple-element.105.refs_0_.refs_1_), channel_id=1, source_target_pairs={{0,1},{1,0},{2,3},{3,2},{4,5},{5,4},{6,7},{7,6}} | collective-permute-start | bytes 25165832 | tf_op jit(solution)/shard_map/ppermute | solution.py:608
  21.5 9.5 %collective-permute-start.1 = (bf16[8,4096]{1,0:T(8,128)(2,1)S(1)}, bf16[8,4096]{1,0:T(8,128)(2,1)S(1)}, u32[]{:S(2)}, u32[]{:S(2)}) collective-permute-start(bf16[8,4096]{1,0:T(8,128)(2,1)S(1)} %bitcast.32), channel_id=1, source_target_pairs={{0,1},{1,0},{2,3},{3,2},{4,5},{5,4},{6,7},{7,6}} | collective-permute-start | bytes 196616 | tf_op jit(solution)/shard_map/ppermute | solution.py:608
  24.7 19.7 %copy-start.4 = (bf16[8,4096]{1,0:T(8,128)(2,1)S(1)}, bf16[8,4096]{1,0:T(8,128)(2,1)}, u32[]{:S(2)}) copy-start(bf16[8,4096]{1,0:T(8,128)(2,1)} %new_ref.1) | copy-start | bytes 196612
  24.7 55.5 %collective-permute-start.6 = (bf16[1,64,4096]{2,1,0:T(8,128)(2,1)}, bf16[1,64,4096]{2,1,0:T(8,128)(2,1)S(1)}, u32[]{:S(2)}, u32[]{:S(2)}) collective-permute-start(bf16[1,64,4096]{2,1,0:T(8,128)(2,1)} %get-tuple-element.121), channel_id=1, source_target_pairs={{0,4},{1,5},{2,6},{3,7},{4,0},{5,1},{6,2},{7,3}} | collective-permute-start | bytes 1572872 | tf_op jit(solution)/shard_map/ppermute | solution.py:608
  31.0 10.4 %collective-permute-start.3 = (bf16[8,2048]{1,0:T(8,128)(2,1)S(1)}, bf16[8,2048]{1,0:T(8,128)(2,1)S(1)}, u32[]{:S(2)}, u32[]{:S(2)}) collective-permute-start(bf16[8,2048]{1,0:T(8,128)(2,1)S(1)} %dynamic-slice_add_fusion), channel_id=1, source_target_pairs={{0,4},{1,5},{2,6},{3,7},{4,0},{5,1},{6,2},{7,3}} | collective-permute-start | bytes 98312 | tf_op jit(solution)/shard_map/ppermute | solution.py:608
  32.8 10.3 %collective-permute-start.2 = (bf16[8,2048]{1,0:T(8,128)(2,1)S(1)}, bf16[8,2048]{1,0:T(8,128)(2,1)S(1)}, u32[]{:S(2)}, u32[]{:S(2)}) collective-permute-start(bf16[8,2048]{1,0:T(8,128)(2,1)S(1)} %dynamic-slice_add_fusion), channel_id=1, source_target_pairs={{0,2},{1,3},{2,0},{3,1},{4,6},{5,7},{6,4},{7,5}} | collective-permute-start | bytes 98312 | tf_op jit(solution)/shard_map/ppermute | solution.py:608
  34.2 8.9 %collective-permute-start.4 = (bf16[8,2048]{1,0:T(8,128)(2,1)S(1)}, bf16[8,2048]{1,0:T(8,128)(2,1)S(1)}, u32[]{:S(2)}, u32[]{:S(2)}) collective-permute-start(bf16[8,2048]{1,0:T(8,128)(2,1)S(1)} %dynamic-slice_add_fusion), channel_id=1, source_target_pairs={{0,6},{1,7},{2,4},{3,5},{4,2},{5,3},{6,0},{7,1}} | collective-permute-start | bytes 98312 | tf_op jit(solution)/shard_map/ppermute | solution.py:608
  41.4 38.8 %collective-permute-start.7 = (bf16[1,64,4096]{2,1,0:T(8,128)(2,1)}, bf16[1,64,4096]{2,1,0:T(8,128)(2,1)S(1)}, u32[]{:S(2)}, u32[]{:S(2)}) collective-permute-start(bf16[1,64,4096]{2,1,0:T(8,128)(2,1)} %copy-done.12), channel_id=1, source_target_pairs={{0,2},{1,3},{2,0},{3,1},{4,6},{5,7},{6,4},{7,5}} | collective-permute-start | bytes 1572872 | tf_op jit(solution)/shard_map/ppermute | solution.py:608
  43.1 1.2 collective-permute-start.5
  80.2 4.3 %collective-permute-start.8 = (bf16[1,64,4096]{2,1,0:T(8,128)(2,1)S(1)}, bf16[1,64,4096]{2,1,0:T(8,128)(2,1)S(1)}, u32[]{:S(2)}, u32[]{:S(2)}) collective-permute-start(bf16[1,64,4096]{2,1,0:T(8,128)(2,1)S(1)} %collective-permute-done.6.refs_0_), channel_id=1, source_target_pairs={{0,1},{1,0},{2,3},{3,2},{4,5},{5,4},{6,7},{7,6}} | collective-permute-start | bytes 1572872 | tf_op jit(solution)/shard_map/ppermute | solution.py:608
  80.4 4.2 %collective-permute-start.9 = (bf16[1,64,4096]{2,1,0:T(8,128)(2,1)S(1)}, bf16[1,64,4096]{2,1,0:T(8,128)(2,1)S(1)}, u32[]{:S(2)}, u32[]{:S(2)}) collective-permute-start(bf16[1,64,4096]{2,1,0:T(8,128)(2,1)S(1)} %collective-permute-done.7.refs_1_), channel_id=1, source_target_pairs={{0,1},{1,0},{2,3},{3,2},{4,5},{5,4},{6,7},{7,6}} | collective-permute-start | bytes 1572872 | tf_op jit(solution)/shard_map/ppermute | solution.py:608
  82.5 14.0 %collective-permute-start.10 = (bf16[1,64,4096]{2,1,0:T(8,128)(2,1)S(1)}, bf16[1,64,4096]{2,1,0:T(8,128)(2,1)S(1)}, u32[]{:S(2)}, u32[]{:S(2)}) collective-permute-start(bf16[1,64,4096]{2,1,0:T(8,128)(2,1)S(1)} %get-tuple-element.129), channel_id=1, source_target_pairs={{0,4},{1,5},{2,6},{3,7},{4,0},{5,1},{6,2},{7,3}} | collective-permute-start | bytes 1572872 | tf_op jit(solution)/shard_map/ppermute | solution.py:608
  84.0 13.7 %collective-permute-start.11 = (bf16[1,64,4096]{2,1,0:T(8,128)(2,1)S(1)}, bf16[1,64,4096]{2,1,0:T(8,128)(2,1)S(1)}, u32[]{:S(2)}, u32[]{:S(2)}) collective-permute-start(bf16[1,64,4096]{2,1,0:T(8,128)(2,1)S(1)} %get-tuple-element.130), channel_id=1, source_target_pairs={{0,2},{1,3},{2,0},{3,1},{4,6},{5,7},{6,4},{7,5}} | collective-permute-start | bytes 1572872 | tf_op jit(solution)/shard_map/ppermute | solution.py:608
  84.6 15.7 %copy-start.7 = (bf16[2,128,4096]{2,1,0:T(8,128)(2,1)S(1)}, bf16[2,128,4096]{2,1,0:T(8,128)(2,1)}, u32[]{:S(2)}) copy-start(bf16[2,128,4096]{2,1,0:T(8,128)(2,1)} %copy-done.6) | copy-start | bytes 6291460
  97.7 2.6 collective-permute-start.12
  97.7 26.0 %collective-permute-start.14 = (bf16[1,128,4096]{2,1,0:T(8,128)(2,1)S(1)}, bf16[1,128,4096]{2,1,0:T(8,128)(2,1)S(1)}, u32[]{:S(2)}, u32[]{:S(2)}) collective-permute-start(bf16[1,128,4096]{2,1,0:T(8,128)(2,1)S(1)} %copy-done.11), channel_id=1, source_target_pairs={{0,4},{1,5},{2,6},{3,7},{4,0},{5,1},{6,2},{7,3}} | collective-permute-start | bytes 3145736 | tf_op jit(solution)/shard_map/ppermute | solution.py:608
  98.2 26.0 %collective-permute-start.15 = (bf16[1,128,4096]{2,1,0:T(8,128)(2,1)S(1)}, bf16[1,128,4096]{2,1,0:T(8,128)(2,1)S(1)}, u32[]{:S(2)}, u32[]{:S(2)}) collective-permute-start(bf16[1,128,4096]{2,1,0:T(8,128)(2,1)S(1)} %get-tuple-element.138), channel_id=1, source_target_pairs={{0,2},{1,3},{2,0},{3,1},{4,6},{5,7},{6,4},{7,5}} | collective-permute-start | bytes 3145736 | tf_op jit(solution)/shard_map/ppermute | solution.py:608
  98.6 3.2 collective-permute-start.13
  98.6 69.7 %collective-permute-start.18 = (bf16[2,128,4096]{2,1,0:T(8,128)(2,1)S(1)}, bf16[2,128,4096]{2,1,0:T(8,128)(2,1)S(1)}, u32[]{:S(2)}, u32[]{:S(2)}) collective-permute-start(bf16[2,128,4096]{2,1,0:T(8,128)(2,1)S(1)} %copy-done.9), channel_id=1, source_target_pairs={{0,4},{1,5},{2,6},{3,7},{4,0},{5,1},{6,2},{7,3}} | collective-permute-start | bytes 6291464 | tf_op jit(solution)/shard_map/ppermute | solution.py:608
  100.3 68.2 %collective-permute-start.19 = (bf16[2,128,4096]{2,1,0:T(8,128)(2,1)S(1)}, bf16[2,128,4096]{2,1,0:T(8,128)(2,1)S(1)}, u32[]{:S(2)}, u32[]{:S(2)}) collective-permute-start(bf16[2,128,4096]{2,1,0:T(8,128)(2,1)S(1)} %copy-done.7), channel_id=1, source_target_pairs={{0,2},{1,3},{2,0},{3,1},{4,6},{5,7},{6,4},{7,5}} | collective-permute-start | bytes 6291464 | tf_op jit(solution)/shard_map/ppermute | solution.py:608
  124.3 2.7 collective-permute-start.16
  124.3 4.2 %collective-permute-start.17 = (bf16[1,128,4096]{2,1,0:T(8,128)(2,1)S(1)}, bf16[1,128,4096]{2,1,0:T(8,128)(2,1)S(1)}, u32[]{:S(2)}, u32[]{:S(2)}) collective-permute-start(bf16[1,128,4096]{2,1,0:T(8,128)(2,1)S(1)} %collective-permute-done.15.refs_1_), channel_id=1, source_target_pairs={{0,1},{1,0},{2,3},{3,2},{4,5},{5,4},{6,7},{7,6}} | collective-permute-start | bytes 3145736 | tf_op jit(solution)/shard_map/ppermute | solution.py:608
  168.5 4.2 %collective-permute-start.20 = (bf16[2,128,4096]{2,1,0:T(8,128)(2,1)S(1)}, bf16[2,128,4096]{2,1,0:T(8,128)(2,1)S(1)}, u32[]{:S(2)}, u32[]{:S(2)}) collective-permute-start(bf16[2,128,4096]{2,1,0:T(8,128)(2,1)S(1)} %collective-permute-done.18.refs_0_), channel_id=1, source_target_pairs={{0,1},{1,0},{2,3},{3,2},{4,5},{5,4},{6,7},{7,6}} | collective-permute-start | bytes 6291464 | tf_op jit(solution)/shard_map/ppermute | solution.py:608
  168.5 7.2 %collective-permute-start.21 = (bf16[2,128,4096]{2,1,0:T(8,128)(2,1)S(1)}, bf16[2,128,4096]{2,1,0:T(8,128)(2,1)S(1)}, u32[]{:S(2)}, u32[]{:S(2)}) collective-permute-start(bf16[2,128,4096]{2,1,0:T(8,128)(2,1)S(1)} %collective-permute-done.19.refs_1_), channel_id=1, source_target_pairs={{0,1},{1,0},{2,3},{3,2},{4,5},{5,4},{6,7},{7,6}} | collective-permute-start | bytes 6291464 | tf_op jit(solution)/shard_map/ppermute | solution.py:608
  169.0 47.5 %collective-permute-start.23 = (bf16[2,128,4096]{2,1,0:T(8,128)(2,1)S(1)}, bf16[2,128,4096]{2,1,0:T(8,128)(2,1)S(1)}, u32[]{:S(2)}, u32[]{:S(2)}) collective-permute-start(bf16[2,128,4096]{2,1,0:T(8,128)(2,1)S(1)} %copy-done.9), channel_id=1, source_target_pairs={{0,2},{1,3},{2,0},{3,1},{4,6},{5,7},{6,4},{7,5}} | collective-permute-start | bytes 6291464 | tf_op jit(solution)/shard_map/ppermute | solution.py:608
  169.3 47.3 %collective-permute-start.22 = (bf16[2,128,4096]{2,1,0:T(8,128)(2,1)S(1)}, bf16[2,128,4096]{2,1,0:T(8,128)(2,1)S(1)}, u32[]{:S(2)}, u32[]{:S(2)}) collective-permute-start(bf16[2,128,4096]{2,1,0:T(8,128)(2,1)S(1)} %copy-done.7), channel_id=1, source_target_pairs={{0,4},{1,5},{2,6},{3,7},{4,0},{5,1},{6,2},{7,3}} | collective-permute-start | bytes 6291464 | tf_op jit(solution)/shard_map/ppermute | solution.py:608
  216.6 8.4 %collective-permute-start.24 = (bf16[2,128,4096]{2,1,0:T(8,128)(2,1)S(1)}, bf16[2,128,4096]{2,1,0:T(8,128)(2,1)S(1)}, u32[]{:S(2)}, u32[]{:S(2)}) collective-permute-start(bf16[2,128,4096]{2,1,0:T(8,128)(2,1)S(1)} %collective-permute-done.22.refs_0_), channel_id=1, source_target_pairs={{0,1},{1,0},{2,3},{3,2},{4,5},{5,4},{6,7},{7,6}} | collective-permute-start | bytes 6291464 | tf_op jit(solution)/shard_map/ppermute | solution.py:608
  216.6 8.4 %collective-permute-start.25 = (bf16[2,128,4096]{2,1,0:T(8,128)(2,1)S(1)}, bf16[2,128,4096]{2,1,0:T(8,128)(2,1)S(1)}, u32[]{:S(2)}, u32[]{:S(2)}) collective-permute-start(bf16[2,128,4096]{2,1,0:T(8,128)(2,1)S(1)} %collective-permute-done.23.refs_1_), channel_id=1, source_target_pairs={{0,1},{1,0},{2,3},{3,2},{4,5},{5,4},{6,7},{7,6}} | collective-permute-start | bytes 6291464 | tf_op jit(solution)/shard_map/ppermute | solution.py:608
  221.7 47.7 %collective-permute-start.27 = (bf16[2,128,4096]{2,1,0:T(8,128)(2,1)}, bf16[2,128,4096]{2,1,0:T(8,128)(2,1)S(1)}, u32[]{:S(2)}, u32[]{:S(2)}) collective-permute-start(bf16[2,128,4096]{2,1,0:T(8,128)(2,1)} %get-tuple-element.206), channel_id=1, source_target_pairs={{0,2},{1,3},{2,0},{3,1},{4,6},{5,7},{6,4},{7,5}} | collective-permute-start | bytes 6291464 | tf_op jit(solution)/shard_map/ppermute | solution.py:608
  223.4 47.5 %collective-permute-start.26 = (bf16[2,128,4096]{2,1,0:T(8,128)(2,1)}, bf16[2,128,4096]{2,1,0:T(8,128)(2,1)S(1)}, u32[]{:S(2)}, u32[]{:S(2)}) collective-permute-start(bf16[2,128,4096]{2,1,0:T(8,128)(2,1)} %get-tuple-element.207), channel_id=1, source_target_pairs={{0,4},{1,5},{2,6},{3,7},{4,0},{5,1},{6,2},{7,3}} | collective-permute-start | bytes 6291464 | tf_op jit(solution)/shard_map/ppermute | solution.py:608
  270.9 4.2 %collective-permute-start.28 = (bf16[2,128,4096]{2,1,0:T(8,128)(2,1)S(1)}, bf16[2,128,4096]{2,1,0:T(8,128)(2,1)S(1)}, u32[]{:S(2)}, u32[]{:S(2)}) collective-permute-start(bf16[2,128,4096]{2,1,0:T(8,128)(2,1)S(1)} %collective-permute-done.26.refs_0_), channel_id=1, source_target_pairs={{0,1},{1,0},{2,3},{3,2},{4,5},{5,4},{6,7},{7,6}} | collective-permute-start | bytes 6291464 | tf_op jit(solution)/shard_map/ppermute | solution.py:608
  270.9 7.2 %collective-permute-start.29 = (bf16[2,128,4096]{2,1,0:T(8,128)(2,1)S(1)}, bf16[2,128,4096]{2,1,0:T(8,128)(2,1)S(1)}, u32[]{:S(2)}, u32[]{:S(2)}) collective-permute-start(bf16[2,128,4096]{2,1,0:T(8,128)(2,1)S(1)} %collective-permute-done.27.refs_1_), channel_id=1, source_target_pairs={{0,1},{1,0},{2,3},{3,2},{4,5},{5,4},{6,7},{7,6}} | collective-permute-start | bytes 6291464 | tf_op jit(solution)/shard_map/ppermute | solution.py:608
  271.4 47.5 %collective-permute-start.30 = (bf16[2,128,4096]{2,1,0:T(8,128)(2,1)S(1)}, bf16[2,128,4096]{2,1,0:T(8,128)(2,1)S(1)}, u32[]{:S(2)}, u32[]{:S(2)}) collective-permute-start(bf16[2,128,4096]{2,1,0:T(8,128)(2,1)S(1)} %collective-permute-done.19.refs_1_), channel_id=1, source_target_pairs={{0,4},{1,5},{2,6},{3,7},{4,0},{5,1},{6,2},{7,3}} | collective-permute-start | bytes 6291464 | tf_op jit(solution)/shard_map/ppermute | solution.py:608
  272.9 47.3 %collective-permute-start.31 = (bf16[2,128,4096]{2,1,0:T(8,128)(2,1)S(1)}, bf16[2,128,4096]{2,1,0:T(8,128)(2,1)S(1)}, u32[]{:S(2)}, u32[]{:S(2)}) collective-permute-start(bf16[2,128,4096]{2,1,0:T(8,128)(2,1)S(1)} %collective-permute-done.18.refs_0_), channel_id=1, source_target_pairs={{0,2},{1,3},{2,0},{3,1},{4,6},{5,7},{6,4},{7,5}} | collective-permute-start | bytes 6291464 | tf_op jit(solution)/shard_map/ppermute | solution.py:608
  320.2 4.2 %collective-permute-start.32 = (bf16[2,128,4096]{2,1,0:T(8,128)(2,1)S(1)}, bf16[2,128,4096]{2,1,0:T(8,128)(2,1)S(1)}, u32[]{:S(2)}, u32[]{:S(2)}) collective-permute-start(bf16[2,128,4096]{2,1,0:T(8,128)(2,1)S(1)} %collective-permute-done.31.refs_0_), channel_id=1, source_target_pairs={{0,1},{1,0},{2,3},{3,2},{4,5},{5,4},{6,7},{7,6}} | collective-permute-start | bytes 6291464 | tf_op jit(solution)/shard_map/ppermute | solution.py:608
  320.2 7.2 %collective-permute-start.33 = (bf16[2,128,4096]{2,1,0:T(8,128)(2,1)S(1)}, bf16[2,128,4096]{2,1,0:T(8,128)(2,1)S(1)}, u32[]{:S(2)}, u32[]{:S(2)}) collective-permute-start(bf16[2,128,4096]{2,1,0:T(8,128)(2,1)S(1)} %collective-permute-done.30.refs_1_), channel_id=1, source_target_pairs={{0,1},{1,0},{2,3},{3,2},{4,5},{5,4},{6,7},{7,6}} | collective-permute-start | bytes 6291464 | tf_op jit(solution)/shard_map/ppermute | solution.py:608
  320.7 25.1 %collective-permute-start.34 = (bf16[1,128,4096]{2,1,0:T(8,128)(2,1)S(1)}, bf16[1,128,4096]{2,1,0:T(8,128)(2,1)S(1)}, u32[]{:S(2)}, u32[]{:S(2)}) collective-permute-start(bf16[1,128,4096]{2,1,0:T(8,128)(2,1)S(1)} %collective-permute-done.15.refs_1_), channel_id=1, source_target_pairs={{0,4},{1,5},{2,6},{3,7},{4,0},{5,1},{6,2},{7,3}} | collective-permute-start | bytes 3145736 | tf_op jit(solution)/shard_map/ppermute | solution.py:608
  321.2 24.8 %collective-permute-start.35 = (bf16[1,128,4096]{2,1,0:T(8,128)(2,1)S(1)}, bf16[1,128,4096]{2,1,0:T(8,128)(2,1)S(1)}, u32[]{:S(2)}, u32[]{:S(2)}) collective-permute-start(bf16[1,128,4096]{2,1,0:T(8,128)(2,1)S(1)} %collective-permute-done.14.refs_0_), channel_id=1, source_target_pairs={{0,2},{1,3},{2,0},{3,1},{4,6},{5,7},{6,4},{7,5}} | collective-permute-start | bytes 3145736 | tf_op jit(solution)/shard_map/ppermute | solution.py:608
  346.0 2.7 collective-permute-start.36
  346.0 4.2 %collective-permute-start.37 = (bf16[1,128,4096]{2,1,0:T(8,128)(2,1)S(1)}, bf16[1,128,4096]{2,1,0:T(8,128)(2,1)S(1)}, u32[]{:S(2)}, u32[]{:S(2)}) collective-permute-start(bf16[1,128,4096]{2,1,0:T(8,128)(2,1)S(1)} %collective-permute-done.34.refs_1_), channel_id=1, source_target_pairs={{0,1},{1,0},{2,3},{3,2},{4,5},{5,4},{6,7},{7,6}} | collective-permute-start | bytes 3145736 | tf_op jit(solution)/shard_map/ppermute | solution.py:608
  346.5 13.8 %collective-permute-start.38 = (bf16[1,64,4096]{2,1,0:T(8,128)(2,1)S(1)}, bf16[1,64,4096]{2,1,0:T(8,128)(2,1)S(1)}, u32[]{:S(2)}, u32[]{:S(2)}) collective-permute-start(bf16[1,64,4096]{2,1,0:T(8,128)(2,1)S(1)} %collective-permute-done.7.refs_1_), channel_id=1, source_target_pairs={{0,4},{1,5},{2,6},{3,7},{4,0},{5,1},{6,2},{7,3}} | collective-permute-start | bytes 1572872 | tf_op jit(solution)/shard_map/ppermute | solution.py:608
  348.0 13.6 %collective-permute-start.39 = (bf16[1,64,4096]{2,1,0:T(8,128)(2,1)S(1)}, bf16[1,64,4096]{2,1,0:T(8,128)(2,1)S(1)}, u32[]{:S(2)}, u32[]{:S(2)}) collective-permute-start(bf16[1,64,4096]{2,1,0:T(8,128)(2,1)S(1)} %collective-permute-done.6.refs_0_), channel_id=1, source_target_pairs={{0,2},{1,3},{2,0},{3,1},{4,6},{5,7},{6,4},{7,5}} | collective-permute-start | bytes 1572872 | tf_op jit(solution)/shard_map/ppermute | solution.py:608
  361.6 1.9 collective-permute-start.40
  361.6 2.7 collective-permute-start.41
  362.1 13.8 %collective-permute-start.42 = (bf16[1,64,4096]{2,1,0:T(8,128)(2,1)S(1)}, bf16[1,64,4096]{2,1,0:T(8,128)(2,1)S(1)}, u32[]{:S(2)}, u32[]{:S(2)}) collective-permute-start(bf16[1,64,4096]{2,1,0:T(8,128)(2,1)S(1)} %collective-permute-done.11.refs_1_), channel_id=1, source_target_pairs={{0,4},{1,5},{2,6},{3,7},{4,0},{5,1},{6,2},{7,3}} | collective-permute-start | bytes 1572872 | tf_op jit(solution)/shard_map/ppermute | solution.py:608
  362.6 13.6 %collective-permute-start.43 = (bf16[1,64,4096]{2,1,0:T(8,128)(2,1)S(1)}, bf16[1,64,4096]{2,1,0:T(8,128)(2,1)S(1)}, u32[]{:S(2)}, u32[]{:S(2)}) collective-permute-start(bf16[1,64,4096]{2,1,0:T(8,128)(2,1)S(1)} %collective-permute-done.10.refs_0_), channel_id=1, source_target_pairs={{0,2},{1,3},{2,0},{3,1},{4,6},{5,7},{6,4},{7,5}} | collective-permute-start | bytes 1572872 | tf_op jit(solution)/shard_map/ppermute | solution.py:608
  376.1 1.9 collective-permute-start.44
  376.1 2.7 collective-permute-start.45
  (12 other events, 64.7 us)

commit v9 on v8

--- a/solution.py
+++ b/solution.py
@@ -125,17 +125,21 @@
     out_refs = refs[:n]
     x_buf, gain_ref, sem = refs[n:]
     d_model = x_hbm.shape[2]
-    loads = [pltpu.make_async_copy(x_hbm.at[bat, pl.ds(row0, rows)], x_buf.at[i], sem.at[i]) for i, (bat, row0) in enumerate(places)]
-    loads.append(pltpu.make_async_copy(gain_hbm, gain_ref, sem.at[n]))
-    for load in loads:
-        load.start()
-    loads[n].wait()
+    pieces = rows // NORM_ROWS
+    gain_load = pltpu.make_async_copy(gain_hbm, gain_ref, sem.at[n * pieces])
+    gain_load.start()
+    loads = {}
+    for k in range(pieces):
+        for i, (bat, row0) in enumerate(places):
+            loads[k, i] = pltpu.make_async_copy(x_hbm.at[bat, pl.ds(row0 + k * NORM_ROWS, NORM_ROWS)],
+                                                x_buf.at[i, pl.ds(k * NORM_ROWS, NORM_ROWS)], sem.at[k * n + i])
+            loads[k, i].start()
+    gain_load.wait()
     lanes = [slice(c * HEAD_DIM, (c + 1) * HEAD_DIM) for c in range(d_model // HEAD_DIM)]
-    for i in range(n):
-        loads[i].wait()
-
-        def norm_rows(r, carry):
-            at = pl.ds(pl.multiple_of(r * NORM_ROWS, NORM_ROWS), NORM_ROWS)
+    for k in range(pieces):
+        at = slice(k * NORM_ROWS, (k + 1) * NORM_ROWS)
+        for i in range(n):
+            loads[k, i].wait()
             acc = [jnp.zeros((NORM_ROWS, HEAD_DIM), jnp.float32) for _ in range(2)]
             for c, lane in enumerate(lanes):
                 xf = x_buf[i, at, lane].astype(jnp.float32)
@@ -144,9 +148,6 @@
             for lane in lanes:
                 xf = x_buf[i, at, lane].astype(jnp.float32)
                 out_refs[i][0, at, lane] = (xf * inv_rms * gain_ref[:, lane].astype(jnp.float32)).astype(jnp.bfloat16)
-            return carry
-
-        lax.fori_loop(0, rows // NORM_ROWS, norm_rows, 0)
 
 
 def first_call(x, gain, places, rows):
@@ -159,7 +160,7 @@
         scratch_shapes=[
             pltpu.VMEM((len(places), rows, d_model), jnp.bfloat16),
             pltpu.VMEM(gain.shape, gain.dtype),
-            pltpu.SemaphoreType.DMA((len(places) + 1,)),
+            pltpu.SemaphoreType.DMA((len(places) * rows // NORM_ROWS + 1,)),
         ],
         compiler_params=pltpu.CompilerParams(vmem_limit_bytes=8 * 2 ** 20),
         cost_estimate=pl.CostEstimate(flops=len(places) * rows * d_model * 8, bytes_accessed=len(places) * rows * d_model * 4, transcendentals=0),
@@ -471,14 +472,14 @@
     cols = d_model // n_dev
     heads = STAT_ROWS // 2
     loads = [pltpu.make_async_copy(src, dst, w_sem.at[i]) for i, (src, dst) in enumerate(((wg_hbm, wg), (wu_hbm, wu), (wd_hbm, wd)))]
-    for load in loads:
-        load.start()
+    loads[0].start()
+    loads[1].start()
     barrier = pltpu.get_barrier_semaphore()
 
     def peer_of(mask):
         return sum(lax.rem(me // bit + mask // bit, 2) * bit for bit in (1, 2, 4))
 
-    far_first = ((6, 7), (2, 3, 4, 5), (1,))
+    far_first = ((6,), (7, 2), (4, 5, 3), (1,))
     for mask in sum(far_first, ()):
         pl.semaphore_signal(barrier, inc=1, device_id={"model": peer_of(mask)}, device_id_type=MESH)
 
@@ -515,6 +516,8 @@
         for mask in sum(far_first, ()):
             outs.append(send(phase + 1, mask, xo, xg.at[me]))
             outs[-1].start()
+        if phase == 0:
+            loads[2].start()
         for out in outs:
             out.wait_recv()
         return [copy for copy, _ in copies] + outs
@@ -698,6 +701,8 @@
             caches, (via_y,) = after(caches, diag[step][1])
             caches, (via_x,) = after(caches, diag[step][0])
             other_y = swap(via_y, 1)
+            if step == "0b":
+                via_x, other_y = lax.optimization_barrier((via_x, other_y))
             other_x = swap(via_x, 1)
             start = starts[step]
             streams = [[(via_x, 0), (via_y, 0)], [(other_x, 0), (other_y, 0)]]

time: 407 us -> 407 us (level)
  no operation moved by 1% of the time
where the time goes in v9:
time: 407 us; the launch traced here: 406 us
  Pallas kernels  174 us (43%)
  waiting for transfers between devices  172 us (42%)
  starting transfers between devices  30.5 us (7%)
  local copies, waits for them, and re-layouts  19.1 us (5%)
  other arithmetic  5.18 us (1%)
  matrix products  4.57 us (1%)
    ppermute x46, waiting for transfers between devices, swap(): return lax.ppermute(arr, 'model', [(i, i ^ bit) for i in range(n_dev)])  172 us
    pallas_call x11, Pallas kernels, kv_call(): pl.pallas_call(functools.partial(kv_kernel, n_in, n_steps, masks, batches...  113 us
    ppermute x46, starting transfers between devices, swap(): return lax.ppermute(arr, 'model', [(i, i ^ bit) for i in range(n_dev)])  30.5 us
    pallas_call x1, Pallas kernels, tail_call(): pl.pallas_call(functools.partial(tail_kernel, n_dev, parts_of), out_shape...  22.1 us
    pallas_call x2, Pallas kernels, turn_call(): pl.pallas_call(turn_kernel, grid=(d // cols,), in_specs=[pl.BlockSpec((n,...  15.8 us
    unnamed x28, local copies, waits for them, and re-layouts  13.6 us
    pallas_call x1, Pallas kernels, norm_call(): pl.pallas_call(functools.partial(norm_kernel, outs_of), grid=(len(order),...  10.8 us
  transfers between devices with their start and end apart: 46, of which 34 were waited for; matrix products, arithmetic and copies ran while one was open for 4% of the time, Pallas kernels for 34%

profile of v9, /device:TPU:0, one launch (start us, length us, event | category | flops | bytes accessed | tf_op | source)
XLA Modules:
  0.0 406.2 jit_solution(9672008167524574335)
XLA Ops:
  1.4 10.8 %norm_rows.1 = (bf16[1,128,4096]{2,1,0:T(8,128)(2,1)S(1)}, bf16[1,128,4096]{2,1,0:T(8,128)(2,1)S(1)}, bf16[2,128,4096]{2,1,0:T(8,128)(2,1)S(1)}, bf16[2,128,4096]{2,1,0:T(8,128)(2,1)S(1)}, bf16[8,128,4096]{2,1,0:T(8,128)(2,1)}) custom-call(bf16[8,128,4096]{2,1,0:T(8,128)(2,1)} %x_hbm.3, bf16[1,4096]{1,0:T(2,128)(2,1)S(1)} %copy-done.2), custom_call_target="tpu_custom_call" | custom-call | flops 33554432 | bytes 25165824 | tf_op jit(solution)/shard_map/norm_rows/pallas_call | solution.py:181
  16.8 4.6 %fusion.2 = bf16[8,1,4096]{2,1,0:T(2,128)(2,1)S(1)} fusion(bf16[8,128,4096]{2,1,0:T(8,128)(2,1)} %x_hbm.3, pred[8,128,1]{1,0,2:T(8,128)(4,1)S(1)} %compare_bitcast_fusion), kind=kOutput, calls=%fused_computation.14 | convolution fusion | flops 8388608 | bytes 8455168 | tf_op jit(solution)/shard_map/bs,bsd->bd/dot_general | solution.py:646
  21.5 2.3 first_rows.2
  24.6 3.0 collective-permute-start.6
  27.7 3.0 fusion
  30.9 1.9 collective-permute-start.3
  34.4 1.7 pad_maximum_fusion
  36.1 5.2 %collective-permute-done.3 = bf16[8,2048]{1,0:T(8,128)(2,1)S(1)} collective-permute-done((bf16[8,2048]{1,0:T(8,128)(2,1)S(1)}, bf16[8,2048]{1,0:T(8,128)(2,1)S(1)}, u32[]{:S(2)}, u32[]{:S(2)}) %collective-permute-start.3) | collective-permute-done | bytes 32800 | tf_op jit(solution)/shard_map/ppermute | solution.py:611
  41.3 1.7 collective-permute-start.7
  44.4 4.7 %keep.1 = (bf16[4096,512]{1,0:T(8,128)(2,1)S(1)}, bf16[4096,512]{1,0:T(8,128)(2,1)S(1)}, bf16[512,4096]{1,0:T(8,128)(2,1)S(1)}) custom-call(bf16[4096,512]{1,0:T(8,128)(2,1)} %bitcast.28, bf16[4096,512]{1,0:T(8,128)(2,1)} %bitcast.29, bf16[512,4096]{1,0:T(8,128)(2,1)} %bitcast.30), custom_call_target="tpu_custom_call" | custom-call | tf_op jit(solution)/shard_map/keep/pallas_call | solution.py:39
  49.1 3.1 query_rows.1
  52.2 27.9 %kv_chunk.11 = (bf16[8,1025,4,128]{3,2,1,0:T(4,128)(2,1)}, bf16[8,1025,4,128]{3,2,1,0:T(4,128)(2,1)}, f32[14,8,3,8,128]{4,3,2,1,0:T(8,128)S(1)}) custom-call(bf16[8,128,4096]{2,1,0:T(8,128)(2,1)} %get-tuple-element.107.refs_0_.refs_1_, bf16[8,128,4096]{2,1,0:T(8,128)(2,1)} %get-tuple-element.107.refs_0_.refs_1_, ...), custom_call_target="tpu_custom_call" | custom-call | flops 17179869184 | bytes 20971520 | tf_op jit(solution)/shard_map/kv_chunk/pallas_call | solution.py:442
  80.7 1.7 first_rows.3
  84.5 3.6 kv_chunk.12
  88.0 8.3 %collective-permute-done.10.refs_0_ = bf16[1,64,4096]{2,1,0:T(8,128)(2,1)S(1)} collective-permute-done((bf16[1,64,4096]{2,1,0:T(8,128)(2,1)S(1)}, bf16[1,64,4096]{2,1,0:T(8,128)(2,1)S(1)}, u32[]{:S(2)}, u32[]{:S(2)}) %collective-permute-start.10) | collective-permute-done | bytes 524320 | tf_op jit(solution)/shard_map/ppermute | solution.py:611
  98.5 1.7 collective-permute-start.18
  101.7 3.5 kv_chunk.13
  105.2 18.4 %collective-permute-done.14.refs_0_ = bf16[1,128,4096]{2,1,0:T(8,128)(2,1)S(1)} collective-permute-done((bf16[1,128,4096]{2,1,0:T(8,128)(2,1)S(1)}, bf16[1,128,4096]{2,1,0:T(8,128)(2,1)S(1)}, u32[]{:S(2)}, u32[]{:S(2)}) %collective-permute-start.14) | collective-permute-done | bytes 1048608 | tf_op jit(solution)/shard_map/ppermute | solution.py:611
  124.7 2.1 collective-permute-done.16.refs_2_
  128.3 7.4 %kv_chunk.14 = (bf16[8,1025,4,128]{3,2,1,0:T(4,128)(2,1)}, bf16[8,1025,4,128]{3,2,1,0:T(4,128)(2,1)}, f32[14,8,3,8,128]{4,3,2,1,0:T(8,128)S(1)}) custom-call(bf16[1,128,4096]{2,1,0:T(8,128)(2,1)S(1)} %collective-permute-done.14.refs_0_, ...), custom_call_target="tpu_custom_call", output_to_operand_aliasing={{0}: (10, {}), {1}: (11, {}), {2}: (12, {})} | custom-call | flops 4294967296 | bytes 5242880 | tf_op jit(solution)/shard_map/kv_chunk/pallas_call | solution.py:442
  135.7 32.4 %collective-permute-done.18.refs_0_ = bf16[2,128,4096]{2,1,0:T(8,128)(2,1)S(1)} collective-permute-done((bf16[2,128,4096]{2,1,0:T(8,128)(2,1)S(1)}, bf16[2,128,4096]{2,1,0:T(8,128)(2,1)S(1)}, u32[]{:S(2)}, u32[]{:S(2)}) %collective-permute-start.18) | collective-permute-done | bytes 2097184 | tf_op jit(solution)/shard_map/ppermute | solution.py:611
  169.2 1.7 collective-permute-start.22
  172.5 3.0 collective-permute-done.21.refs_3_
  175.5 14.0 %kv_chunk.15 = (bf16[8,1025,4,128]{3,2,1,0:T(4,128)(2,1)}, bf16[8,1025,4,128]{3,2,1,0:T(4,128)(2,1)}, f32[14,8,3,8,128]{4,3,2,1,0:T(8,128)S(1)}) custom-call(bf16[2,128,4096]{2,1,0:T(8,128)(2,1)S(1)} %collective-permute-done.18.refs_0_, ...), custom_call_target="tpu_custom_call", output_to_operand_aliasing={{0}: (10, {}), {1}: (11, {}), {2}: (12, {})} | custom-call | flops 8589934592 | bytes 10485760 | tf_op jit(solution)/shard_map/kv_chunk/pallas_call | solution.py:442
  189.5 26.9 %collective-permute-done.23.refs_1_ = bf16[2,128,4096]{2,1,0:T(8,128)(2,1)S(1)} collective-permute-done((bf16[2,128,4096]{2,1,0:T(8,128)(2,1)S(1)}, bf16[2,128,4096]{2,1,0:T(8,128)(2,1)S(1)}, u32[]{:S(2)}, u32[]{:S(2)}) %collective-permute-start.23) | collective-permute-done | bytes 2097184 | tf_op jit(solution)/shard_map/ppermute | solution.py:611
  217.0 4.7 %fusion.5 = (bf16[2,128,4096]{2,1,0:T(8,128)(2,1)}, bf16[2,128,4096]{2,1,0:T(8,128)(2,1)}) fusion(bf16[8,128,4096]{2,1,0:T(8,128)(2,1)} %get-tuple-element.107.refs_0_.refs_1_), kind=kLoop, calls=%fused_computation.27 | loop fusion | bytes 8388608 | tf_op jit(solution)/shard_map/slice | solution.py:655
  221.6 1.7 collective-permute-start.27
  224.8 14.0 %kv_chunk.16 = (bf16[8,1025,4,128]{3,2,1,0:T(4,128)(2,1)}, bf16[8,1025,4,128]{3,2,1,0:T(4,128)(2,1)}, f32[14,8,3,8,128]{4,3,2,1,0:T(8,128)S(1)}) custom-call(bf16[2,128,4096]{2,1,0:T(8,128)(2,1)S(1)} %collective-permute-done.22.refs_0_, ...), custom_call_target="tpu_custom_call", output_to_operand_aliasing={{0}: (10, {}), {1}: (11, {}), {2}: (12, {})} | custom-call | flops 8589934592 | bytes 10485760 | tf_op jit(solution)/shard_map/kv_chunk/pallas_call | solution.py:442
  238.8 7.9 %turn.2.wg_hbm = bf16[4096,1376]{1,0:T(8,128)(2,1)S(1)} custom-call(bf16[1376,4096]{1,0:T(8,128)(2,1)} %bitcast.25), custom_call_target="tpu_custom_call" | custom-call | flops 1442840576 | bytes 22544384 | tf_op jit(solution)/shard_map/turn/pallas_call | solution.py:57
  246.8 4.2 %copy-done = bf16[4096,1376]{1,0:T(8,128)(2,1)} copy-done((bf16[4096,1376]{1,0:T(8,128)(2,1)}, bf16[4096,1376]{1,0:T(8,128)(2,1)S(1)}, u32[]{:S(2)}) %copy-start) | copy-done | bytes 11272216
  251.0 18.4 %collective-permute-done.27.refs_1_ = bf16[2,128,4096]{2,1,0:T(8,128)(2,1)S(1)} collective-permute-done((bf16[2,128,4096]{2,1,0:T(8,128)(2,1)}, bf16[2,128,4096]{2,1,0:T(8,128)(2,1)S(1)}, u32[]{:S(2)}, u32[]{:S(2)}) %collective-permute-start.27) | collective-permute-done | bytes 2097184 | tf_op jit(solution)/shard_map/ppermute | solution.py:611
  274.9 3.0 collective-permute-done.29.refs_3_
  277.9 14.0 %kv_chunk.17 = (bf16[8,1025,4,128]{3,2,1,0:T(4,128)(2,1)}, bf16[8,1025,4,128]{3,2,1,0:T(4,128)(2,1)}, f32[14,8,3,8,128]{4,3,2,1,0:T(8,128)S(1)}) custom-call(bf16[2,128,4096]{2,1,0:T(8,128)(2,1)S(1)} %collective-permute-done.26.refs_0_, ...), custom_call_target="tpu_custom_call", output_to_operand_aliasing={{0}: (10, {}), {1}: (11, {}), {2}: (12, {})} | custom-call | flops 8589934592 | bytes 10485760 | tf_op jit(solution)/shard_map/kv_chunk/pallas_call | solution.py:442
  292.0 7.9 %turn.3.wu_hbm = bf16[4096,1376]{1,0:T(8,128)(2,1)S(1)} custom-call(bf16[1376,4096]{1,0:T(8,128)(2,1)} %bitcast.26), custom_call_target="tpu_custom_call" | custom-call | flops 1442840576 | bytes 22544384 | tf_op jit(solution)/shard_map/turn/pallas_call | solution.py:57
  299.9 4.2 %copy-done.1 = bf16[4096,1376]{1,0:T(8,128)(2,1)} copy-done((bf16[4096,1376]{1,0:T(8,128)(2,1)}, bf16[4096,1376]{1,0:T(8,128)(2,1)S(1)}, u32[]{:S(2)}) %copy-start.1) | copy-done | bytes 11272216
  304.1 14.8 %collective-permute-done.30.refs_1_ = bf16[2,128,4096]{2,1,0:T(8,128)(2,1)S(1)} collective-permute-done((bf16[2,128,4096]{2,1,0:T(8,128)(2,1)S(1)}, bf16[2,128,4096]{2,1,0:T(8,128)(2,1)S(1)}, u32[]{:S(2)}, u32[]{:S(2)}) %collective-permute-start.30) | collective-permute-done | bytes 2097184 | tf_op jit(solution)/shard_map/ppermute | solution.py:611
  321.4 2.8 collective-permute-done.32.refs_2_
  324.2 3.0 collective-permute-done.33.refs_3_
  327.2 14.0 %kv_chunk.18 = (bf16[8,1025,4,128]{3,2,1,0:T(4,128)(2,1)}, bf16[8,1025,4,128]{3,2,1,0:T(4,128)(2,1)}, f32[14,8,3,8,128]{4,3,2,1,0:T(8,128)S(1)}) custom-call(bf16[2,128,4096]{2,1,0:T(8,128)(2,1)S(1)} %collective-permute-done.31.refs_0_, ...), custom_call_target="tpu_custom_call", output_to_operand_aliasing={{0}: (10, {}), {1}: (11, {}), {2}: (12, {})} | custom-call | flops 8589934592 | bytes 10485760 | tf_op jit(solution)/shard_map/kv_chunk/pallas_call | solution.py:442
  341.2 4.4 %collective-permute-done.34.refs_1_ = bf16[1,128,4096]{2,1,0:T(8,128)(2,1)S(1)} collective-permute-done((bf16[1,128,4096]{2,1,0:T(8,128)(2,1)S(1)}, bf16[1,128,4096]{2,1,0:T(8,128)(2,1)S(1)}, u32[]{:S(2)}, u32[]{:S(2)}) %collective-permute-start.34) | collective-permute-done | bytes 1048608 | tf_op jit(solution)/shard_map/ppermute | solution.py:611
  350.0 7.4 %kv_chunk.19 = (bf16[8,1025,4,128]{3,2,1,0:T(4,128)(2,1)}, bf16[8,1025,4,128]{3,2,1,0:T(4,128)(2,1)}, f32[14,8,3,8,128]{4,3,2,1,0:T(8,128)S(1)}) custom-call(bf16[1,128,4096]{2,1,0:T(8,128)(2,1)S(1)} %collective-permute-done.35.refs_0_, ...), custom_call_target="tpu_custom_call", output_to_operand_aliasing={{0}: (10, {}), {1}: (11, {}), {2}: (12, {})} | custom-call | flops 4294967296 | bytes 5242880 | tf_op jit(solution)/shard_map/kv_chunk/pallas_call | solution.py:442
  357.4 2.8 collective-permute-done.38.refs_1_
  364.1 3.6 kv_chunk.20
  367.7 8.1 %collective-permute-done.42.refs_1_ = bf16[1,64,4096]{2,1,0:T(8,128)(2,1)S(1)} collective-permute-done((bf16[1,64,4096]{2,1,0:T(8,128)(2,1)S(1)}, bf16[1,64,4096]{2,1,0:T(8,128)(2,1)S(1)}, u32[]{:S(2)}, u32[]{:S(2)}) %collective-permute-start.42) | collective-permute-done | bytes 524320 | tf_op jit(solution)/shard_map/ppermute | solution.py:611
  376.0 1.7 collective-permute-done.44.refs_3_
  377.9 1.8 collective-permute-done.45.refs_2_
  379.6 3.8 kv_chunk.21
  383.4 22.1 %tail.1 = bf16[2,8,4096]{2,1,0:T(8,128)(2,1)S(1)} custom-call(f32[14,8,3,8,128]{4,3,2,1,0:T(8,128)S(1)} %get-tuple-element.202.stv, f32[3,8,8,128]{3,2,1,0:T(8,128)S(1)} %get-tuple-element.203.self_ref, bf16[16,512]{1,0:T(8,128)(2,1)S(1)} %fusion.1.xs_ref, bf16[1,4096]{1,0:T(2,128)(2,1)S(1)} %copy-done.5, bf16[512,4096]{1,0:T(8,128)(2,1)S(1)} %get-tuple-element.205.wo, ...), custom_call_target="tpu_custom_call" | custom-call | tf_op jit(solution)/shard_map/tail/pallas_call | solution.py:576
  (110 shorter events, 40.4 us)
Async XLA Ops:
  15.9 36.3 %collective-permute-start = (bf16[8,128,4096]{2,1,0:T(8,128)(2,1)}, bf16[8,128,4096]{2,1,0:T(8,128)(2,1)}, u32[]{:S(2)}, u32[]{:S(2)}) collective-permute-start(bf16[8,128,4096]{2,1,0:T(8,128)(2,1)} %get-tuple-element.107.refs_0_.refs_1_), channel_id=1, source_target_pairs={{0,1},{1,0},{2,3},{3,2},{4,5},{5,4},{6,7},{7,6}} | collective-permute-start | bytes 25165832 | tf_op jit(solution)/shard_map/ppermute | solution.py:611
  21.5 9.4 %collective-permute-start.1 = (bf16[8,4096]{1,0:T(8,128)(2,1)S(1)}, bf16[8,4096]{1,0:T(8,128)(2,1)S(1)}, u32[]{:S(2)}, u32[]{:S(2)}) collective-permute-start(bf16[8,4096]{1,0:T(8,128)(2,1)S(1)} %bitcast.32), channel_id=1, source_target_pairs={{0,1},{1,0},{2,3},{3,2},{4,5},{5,4},{6,7},{7,6}} | collective-permute-start | bytes 196616 | tf_op jit(solution)/shard_map/ppermute | solution.py:611
  24.6 19.7 %copy-start.4 = (bf16[8,4096]{1,0:T(8,128)(2,1)S(1)}, bf16[8,4096]{1,0:T(8,128)(2,1)}, u32[]{:S(2)}) copy-start(bf16[8,4096]{1,0:T(8,128)(2,1)} %new_ref.1) | copy-start | bytes 196612
  24.6 55.5 %collective-permute-start.6 = (bf16[1,64,4096]{2,1,0:T(8,128)(2,1)}, bf16[1,64,4096]{2,1,0:T(8,128)(2,1)S(1)}, u32[]{:S(2)}, u32[]{:S(2)}) collective-permute-start(bf16[1,64,4096]{2,1,0:T(8,128)(2,1)} %get-tuple-element.123), channel_id=1, source_target_pairs={{0,4},{1,5},{2,6},{3,7},{4,0},{5,1},{6,2},{7,3}} | collective-permute-start | bytes 1572872 | tf_op jit(solution)/shard_map/ppermute | solution.py:611
  30.9 10.4 %collective-permute-start.3 = (bf16[8,2048]{1,0:T(8,128)(2,1)S(1)}, bf16[8,2048]{1,0:T(8,128)(2,1)S(1)}, u32[]{:S(2)}, u32[]{:S(2)}) collective-permute-start(bf16[8,2048]{1,0:T(8,128)(2,1)S(1)} %dynamic-slice_add_fusion), channel_id=1, source_target_pairs={{0,4},{1,5},{2,6},{3,7},{4,0},{5,1},{6,2},{7,3}} | collective-permute-start | bytes 98312 | tf_op jit(solution)/shard_map/ppermute | solution.py:611
  32.8 10.3 %collective-permute-start.2 = (bf16[8,2048]{1,0:T(8,128)(2,1)S(1)}, bf16[8,2048]{1,0:T(8,128)(2,1)S(1)}, u32[]{:S(2)}, u32[]{:S(2)}) collective-permute-start(bf16[8,2048]{1,0:T(8,128)(2,1)S(1)} %dynamic-slice_add_fusion), channel_id=1, source_target_pairs={{0,2},{1,3},{2,0},{3,1},{4,6},{5,7},{6,4},{7,5}} | collective-permute-start | bytes 98312 | tf_op jit(solution)/shard_map/ppermute | solution.py:611
  34.2 8.8 %collective-permute-start.4 = (bf16[8,2048]{1,0:T(8,128)(2,1)S(1)}, bf16[8,2048]{1,0:T(8,128)(2,1)S(1)}, u32[]{:S(2)}, u32[]{:S(2)}) collective-permute-start(bf16[8,2048]{1,0:T(8,128)(2,1)S(1)} %dynamic-slice_add_fusion), channel_id=1, source_target_pairs={{0,6},{1,7},{2,4},{3,5},{4,2},{5,3},{6,0},{7,1}} | collective-permute-start | bytes 98312 | tf_op jit(solution)/shard_map/ppermute | solution.py:611
  41.3 38.8 %collective-permute-start.7 = (bf16[1,64,4096]{2,1,0:T(8,128)(2,1)}, bf16[1,64,4096]{2,1,0:T(8,128)(2,1)S(1)}, u32[]{:S(2)}, u32[]{:S(2)}) collective-permute-start(bf16[1,64,4096]{2,1,0:T(8,128)(2,1)} %copy-done.12), channel_id=1, source_target_pairs={{0,2},{1,3},{2,0},{3,1},{4,6},{5,7},{6,4},{7,5}} | collective-permute-start | bytes 1572872 | tf_op jit(solution)/shard_map/ppermute | solution.py:611
  43.1 1.2 collective-permute-start.5
  80.2 4.3 %collective-permute-start.8 = (bf16[1,64,4096]{2,1,0:T(8,128)(2,1)S(1)}, bf16[1,64,4096]{2,1,0:T(8,128)(2,1)S(1)}, u32[]{:S(2)}, u32[]{:S(2)}) collective-permute-start(bf16[1,64,4096]{2,1,0:T(8,128)(2,1)S(1)} %collective-permute-done.6.refs_0_), channel_id=1, source_target_pairs={{0,1},{1,0},{2,3},{3,2},{4,5},{5,4},{6,7},{7,6}} | collective-permute-start | bytes 1572872 | tf_op jit(solution)/shard_map/ppermute | solution.py:611
  80.3 4.1 %collective-permute-start.9 = (bf16[1,64,4096]{2,1,0:T(8,128)(2,1)S(1)}, bf16[1,64,4096]{2,1,0:T(8,128)(2,1)S(1)}, u32[]{:S(2)}, u32[]{:S(2)}) collective-permute-start(bf16[1,64,4096]{2,1,0:T(8,128)(2,1)S(1)} %collective-permute-done.7.refs_1_), channel_id=1, source_target_pairs={{0,1},{1,0},{2,3},{3,2},{4,5},{5,4},{6,7},{7,6}} | collective-permute-start | bytes 1572872 | tf_op jit(solution)/shard_map/ppermute | solution.py:611
  82.4 14.0 %collective-permute-start.10 = (bf16[1,64,4096]{2,1,0:T(8,128)(2,1)S(1)}, bf16[1,64,4096]{2,1,0:T(8,128)(2,1)S(1)}, u32[]{:S(2)}, u32[]{:S(2)}) collective-permute-start(bf16[1,64,4096]{2,1,0:T(8,128)(2,1)S(1)} %get-tuple-element.131), channel_id=1, source_target_pairs={{0,4},{1,5},{2,6},{3,7},{4,0},{5,1},{6,2},{7,3}} | collective-permute-start | bytes 1572872 | tf_op jit(solution)/shard_map/ppermute | solution.py:611
  83.9 13.7 %collective-permute-start.11 = (bf16[1,64,4096]{2,1,0:T(8,128)(2,1)S(1)}, bf16[1,64,4096]{2,1,0:T(8,128)(2,1)S(1)}, u32[]{:S(2)}, u32[]{:S(2)}) collective-permute-start(bf16[1,64,4096]{2,1,0:T(8,128)(2,1)S(1)} %get-tuple-element.132), channel_id=1, source_target_pairs={{0,2},{1,3},{2,0},{3,1},{4,6},{5,7},{6,4},{7,5}} | collective-permute-start | bytes 1572872 | tf_op jit(solution)/shard_map/ppermute | solution.py:611
  84.5 15.7 %copy-start.7 = (bf16[2,128,4096]{2,1,0:T(8,128)(2,1)S(1)}, bf16[2,128,4096]{2,1,0:T(8,128)(2,1)}, u32[]{:S(2)}) copy-start(bf16[2,128,4096]{2,1,0:T(8,128)(2,1)} %copy-done.6) | copy-start | bytes 6291460
  97.6 2.6 collective-permute-start.12
  97.6 26.0 %collective-permute-start.14 = (bf16[1,128,4096]{2,1,0:T(8,128)(2,1)S(1)}, bf16[1,128,4096]{2,1,0:T(8,128)(2,1)S(1)}, u32[]{:S(2)}, u32[]{:S(2)}) collective-permute-start(bf16[1,128,4096]{2,1,0:T(8,128)(2,1)S(1)} %copy-done.11), channel_id=1, source_target_pairs={{0,4},{1,5},{2,6},{3,7},{4,0},{5,1},{6,2},{7,3}} | collective-permute-start | bytes 3145736 | tf_op jit(solution)/shard_map/ppermute | solution.py:611
  98.1 26.0 %collective-permute-start.15 = (bf16[1,128,4096]{2,1,0:T(8,128)(2,1)S(1)}, bf16[1,128,4096]{2,1,0:T(8,128)(2,1)S(1)}, u32[]{:S(2)}, u32[]{:S(2)}) collective-permute-start(bf16[1,128,4096]{2,1,0:T(8,128)(2,1)S(1)} %get-tuple-element.140), channel_id=1, source_target_pairs={{0,2},{1,3},{2,0},{3,1},{4,6},{5,7},{6,4},{7,5}} | collective-permute-start | bytes 3145736 | tf_op jit(solution)/shard_map/ppermute | solution.py:611
  98.5 3.2 collective-permute-start.13
  98.5 69.7 %collective-permute-start.18 = (bf16[2,128,4096]{2,1,0:T(8,128)(2,1)S(1)}, bf16[2,128,4096]{2,1,0:T(8,128)(2,1)S(1)}, u32[]{:S(2)}, u32[]{:S(2)}) collective-permute-start(bf16[2,128,4096]{2,1,0:T(8,128)(2,1)S(1)} %copy-done.9), channel_id=1, source_target_pairs={{0,4},{1,5},{2,6},{3,7},{4,0},{5,1},{6,2},{7,3}} | collective-permute-start | bytes 6291464 | tf_op jit(solution)/shard_map/ppermute | solution.py:611
  100.2 68.2 %collective-permute-start.19 = (bf16[2,128,4096]{2,1,0:T(8,128)(2,1)S(1)}, bf16[2,128,4096]{2,1,0:T(8,128)(2,1)S(1)}, u32[]{:S(2)}, u32[]{:S(2)}) collective-permute-start(bf16[2,128,4096]{2,1,0:T(8,128)(2,1)S(1)} %copy-done.7), channel_id=1, source_target_pairs={{0,2},{1,3},{2,0},{3,1},{4,6},{5,7},{6,4},{7,5}} | collective-permute-start | bytes 6291464 | tf_op jit(solution)/shard_map/ppermute | solution.py:611
  124.2 2.7 collective-permute-start.16
  124.2 4.2 %collective-permute-start.17 = (bf16[1,128,4096]{2,1,0:T(8,128)(2,1)S(1)}, bf16[1,128,4096]{2,1,0:T(8,128)(2,1)S(1)}, u32[]{:S(2)}, u32[]{:S(2)}) collective-permute-start(bf16[1,128,4096]{2,1,0:T(8,128)(2,1)S(1)} %collective-permute-done.15.refs_1_), channel_id=1, source_target_pairs={{0,1},{1,0},{2,3},{3,2},{4,5},{5,4},{6,7},{7,6}} | collective-permute-start | bytes 3145736 | tf_op jit(solution)/shard_map/ppermute | solution.py:611
  168.4 4.2 %collective-permute-start.20 = (bf16[2,128,4096]{2,1,0:T(8,128)(2,1)S(1)}, bf16[2,128,4096]{2,1,0:T(8,128)(2,1)S(1)}, u32[]{:S(2)}, u32[]{:S(2)}) collective-permute-start(bf16[2,128,4096]{2,1,0:T(8,128)(2,1)S(1)} %collective-permute-done.18.refs_0_), channel_id=1, source_target_pairs={{0,1},{1,0},{2,3},{3,2},{4,5},{5,4},{6,7},{7,6}} | collective-permute-start | bytes 6291464 | tf_op jit(solution)/shard_map/ppermute | solution.py:611
  168.4 7.2 %collective-permute-start.21 = (bf16[2,128,4096]{2,1,0:T(8,128)(2,1)S(1)}, bf16[2,128,4096]{2,1,0:T(8,128)(2,1)S(1)}, u32[]{:S(2)}, u32[]{:S(2)}) collective-permute-start(bf16[2,128,4096]{2,1,0:T(8,128)(2,1)S(1)} %collective-permute-done.19.refs_1_), channel_id=1, source_target_pairs={{0,1},{1,0},{2,3},{3,2},{4,5},{5,4},{6,7},{7,6}} | collective-permute-start | bytes 6291464 | tf_op jit(solution)/shard_map/ppermute | solution.py:611
  168.9 47.5 %collective-permute-start.23 = (bf16[2,128,4096]{2,1,0:T(8,128)(2,1)S(1)}, bf16[2,128,4096]{2,1,0:T(8,128)(2,1)S(1)}, u32[]{:S(2)}, u32[]{:S(2)}) collective-permute-start(bf16[2,128,4096]{2,1,0:T(8,128)(2,1)S(1)} %copy-done.9), channel_id=1, source_target_pairs={{0,2},{1,3},{2,0},{3,1},{4,6},{5,7},{6,4},{7,5}} | collective-permute-start | bytes 6291464 | tf_op jit(solution)/shard_map/ppermute | solution.py:611
  169.2 47.3 %collective-permute-start.22 = (bf16[2,128,4096]{2,1,0:T(8,128)(2,1)S(1)}, bf16[2,128,4096]{2,1,0:T(8,128)(2,1)S(1)}, u32[]{:S(2)}, u32[]{:S(2)}) collective-permute-start(bf16[2,128,4096]{2,1,0:T(8,128)(2,1)S(1)} %copy-done.7), channel_id=1, source_target_pairs={{0,4},{1,5},{2,6},{3,7},{4,0},{5,1},{6,2},{7,3}} | collective-permute-start | bytes 6291464 | tf_op jit(solution)/shard_map/ppermute | solution.py:611
  216.5 8.4 %collective-permute-start.24 = (bf16[2,128,4096]{2,1,0:T(8,128)(2,1)S(1)}, bf16[2,128,4096]{2,1,0:T(8,128)(2,1)S(1)}, u32[]{:S(2)}, u32[]{:S(2)}) collective-permute-start(bf16[2,128,4096]{2,1,0:T(8,128)(2,1)S(1)} %collective-permute-done.22.refs_0_), channel_id=1, source_target_pairs={{0,1},{1,0},{2,3},{3,2},{4,5},{5,4},{6,7},{7,6}} | collective-permute-start | bytes 6291464 | tf_op jit(solution)/shard_map/ppermute | solution.py:611
  216.5 8.4 %collective-permute-start.25 = (bf16[2,128,4096]{2,1,0:T(8,128)(2,1)S(1)}, bf16[2,128,4096]{2,1,0:T(8,128)(2,1)S(1)}, u32[]{:S(2)}, u32[]{:S(2)}) collective-permute-start(bf16[2,128,4096]{2,1,0:T(8,128)(2,1)S(1)} %collective-permute-done.23.refs_1_), channel_id=1, source_target_pairs={{0,1},{1,0},{2,3},{3,2},{4,5},{5,4},{6,7},{7,6}} | collective-permute-start | bytes 6291464 | tf_op jit(solution)/shard_map/ppermute | solution.py:611
  221.6 47.7 %collective-permute-start.27 = (bf16[2,128,4096]{2,1,0:T(8,128)(2,1)}, bf16[2,128,4096]{2,1,0:T(8,128)(2,1)S(1)}, u32[]{:S(2)}, u32[]{:S(2)}) collective-permute-start(bf16[2,128,4096]{2,1,0:T(8,128)(2,1)} %get-tuple-element.210), channel_id=1, source_target_pairs={{0,2},{1,3},{2,0},{3,1},{4,6},{5,7},{6,4},{7,5}} | collective-permute-start | bytes 6291464 | tf_op jit(solution)/shard_map/ppermute | solution.py:611
  223.3 47.5 %collective-permute-start.26 = (bf16[2,128,4096]{2,1,0:T(8,128)(2,1)}, bf16[2,128,4096]{2,1,0:T(8,128)(2,1)S(1)}, u32[]{:S(2)}, u32[]{:S(2)}) collective-permute-start(bf16[2,128,4096]{2,1,0:T(8,128)(2,1)} %get-tuple-element.211), channel_id=1, source_target_pairs={{0,4},{1,5},{2,6},{3,7},{4,0},{5,1},{6,2},{7,3}} | collective-permute-start | bytes 6291464 | tf_op jit(solution)/shard_map/ppermute | solution.py:611
  270.8 4.2 %collective-permute-start.28 = (bf16[2,128,4096]{2,1,0:T(8,128)(2,1)S(1)}, bf16[2,128,4096]{2,1,0:T(8,128)(2,1)S(1)}, u32[]{:S(2)}, u32[]{:S(2)}) collective-permute-start(bf16[2,128,4096]{2,1,0:T(8,128)(2,1)S(1)} %collective-permute-done.26.refs_0_), channel_id=1, source_target_pairs={{0,1},{1,0},{2,3},{3,2},{4,5},{5,4},{6,7},{7,6}} | collective-permute-start | bytes 6291464 | tf_op jit(solution)/shard_map/ppermute | solution.py:611
  270.8 7.2 %collective-permute-start.29 = (bf16[2,128,4096]{2,1,0:T(8,128)(2,1)S(1)}, bf16[2,128,4096]{2,1,0:T(8,128)(2,1)S(1)}, u32[]{:S(2)}, u32[]{:S(2)}) collective-permute-start(bf16[2,128,4096]{2,1,0:T(8,128)(2,1)S(1)} %collective-permute-done.27.refs_1_), channel_id=1, source_target_pairs={{0,1},{1,0},{2,3},{3,2},{4,5},{5,4},{6,7},{7,6}} | collective-permute-start | bytes 6291464 | tf_op jit(solution)/shard_map/ppermute | solution.py:611
  271.3 47.5 %collective-permute-start.30 = (bf16[2,128,4096]{2,1,0:T(8,128)(2,1)S(1)}, bf16[2,128,4096]{2,1,0:T(8,128)(2,1)S(1)}, u32[]{:S(2)}, u32[]{:S(2)}) collective-permute-start(bf16[2,128,4096]{2,1,0:T(8,128)(2,1)S(1)} %collective-permute-done.19.refs_1_), channel_id=1, source_target_pairs={{0,4},{1,5},{2,6},{3,7},{4,0},{5,1},{6,2},{7,3}} | collective-permute-start | bytes 6291464 | tf_op jit(solution)/shard_map/ppermute | solution.py:611
  272.8 47.3 %collective-permute-start.31 = (bf16[2,128,4096]{2,1,0:T(8,128)(2,1)S(1)}, bf16[2,128,4096]{2,1,0:T(8,128)(2,1)S(1)}, u32[]{:S(2)}, u32[]{:S(2)}) collective-permute-start(bf16[2,128,4096]{2,1,0:T(8,128)(2,1)S(1)} %collective-permute-done.18.refs_0_), channel_id=1, source_target_pairs={{0,2},{1,3},{2,0},{3,1},{4,6},{5,7},{6,4},{7,5}} | collective-permute-start | bytes 6291464 | tf_op jit(solution)/shard_map/ppermute | solution.py:611
  320.1 4.2 %collective-permute-start.32 = (bf16[2,128,4096]{2,1,0:T(8,128)(2,1)S(1)}, bf16[2,128,4096]{2,1,0:T(8,128)(2,1)S(1)}, u32[]{:S(2)}, u32[]{:S(2)}) collective-permute-start(bf16[2,128,4096]{2,1,0:T(8,128)(2,1)S(1)} %collective-permute-done.31.refs_0_), channel_id=1, source_target_pairs={{0,1},{1,0},{2,3},{3,2},{4,5},{5,4},{6,7},{7,6}} | collective-permute-start | bytes 6291464 | tf_op jit(solution)/shard_map/ppermute | solution.py:611
  320.1 7.2 %collective-permute-start.33 = (bf16[2,128,4096]{2,1,0:T(8,128)(2,1)S(1)}, bf16[2,128,4096]{2,1,0:T(8,128)(2,1)S(1)}, u32[]{:S(2)}, u32[]{:S(2)}) collective-permute-start(bf16[2,128,4096]{2,1,0:T(8,128)(2,1)S(1)} %collective-permute-done.30.refs_1_), channel_id=1, source_target_pairs={{0,1},{1,0},{2,3},{3,2},{4,5},{5,4},{6,7},{7,6}} | collective-permute-start | bytes 6291464 | tf_op jit(solution)/shard_map/ppermute | solution.py:611
  320.6 25.1 %collective-permute-start.34 = (bf16[1,128,4096]{2,1,0:T(8,128)(2,1)S(1)}, bf16[1,128,4096]{2,1,0:T(8,128)(2,1)S(1)}, u32[]{:S(2)}, u32[]{:S(2)}) collective-permute-start(bf16[1,128,4096]{2,1,0:T(8,128)(2,1)S(1)} %collective-permute-done.15.refs_1_), channel_id=1, source_target_pairs={{0,4},{1,5},{2,6},{3,7},{4,0},{5,1},{6,2},{7,3}} | collective-permute-start | bytes 3145736 | tf_op jit(solution)/shard_map/ppermute | solution.py:611
  321.1 24.8 %collective-permute-start.35 = (bf16[1,128,4096]{2,1,0:T(8,128)(2,1)S(1)}, bf16[1,128,4096]{2,1,0:T(8,128)(2,1)S(1)}, u32[]{:S(2)}, u32[]{:S(2)}) collective-permute-start(bf16[1,128,4096]{2,1,0:T(8,128)(2,1)S(1)} %collective-permute-done.14.refs_0_), channel_id=1, source_target_pairs={{0,2},{1,3},{2,0},{3,1},{4,6},{5,7},{6,4},{7,5}} | collective-permute-start | bytes 3145736 | tf_op jit(solution)/shard_map/ppermute | solution.py:611
  345.9 2.7 collective-permute-start.36
  345.9 4.2 %collective-permute-start.37 = (bf16[1,128,4096]{2,1,0:T(8,128)(2,1)S(1)}, bf16[1,128,4096]{2,1,0:T(8,128)(2,1)S(1)}, u32[]{:S(2)}, u32[]{:S(2)}) collective-permute-start(bf16[1,128,4096]{2,1,0:T(8,128)(2,1)S(1)} %collective-permute-done.34.refs_1_), channel_id=1, source_target_pairs={{0,1},{1,0},{2,3},{3,2},{4,5},{5,4},{6,7},{7,6}} | collective-permute-start | bytes 3145736 | tf_op jit(solution)/shard_map/ppermute | solution.py:611
  346.4 13.8 %collective-permute-start.38 = (bf16[1,64,4096]{2,1,0:T(8,128)(2,1)S(1)}, bf16[1,64,4096]{2,1,0:T(8,128)(2,1)S(1)}, u32[]{:S(2)}, u32[]{:S(2)}) collective-permute-start(bf16[1,64,4096]{2,1,0:T(8,128)(2,1)S(1)} %collective-permute-done.7.refs_1_), channel_id=1, source_target_pairs={{0,4},{1,5},{2,6},{3,7},{4,0},{5,1},{6,2},{7,3}} | collective-permute-start | bytes 1572872 | tf_op jit(solution)/shard_map/ppermute | solution.py:611
  347.9 13.6 %collective-permute-start.39 = (bf16[1,64,4096]{2,1,0:T(8,128)(2,1)S(1)}, bf16[1,64,4096]{2,1,0:T(8,128)(2,1)S(1)}, u32[]{:S(2)}, u32[]{:S(2)}) collective-permute-start(bf16[1,64,4096]{2,1,0:T(8,128)(2,1)S(1)} %collective-permute-done.6.refs_0_), channel_id=1, source_target_pairs={{0,2},{1,3},{2,0},{3,1},{4,6},{5,7},{6,4},{7,5}} | collective-permute-start | bytes 1572872 | tf_op jit(solution)/shard_map/ppermute | solution.py:611
  361.5 1.9 collective-permute-start.40
  361.5 2.7 collective-permute-start.41
  362.0 13.8 %collective-permute-start.42 = (bf16[1,64,4096]{2,1,0:T(8,128)(2,1)S(1)}, bf16[1,64,4096]{2,1,0:T(8,128)(2,1)S(1)}, u32[]{:S(2)}, u32[]{:S(2)}) collective-permute-start(bf16[1,64,4096]{2,1,0:T(8,128)(2,1)S(1)} %collective-permute-done.11.refs_1_), channel_id=1, source_target_pairs={{0,4},{1,5},{2,6},{3,7},{4,0},{5,1},{6,2},{7,3}} | collective-permute-start | bytes 1572872 | tf_op jit(solution)/shard_map/ppermute | solution.py:611
  362.5 13.6 %collective-permute-start.43 = (bf16[1,64,4096]{2,1,0:T(8,128)(2,1)S(1)}, bf16[1,64,4096]{2,1,0:T(8,128)(2,1)S(1)}, u32[]{:S(2)}, u32[]{:S(2)}) collective-permute-start(bf16[1,64,4096]{2,1,0:T(8,128)(2,1)S(1)} %collective-permute-done.10.refs_0_), channel_id=1, source_target_pairs={{0,2},{1,3},{2,0},{3,1},{4,6},{5,7},{6,4},{7,5}} | collective-permute-start | bytes 1572872 | tf_op jit(solution)/shard_map/ppermute | solution.py:611
  375.8 1.9 collective-permute-start.44
  377.7 1.9 collective-permute-start.45
  (12 other events, 64.7 us)

commit v10 on v8

--- a/solution.py
+++ b/solution.py
@@ -13,6 +13,7 @@
 STAT_ROWS = 8
 NORM_ROWS = 32
 COL_TILE = 256
+FIRST_ROWS = 16
 MESH = pl.DeviceIdType.MESH
 
 
@@ -135,8 +136,8 @@
         loads[i].wait()
 
         def norm_rows(r, carry):
-            at = pl.ds(pl.multiple_of(r * NORM_ROWS, NORM_ROWS), NORM_ROWS)
-            acc = [jnp.zeros((NORM_ROWS, HEAD_DIM), jnp.float32) for _ in range(2)]
+            at = pl.ds(pl.multiple_of(r * FIRST_ROWS, FIRST_ROWS), FIRST_ROWS)
+            acc = [jnp.zeros((FIRST_ROWS, HEAD_DIM), jnp.float32) for _ in range(2)]
             for c, lane in enumerate(lanes):
                 xf = x_buf[i, at, lane].astype(jnp.float32)
                 acc[c % 2] += xf * xf
@@ -146,7 +147,7 @@
                 out_refs[i][0, at, lane] = (xf * inv_rms * gain_ref[:, lane].astype(jnp.float32)).astype(jnp.bfloat16)
             return carry
 
-        lax.fori_loop(0, rows // NORM_ROWS, norm_rows, 0)
+        lax.fori_loop(0, rows // FIRST_ROWS, norm_rows, 0, unroll=True)
 
 
 def first_call(x, gain, places, rows):
@@ -617,18 +618,19 @@
         wq = w_q[0]
         gain = norm_attn
 
-        q1, q2, rows_h = 1, n_batch // 4, blk // 2
+        q1, q2 = 1, n_batch // 4
+        pieces = {"0b": (blk - 3 * blk // 8, 3 * blk // 8), "0a": (0, blk - 3 * blk // 8)}
         a_parts, b_parts = {}, {}
-        for h, name in enumerate(("0a", "0b")):
-            a_parts[name], b_parts[name] = first_call(prompt, norm_attn, [(0, h * rows_h), (half, h * rows_h)], rows_h)
+        for name, (lo, rows) in pieces.items():
+            a_parts[name], b_parts[name] = first_call(prompt, norm_attn, [(0, lo), (half, lo)], rows)
         from_y, from_x = {}, {}
 
         def send_part(step, along_y, along_x):
             from_y[step] = swap(along_y, 4)
             from_x[step] = swap(along_x, 2)
 
-        send_part("0a", a_parts["0a"], b_parts["0a"])
-        send_part("0b", a_parts["0b"], b_parts["0b"])
+        for name in pieces:
+            send_part(name, a_parts[name], b_parts[name])
         order, outs_of = [], []
         for part, (lo, hi) in ((1, (q1, q2)), (2, (q2, half)), (0, (0, q1))):
             for k in range(lo, hi):
@@ -667,8 +669,8 @@
         def run(groups, per_group, masks, batches, caches, **kw):
             return kv_call(groups, per_group, masks, batches, len_rows, tabs, wk, wv, q_diag, caches, **kw)
 
-        def half_rows(step):
-            return {"row0": rows_h * (step == "0b"), "stat_of": (n_dev - 2) * (step == "0b")}
+        def piece_of(step):
+            return {"row0": pieces[step][0], "stat_of": (n_dev - 2) * (step == "0b")}
 
         def after(caches, *arrays):
             out = lax.optimization_barrier((caches[2], *arrays))
@@ -677,7 +679,7 @@
         caches = run([[(arr, 0), (arr, half)] for arr in (normed, core_all)], half,
                      [[0] * 2, [1] * 2], [[0, half]] * 2, caches, new_rows=[k_new, v_new])
         diag, turned = {}, {}
-        starts = {"0a": (0, half), "0b": (0, half), "1": (q1, half + q1), "2": (q2, half + q2), "3": (half + q2, q2), "4": (half, 0)}
+        starts = {"0b": (0, half), "0a": (0, half), "1": (q1, half + q1), "2": (q2, half + q2), "3": (half + q2, q2), "4": (half, 0)}
         for step, start in starts.items():
             caches, (got_y, got_x) = after(caches, from_y[step], from_x[step])
             other_y, other_x = swap(got_y, 1), swap(got_x, 1)
@@ -687,7 +689,7 @@
                 diag[step] = (via_x, via_y)
             streams = [[(got_y, 0), (got_x, 0)], [(other_y, 0), (other_x, 0)]]
             if step in ("0a", "0b"):
-                caches = run([streams[0] + streams[1]], q1, [[4, 2, 5, 3]], [[*start, *start]], caches, **half_rows(step))
+                caches = run([streams[0] + streams[1]], q1, [[4, 2, 5, 3]], [[*start, *start]], caches, **piece_of(step))
             else:
                 caches = run(streams, got_y.shape[0], [[4, 2], [5, 3]], [list(start)] * 2, caches)
             if step in "34":
@@ -702,7 +704,7 @@
             start = starts[step]
             streams = [[(via_x, 0), (via_y, 0)], [(other_x, 0), (other_y, 0)]]
             if step in ("0a", "0b"):
-                caches = run([streams[0] + streams[1]], q1, [[6, 6, 7, 7]], [[*start, *start]], caches, **half_rows(step))
+                caches = run([streams[0] + streams[1]], q1, [[6, 6, 7, 7]], [[*start, *start]], caches, **piece_of(step))
             else:
                 caches = run(streams, via_x.shape[0], [[6] * 2, [7] * 2], [list(start)] * 2, caches)
 

time: 407 us -> 394 us (0.968)
  waiting for transfers between devices: 171 us -> 150 us
  starting transfers between devices: 30.9 us -> 37.7 us
    ppermute x46, waiting for transfers between devices: 171 us -> 150 us  [swap(): return lax.ppermute(arr, 'model', [(i, i ^ bit) for i in range(n_dev)])]
    ppermute x46, starting transfers between devices: 30.9 us -> 37.7 us  [swap(): return lax.ppermute(arr, 'model', [(i, i ^ bit) for i in range(n_dev)])]
    unnamed x28 -> x30, local copies, waits for them, and re-layouts: 13.6 us -> 13.8 us
  transfers between devices with their start and end apart: 46 -> 46, of which waited for: 34 -> 28; matrix products, arithmetic and copies ran while one was open for 4% -> 3% of each run, Pallas kernels for 34% -> 36%
where the time goes in v10:
time: 394 us
  Pallas kernels  178 us (45%)
  waiting for transfers between devices  150 us (38%)
  starting transfers between devices  37.7 us (10%)
  local copies, waits for them, and re-layouts  19.3 us (5%)
  matrix products  4.57 us (1%)
    ppermute x46, waiting for transfers between devices, swap(): return lax.ppermute(arr, 'model', [(i, i ^ bit) for i in range(n_dev)])  150 us
    pallas_call x11, Pallas kernels, kv_call(): pl.pallas_call(functools.partial(kv_kernel, n_in, n_steps, masks, batches...  116 us
    ppermute x46, starting transfers between devices, swap(): return lax.ppermute(arr, 'model', [(i, i ^ bit) for i in range(n_dev)])  37.7 us
    pallas_call x1, Pallas kernels, tail_call(): pl.pallas_call(functools.partial(tail_kernel, n_dev, parts_of), out_shape...  23.6 us
    pallas_call x2, Pallas kernels, turn_call(): pl.pallas_call(turn_kernel, grid=(d // cols,), in_specs=[pl.BlockSpec((n,...  15.8 us
    unnamed x30, local copies, waits for them, and re-layouts  13.8 us
    pallas_call x1, Pallas kernels, norm_call(): pl.pallas_call(functools.partial(norm_kernel, outs_of), grid=(len(order),...  10.8 us
  transfers between devices with their start and end apart: 46, of which 28 were waited for; matrix products, arithmetic and copies ran while one was open for 3% of the time, Pallas kernels for 36%

profile of v10, /device:TPU:0, one launch (start us, length us, event | category | flops | bytes accessed | tf_op | source)
XLA Modules:
  0.0 393.6 jit_solution(6028982378751449815)
XLA Ops:
  1.4 10.8 %norm_rows.1 = (bf16[1,128,4096]{2,1,0:T(8,128)(2,1)S(1)}, bf16[1,128,4096]{2,1,0:T(8,128)(2,1)S(1)}, bf16[2,128,4096]{2,1,0:T(8,128)(2,1)S(1)}, bf16[2,128,4096]{2,1,0:T(8,128)(2,1)S(1)}, bf16[8,128,4096]{2,1,0:T(8,128)(2,1)}) custom-call(bf16[8,128,4096]{2,1,0:T(8,128)(2,1)} %x_hbm.3, bf16[1,4096]{1,0:T(2,128)(2,1)S(1)} %copy-done.2), custom_call_target="tpu_custom_call" | custom-call | flops 33554432 | bytes 25165824 | tf_op jit(solution)/shard_map/norm_rows/pallas_call | solution.py:181
  17.8 4.6 %fusion.2 = bf16[8,1,4096]{2,1,0:T(2,128)(2,1)S(1)} fusion(bf16[8,128,4096]{2,1,0:T(8,128)(2,1)} %x_hbm.3, pred[8,128,1]{1,0,2:T(8,128)(4,1)S(1)} %compare_bitcast_fusion), kind=kOutput, calls=%fused_computation.14 | convolution fusion | flops 8388608 | bytes 8455168 | tf_op jit(solution)/shard_map/bs,bsd->bd/dot_general | solution.py:645
  22.5 2.2 first_rows.2
  24.7 3.0 collective-permute-start.6
  27.8 1.9 fusion
  30.9 2.9 collective-permute-start.3
  35.6 2.4 first_rows.3
  38.0 2.0 collective-permute-start.7
  40.0 1.9 collective-permute-start.10
  43.4 4.7 %keep.1 = (bf16[4096,512]{1,0:T(8,128)(2,1)S(1)}, bf16[4096,512]{1,0:T(8,128)(2,1)S(1)}, bf16[512,4096]{1,0:T(8,128)(2,1)S(1)}) custom-call(bf16[4096,512]{1,0:T(8,128)(2,1)} %bitcast.28, bf16[4096,512]{1,0:T(8,128)(2,1)} %bitcast.29, bf16[512,4096]{1,0:T(8,128)(2,1)} %bitcast.30), custom_call_target="tpu_custom_call" | custom-call | tf_op jit(solution)/shard_map/keep/pallas_call | solution.py:40
  48.1 3.1 query_rows.1
  51.3 27.9 %kv_chunk.11 = (bf16[8,1025,4,128]{3,2,1,0:T(4,128)(2,1)}, bf16[8,1025,4,128]{3,2,1,0:T(4,128)(2,1)}, f32[14,8,3,8,128]{4,3,2,1,0:T(8,128)S(1)}) custom-call(bf16[8,128,4096]{2,1,0:T(8,128)(2,1)} %get-tuple-element.105.refs_0_.refs_1_, bf16[8,128,4096]{2,1,0:T(8,128)(2,1)} %get-tuple-element.105.refs_0_.refs_1_, ...), custom_call_target="tpu_custom_call" | custom-call | flops 17179869184 | bytes 20971520 | tf_op jit(solution)/shard_map/kv_chunk/pallas_call | solution.py:442
  81.5 3.6 kv_chunk.12
  85.3 2.0 collective-permute-start.15
  87.3 1.9 collective-permute-start.18
  89.4 5.0 %kv_chunk.13 = (bf16[8,1025,4,128]{3,2,1,0:T(4,128)(2,1)}, bf16[8,1025,4,128]{3,2,1,0:T(4,128)(2,1)}, f32[14,8,3,8,128]{4,3,2,1,0:T(8,128)S(1)}) custom-call(bf16[1,80,4096]{2,1,0:T(8,128)(2,1)S(1)} %collective-permute-done.10.refs_0_, ...), custom_call_target="tpu_custom_call", output_to_operand_aliasing={{0}: (10, {}), {1}: (11, {}), {2}: (12, {})} | custom-call | flops 2684354560 | bytes 3276800 | tf_op jit(solution)/shard_map/kv_chunk/pallas_call | solution.py:442
  94.4 16.9 %collective-permute-done.14.refs_0_ = bf16[1,128,4096]{2,1,0:T(8,128)(2,1)S(1)} collective-permute-done((bf16[1,128,4096]{2,1,0:T(8,128)(2,1)S(1)}, bf16[1,128,4096]{2,1,0:T(8,128)(2,1)S(1)}, u32[]{:S(2)}, u32[]{:S(2)}) %collective-permute-start.14) | collective-permute-done | bytes 1048608 | tf_op jit(solution)/shard_map/ppermute | solution.py:609
  111.8 2.1 collective-permute-done.16.refs_2_
  115.5 7.4 %kv_chunk.14 = (bf16[8,1025,4,128]{3,2,1,0:T(4,128)(2,1)}, bf16[8,1025,4,128]{3,2,1,0:T(4,128)(2,1)}, f32[14,8,3,8,128]{4,3,2,1,0:T(8,128)S(1)}) custom-call(bf16[1,128,4096]{2,1,0:T(8,128)(2,1)S(1)} %collective-permute-done.14.refs_0_, ...), custom_call_target="tpu_custom_call", output_to_operand_aliasing={{0}: (10, {}), {1}: (11, {}), {2}: (12, {})} | custom-call | flops 4294967296 | bytes 5242880 | tf_op jit(solution)/shard_map/kv_chunk/pallas_call | solution.py:442
  122.9 32.8 %collective-permute-done.18.refs_0_ = bf16[2,128,4096]{2,1,0:T(8,128)(2,1)S(1)} collective-permute-done((bf16[2,128,4096]{2,1,0:T(8,128)(2,1)S(1)}, bf16[2,128,4096]{2,1,0:T(8,128)(2,1)S(1)}, u32[]{:S(2)}, u32[]{:S(2)}) %collective-permute-start.18) | collective-permute-done | bytes 2097184 | tf_op jit(solution)/shard_map/ppermute | solution.py:609
  156.3 1.7 collective-permute-start.23
  158.0 1.7 collective-permute-start.22
  159.9 3.0 collective-permute-done.21.refs_3_
  162.9 14.0 %kv_chunk.15 = (bf16[8,1025,4,128]{3,2,1,0:T(4,128)(2,1)}, bf16[8,1025,4,128]{3,2,1,0:T(4,128)(2,1)}, f32[14,8,3,8,128]{4,3,2,1,0:T(8,128)S(1)}) custom-call(bf16[2,128,4096]{2,1,0:T(8,128)(2,1)S(1)} %collective-permute-done.18.refs_0_, ...), custom_call_target="tpu_custom_call", output_to_operand_aliasing={{0}: (10, {}), {1}: (11, {}), {2}: (12, {})} | custom-call | flops 8589934592 | bytes 10485760 | tf_op jit(solution)/shard_map/kv_chunk/pallas_call | solution.py:442
  177.0 26.9 %collective-permute-done.23.refs_1_ = bf16[2,128,4096]{2,1,0:T(8,128)(2,1)S(1)} collective-permute-done((bf16[2,128,4096]{2,1,0:T(8,128)(2,1)S(1)}, bf16[2,128,4096]{2,1,0:T(8,128)(2,1)S(1)}, u32[]{:S(2)}, u32[]{:S(2)}) %collective-permute-start.23) | collective-permute-done | bytes 2097184 | tf_op jit(solution)/shard_map/ppermute | solution.py:609
  205.8 4.6 %fusion.5 = (bf16[2,128,4096]{2,1,0:T(8,128)(2,1)}, bf16[2,128,4096]{2,1,0:T(8,128)(2,1)}) fusion(bf16[8,128,4096]{2,1,0:T(8,128)(2,1)} %get-tuple-element.105.refs_0_.refs_1_), kind=kLoop, calls=%fused_computation.27 | loop fusion | bytes 8388608 | tf_op jit(solution)/shard_map/slice | solution.py:654
  212.5 14.0 %kv_chunk.16 = (bf16[8,1025,4,128]{3,2,1,0:T(4,128)(2,1)}, bf16[8,1025,4,128]{3,2,1,0:T(4,128)(2,1)}, f32[14,8,3,8,128]{4,3,2,1,0:T(8,128)S(1)}) custom-call(bf16[2,128,4096]{2,1,0:T(8,128)(2,1)S(1)} %collective-permute-done.22.refs_0_, ...), custom_call_target="tpu_custom_call", output_to_operand_aliasing={{0}: (10, {}), {1}: (11, {}), {2}: (12, {})} | custom-call | flops 8589934592 | bytes 10485760 | tf_op jit(solution)/shard_map/kv_chunk/pallas_call | solution.py:442
  226.5 7.9 %turn.2.wg_hbm = bf16[4096,1376]{1,0:T(8,128)(2,1)S(1)} custom-call(bf16[1376,4096]{1,0:T(8,128)(2,1)} %bitcast.25), custom_call_target="tpu_custom_call" | custom-call | flops 1442840576 | bytes 22544384 | tf_op jit(solution)/shard_map/turn/pallas_call | solution.py:58
  234.4 4.2 %copy-done = bf16[4096,1376]{1,0:T(8,128)(2,1)} copy-done((bf16[4096,1376]{1,0:T(8,128)(2,1)}, bf16[4096,1376]{1,0:T(8,128)(2,1)S(1)}, u32[]{:S(2)}) %copy-start) | copy-done | bytes 11272216
  238.6 19.6 %collective-permute-done.27.refs_1_ = bf16[2,128,4096]{2,1,0:T(8,128)(2,1)S(1)} collective-permute-done((bf16[2,128,4096]{2,1,0:T(8,128)(2,1)}, bf16[2,128,4096]{2,1,0:T(8,128)(2,1)S(1)}, u32[]{:S(2)}, u32[]{:S(2)}) %collective-permute-start.27) | collective-permute-done | bytes 2097184 | tf_op jit(solution)/shard_map/ppermute | solution.py:609
  260.4 1.7 collective-permute-start.31
  262.4 3.0 collective-permute-done.29.refs_3_
  265.4 14.0 %kv_chunk.17 = (bf16[8,1025,4,128]{3,2,1,0:T(4,128)(2,1)}, bf16[8,1025,4,128]{3,2,1,0:T(4,128)(2,1)}, f32[14,8,3,8,128]{4,3,2,1,0:T(8,128)S(1)}) custom-call(bf16[2,128,4096]{2,1,0:T(8,128)(2,1)S(1)} %collective-permute-done.26.refs_0_, ...), custom_call_target="tpu_custom_call", output_to_operand_aliasing={{0}: (10, {}), {1}: (11, {}), {2}: (12, {})} | custom-call | flops 8589934592 | bytes 10485760 | tf_op jit(solution)/shard_map/kv_chunk/pallas_call | solution.py:442
  279.4 7.9 %turn.3.wu_hbm = bf16[4096,1376]{1,0:T(8,128)(2,1)S(1)} custom-call(bf16[1376,4096]{1,0:T(8,128)(2,1)} %bitcast.26), custom_call_target="tpu_custom_call" | custom-call | flops 1442840576 | bytes 22544384 | tf_op jit(solution)/shard_map/turn/pallas_call | solution.py:58
  287.3 4.2 %copy-done.1 = bf16[4096,1376]{1,0:T(8,128)(2,1)} copy-done((bf16[4096,1376]{1,0:T(8,128)(2,1)}, bf16[4096,1376]{1,0:T(8,128)(2,1)S(1)}, u32[]{:S(2)}) %copy-start.1) | copy-done | bytes 11272216
  291.5 14.8 %collective-permute-done.30.refs_1_ = bf16[2,128,4096]{2,1,0:T(8,128)(2,1)S(1)} collective-permute-done((bf16[2,128,4096]{2,1,0:T(8,128)(2,1)S(1)}, bf16[2,128,4096]{2,1,0:T(8,128)(2,1)S(1)}, u32[]{:S(2)}, u32[]{:S(2)}) %collective-permute-start.30) | collective-permute-done | bytes 2097184 | tf_op jit(solution)/shard_map/ppermute | solution.py:609
  308.5 1.7 collective-permute-start.35
  311.9 3.0 collective-permute-done.33.refs_3_
  314.9 14.0 %kv_chunk.18 = (bf16[8,1025,4,128]{3,2,1,0:T(4,128)(2,1)}, bf16[8,1025,4,128]{3,2,1,0:T(4,128)(2,1)}, f32[14,8,3,8,128]{4,3,2,1,0:T(8,128)S(1)}) custom-call(bf16[2,128,4096]{2,1,0:T(8,128)(2,1)S(1)} %collective-permute-done.31.refs_0_, ...), custom_call_target="tpu_custom_call", output_to_operand_aliasing={{0}: (10, {}), {1}: (11, {}), {2}: (12, {})} | custom-call | flops 8589934592 | bytes 10485760 | tf_op jit(solution)/shard_map/kv_chunk/pallas_call | solution.py:442
  328.8 4.4 %collective-permute-done.34.refs_1_ = bf16[1,128,4096]{2,1,0:T(8,128)(2,1)S(1)} collective-permute-done((bf16[1,128,4096]{2,1,0:T(8,128)(2,1)S(1)}, bf16[1,128,4096]{2,1,0:T(8,128)(2,1)S(1)}, u32[]{:S(2)}, u32[]{:S(2)}) %collective-permute-start.34) | collective-permute-done | bytes 1048608 | tf_op jit(solution)/shard_map/ppermute | solution.py:609
  335.5 1.7 collective-permute-start.39
  337.5 7.4 %kv_chunk.19 = (bf16[8,1025,4,128]{3,2,1,0:T(4,128)(2,1)}, bf16[8,1025,4,128]{3,2,1,0:T(4,128)(2,1)}, f32[14,8,3,8,128]{4,3,2,1,0:T(8,128)S(1)}) custom-call(bf16[1,128,4096]{2,1,0:T(8,128)(2,1)S(1)} %collective-permute-done.35.refs_0_, ...), custom_call_target="tpu_custom_call", output_to_operand_aliasing={{0}: (10, {}), {1}: (11, {}), {2}: (12, {})} | custom-call | flops 4294967296 | bytes 5242880 | tf_op jit(solution)/shard_map/kv_chunk/pallas_call | solution.py:442
  344.9 5.6 %collective-permute-done.38.refs_1_ = bf16[1,80,4096]{2,1,0:T(8,128)(2,1)S(1)} collective-permute-done((bf16[1,80,4096]{2,1,0:T(8,128)(2,1)S(1)}, bf16[1,80,4096]{2,1,0:T(8,128)(2,1)S(1)}, u32[]{:S(2)}, u32[]{:S(2)}) %collective-permute-start.38) | collective-permute-done | bytes 655392 | tf_op jit(solution)/shard_map/ppermute | solution.py:609
  352.7 1.7 collective-permute-start.43
  354.9 4.8 %kv_chunk.20 = (bf16[8,1025,4,128]{3,2,1,0:T(4,128)(2,1)}, bf16[8,1025,4,128]{3,2,1,0:T(4,128)(2,1)}, f32[14,8,3,8,128]{4,3,2,1,0:T(8,128)S(1)}) custom-call(bf16[1,80,4096]{2,1,0:T(8,128)(2,1)S(1)} %collective-permute-done.39.refs_0_, ...), custom_call_target="tpu_custom_call", output_to_operand_aliasing={{0}: (10, {}), {1}: (11, {}), {2}: (12, {})} | custom-call | flops 2684354560 | bytes 3276800 | tf_op jit(solution)/shard_map/kv_chunk/pallas_call | solution.py:442
  359.7 3.7 collective-permute-done.42.refs_1_
  365.7 3.6 kv_chunk.21
  369.3 23.6 %tail.1 = bf16[2,8,4096]{2,1,0:T(8,128)(2,1)S(1)} custom-call(f32[14,8,3,8,128]{4,3,2,1,0:T(8,128)S(1)} %get-tuple-element.198.stv, f32[3,8,8,128]{3,2,1,0:T(8,128)S(1)} %get-tuple-element.199.self_ref, bf16[16,512]{1,0:T(8,128)(2,1)S(1)} %fusion.1.xs_ref, bf16[1,4096]{1,0:T(2,128)(2,1)S(1)} %copy-done.5, bf16[512,4096]{1,0:T(8,128)(2,1)S(1)} %get-tuple-element.201.wo, ...), custom_call_target="tpu_custom_call" | custom-call | tf_op jit(solution)/shard_map/tail/pallas_call | solution.py:574
  (112 shorter events, 34.9 us)
Async XLA Ops:
  1.4 16.4 %copy-start.14 = (s32[8]{0:T(128)S(1)}, s32[8]{0:T(128)}, u32[]{:S(2)}) copy-start(s32[8]{0:T(128)} %param.13) | copy-start | bytes 100
  16.9 34.4 %collective-permute-start = (bf16[8,128,4096]{2,1,0:T(8,128)(2,1)}, bf16[8,128,4096]{2,1,0:T(8,128)(2,1)}, u32[]{:S(2)}, u32[]{:S(2)}) collective-permute-start(bf16[8,128,4096]{2,1,0:T(8,128)(2,1)} %get-tuple-element.105.refs_0_.refs_1_), channel_id=1, source_target_pairs={{0,1},{1,0},{2,3},{3,2},{4,5},{5,4},{6,7},{7,6}} | collective-permute-start | bytes 25165832 | tf_op jit(solution)/shard_map/ppermute | solution.py:609
  22.5 8.4 %collective-permute-start.1 = (bf16[8,4096]{1,0:T(8,128)(2,1)S(1)}, bf16[8,4096]{1,0:T(8,128)(2,1)S(1)}, u32[]{:S(2)}, u32[]{:S(2)}) collective-permute-start(bf16[8,4096]{1,0:T(8,128)(2,1)S(1)} %bitcast.32), channel_id=1, source_target_pairs={{0,1},{1,0},{2,3},{3,2},{4,5},{5,4},{6,7},{7,6}} | collective-permute-start | bytes 196616 | tf_op jit(solution)/shard_map/ppermute | solution.py:609
  24.7 54.5 %collective-permute-start.6 = (bf16[1,48,4096]{2,1,0:T(8,128)(2,1)}, bf16[1,48,4096]{2,1,0:T(8,128)(2,1)S(1)}, u32[]{:S(2)}, u32[]{:S(2)}) collective-permute-start(bf16[1,48,4096]{2,1,0:T(8,128)(2,1)} %get-tuple-element.121), channel_id=1, source_target_pairs={{0,4},{1,5},{2,6},{3,7},{4,0},{5,1},{6,2},{7,3}} | collective-permute-start | bytes 1179656 | tf_op jit(solution)/shard_map/ppermute | solution.py:609
  30.9 7.1 %collective-permute-start.3 = (bf16[8,2048]{1,0:T(8,128)(2,1)S(1)}, bf16[8,2048]{1,0:T(8,128)(2,1)S(1)}, u32[]{:S(2)}, u32[]{:S(2)}) collective-permute-start(bf16[8,2048]{1,0:T(8,128)(2,1)S(1)} %dynamic-slice_add_fusion), channel_id=1, source_target_pairs={{0,4},{1,5},{2,6},{3,7},{4,0},{5,1},{6,2},{7,3}} | collective-permute-start | bytes 98312 | tf_op jit(solution)/shard_map/ppermute | solution.py:609
  33.7 6.3 %collective-permute-start.2 = (bf16[8,2048]{1,0:T(8,128)(2,1)S(1)}, bf16[8,2048]{1,0:T(8,128)(2,1)S(1)}, u32[]{:S(2)}, u32[]{:S(2)}) collective-permute-start(bf16[8,2048]{1,0:T(8,128)(2,1)S(1)} %dynamic-slice_add_fusion), channel_id=1, source_target_pairs={{0,2},{1,3},{2,0},{3,1},{4,6},{5,7},{6,4},{7,5}} | collective-permute-start | bytes 98312 | tf_op jit(solution)/shard_map/ppermute | solution.py:609
  35.2 6.7 %collective-permute-start.4 = (bf16[8,2048]{1,0:T(8,128)(2,1)S(1)}, bf16[8,2048]{1,0:T(8,128)(2,1)S(1)}, u32[]{:S(2)}, u32[]{:S(2)}) collective-permute-start(bf16[8,2048]{1,0:T(8,128)(2,1)S(1)} %dynamic-slice_add_fusion), channel_id=1, source_target_pairs={{0,6},{1,7},{2,4},{3,5},{4,2},{5,3},{6,0},{7,1}} | collective-permute-start | bytes 98312 | tf_op jit(solution)/shard_map/ppermute | solution.py:609
  35.6 7.8 %copy-start.4 = (bf16[8,4096]{1,0:T(8,128)(2,1)S(1)}, bf16[8,4096]{1,0:T(8,128)(2,1)}, u32[]{:S(2)}) copy-start(bf16[8,4096]{1,0:T(8,128)(2,1)} %new_ref.1) | copy-start | bytes 196612
  38.0 41.2 %collective-permute-start.7 = (bf16[1,48,4096]{2,1,0:T(8,128)(2,1)}, bf16[1,48,4096]{2,1,0:T(8,128)(2,1)S(1)}, u32[]{:S(2)}, u32[]{:S(2)}) collective-permute-start(bf16[1,48,4096]{2,1,0:T(8,128)(2,1)} %get-tuple-element.122), channel_id=1, source_target_pairs={{0,2},{1,3},{2,0},{3,1},{4,6},{5,7},{6,4},{7,5}} | collective-permute-start | bytes 1179656 | tf_op jit(solution)/shard_map/ppermute | solution.py:609
  40.0 45.1 %collective-permute-start.10 = (bf16[1,80,4096]{2,1,0:T(8,128)(2,1)}, bf16[1,80,4096]{2,1,0:T(8,128)(2,1)S(1)}, u32[]{:S(2)}, u32[]{:S(2)}) collective-permute-start(bf16[1,80,4096]{2,1,0:T(8,128)(2,1)} %get-tuple-element.129), channel_id=1, source_target_pairs={{0,4},{1,5},{2,6},{3,7},{4,0},{5,1},{6,2},{7,3}} | collective-permute-start | bytes 1966088 | tf_op jit(solution)/shard_map/ppermute | solution.py:609
  41.9 1.2 collective-permute-start.5
  43.1 42.0 %collective-permute-start.11 = (bf16[1,80,4096]{2,1,0:T(8,128)(2,1)S(1)}, bf16[1,80,4096]{2,1,0:T(8,128)(2,1)S(1)}, u32[]{:S(2)}, u32[]{:S(2)}) collective-permute-start(bf16[1,80,4096]{2,1,0:T(8,128)(2,1)S(1)} %get-tuple-element.130), channel_id=1, source_target_pairs={{0,2},{1,3},{2,0},{3,1},{4,6},{5,7},{6,4},{7,5}} | collective-permute-start | bytes 1966088 | tf_op jit(solution)/shard_map/ppermute | solution.py:609
  79.2 1.7 collective-permute-start.8
  79.2 2.3 collective-permute-start.9
  85.1 4.0 %collective-permute-start.12 = (bf16[1,80,4096]{2,1,0:T(8,128)(2,1)S(1)}, bf16[1,80,4096]{2,1,0:T(8,128)(2,1)S(1)}, u32[]{:S(2)}, u32[]{:S(2)}) collective-permute-start(bf16[1,80,4096]{2,1,0:T(8,128)(2,1)S(1)} %collective-permute-done.10.refs_0_), channel_id=1, source_target_pairs={{0,1},{1,0},{2,3},{3,2},{4,5},{5,4},{6,7},{7,6}} | collective-permute-start | bytes 1966088 | tf_op jit(solution)/shard_map/ppermute | solution.py:609
  85.3 26.0 %collective-permute-start.14 = (bf16[1,128,4096]{2,1,0:T(8,128)(2,1)S(1)}, bf16[1,128,4096]{2,1,0:T(8,128)(2,1)S(1)}, u32[]{:S(2)}, u32[]{:S(2)}) collective-permute-start(bf16[1,128,4096]{2,1,0:T(8,128)(2,1)S(1)} %copy-done.13), channel_id=1, source_target_pairs={{0,4},{1,5},{2,6},{3,7},{4,0},{5,1},{6,2},{7,3}} | collective-permute-start | bytes 3145736 | tf_op jit(solution)/shard_map/ppermute | solution.py:609
  85.3 26.0 %collective-permute-start.15 = (bf16[1,128,4096]{2,1,0:T(8,128)(2,1)S(1)}, bf16[1,128,4096]{2,1,0:T(8,128)(2,1)S(1)}, u32[]{:S(2)}, u32[]{:S(2)}) collective-permute-start(bf16[1,128,4096]{2,1,0:T(8,128)(2,1)S(1)} %copy-done.11), channel_id=1, source_target_pairs={{0,2},{1,3},{2,0},{3,1},{4,6},{5,7},{6,4},{7,5}} | collective-permute-start | bytes 3145736 | tf_op jit(solution)/shard_map/ppermute | solution.py:609
  87.3 2.1 collective-permute-start.13
  87.3 68.4 %collective-permute-start.18 = (bf16[2,128,4096]{2,1,0:T(8,128)(2,1)S(1)}, bf16[2,128,4096]{2,1,0:T(8,128)(2,1)S(1)}, u32[]{:S(2)}, u32[]{:S(2)}) collective-permute-start(bf16[2,128,4096]{2,1,0:T(8,128)(2,1)S(1)} %copy-done.9), channel_id=1, source_target_pairs={{0,4},{1,5},{2,6},{3,7},{4,0},{5,1},{6,2},{7,3}} | collective-permute-start | bytes 6291464 | tf_op jit(solution)/shard_map/ppermute | solution.py:609
  89.2 66.6 %collective-permute-start.19 = (bf16[2,128,4096]{2,1,0:T(8,128)(2,1)S(1)}, bf16[2,128,4096]{2,1,0:T(8,128)(2,1)S(1)}, u32[]{:S(2)}, u32[]{:S(2)}) collective-permute-start(bf16[2,128,4096]{2,1,0:T(8,128)(2,1)S(1)} %copy-done.7), channel_id=1, source_target_pairs={{0,2},{1,3},{2,0},{3,1},{4,6},{5,7},{6,4},{7,5}} | collective-permute-start | bytes 6291464 | tf_op jit(solution)/shard_map/ppermute | solution.py:609
  111.3 2.7 collective-permute-start.16
  111.3 4.2 %collective-permute-start.17 = (bf16[1,128,4096]{2,1,0:T(8,128)(2,1)S(1)}, bf16[1,128,4096]{2,1,0:T(8,128)(2,1)S(1)}, u32[]{:S(2)}, u32[]{:S(2)}) collective-permute-start(bf16[1,128,4096]{2,1,0:T(8,128)(2,1)S(1)} %collective-permute-done.15.refs_1_), channel_id=1, source_target_pairs={{0,1},{1,0},{2,3},{3,2},{4,5},{5,4},{6,7},{7,6}} | collective-permute-start | bytes 3145736 | tf_op jit(solution)/shard_map/ppermute | solution.py:609
  155.8 4.2 %collective-permute-start.20 = (bf16[2,128,4096]{2,1,0:T(8,128)(2,1)S(1)}, bf16[2,128,4096]{2,1,0:T(8,128)(2,1)S(1)}, u32[]{:S(2)}, u32[]{:S(2)}) collective-permute-start(bf16[2,128,4096]{2,1,0:T(8,128)(2,1)S(1)} %collective-permute-done.18.refs_0_), channel_id=1, source_target_pairs={{0,1},{1,0},{2,3},{3,2},{4,5},{5,4},{6,7},{7,6}} | collective-permute-start | bytes 6291464 | tf_op jit(solution)/shard_map/ppermute | solution.py:609
  155.8 7.2 %collective-permute-start.21 = (bf16[2,128,4096]{2,1,0:T(8,128)(2,1)S(1)}, bf16[2,128,4096]{2,1,0:T(8,128)(2,1)S(1)}, u32[]{:S(2)}, u32[]{:S(2)}) collective-permute-start(bf16[2,128,4096]{2,1,0:T(8,128)(2,1)S(1)} %collective-permute-done.19.refs_1_), channel_id=1, source_target_pairs={{0,1},{1,0},{2,3},{3,2},{4,5},{5,4},{6,7},{7,6}} | collective-permute-start | bytes 6291464 | tf_op jit(solution)/shard_map/ppermute | solution.py:609
  156.3 47.5 %collective-permute-start.23 = (bf16[2,128,4096]{2,1,0:T(8,128)(2,1)S(1)}, bf16[2,128,4096]{2,1,0:T(8,128)(2,1)S(1)}, u32[]{:S(2)}, u32[]{:S(2)}) collective-permute-start(bf16[2,128,4096]{2,1,0:T(8,128)(2,1)S(1)} %copy-done.9), channel_id=1, source_target_pairs={{0,2},{1,3},{2,0},{3,1},{4,6},{5,7},{6,4},{7,5}} | collective-permute-start | bytes 6291464 | tf_op jit(solution)/shard_map/ppermute | solution.py:609
  158.0 47.3 %collective-permute-start.22 = (bf16[2,128,4096]{2,1,0:T(8,128)(2,1)S(1)}, bf16[2,128,4096]{2,1,0:T(8,128)(2,1)S(1)}, u32[]{:S(2)}, u32[]{:S(2)}) collective-permute-start(bf16[2,128,4096]{2,1,0:T(8,128)(2,1)S(1)} %copy-done.7), channel_id=1, source_target_pairs={{0,4},{1,5},{2,6},{3,7},{4,0},{5,1},{6,2},{7,3}} | collective-permute-start | bytes 6291464 | tf_op jit(solution)/shard_map/ppermute | solution.py:609
  205.3 7.2 %collective-permute-start.24 = (bf16[2,128,4096]{2,1,0:T(8,128)(2,1)S(1)}, bf16[2,128,4096]{2,1,0:T(8,128)(2,1)S(1)}, u32[]{:S(2)}, u32[]{:S(2)}) collective-permute-start(bf16[2,128,4096]{2,1,0:T(8,128)(2,1)S(1)} %collective-permute-done.22.refs_0_), channel_id=1, source_target_pairs={{0,1},{1,0},{2,3},{3,2},{4,5},{5,4},{6,7},{7,6}} | collective-permute-start | bytes 6291464 | tf_op jit(solution)/shard_map/ppermute | solution.py:609
  205.3 7.2 %collective-permute-start.25 = (bf16[2,128,4096]{2,1,0:T(8,128)(2,1)S(1)}, bf16[2,128,4096]{2,1,0:T(8,128)(2,1)S(1)}, u32[]{:S(2)}, u32[]{:S(2)}) collective-permute-start(bf16[2,128,4096]{2,1,0:T(8,128)(2,1)S(1)} %collective-permute-done.23.refs_1_), channel_id=1, source_target_pairs={{0,1},{1,0},{2,3},{3,2},{4,5},{5,4},{6,7},{7,6}} | collective-permute-start | bytes 6291464 | tf_op jit(solution)/shard_map/ppermute | solution.py:609
  210.5 47.7 %collective-permute-start.27 = (bf16[2,128,4096]{2,1,0:T(8,128)(2,1)}, bf16[2,128,4096]{2,1,0:T(8,128)(2,1)S(1)}, u32[]{:S(2)}, u32[]{:S(2)}) collective-permute-start(bf16[2,128,4096]{2,1,0:T(8,128)(2,1)} %get-tuple-element.206), channel_id=1, source_target_pairs={{0,2},{1,3},{2,0},{3,1},{4,6},{5,7},{6,4},{7,5}} | collective-permute-start | bytes 6291464 | tf_op jit(solution)/shard_map/ppermute | solution.py:609
  210.7 47.5 %collective-permute-start.26 = (bf16[2,128,4096]{2,1,0:T(8,128)(2,1)}, bf16[2,128,4096]{2,1,0:T(8,128)(2,1)S(1)}, u32[]{:S(2)}, u32[]{:S(2)}) collective-permute-start(bf16[2,128,4096]{2,1,0:T(8,128)(2,1)} %get-tuple-element.207), channel_id=1, source_target_pairs={{0,4},{1,5},{2,6},{3,7},{4,0},{5,1},{6,2},{7,3}} | collective-permute-start | bytes 6291464 | tf_op jit(solution)/shard_map/ppermute | solution.py:609
  258.2 4.2 %collective-permute-start.28 = (bf16[2,128,4096]{2,1,0:T(8,128)(2,1)S(1)}, bf16[2,128,4096]{2,1,0:T(8,128)(2,1)S(1)}, u32[]{:S(2)}, u32[]{:S(2)}) collective-permute-start(bf16[2,128,4096]{2,1,0:T(8,128)(2,1)S(1)} %collective-permute-done.26.refs_0_), channel_id=1, source_target_pairs={{0,1},{1,0},{2,3},{3,2},{4,5},{5,4},{6,7},{7,6}} | collective-permute-start | bytes 6291464 | tf_op jit(solution)/shard_map/ppermute | solution.py:609
  258.2 7.2 %collective-permute-start.29 = (bf16[2,128,4096]{2,1,0:T(8,128)(2,1)S(1)}, bf16[2,128,4096]{2,1,0:T(8,128)(2,1)S(1)}, u32[]{:S(2)}, u32[]{:S(2)}) collective-permute-start(bf16[2,128,4096]{2,1,0:T(8,128)(2,1)S(1)} %collective-permute-done.27.refs_1_), channel_id=1, source_target_pairs={{0,1},{1,0},{2,3},{3,2},{4,5},{5,4},{6,7},{7,6}} | collective-permute-start | bytes 6291464 | tf_op jit(solution)/shard_map/ppermute | solution.py:609
  258.7 47.5 %collective-permute-start.30 = (bf16[2,128,4096]{2,1,0:T(8,128)(2,1)S(1)}, bf16[2,128,4096]{2,1,0:T(8,128)(2,1)S(1)}, u32[]{:S(2)}, u32[]{:S(2)}) collective-permute-start(bf16[2,128,4096]{2,1,0:T(8,128)(2,1)S(1)} %collective-permute-done.19.refs_1_), channel_id=1, source_target_pairs={{0,4},{1,5},{2,6},{3,7},{4,0},{5,1},{6,2},{7,3}} | collective-permute-start | bytes 6291464 | tf_op jit(solution)/shard_map/ppermute | solution.py:609
  260.4 47.3 %collective-permute-start.31 = (bf16[2,128,4096]{2,1,0:T(8,128)(2,1)S(1)}, bf16[2,128,4096]{2,1,0:T(8,128)(2,1)S(1)}, u32[]{:S(2)}, u32[]{:S(2)}) collective-permute-start(bf16[2,128,4096]{2,1,0:T(8,128)(2,1)S(1)} %collective-permute-done.18.refs_0_), channel_id=1, source_target_pairs={{0,2},{1,3},{2,0},{3,1},{4,6},{5,7},{6,4},{7,5}} | collective-permute-start | bytes 6291464 | tf_op jit(solution)/shard_map/ppermute | solution.py:609
  307.7 4.2 %collective-permute-start.32 = (bf16[2,128,4096]{2,1,0:T(8,128)(2,1)S(1)}, bf16[2,128,4096]{2,1,0:T(8,128)(2,1)S(1)}, u32[]{:S(2)}, u32[]{:S(2)}) collective-permute-start(bf16[2,128,4096]{2,1,0:T(8,128)(2,1)S(1)} %collective-permute-done.31.refs_0_), channel_id=1, source_target_pairs={{0,1},{1,0},{2,3},{3,2},{4,5},{5,4},{6,7},{7,6}} | collective-permute-start | bytes 6291464 | tf_op jit(solution)/shard_map/ppermute | solution.py:609
  307.7 7.2 %collective-permute-start.33 = (bf16[2,128,4096]{2,1,0:T(8,128)(2,1)S(1)}, bf16[2,128,4096]{2,1,0:T(8,128)(2,1)S(1)}, u32[]{:S(2)}, u32[]{:S(2)}) collective-permute-start(bf16[2,128,4096]{2,1,0:T(8,128)(2,1)S(1)} %collective-permute-done.30.refs_1_), channel_id=1, source_target_pairs={{0,1},{1,0},{2,3},{3,2},{4,5},{5,4},{6,7},{7,6}} | collective-permute-start | bytes 6291464 | tf_op jit(solution)/shard_map/ppermute | solution.py:609
  308.2 25.1 %collective-permute-start.34 = (bf16[1,128,4096]{2,1,0:T(8,128)(2,1)S(1)}, bf16[1,128,4096]{2,1,0:T(8,128)(2,1)S(1)}, u32[]{:S(2)}, u32[]{:S(2)}) collective-permute-start(bf16[1,128,4096]{2,1,0:T(8,128)(2,1)S(1)} %collective-permute-done.15.refs_1_), channel_id=1, source_target_pairs={{0,4},{1,5},{2,6},{3,7},{4,0},{5,1},{6,2},{7,3}} | collective-permute-start | bytes 3145736 | tf_op jit(solution)/shard_map/ppermute | solution.py:609
  308.5 24.8 %collective-permute-start.35 = (bf16[1,128,4096]{2,1,0:T(8,128)(2,1)S(1)}, bf16[1,128,4096]{2,1,0:T(8,128)(2,1)S(1)}, u32[]{:S(2)}, u32[]{:S(2)}) collective-permute-start(bf16[1,128,4096]{2,1,0:T(8,128)(2,1)S(1)} %collective-permute-done.14.refs_0_), channel_id=1, source_target_pairs={{0,2},{1,3},{2,0},{3,1},{4,6},{5,7},{6,4},{7,5}} | collective-permute-start | bytes 3145736 | tf_op jit(solution)/shard_map/ppermute | solution.py:609
  333.3 4.0 %collective-permute-start.36 = (bf16[1,128,4096]{2,1,0:T(8,128)(2,1)S(1)}, bf16[1,128,4096]{2,1,0:T(8,128)(2,1)S(1)}, u32[]{:S(2)}, u32[]{:S(2)}) collective-permute-start(bf16[1,128,4096]{2,1,0:T(8,128)(2,1)S(1)} %collective-permute-done.35.refs_0_), channel_id=1, source_target_pairs={{0,1},{1,0},{2,3},{3,2},{4,5},{5,4},{6,7},{7,6}} | collective-permute-start | bytes 3145736 | tf_op jit(solution)/shard_map/ppermute | solution.py:609
  333.3 4.2 %collective-permute-start.37 = (bf16[1,128,4096]{2,1,0:T(8,128)(2,1)S(1)}, bf16[1,128,4096]{2,1,0:T(8,128)(2,1)S(1)}, u32[]{:S(2)}, u32[]{:S(2)}) collective-permute-start(bf16[1,128,4096]{2,1,0:T(8,128)(2,1)S(1)} %collective-permute-done.34.refs_1_), channel_id=1, source_target_pairs={{0,1},{1,0},{2,3},{3,2},{4,5},{5,4},{6,7},{7,6}} | collective-permute-start | bytes 3145736 | tf_op jit(solution)/shard_map/ppermute | solution.py:609
  333.8 16.6 %collective-permute-start.38 = (bf16[1,80,4096]{2,1,0:T(8,128)(2,1)S(1)}, bf16[1,80,4096]{2,1,0:T(8,128)(2,1)S(1)}, u32[]{:S(2)}, u32[]{:S(2)}) collective-permute-start(bf16[1,80,4096]{2,1,0:T(8,128)(2,1)S(1)} %collective-permute-done.11.refs_1_), channel_id=1, source_target_pairs={{0,4},{1,5},{2,6},{3,7},{4,0},{5,1},{6,2},{7,3}} | collective-permute-start | bytes 1966088 | tf_op jit(solution)/shard_map/ppermute | solution.py:609
  335.5 16.4 %collective-permute-start.39 = (bf16[1,80,4096]{2,1,0:T(8,128)(2,1)S(1)}, bf16[1,80,4096]{2,1,0:T(8,128)(2,1)S(1)}, u32[]{:S(2)}, u32[]{:S(2)}) collective-permute-start(bf16[1,80,4096]{2,1,0:T(8,128)(2,1)S(1)} %collective-permute-done.10.refs_0_), channel_id=1, source_target_pairs={{0,2},{1,3},{2,0},{3,1},{4,6},{5,7},{6,4},{7,5}} | collective-permute-start | bytes 1966088 | tf_op jit(solution)/shard_map/ppermute | solution.py:609
  351.9 2.6 collective-permute-start.40
  351.9 3.0 collective-permute-start.41
  352.4 11.0 %collective-permute-start.42 = (bf16[1,48,4096]{2,1,0:T(8,128)(2,1)S(1)}, bf16[1,48,4096]{2,1,0:T(8,128)(2,1)S(1)}, u32[]{:S(2)}, u32[]{:S(2)}) collective-permute-start(bf16[1,48,4096]{2,1,0:T(8,128)(2,1)S(1)} %collective-permute-done.7.refs_1_), channel_id=1, source_target_pairs={{0,4},{1,5},{2,6},{3,7},{4,0},{5,1},{6,2},{7,3}} | collective-permute-start | bytes 1179656 | tf_op jit(solution)/shard_map/ppermute | solution.py:609
  352.7 10.7 %collective-permute-start.43 = (bf16[1,48,4096]{2,1,0:T(8,128)(2,1)S(1)}, bf16[1,48,4096]{2,1,0:T(8,128)(2,1)S(1)}, u32[]{:S(2)}, u32[]{:S(2)}) collective-permute-start(bf16[1,48,4096]{2,1,0:T(8,128)(2,1)S(1)} %collective-permute-done.6.refs_0_), channel_id=1, source_target_pairs={{0,2},{1,3},{2,0},{3,1},{4,6},{5,7},{6,4},{7,5}} | collective-permute-start | bytes 1179656 | tf_op jit(solution)/shard_map/ppermute | solution.py:609
  363.5 1.7 collective-permute-start.44
  363.5 2.3 collective-permute-start.45
  (13 other events, 43.0 us)

commit v11 on v8

--- a/solution.py
+++ b/solution.py
@@ -147,6 +147,28 @@
             return carry
 
         lax.fori_loop(0, rows // NORM_ROWS, norm_rows, 0)
+
+
+def raw_kernel(places, rows, x_hbm, *refs):
+    n = len(places)
+    copies = [pltpu.make_async_copy(x_hbm.at[bat, pl.ds(row0, rows)], refs[i].at[0], refs[n].at[i]) for i, (bat, row0) in enumerate(places)]
+    for copy in copies:
+        copy.start()
+    for copy in copies:
+        copy.wait()
+
+
+def raw_call(x, places, rows):
+    d_model = x.shape[2]
+    return pl.pallas_call(
+        functools.partial(raw_kernel, places, rows),
+        out_shape=[pltpu.VMEM((1, rows, d_model), jnp.bfloat16)] * len(places),
+        in_specs=[pl.BlockSpec(memory_space=pl.ANY)],
+        out_specs=[pl.BlockSpec(memory_space=pltpu.VMEM)] * len(places),
+        scratch_shapes=[pltpu.SemaphoreType.DMA((len(places),))],
+        compiler_params=pltpu.CompilerParams(vmem_limit_bytes=8 * 2 ** 20),
+        name="raw_rows",
+    )(pltpu.with_memory_space_constraint(x, pltpu.HBM))
 
 
 def first_call(x, gain, places, rows):
@@ -270,12 +292,14 @@
     return out
 
 
-def kv_kernel(n_in, n_steps, masks, batches, firsts, row0, stat_of, with_new, *refs):
+def kv_kernel(n_in, n_steps, masks, batches, firsts, row0, stat_of, with_new, raw, *refs):
     n_groups = len(masks)
     n_arr = n_in * n_groups
     x_refs = refs[:n_arr]
     cos_ref, sin_ref, len_ref, wk, wv, q_ref = refs[n_arr:n_arr + 6]
     rest = refs[n_arr + 6:]
+    if raw:
+        gain_ref, *rest = rest
     if with_new:
         new_refs = rest[:2]
         rest = rest[2:]
@@ -342,6 +366,22 @@
     for copy in x_copies(0, slot, 0):
         copy.wait()
     x_rows = x_buf.at[slot]
+    if raw:
+        lanes = [slice(c * HEAD_DIM, (c + 1) * HEAD_DIM) for c in range(x_buf.shape[3] // HEAD_DIM)]
+        for i in range(n_in):
+            def norm_rows(r, carry, i=i):
+                at = pl.ds(pl.multiple_of(r * NORM_ROWS, NORM_ROWS), NORM_ROWS)
+                acc = [jnp.zeros((NORM_ROWS, HEAD_DIM), jnp.float32) for _ in range(2)]
+                for c, lane in enumerate(lanes):
+                    xf = x_rows[i, at, lane].astype(jnp.float32)
+                    acc[c % 2] += xf * xf
+                inv_rms = lax.rsqrt(jnp.sum(acc[0] + acc[1], axis=-1, keepdims=True) / x_buf.shape[3] + 1e-5)
+                for lane in lanes:
+                    xf = x_rows[i, at, lane].astype(jnp.float32)
+                    x_rows[i, at, lane] = (xf * inv_rms * gain_ref[:, lane].astype(jnp.float32)).astype(jnp.bfloat16)
+                return carry
+
+            lax.fori_loop(0, blk // NORM_ROWS, norm_rows, 0)
 
     def col_tile(c, carry):
         cols = pl.ds(pl.multiple_of(c * COL_TILE, COL_TILE), COL_TILE) if n_steps > 1 else slice(c * COL_TILE, (c + 1) * COL_TILE)
@@ -414,7 +454,7 @@
                 copy.wait()
 
 
-def kv_call(groups, per_group, masks, batches, lengths, tabs, w_k, w_v, q_diag, caches, new_rows=None, row0=0, stat_of=0):
+def kv_call(groups, per_group, masks, batches, lengths, tabs, w_k, w_v, q_diag, caches, new_rows=None, row0=0, stat_of=0, gain=None):
     n_groups = len(groups)
     n_in = len(groups[0])
     n_steps = n_groups * per_group
@@ -426,6 +466,9 @@
     operands = [arr for group in groups for arr, _ in group]
     in_specs = [any_spec] * len(operands) + [pl.BlockSpec(memory_space=pltpu.VMEM)] * 6
     operands += [cos_tab, sin_tab, lengths, w_k, w_v, q_diag]
+    if gain is not None:
+        in_specs.append(pl.BlockSpec(memory_space=pltpu.VMEM))
+        operands.append(gain)
     with_new = new_rows is not None
     if with_new:
         operands += new_rows
@@ -439,7 +482,7 @@
     n_batch = q_diag.shape[0]
     slots = min(n_steps, 2)
     return pl.pallas_call(
-        functools.partial(kv_kernel, n_in, n_steps, masks, batches, [[first for _, first in group] for group in groups], row0, stat_of, with_new),
+        functools.partial(kv_kernel, n_in, n_steps, masks, batches, [[first for _, first in group] for group in groups], row0, stat_of, with_new, gain is not None),
         grid=(n_steps,) if n_steps > 1 else (),
         in_specs=in_specs,
         out_specs=[any_spec] * 3,
@@ -619,8 +662,8 @@
 
         q1, q2, rows_h = 1, n_batch // 4, blk // 2
         a_parts, b_parts = {}, {}
-        for h, name in enumerate(("0a", "0b")):
-            a_parts[name], b_parts[name] = first_call(prompt, norm_attn, [(0, h * rows_h), (half, h * rows_h)], rows_h)
+        a_parts["0a"], b_parts["0a"] = raw_call(prompt, [(0, 0), (half, 0)], rows_h)
+        a_parts["0b"], b_parts["0b"] = first_call(prompt, norm_attn, [(0, rows_h), (half, rows_h)], rows_h)
         from_y, from_x = {}, {}
 
         def send_part(step, along_y, along_x):
@@ -644,7 +687,8 @@
         core, cols_h = my_idx % 2, d_model // 2
         last_x = last_x + swap(last_x, 1)
         last_x = lax.dynamic_slice_in_dim(last_x, core * cols_h, cols_h, axis=1)
-        last_x = (last_x + swap(last_x, 2)) + (swap(last_x, 4) + swap(last_x, 6))
+        last_x = last_x + swap(last_x, 2)
+        last_x = last_x + swap(last_x, 4)
         other_x = swap(last_x, 1)
         last_x = jnp.where(core == 0, jnp.concatenate([last_x, other_x], axis=1), jnp.concatenate([other_x, last_x], axis=1))
         send_part("2", a_parts["2"], b_parts["2"])
@@ -668,7 +712,7 @@
             return kv_call(groups, per_group, masks, batches, len_rows, tabs, wk, wv, q_diag, caches, **kw)
 
         def half_rows(step):
-            return {"row0": rows_h * (step == "0b"), "stat_of": (n_dev - 2) * (step == "0b")}
+            return {"row0": rows_h * (step == "0b"), "stat_of": (n_dev - 2) * (step == "0b"), "gain": norm_attn if step == "0a" else None}
 
         def after(caches, *arrays):
             out = lax.optimization_barrier((caches[2], *arrays))

time: 407 us -> 408 us (level)
    ppermute x46 -> x45, waiting for transfers between devices: 171 us -> 172 us  [swap(): return lax.ppermute(arr, 'model', [(i, i ^ bit) for i in range(n_dev)])]
    ppermute x46 -> x45, starting transfers between devices: 30.9 us -> 32.1 us  [swap(): return lax.ppermute(arr, 'model', [(i, i ^ bit) for i in range(n_dev)])]
  transfers between devices with their start and end apart: 46 -> 45, of which waited for: 34 -> 32; matrix products, arithmetic and copies ran while one was open for 4% -> 3% of each run, Pallas kernels for 34% -> 34%
where the time goes in v11:
time: 408 us
  Pallas kernels  177 us (43%)
  waiting for transfers between devices  172 us (42%)
  starting transfers between devices  32.1 us (8%)
  local copies, waits for them, and re-layouts  18.3 us (4%)
  matrix products  4.57 us (1%)
    ppermute x45, waiting for transfers between devices, swap(): return lax.ppermute(arr, 'model', [(i, i ^ bit) for i in range(n_dev)])  172 us
    pallas_call x11, Pallas kernels, kv_call(): pl.pallas_call(functools.partial(kv_kernel, n_in, n_steps, masks, batches...  116 us
    ppermute x45, starting transfers between devices, swap(): return lax.ppermute(arr, 'model', [(i, i ^ bit) for i in range(n_dev)])  32.1 us
    pallas_call x1, Pallas kernels, tail_call(): pl.pallas_call(functools.partial(tail_kernel, n_dev, parts_of), out_shape...  22.5 us
    pallas_call x2, Pallas kernels, turn_call(): pl.pallas_call(turn_kernel, grid=(d // cols,), in_specs=[pl.BlockSpec((n,...  15.8 us
    unnamed x28, local copies, waits for them, and re-layouts  12.8 us
    pallas_call x1, Pallas kernels, norm_call(): pl.pallas_call(functools.partial(norm_kernel, outs_of), grid=(len(order),...  10.8 us
  transfers between devices with their start and end apart: 45, of which 32 were waited for; matrix products, arithmetic and copies ran while one was open for 3% of the time, Pallas kernels for 34%

profile of v11, /device:TPU:0, one launch (start us, length us, event | category | flops | bytes accessed | tf_op | source)
XLA Modules:
  0.0 407.7 jit_solution(7282191581972972022)
XLA Ops:
  1.4 10.8 %norm_rows.1 = (bf16[1,128,4096]{2,1,0:T(8,128)(2,1)S(1)}, bf16[1,128,4096]{2,1,0:T(8,128)(2,1)S(1)}, bf16[2,128,4096]{2,1,0:T(8,128)(2,1)S(1)}, bf16[2,128,4096]{2,1,0:T(8,128)(2,1)S(1)}, bf16[8,128,4096]{2,1,0:T(8,128)(2,1)}) custom-call(bf16[8,128,4096]{2,1,0:T(8,128)(2,1)} %x_hbm.3, bf16[1,4096]{1,0:T(2,128)(2,1)S(1)} %copy-done.2), custom_call_target="tpu_custom_call" | custom-call | flops 33554432 | bytes 25165824 | tf_op jit(solution)/shard_map/norm_rows/pallas_call | solution.py:202
  16.8 4.6 %fusion.2 = bf16[8,1,4096]{2,1,0:T(2,128)(2,1)S(1)} fusion(bf16[8,128,4096]{2,1,0:T(8,128)(2,1)} %x_hbm.3, pred[8,128,1]{1,0,2:T(8,128)(4,1)S(1)} %compare_bitcast_fusion), kind=kOutput, calls=%fused_computation.13 | convolution fusion | flops 8388608 | bytes 8455168 | tf_op jit(solution)/shard_map/bs,bsd->bd/dot_general | solution.py:686
  21.5 2.2 raw_rows.1
  23.7 3.0 collective-permute-start.5
  28.3 1.9 fusion
  30.3 2.5 collective-permute-start.2
  32.9 8.4 %collective-permute-done.2 = bf16[8,2048]{1,0:T(8,128)(2,1)S(1)} collective-permute-done((bf16[8,2048]{1,0:T(8,128)(2,1)S(1)}, bf16[8,2048]{1,0:T(8,128)(2,1)S(1)}, u32[]{:S(2)}, u32[]{:S(2)}) %collective-permute-start.2) | collective-permute-done | bytes 32800 | tf_op jit(solution)/shard_map/ppermute | solution.py:651
  41.9 3.3 collective-permute-done.3
  46.5 4.7 %keep.1 = (bf16[4096,512]{1,0:T(8,128)(2,1)S(1)}, bf16[4096,512]{1,0:T(8,128)(2,1)S(1)}, bf16[512,4096]{1,0:T(8,128)(2,1)S(1)}) custom-call(bf16[4096,512]{1,0:T(8,128)(2,1)} %bitcast.28, bf16[4096,512]{1,0:T(8,128)(2,1)} %bitcast.29, bf16[512,4096]{1,0:T(8,128)(2,1)} %bitcast.30), custom_call_target="tpu_custom_call" | custom-call | tf_op jit(solution)/shard_map/keep/pallas_call | solution.py:39
  51.3 3.1 query_rows.1
  54.4 27.9 %kv_chunk.11 = (bf16[8,1025,4,128]{3,2,1,0:T(4,128)(2,1)}, bf16[8,1025,4,128]{3,2,1,0:T(4,128)(2,1)}, f32[14,8,3,8,128]{4,3,2,1,0:T(8,128)S(1)}) custom-call(bf16[8,128,4096]{2,1,0:T(8,128)(2,1)} %get-tuple-element.105.refs_0_.refs_1_, bf16[8,128,4096]{2,1,0:T(8,128)(2,1)} %get-tuple-element.105.refs_0_.refs_1_, ...), custom_call_target="tpu_custom_call" | custom-call | flops 17179869184 | bytes 20971520 | tf_op jit(solution)/shard_map/kv_chunk/pallas_call | solution.py:484
  82.8 1.7 first_rows.1
  84.9 1.7 collective-permute-start.10
  86.6 4.9 %kv_chunk.12 = (bf16[8,1025,4,128]{3,2,1,0:T(4,128)(2,1)}, bf16[8,1025,4,128]{3,2,1,0:T(4,128)(2,1)}, f32[14,8,3,8,128]{4,3,2,1,0:T(8,128)S(1)}) custom-call(bf16[1,64,4096]{2,1,0:T(8,128)(2,1)S(1)} %collective-permute-done.5.refs_0_, ...), custom_call_target="tpu_custom_call", output_to_operand_aliasing={{0}: (11, {}), {1}: (12, {}), {2}: (13, {})} | custom-call | flops 2147483648 | bytes 2621440 | tf_op jit(solution)/shard_map/kv_chunk/pallas_call | solution.py:484
  91.5 7.1 %collective-permute-done.9.refs_0_ = bf16[1,64,4096]{2,1,0:T(8,128)(2,1)S(1)} collective-permute-done((bf16[1,64,4096]{2,1,0:T(8,128)(2,1)S(1)}, bf16[1,64,4096]{2,1,0:T(8,128)(2,1)S(1)}, u32[]{:S(2)}, u32[]{:S(2)}) %collective-permute-start.9) | collective-permute-done | bytes 524320 | tf_op jit(solution)/shard_map/ppermute | solution.py:651
  98.6 1.7 collective-permute-start.13
  103.7 3.7 kv_chunk.13
  107.5 17.2 %collective-permute-done.13.refs_0_ = bf16[1,128,4096]{2,1,0:T(8,128)(2,1)S(1)} collective-permute-done((bf16[1,128,4096]{2,1,0:T(8,128)(2,1)S(1)}, bf16[1,128,4096]{2,1,0:T(8,128)(2,1)S(1)}, u32[]{:S(2)}, u32[]{:S(2)}) %collective-permute-start.13) | collective-permute-done | bytes 1048608 | tf_op jit(solution)/shard_map/ppermute | solution.py:651
  124.7 1.7 collective-permute-done.14.refs_1_
  126.9 2.1 collective-permute-done.15.refs_2_
  130.5 7.4 %kv_chunk.14 = (bf16[8,1025,4,128]{3,2,1,0:T(4,128)(2,1)}, bf16[8,1025,4,128]{3,2,1,0:T(4,128)(2,1)}, f32[14,8,3,8,128]{4,3,2,1,0:T(8,128)S(1)}) custom-call(bf16[1,128,4096]{2,1,0:T(8,128)(2,1)S(1)} %collective-permute-done.13.refs_0_, ...), custom_call_target="tpu_custom_call", output_to_operand_aliasing={{0}: (10, {}), {1}: (11, {}), {2}: (12, {})} | custom-call | flops 4294967296 | bytes 5242880 | tf_op jit(solution)/shard_map/kv_chunk/pallas_call | solution.py:484
  137.9 31.2 %collective-permute-done.17.refs_0_ = bf16[2,128,4096]{2,1,0:T(8,128)(2,1)S(1)} collective-permute-done((bf16[2,128,4096]{2,1,0:T(8,128)(2,1)S(1)}, bf16[2,128,4096]{2,1,0:T(8,128)(2,1)S(1)}, u32[]{:S(2)}, u32[]{:S(2)}) %collective-permute-start.17) | collective-permute-done | bytes 2097184 | tf_op jit(solution)/shard_map/ppermute | solution.py:651
  174.7 3.0 collective-permute-done.20.refs_3_
  177.7 14.0 %kv_chunk.15 = (bf16[8,1025,4,128]{3,2,1,0:T(4,128)(2,1)}, bf16[8,1025,4,128]{3,2,1,0:T(4,128)(2,1)}, f32[14,8,3,8,128]{4,3,2,1,0:T(8,128)S(1)}) custom-call(bf16[2,128,4096]{2,1,0:T(8,128)(2,1)S(1)} %collective-permute-done.17.refs_0_, ...), custom_call_target="tpu_custom_call", output_to_operand_aliasing={{0}: (10, {}), {1}: (11, {}), {2}: (12, {})} | custom-call | flops 8589934592 | bytes 10485760 | tf_op jit(solution)/shard_map/kv_chunk/pallas_call | solution.py:484
  191.8 26.9 %collective-permute-done.22.refs_1_ = bf16[2,128,4096]{2,1,0:T(8,128)(2,1)S(1)} collective-permute-done((bf16[2,128,4096]{2,1,0:T(8,128)(2,1)S(1)}, bf16[2,128,4096]{2,1,0:T(8,128)(2,1)S(1)}, u32[]{:S(2)}, u32[]{:S(2)}) %collective-permute-start.22) | collective-permute-done | bytes 2097184 | tf_op jit(solution)/shard_map/ppermute | solution.py:651
  220.3 4.7 %fusion.5 = (bf16[2,128,4096]{2,1,0:T(8,128)(2,1)}, bf16[2,128,4096]{2,1,0:T(8,128)(2,1)}) fusion(bf16[8,128,4096]{2,1,0:T(8,128)(2,1)} %get-tuple-element.105.refs_0_.refs_1_), kind=kLoop, calls=%fused_computation.26 | loop fusion | bytes 8388608 | tf_op jit(solution)/shard_map/slice | solution.py:696
  227.0 14.0 %kv_chunk.16 = (bf16[8,1025,4,128]{3,2,1,0:T(4,128)(2,1)}, bf16[8,1025,4,128]{3,2,1,0:T(4,128)(2,1)}, f32[14,8,3,8,128]{4,3,2,1,0:T(8,128)S(1)}) custom-call(bf16[2,128,4096]{2,1,0:T(8,128)(2,1)S(1)} %collective-permute-done.21.refs_0_, ...), custom_call_target="tpu_custom_call", output_to_operand_aliasing={{0}: (10, {}), {1}: (11, {}), {2}: (12, {})} | custom-call | flops 8589934592 | bytes 10485760 | tf_op jit(solution)/shard_map/kv_chunk/pallas_call | solution.py:484
  241.0 7.9 %turn.2.wg_hbm = bf16[4096,1376]{1,0:T(8,128)(2,1)S(1)} custom-call(bf16[1376,4096]{1,0:T(8,128)(2,1)} %bitcast.25), custom_call_target="tpu_custom_call" | custom-call | flops 1442840576 | bytes 22544384 | tf_op jit(solution)/shard_map/turn/pallas_call | solution.py:57
  248.9 4.2 %copy-done = bf16[4096,1376]{1,0:T(8,128)(2,1)} copy-done((bf16[4096,1376]{1,0:T(8,128)(2,1)}, bf16[4096,1376]{1,0:T(8,128)(2,1)S(1)}, u32[]{:S(2)}) %copy-start) | copy-done | bytes 11272216
  253.1 19.6 %collective-permute-done.26.refs_1_ = bf16[2,128,4096]{2,1,0:T(8,128)(2,1)S(1)} collective-permute-done((bf16[2,128,4096]{2,1,0:T(8,128)(2,1)}, bf16[2,128,4096]{2,1,0:T(8,128)(2,1)S(1)}, u32[]{:S(2)}, u32[]{:S(2)}) %collective-permute-start.26) | collective-permute-done | bytes 2097184 | tf_op jit(solution)/shard_map/ppermute | solution.py:651
  273.8 1.7 collective-permute-start.30
  277.2 3.0 collective-permute-done.28.refs_3_
  280.2 14.0 %kv_chunk.17 = (bf16[8,1025,4,128]{3,2,1,0:T(4,128)(2,1)}, bf16[8,1025,4,128]{3,2,1,0:T(4,128)(2,1)}, f32[14,8,3,8,128]{4,3,2,1,0:T(8,128)S(1)}) custom-call(bf16[2,128,4096]{2,1,0:T(8,128)(2,1)S(1)} %collective-permute-done.25.refs_0_, ...), custom_call_target="tpu_custom_call", output_to_operand_aliasing={{0}: (10, {}), {1}: (11, {}), {2}: (12, {})} | custom-call | flops 8589934592 | bytes 10485760 | tf_op jit(solution)/shard_map/kv_chunk/pallas_call | solution.py:484
  294.2 7.9 %turn.3.wu_hbm = bf16[4096,1376]{1,0:T(8,128)(2,1)S(1)} custom-call(bf16[1376,4096]{1,0:T(8,128)(2,1)} %bitcast.26), custom_call_target="tpu_custom_call" | custom-call | flops 1442840576 | bytes 22544384 | tf_op jit(solution)/shard_map/turn/pallas_call | solution.py:57
  302.1 4.2 %copy-done.1 = bf16[4096,1376]{1,0:T(8,128)(2,1)} copy-done((bf16[4096,1376]{1,0:T(8,128)(2,1)}, bf16[4096,1376]{1,0:T(8,128)(2,1)S(1)}, u32[]{:S(2)}) %copy-start.1) | copy-done | bytes 11272216
  306.3 14.8 %collective-permute-done.29.refs_1_ = bf16[2,128,4096]{2,1,0:T(8,128)(2,1)S(1)} collective-permute-done((bf16[2,128,4096]{2,1,0:T(8,128)(2,1)S(1)}, bf16[2,128,4096]{2,1,0:T(8,128)(2,1)S(1)}, u32[]{:S(2)}, u32[]{:S(2)}) %collective-permute-start.29) | collective-permute-done | bytes 2097184 | tf_op jit(solution)/shard_map/ppermute | solution.py:651
  321.6 1.7 collective-permute-start.33
  325.2 3.0 collective-permute-done.32.refs_3_
  328.2 14.0 %kv_chunk.18 = (bf16[8,1025,4,128]{3,2,1,0:T(4,128)(2,1)}, bf16[8,1025,4,128]{3,2,1,0:T(4,128)(2,1)}, f32[14,8,3,8,128]{4,3,2,1,0:T(8,128)S(1)}) custom-call(bf16[2,128,4096]{2,1,0:T(8,128)(2,1)S(1)} %collective-permute-done.30.refs_0_, ...), custom_call_target="tpu_custom_call", output_to_operand_aliasing={{0}: (10, {}), {1}: (11, {}), {2}: (12, {})} | custom-call | flops 8589934592 | bytes 10485760 | tf_op jit(solution)/shard_map/kv_chunk/pallas_call | solution.py:484
  342.2 4.4 %collective-permute-done.33.refs_1_ = bf16[1,128,4096]{2,1,0:T(8,128)(2,1)S(1)} collective-permute-done((bf16[1,128,4096]{2,1,0:T(8,128)(2,1)S(1)}, bf16[1,128,4096]{2,1,0:T(8,128)(2,1)S(1)}, u32[]{:S(2)}, u32[]{:S(2)}) %collective-permute-start.33) | collective-permute-done | bytes 1048608 | tf_op jit(solution)/shard_map/ppermute | solution.py:651
  348.9 1.7 collective-permute-start.38
  352.3 7.4 %kv_chunk.19 = (bf16[8,1025,4,128]{3,2,1,0:T(4,128)(2,1)}, bf16[8,1025,4,128]{3,2,1,0:T(4,128)(2,1)}, f32[14,8,3,8,128]{4,3,2,1,0:T(8,128)S(1)}) custom-call(bf16[1,128,4096]{2,1,0:T(8,128)(2,1)S(1)} %collective-permute-done.34.refs_0_, ...), custom_call_target="tpu_custom_call", output_to_operand_aliasing={{0}: (10, {}), {1}: (11, {}), {2}: (12, {})} | custom-call | flops 4294967296 | bytes 5242880 | tf_op jit(solution)/shard_map/kv_chunk/pallas_call | solution.py:484
  359.6 2.8 collective-permute-done.37.refs_1_
  363.0 1.7 collective-permute-start.41
  366.2 5.1 %kv_chunk.20 = (bf16[8,1025,4,128]{3,2,1,0:T(4,128)(2,1)}, bf16[8,1025,4,128]{3,2,1,0:T(4,128)(2,1)}, f32[14,8,3,8,128]{4,3,2,1,0:T(8,128)S(1)}) custom-call(bf16[1,64,4096]{2,1,0:T(8,128)(2,1)S(1)} %collective-permute-done.38.refs_0_, ...), custom_call_target="tpu_custom_call", output_to_operand_aliasing={{0}: (11, {}), {1}: (12, {}), {2}: (13, {})} | custom-call | flops 2147483648 | bytes 2621440 | tf_op jit(solution)/shard_map/kv_chunk/pallas_call | solution.py:484
  371.3 5.5 %collective-permute-done.41.refs_1_ = bf16[1,64,4096]{2,1,0:T(8,128)(2,1)S(1)} collective-permute-done((bf16[1,64,4096]{2,1,0:T(8,128)(2,1)S(1)}, bf16[1,64,4096]{2,1,0:T(8,128)(2,1)S(1)}, u32[]{:S(2)}, u32[]{:S(2)}) %collective-permute-start.41) | collective-permute-done | bytes 524320 | tf_op jit(solution)/shard_map/ppermute | solution.py:651
  380.9 3.6 kv_chunk.21
  384.5 22.5 %tail.1 = bf16[2,8,4096]{2,1,0:T(8,128)(2,1)S(1)} custom-call(f32[14,8,3,8,128]{4,3,2,1,0:T(8,128)S(1)} %get-tuple-element.198.stv, f32[3,8,8,128]{3,2,1,0:T(8,128)S(1)} %get-tuple-element.199.self_ref, bf16[16,512]{1,0:T(8,128)(2,1)S(1)} %fusion.1.xs_ref, bf16[1,4096]{1,0:T(2,128)(2,1)S(1)} %copy-done.6, bf16[512,4096]{1,0:T(8,128)(2,1)S(1)} %get-tuple-element.201.wo, ...), custom_call_target="tpu_custom_call" | custom-call | tf_op jit(solution)/shard_map/tail/pallas_call | solution.py:616
  (109 shorter events, 40.7 us)
Async XLA Ops:
  1.4 15.4 %copy-start.13 = (s32[8]{0:T(128)S(1)}, s32[8]{0:T(128)}, u32[]{:S(2)}) copy-start(s32[8]{0:T(128)} %param.13) | copy-start | bytes 100
  15.9 38.5 %collective-permute-start = (bf16[8,128,4096]{2,1,0:T(8,128)(2,1)}, bf16[8,128,4096]{2,1,0:T(8,128)(2,1)}, u32[]{:S(2)}, u32[]{:S(2)}) collective-permute-start(bf16[8,128,4096]{2,1,0:T(8,128)(2,1)} %get-tuple-element.105.refs_0_.refs_1_), channel_id=1, source_target_pairs={{0,1},{1,0},{2,3},{3,2},{4,5},{5,4},{6,7},{7,6}} | collective-permute-start | bytes 25165832 | tf_op jit(solution)/shard_map/ppermute | solution.py:651
  21.5 8.8 %collective-permute-start.1 = (bf16[8,4096]{1,0:T(8,128)(2,1)S(1)}, bf16[8,4096]{1,0:T(8,128)(2,1)S(1)}, u32[]{:S(2)}, u32[]{:S(2)}) collective-permute-start(bf16[8,4096]{1,0:T(8,128)(2,1)S(1)} %bitcast.32), channel_id=1, source_target_pairs={{0,1},{1,0},{2,3},{3,2},{4,5},{5,4},{6,7},{7,6}} | collective-permute-start | bytes 196616 | tf_op jit(solution)/shard_map/ppermute | solution.py:651
  23.7 22.7 %copy-start.5 = (bf16[8,4096]{1,0:T(8,128)(2,1)S(1)}, bf16[8,4096]{1,0:T(8,128)(2,1)}, u32[]{:S(2)}) copy-start(bf16[8,4096]{1,0:T(8,128)(2,1)} %new_ref.1) | copy-start | bytes 196612
  23.7 58.5 %collective-permute-start.5 = (bf16[1,64,4096]{2,1,0:T(8,128)(2,1)}, bf16[1,64,4096]{2,1,0:T(8,128)(2,1)S(1)}, u32[]{:S(2)}, u32[]{:S(2)}) collective-permute-start(bf16[1,64,4096]{2,1,0:T(8,128)(2,1)} %get-tuple-element.121), channel_id=1, source_target_pairs={{0,4},{1,5},{2,6},{3,7},{4,0},{5,1},{6,2},{7,3}} | collective-permute-start | bytes 1572872 | tf_op jit(solution)/shard_map/ppermute | solution.py:651
  26.8 55.5 %collective-permute-start.6 = (bf16[1,64,4096]{2,1,0:T(8,128)(2,1)}, bf16[1,64,4096]{2,1,0:T(8,128)(2,1)S(1)}, u32[]{:S(2)}, u32[]{:S(2)}) collective-permute-start(bf16[1,64,4096]{2,1,0:T(8,128)(2,1)} %get-tuple-element.122), channel_id=1, source_target_pairs={{0,2},{1,3},{2,0},{3,1},{4,6},{5,7},{6,4},{7,5}} | collective-permute-start | bytes 1572872 | tf_op jit(solution)/shard_map/ppermute | solution.py:651
  30.3 11.0 %collective-permute-start.2 = (bf16[8,2048]{1,0:T(8,128)(2,1)S(1)}, bf16[8,2048]{1,0:T(8,128)(2,1)S(1)}, u32[]{:S(2)}, u32[]{:S(2)}) collective-permute-start(bf16[8,2048]{1,0:T(8,128)(2,1)S(1)} %dynamic-slice_add_fusion), channel_id=1, source_target_pairs={{0,2},{1,3},{2,0},{3,1},{4,6},{5,7},{6,4},{7,5}} | collective-permute-start | bytes 98312 | tf_op jit(solution)/shard_map/ppermute | solution.py:651
  41.2 3.9 collective-permute-start.3
  45.2 1.2 collective-permute-start.4
  82.3 4.3 %collective-permute-start.7 = (bf16[1,64,4096]{2,1,0:T(8,128)(2,1)S(1)}, bf16[1,64,4096]{2,1,0:T(8,128)(2,1)S(1)}, u32[]{:S(2)}, u32[]{:S(2)}) collective-permute-start(bf16[1,64,4096]{2,1,0:T(8,128)(2,1)S(1)} %collective-permute-done.5.refs_0_), channel_id=1, source_target_pairs={{0,1},{1,0},{2,3},{3,2},{4,5},{5,4},{6,7},{7,6}} | collective-permute-start | bytes 1572872 | tf_op jit(solution)/shard_map/ppermute | solution.py:651
  82.5 4.1 %collective-permute-start.8 = (bf16[1,64,4096]{2,1,0:T(8,128)(2,1)S(1)}, bf16[1,64,4096]{2,1,0:T(8,128)(2,1)S(1)}, u32[]{:S(2)}, u32[]{:S(2)}) collective-permute-start(bf16[1,64,4096]{2,1,0:T(8,128)(2,1)S(1)} %collective-permute-done.6.refs_1_), channel_id=1, source_target_pairs={{0,1},{1,0},{2,3},{3,2},{4,5},{5,4},{6,7},{7,6}} | collective-permute-start | bytes 1572872 | tf_op jit(solution)/shard_map/ppermute | solution.py:651
  84.6 14.0 %collective-permute-start.9 = (bf16[1,64,4096]{2,1,0:T(8,128)(2,1)S(1)}, bf16[1,64,4096]{2,1,0:T(8,128)(2,1)S(1)}, u32[]{:S(2)}, u32[]{:S(2)}) collective-permute-start(bf16[1,64,4096]{2,1,0:T(8,128)(2,1)S(1)} %get-tuple-element.129), channel_id=1, source_target_pairs={{0,4},{1,5},{2,6},{3,7},{4,0},{5,1},{6,2},{7,3}} | collective-permute-start | bytes 1572872 | tf_op jit(solution)/shard_map/ppermute | solution.py:651
  84.9 13.7 %collective-permute-start.10 = (bf16[1,64,4096]{2,1,0:T(8,128)(2,1)S(1)}, bf16[1,64,4096]{2,1,0:T(8,128)(2,1)S(1)}, u32[]{:S(2)}, u32[]{:S(2)}) collective-permute-start(bf16[1,64,4096]{2,1,0:T(8,128)(2,1)S(1)} %get-tuple-element.130), channel_id=1, source_target_pairs={{0,2},{1,3},{2,0},{3,1},{4,6},{5,7},{6,4},{7,5}} | collective-permute-start | bytes 1572872 | tf_op jit(solution)/shard_map/ppermute | solution.py:651
  86.6 15.7 %copy-start.8 = (bf16[2,128,4096]{2,1,0:T(8,128)(2,1)S(1)}, bf16[2,128,4096]{2,1,0:T(8,128)(2,1)}, u32[]{:S(2)}) copy-start(bf16[2,128,4096]{2,1,0:T(8,128)(2,1)} %copy-done.7) | copy-start | bytes 6291460
  98.6 3.7 collective-permute-start.11
  98.6 26.0 %collective-permute-start.13 = (bf16[1,128,4096]{2,1,0:T(8,128)(2,1)S(1)}, bf16[1,128,4096]{2,1,0:T(8,128)(2,1)S(1)}, u32[]{:S(2)}, u32[]{:S(2)}) collective-permute-start(bf16[1,128,4096]{2,1,0:T(8,128)(2,1)S(1)} %copy-done.12), channel_id=1, source_target_pairs={{0,4},{1,5},{2,6},{3,7},{4,0},{5,1},{6,2},{7,3}} | collective-permute-start | bytes 3145736 | tf_op jit(solution)/shard_map/ppermute | solution.py:651
  100.3 26.0 %collective-permute-start.14 = (bf16[1,128,4096]{2,1,0:T(8,128)(2,1)S(1)}, bf16[1,128,4096]{2,1,0:T(8,128)(2,1)S(1)}, u32[]{:S(2)}, u32[]{:S(2)}) collective-permute-start(bf16[1,128,4096]{2,1,0:T(8,128)(2,1)S(1)} %get-tuple-element.138), channel_id=1, source_target_pairs={{0,2},{1,3},{2,0},{3,1},{4,6},{5,7},{6,4},{7,5}} | collective-permute-start | bytes 3145736 | tf_op jit(solution)/shard_map/ppermute | solution.py:651
  101.8 1.9 collective-permute-start.12
  101.8 67.3 %collective-permute-start.17 = (bf16[2,128,4096]{2,1,0:T(8,128)(2,1)S(1)}, bf16[2,128,4096]{2,1,0:T(8,128)(2,1)S(1)}, u32[]{:S(2)}, u32[]{:S(2)}) collective-permute-start(bf16[2,128,4096]{2,1,0:T(8,128)(2,1)S(1)} %copy-done.10), channel_id=1, source_target_pairs={{0,4},{1,5},{2,6},{3,7},{4,0},{5,1},{6,2},{7,3}} | collective-permute-start | bytes 6291464 | tf_op jit(solution)/shard_map/ppermute | solution.py:651
  102.3 68.2 %collective-permute-start.18 = (bf16[2,128,4096]{2,1,0:T(8,128)(2,1)S(1)}, bf16[2,128,4096]{2,1,0:T(8,128)(2,1)S(1)}, u32[]{:S(2)}, u32[]{:S(2)}) collective-permute-start(bf16[2,128,4096]{2,1,0:T(8,128)(2,1)S(1)} %copy-done.8), channel_id=1, source_target_pairs={{0,2},{1,3},{2,0},{3,1},{4,6},{5,7},{6,4},{7,5}} | collective-permute-start | bytes 6291464 | tf_op jit(solution)/shard_map/ppermute | solution.py:651
  126.4 2.7 collective-permute-start.15
  126.4 4.2 %collective-permute-start.16 = (bf16[1,128,4096]{2,1,0:T(8,128)(2,1)S(1)}, bf16[1,128,4096]{2,1,0:T(8,128)(2,1)S(1)}, u32[]{:S(2)}, u32[]{:S(2)}) collective-permute-start(bf16[1,128,4096]{2,1,0:T(8,128)(2,1)S(1)} %collective-permute-done.14.refs_1_), channel_id=1, source_target_pairs={{0,1},{1,0},{2,3},{3,2},{4,5},{5,4},{6,7},{7,6}} | collective-permute-start | bytes 3145736 | tf_op jit(solution)/shard_map/ppermute | solution.py:651
  170.6 4.2 %collective-permute-start.19 = (bf16[2,128,4096]{2,1,0:T(8,128)(2,1)S(1)}, bf16[2,128,4096]{2,1,0:T(8,128)(2,1)S(1)}, u32[]{:S(2)}, u32[]{:S(2)}) collective-permute-start(bf16[2,128,4096]{2,1,0:T(8,128)(2,1)S(1)} %collective-permute-done.17.refs_0_), channel_id=1, source_target_pairs={{0,1},{1,0},{2,3},{3,2},{4,5},{5,4},{6,7},{7,6}} | collective-permute-start | bytes 6291464 | tf_op jit(solution)/shard_map/ppermute | solution.py:651
  170.6 7.2 %collective-permute-start.20 = (bf16[2,128,4096]{2,1,0:T(8,128)(2,1)S(1)}, bf16[2,128,4096]{2,1,0:T(8,128)(2,1)S(1)}, u32[]{:S(2)}, u32[]{:S(2)}) collective-permute-start(bf16[2,128,4096]{2,1,0:T(8,128)(2,1)S(1)} %collective-permute-done.18.refs_1_), channel_id=1, source_target_pairs={{0,1},{1,0},{2,3},{3,2},{4,5},{5,4},{6,7},{7,6}} | collective-permute-start | bytes 6291464 | tf_op jit(solution)/shard_map/ppermute | solution.py:651
  171.1 47.5 %collective-permute-start.22 = (bf16[2,128,4096]{2,1,0:T(8,128)(2,1)S(1)}, bf16[2,128,4096]{2,1,0:T(8,128)(2,1)S(1)}, u32[]{:S(2)}, u32[]{:S(2)}) collective-permute-start(bf16[2,128,4096]{2,1,0:T(8,128)(2,1)S(1)} %copy-done.10), channel_id=1, source_target_pairs={{0,2},{1,3},{2,0},{3,1},{4,6},{5,7},{6,4},{7,5}} | collective-permute-start | bytes 6291464 | tf_op jit(solution)/shard_map/ppermute | solution.py:651
  172.6 47.3 %collective-permute-start.21 = (bf16[2,128,4096]{2,1,0:T(8,128)(2,1)S(1)}, bf16[2,128,4096]{2,1,0:T(8,128)(2,1)S(1)}, u32[]{:S(2)}, u32[]{:S(2)}) collective-permute-start(bf16[2,128,4096]{2,1,0:T(8,128)(2,1)S(1)} %copy-done.8), channel_id=1, source_target_pairs={{0,4},{1,5},{2,6},{3,7},{4,0},{5,1},{6,2},{7,3}} | collective-permute-start | bytes 6291464 | tf_op jit(solution)/shard_map/ppermute | solution.py:651
  219.8 6.0 %collective-permute-start.23 = (bf16[2,128,4096]{2,1,0:T(8,128)(2,1)S(1)}, bf16[2,128,4096]{2,1,0:T(8,128)(2,1)S(1)}, u32[]{:S(2)}, u32[]{:S(2)}) collective-permute-start(bf16[2,128,4096]{2,1,0:T(8,128)(2,1)S(1)} %collective-permute-done.21.refs_0_), channel_id=1, source_target_pairs={{0,1},{1,0},{2,3},{3,2},{4,5},{5,4},{6,7},{7,6}} | collective-permute-start | bytes 6291464 | tf_op jit(solution)/shard_map/ppermute | solution.py:651
  219.8 7.2 %collective-permute-start.24 = (bf16[2,128,4096]{2,1,0:T(8,128)(2,1)S(1)}, bf16[2,128,4096]{2,1,0:T(8,128)(2,1)S(1)}, u32[]{:S(2)}, u32[]{:S(2)}) collective-permute-start(bf16[2,128,4096]{2,1,0:T(8,128)(2,1)S(1)} %collective-permute-done.22.refs_1_), channel_id=1, source_target_pairs={{0,1},{1,0},{2,3},{3,2},{4,5},{5,4},{6,7},{7,6}} | collective-permute-start | bytes 6291464 | tf_op jit(solution)/shard_map/ppermute | solution.py:651
  225.0 47.7 %collective-permute-start.26 = (bf16[2,128,4096]{2,1,0:T(8,128)(2,1)}, bf16[2,128,4096]{2,1,0:T(8,128)(2,1)S(1)}, u32[]{:S(2)}, u32[]{:S(2)}) collective-permute-start(bf16[2,128,4096]{2,1,0:T(8,128)(2,1)} %get-tuple-element.206), channel_id=1, source_target_pairs={{0,2},{1,3},{2,0},{3,1},{4,6},{5,7},{6,4},{7,5}} | collective-permute-start | bytes 6291464 | tf_op jit(solution)/shard_map/ppermute | solution.py:651
  225.5 47.5 %collective-permute-start.25 = (bf16[2,128,4096]{2,1,0:T(8,128)(2,1)}, bf16[2,128,4096]{2,1,0:T(8,128)(2,1)S(1)}, u32[]{:S(2)}, u32[]{:S(2)}) collective-permute-start(bf16[2,128,4096]{2,1,0:T(8,128)(2,1)} %get-tuple-element.207), channel_id=1, source_target_pairs={{0,4},{1,5},{2,6},{3,7},{4,0},{5,1},{6,2},{7,3}} | collective-permute-start | bytes 6291464 | tf_op jit(solution)/shard_map/ppermute | solution.py:651
  273.0 4.2 %collective-permute-start.27 = (bf16[2,128,4096]{2,1,0:T(8,128)(2,1)S(1)}, bf16[2,128,4096]{2,1,0:T(8,128)(2,1)S(1)}, u32[]{:S(2)}, u32[]{:S(2)}) collective-permute-start(bf16[2,128,4096]{2,1,0:T(8,128)(2,1)S(1)} %collective-permute-done.25.refs_0_), channel_id=1, source_target_pairs={{0,1},{1,0},{2,3},{3,2},{4,5},{5,4},{6,7},{7,6}} | collective-permute-start | bytes 6291464 | tf_op jit(solution)/shard_map/ppermute | solution.py:651
  273.0 7.2 %collective-permute-start.28 = (bf16[2,128,4096]{2,1,0:T(8,128)(2,1)S(1)}, bf16[2,128,4096]{2,1,0:T(8,128)(2,1)S(1)}, u32[]{:S(2)}, u32[]{:S(2)}) collective-permute-start(bf16[2,128,4096]{2,1,0:T(8,128)(2,1)S(1)} %collective-permute-done.26.refs_1_), channel_id=1, source_target_pairs={{0,1},{1,0},{2,3},{3,2},{4,5},{5,4},{6,7},{7,6}} | collective-permute-start | bytes 6291464 | tf_op jit(solution)/shard_map/ppermute | solution.py:651
  273.5 47.5 %collective-permute-start.29 = (bf16[2,128,4096]{2,1,0:T(8,128)(2,1)S(1)}, bf16[2,128,4096]{2,1,0:T(8,128)(2,1)S(1)}, u32[]{:S(2)}, u32[]{:S(2)}) collective-permute-start(bf16[2,128,4096]{2,1,0:T(8,128)(2,1)S(1)} %collective-permute-done.18.refs_1_), channel_id=1, source_target_pairs={{0,4},{1,5},{2,6},{3,7},{4,0},{5,1},{6,2},{7,3}} | collective-permute-start | bytes 6291464 | tf_op jit(solution)/shard_map/ppermute | solution.py:651
  273.8 47.3 %collective-permute-start.30 = (bf16[2,128,4096]{2,1,0:T(8,128)(2,1)S(1)}, bf16[2,128,4096]{2,1,0:T(8,128)(2,1)S(1)}, u32[]{:S(2)}, u32[]{:S(2)}) collective-permute-start(bf16[2,128,4096]{2,1,0:T(8,128)(2,1)S(1)} %collective-permute-done.17.refs_0_), channel_id=1, source_target_pairs={{0,2},{1,3},{2,0},{3,1},{4,6},{5,7},{6,4},{7,5}} | collective-permute-start | bytes 6291464 | tf_op jit(solution)/shard_map/ppermute | solution.py:651
  321.1 4.2 %collective-permute-start.31 = (bf16[2,128,4096]{2,1,0:T(8,128)(2,1)S(1)}, bf16[2,128,4096]{2,1,0:T(8,128)(2,1)S(1)}, u32[]{:S(2)}, u32[]{:S(2)}) collective-permute-start(bf16[2,128,4096]{2,1,0:T(8,128)(2,1)S(1)} %collective-permute-done.30.refs_0_), channel_id=1, source_target_pairs={{0,1},{1,0},{2,3},{3,2},{4,5},{5,4},{6,7},{7,6}} | collective-permute-start | bytes 6291464 | tf_op jit(solution)/shard_map/ppermute | solution.py:651
  321.1 7.2 %collective-permute-start.32 = (bf16[2,128,4096]{2,1,0:T(8,128)(2,1)S(1)}, bf16[2,128,4096]{2,1,0:T(8,128)(2,1)S(1)}, u32[]{:S(2)}, u32[]{:S(2)}) collective-permute-start(bf16[2,128,4096]{2,1,0:T(8,128)(2,1)S(1)} %collective-permute-done.29.refs_1_), channel_id=1, source_target_pairs={{0,1},{1,0},{2,3},{3,2},{4,5},{5,4},{6,7},{7,6}} | collective-permute-start | bytes 6291464 | tf_op jit(solution)/shard_map/ppermute | solution.py:651
  321.6 25.1 %collective-permute-start.33 = (bf16[1,128,4096]{2,1,0:T(8,128)(2,1)S(1)}, bf16[1,128,4096]{2,1,0:T(8,128)(2,1)S(1)}, u32[]{:S(2)}, u32[]{:S(2)}) collective-permute-start(bf16[1,128,4096]{2,1,0:T(8,128)(2,1)S(1)} %collective-permute-done.14.refs_1_), channel_id=1, source_target_pairs={{0,4},{1,5},{2,6},{3,7},{4,0},{5,1},{6,2},{7,3}} | collective-permute-start | bytes 3145736 | tf_op jit(solution)/shard_map/ppermute | solution.py:651
  323.3 24.8 %collective-permute-start.34 = (bf16[1,128,4096]{2,1,0:T(8,128)(2,1)S(1)}, bf16[1,128,4096]{2,1,0:T(8,128)(2,1)S(1)}, u32[]{:S(2)}, u32[]{:S(2)}) collective-permute-start(bf16[1,128,4096]{2,1,0:T(8,128)(2,1)S(1)} %collective-permute-done.13.refs_0_), channel_id=1, source_target_pairs={{0,2},{1,3},{2,0},{3,1},{4,6},{5,7},{6,4},{7,5}} | collective-permute-start | bytes 3145736 | tf_op jit(solution)/shard_map/ppermute | solution.py:651
  348.1 2.7 collective-permute-start.35
  348.1 4.2 %collective-permute-start.36 = (bf16[1,128,4096]{2,1,0:T(8,128)(2,1)S(1)}, bf16[1,128,4096]{2,1,0:T(8,128)(2,1)S(1)}, u32[]{:S(2)}, u32[]{:S(2)}) collective-permute-start(bf16[1,128,4096]{2,1,0:T(8,128)(2,1)S(1)} %collective-permute-done.33.refs_1_), channel_id=1, source_target_pairs={{0,1},{1,0},{2,3},{3,2},{4,5},{5,4},{6,7},{7,6}} | collective-permute-start | bytes 3145736 | tf_op jit(solution)/shard_map/ppermute | solution.py:651
  348.6 13.8 %collective-permute-start.37 = (bf16[1,64,4096]{2,1,0:T(8,128)(2,1)S(1)}, bf16[1,64,4096]{2,1,0:T(8,128)(2,1)S(1)}, u32[]{:S(2)}, u32[]{:S(2)}) collective-permute-start(bf16[1,64,4096]{2,1,0:T(8,128)(2,1)S(1)} %collective-permute-done.6.refs_1_), channel_id=1, source_target_pairs={{0,4},{1,5},{2,6},{3,7},{4,0},{5,1},{6,2},{7,3}} | collective-permute-start | bytes 1572872 | tf_op jit(solution)/shard_map/ppermute | solution.py:651
  348.9 13.6 %collective-permute-start.38 = (bf16[1,64,4096]{2,1,0:T(8,128)(2,1)S(1)}, bf16[1,64,4096]{2,1,0:T(8,128)(2,1)S(1)}, u32[]{:S(2)}, u32[]{:S(2)}) collective-permute-start(bf16[1,64,4096]{2,1,0:T(8,128)(2,1)S(1)} %collective-permute-done.5.refs_0_), channel_id=1, source_target_pairs={{0,2},{1,3},{2,0},{3,1},{4,6},{5,7},{6,4},{7,5}} | collective-permute-start | bytes 1572872 | tf_op jit(solution)/shard_map/ppermute | solution.py:651
  362.5 3.7 collective-permute-start.39
  362.5 3.7 collective-permute-start.40
  363.0 13.8 %collective-permute-start.41 = (bf16[1,64,4096]{2,1,0:T(8,128)(2,1)S(1)}, bf16[1,64,4096]{2,1,0:T(8,128)(2,1)S(1)}, u32[]{:S(2)}, u32[]{:S(2)}) collective-permute-start(bf16[1,64,4096]{2,1,0:T(8,128)(2,1)S(1)} %collective-permute-done.10.refs_1_), channel_id=1, source_target_pairs={{0,4},{1,5},{2,6},{3,7},{4,0},{5,1},{6,2},{7,3}} | collective-permute-start | bytes 1572872 | tf_op jit(solution)/shard_map/ppermute | solution.py:651
  364.7 13.6 %collective-permute-start.42 = (bf16[1,64,4096]{2,1,0:T(8,128)(2,1)S(1)}, bf16[1,64,4096]{2,1,0:T(8,128)(2,1)S(1)}, u32[]{:S(2)}, u32[]{:S(2)}) collective-permute-start(bf16[1,64,4096]{2,1,0:T(8,128)(2,1)S(1)} %collective-permute-done.9.refs_0_), channel_id=1, source_target_pairs={{0,2},{1,3},{2,0},{3,1},{4,6},{5,7},{6,4},{7,5}} | collective-permute-start | bytes 1572872 | tf_op jit(solution)/shard_map/ppermute | solution.py:651
  378.3 1.9 collective-permute-start.43
  378.3 2.7 collective-permute-start.44
  (11 other events, 52.6 us)

commit v12 on v11

--- a/solution.py
+++ b/solution.py
@@ -147,28 +147,6 @@
             return carry
 
         lax.fori_loop(0, rows // NORM_ROWS, norm_rows, 0)
-
-
-def raw_kernel(places, rows, x_hbm, *refs):
-    n = len(places)
-    copies = [pltpu.make_async_copy(x_hbm.at[bat, pl.ds(row0, rows)], refs[i].at[0], refs[n].at[i]) for i, (bat, row0) in enumerate(places)]
-    for copy in copies:
-        copy.start()
-    for copy in copies:
-        copy.wait()
-
-
-def raw_call(x, places, rows):
-    d_model = x.shape[2]
-    return pl.pallas_call(
-        functools.partial(raw_kernel, places, rows),
-        out_shape=[pltpu.VMEM((1, rows, d_model), jnp.bfloat16)] * len(places),
-        in_specs=[pl.BlockSpec(memory_space=pl.ANY)],
-        out_specs=[pl.BlockSpec(memory_space=pltpu.VMEM)] * len(places),
-        scratch_shapes=[pltpu.SemaphoreType.DMA((len(places),))],
-        compiler_params=pltpu.CompilerParams(vmem_limit_bytes=8 * 2 ** 20),
-        name="raw_rows",
-    )(pltpu.with_memory_space_constraint(x, pltpu.HBM))
 
 
 def first_call(x, gain, places, rows):
@@ -662,7 +640,7 @@
 
         q1, q2, rows_h = 1, n_batch // 4, blk // 2
         a_parts, b_parts = {}, {}
-        a_parts["0a"], b_parts["0a"] = raw_call(prompt, [(0, 0), (half, 0)], rows_h)
+        a_parts["0a"], b_parts["0a"] = prompt[:1, :rows_h], prompt[half:half + 1, :rows_h]
         a_parts["0b"], b_parts["0b"] = first_call(prompt, norm_attn, [(0, rows_h), (half, rows_h)], rows_h)
         from_y, from_x = {}, {}
 
@@ -687,8 +665,7 @@
         core, cols_h = my_idx % 2, d_model // 2
         last_x = last_x + swap(last_x, 1)
         last_x = lax.dynamic_slice_in_dim(last_x, core * cols_h, cols_h, axis=1)
-        last_x = last_x + swap(last_x, 2)
-        last_x = last_x + swap(last_x, 4)
+        last_x = (last_x + swap(last_x, 2)) + (swap(last_x, 4) + swap(last_x, 6))
         other_x = swap(last_x, 1)
         last_x = jnp.where(core == 0, jnp.concatenate([last_x, other_x], axis=1), jnp.concatenate([other_x, last_x], axis=1))
         send_part("2", a_parts["2"], b_parts["2"])

time: 408 us -> 405 us (level)
  waiting for transfers between devices: 172 us -> 165 us
    ppermute x45 -> x46, waiting for transfers between devices: 172 us -> 165 us  [swap(): return lax.ppermute(arr, 'model', [(i, i ^ bit) for i in range(n_dev)])]
    ppermute x45 -> x46, starting transfers between devices: 32.1 us -> 34 us  [swap(): return lax.ppermute(arr, 'model', [(i, i ^ bit) for i in range(n_dev)])]
  transfers between devices with their start and end apart: 45 -> 46, of which waited for: 32 -> 32; matrix products, arithmetic and copies ran while one was open for 3% -> 4% of each run, Pallas kernels for 34% -> 34%
where the time goes in v12:
time: 405 us; the launch traced here: 404 us
  Pallas kernels  174 us (43%)
  waiting for transfers between devices  165 us (41%)
  starting transfers between devices  34 us (8%)
  local copies, waits for them, and re-layouts  20.6 us (5%)
  other arithmetic  5.18 us (1%)
  matrix products  4.57 us (1%)
    ppermute x46, waiting for transfers between devices, swap(): return lax.ppermute(arr, 'model', [(i, i ^ bit) for i in range(n_dev)])  165 us
    pallas_call x11, Pallas kernels, kv_call(): pl.pallas_call(functools.partial(kv_kernel, n_in, n_steps, masks, batches...  116 us
    ppermute x46, starting transfers between devices, swap(): return lax.ppermute(arr, 'model', [(i, i ^ bit) for i in range(n_dev)])  34 us
    pallas_call x1, Pallas kernels, tail_call(): pl.pallas_call(functools.partial(tail_kernel, n_dev, parts_of), out_shape...  22.5 us
    pallas_call x2, Pallas kernels, turn_call(): pl.pallas_call(turn_kernel, grid=(d // cols,), in_specs=[pl.BlockSpec((n,...  15.8 us
    unnamed x28, local copies, waits for them, and re-layouts  12.8 us
    pallas_call x1, Pallas kernels, norm_call(): pl.pallas_call(functools.partial(norm_kernel, outs_of), grid=(len(order),...  10.8 us
  transfers between devices with their start and end apart: 46, of which 32 were waited for; matrix products, arithmetic and copies ran while one was open for 4% of the time, Pallas kernels for 34%

profile of v12, /device:TPU:0, one launch (start us, length us, event | category | flops | bytes accessed | tf_op | source)
XLA Modules:
  0.0 404.3 jit_solution(1828964737739943963)
XLA Ops:
  1.4 10.8 %norm_rows.1 = (bf16[1,128,4096]{2,1,0:T(8,128)(2,1)S(1)}, bf16[1,128,4096]{2,1,0:T(8,128)(2,1)S(1)}, bf16[2,128,4096]{2,1,0:T(8,128)(2,1)S(1)}, bf16[2,128,4096]{2,1,0:T(8,128)(2,1)S(1)}, bf16[8,128,4096]{2,1,0:T(8,128)(2,1)}) custom-call(bf16[8,128,4096]{2,1,0:T(8,128)(2,1)} %x_hbm.1, bf16[1,4096]{1,0:T(2,128)(2,1)S(1)} %copy-done.2), custom_call_target="tpu_custom_call" | custom-call | flops 33554432 | bytes 25165824 | tf_op jit(solution)/shard_map/norm_rows/pallas_call | solution.py:180
  16.8 4.6 %fusion.2 = bf16[8,1,4096]{2,1,0:T(2,128)(2,1)S(1)} fusion(bf16[8,128,4096]{2,1,0:T(8,128)(2,1)} %x_hbm.1, pred[8,128,1]{1,0,2:T(8,128)(4,1)S(1)} %compare_bitcast_fusion), kind=kOutput, calls=%fused_computation.14 | convolution fusion | flops 8388608 | bytes 8455168 | tf_op jit(solution)/shard_map/bs,bsd->bd/dot_general | solution.py:664
  21.5 2.3 fusion.6
  23.8 3.0 collective-permute-start.7
  26.9 3.0 fusion
  30.1 2.7 collective-permute-start.3
  34.3 1.7 pad_maximum_fusion
  36.0 2.0 collective-permute-start.6
  38.0 2.1 collective-permute-done.2
  43.2 4.7 %keep.1 = (bf16[4096,512]{1,0:T(8,128)(2,1)S(1)}, bf16[4096,512]{1,0:T(8,128)(2,1)S(1)}, bf16[512,4096]{1,0:T(8,128)(2,1)S(1)}) custom-call(bf16[4096,512]{1,0:T(8,128)(2,1)} %bitcast.28, bf16[4096,512]{1,0:T(8,128)(2,1)} %bitcast.29, bf16[512,4096]{1,0:T(8,128)(2,1)} %bitcast.30), custom_call_target="tpu_custom_call" | custom-call | tf_op jit(solution)/shard_map/keep/pallas_call | solution.py:39
  47.9 3.1 query_rows.1
  51.0 27.9 %kv_chunk.11 = (bf16[8,1025,4,128]{3,2,1,0:T(4,128)(2,1)}, bf16[8,1025,4,128]{3,2,1,0:T(4,128)(2,1)}, f32[14,8,3,8,128]{4,3,2,1,0:T(8,128)S(1)}) custom-call(bf16[8,128,4096]{2,1,0:T(8,128)(2,1)} %get-tuple-element.103.refs_0_.refs_1_, bf16[8,128,4096]{2,1,0:T(8,128)(2,1)} %get-tuple-element.103.refs_0_.refs_1_, ...), custom_call_target="tpu_custom_call" | custom-call | flops 17179869184 | bytes 20971520 | tf_op jit(solution)/shard_map/kv_chunk/pallas_call | solution.py:462
  79.5 1.7 first_rows.1
  81.5 1.7 collective-permute-start.11
  83.2 4.9 %kv_chunk.12 = (bf16[8,1025,4,128]{3,2,1,0:T(4,128)(2,1)}, bf16[8,1025,4,128]{3,2,1,0:T(4,128)(2,1)}, f32[14,8,3,8,128]{4,3,2,1,0:T(8,128)S(1)}) custom-call(bf16[1,64,4096]{2,1,0:T(8,128)(2,1)S(1)} %collective-permute-done.6.refs_0_, ...), custom_call_target="tpu_custom_call", output_to_operand_aliasing={{0}: (11, {}), {1}: (12, {}), {2}: (13, {})} | custom-call | flops 2147483648 | bytes 2621440 | tf_op jit(solution)/shard_map/kv_chunk/pallas_call | solution.py:462
  88.1 7.1 %collective-permute-done.10.refs_0_ = bf16[1,64,4096]{2,1,0:T(8,128)(2,1)S(1)} collective-permute-done((bf16[1,64,4096]{2,1,0:T(8,128)(2,1)S(1)}, bf16[1,64,4096]{2,1,0:T(8,128)(2,1)S(1)}, u32[]{:S(2)}, u32[]{:S(2)}) %collective-permute-start.10) | collective-permute-done | bytes 524320 | tf_op jit(solution)/shard_map/ppermute | solution.py:629
  95.2 1.7 collective-permute-start.14
  100.3 3.5 kv_chunk.13
  103.9 17.4 %collective-permute-done.14.refs_0_ = bf16[1,128,4096]{2,1,0:T(8,128)(2,1)S(1)} collective-permute-done((bf16[1,128,4096]{2,1,0:T(8,128)(2,1)S(1)}, bf16[1,128,4096]{2,1,0:T(8,128)(2,1)S(1)}, u32[]{:S(2)}, u32[]{:S(2)}) %collective-permute-start.14) | collective-permute-done | bytes 1048608 | tf_op jit(solution)/shard_map/ppermute | solution.py:629
  121.3 1.7 collective-permute-done.15.refs_1_
  123.5 2.1 collective-permute-done.16.refs_2_
  127.1 7.4 %kv_chunk.14 = (bf16[8,1025,4,128]{3,2,1,0:T(4,128)(2,1)}, bf16[8,1025,4,128]{3,2,1,0:T(4,128)(2,1)}, f32[14,8,3,8,128]{4,3,2,1,0:T(8,128)S(1)}) custom-call(bf16[1,128,4096]{2,1,0:T(8,128)(2,1)S(1)} %collective-permute-done.14.refs_0_, ...), custom_call_target="tpu_custom_call", output_to_operand_aliasing={{0}: (10, {}), {1}: (11, {}), {2}: (12, {})} | custom-call | flops 4294967296 | bytes 5242880 | tf_op jit(solution)/shard_map/kv_chunk/pallas_call | solution.py:462
  134.5 31.2 %collective-permute-done.18.refs_0_ = bf16[2,128,4096]{2,1,0:T(8,128)(2,1)S(1)} collective-permute-done((bf16[2,128,4096]{2,1,0:T(8,128)(2,1)S(1)}, bf16[2,128,4096]{2,1,0:T(8,128)(2,1)S(1)}, u32[]{:S(2)}, u32[]{:S(2)}) %collective-permute-start.18) | collective-permute-done | bytes 2097184 | tf_op jit(solution)/shard_map/ppermute | solution.py:629
  171.3 3.0 collective-permute-done.21.refs_3_
  174.3 14.0 %kv_chunk.15 = (bf16[8,1025,4,128]{3,2,1,0:T(4,128)(2,1)}, bf16[8,1025,4,128]{3,2,1,0:T(4,128)(2,1)}, f32[14,8,3,8,128]{4,3,2,1,0:T(8,128)S(1)}) custom-call(bf16[2,128,4096]{2,1,0:T(8,128)(2,1)S(1)} %collective-permute-done.18.refs_0_, ...), custom_call_target="tpu_custom_call", output_to_operand_aliasing={{0}: (10, {}), {1}: (11, {}), {2}: (12, {})} | custom-call | flops 8589934592 | bytes 10485760 | tf_op jit(solution)/shard_map/kv_chunk/pallas_call | solution.py:462
  188.4 26.9 %collective-permute-done.23.refs_1_ = bf16[2,128,4096]{2,1,0:T(8,128)(2,1)S(1)} collective-permute-done((bf16[2,128,4096]{2,1,0:T(8,128)(2,1)S(1)}, bf16[2,128,4096]{2,1,0:T(8,128)(2,1)S(1)}, u32[]{:S(2)}, u32[]{:S(2)}) %collective-permute-start.23) | collective-permute-done | bytes 2097184 | tf_op jit(solution)/shard_map/ppermute | solution.py:629
  216.9 4.7 %fusion.5 = (bf16[2,128,4096]{2,1,0:T(8,128)(2,1)}, bf16[2,128,4096]{2,1,0:T(8,128)(2,1)}) fusion(bf16[8,128,4096]{2,1,0:T(8,128)(2,1)} %get-tuple-element.103.refs_0_.refs_1_), kind=kLoop, calls=%fused_computation.27 | loop fusion | bytes 8388608 | tf_op jit(solution)/shard_map/slice | solution.py:673
  223.6 14.0 %kv_chunk.16 = (bf16[8,1025,4,128]{3,2,1,0:T(4,128)(2,1)}, bf16[8,1025,4,128]{3,2,1,0:T(4,128)(2,1)}, f32[14,8,3,8,128]{4,3,2,1,0:T(8,128)S(1)}) custom-call(bf16[2,128,4096]{2,1,0:T(8,128)(2,1)S(1)} %collective-permute-done.22.refs_0_, ...), custom_call_target="tpu_custom_call", output_to_operand_aliasing={{0}: (10, {}), {1}: (11, {}), {2}: (12, {})} | custom-call | flops 8589934592 | bytes 10485760 | tf_op jit(solution)/shard_map/kv_chunk/pallas_call | solution.py:462
  237.6 7.9 %turn.2.wg_hbm = bf16[4096,1376]{1,0:T(8,128)(2,1)S(1)} custom-call(bf16[1376,4096]{1,0:T(8,128)(2,1)} %bitcast.25), custom_call_target="tpu_custom_call" | custom-call | flops 1442840576 | bytes 22544384 | tf_op jit(solution)/shard_map/turn/pallas_call | solution.py:57
  245.5 4.2 %copy-done = bf16[4096,1376]{1,0:T(8,128)(2,1)} copy-done((bf16[4096,1376]{1,0:T(8,128)(2,1)}, bf16[4096,1376]{1,0:T(8,128)(2,1)S(1)}, u32[]{:S(2)}) %copy-start) | copy-done | bytes 11272216
  249.7 19.6 %collective-permute-done.27.refs_1_ = bf16[2,128,4096]{2,1,0:T(8,128)(2,1)S(1)} collective-permute-done((bf16[2,128,4096]{2,1,0:T(8,128)(2,1)}, bf16[2,128,4096]{2,1,0:T(8,128)(2,1)S(1)}, u32[]{:S(2)}, u32[]{:S(2)}) %collective-permute-start.27) | collective-permute-done | bytes 2097184 | tf_op jit(solution)/shard_map/ppermute | solution.py:629
  270.4 1.7 collective-permute-start.31
  273.8 3.0 collective-permute-done.29.refs_3_
  276.8 14.0 %kv_chunk.17 = (bf16[8,1025,4,128]{3,2,1,0:T(4,128)(2,1)}, bf16[8,1025,4,128]{3,2,1,0:T(4,128)(2,1)}, f32[14,8,3,8,128]{4,3,2,1,0:T(8,128)S(1)}) custom-call(bf16[2,128,4096]{2,1,0:T(8,128)(2,1)S(1)} %collective-permute-done.26.refs_0_, ...), custom_call_target="tpu_custom_call", output_to_operand_aliasing={{0}: (10, {}), {1}: (11, {}), {2}: (12, {})} | custom-call | flops 8589934592 | bytes 10485760 | tf_op jit(solution)/shard_map/kv_chunk/pallas_call | solution.py:462
  290.8 7.9 %turn.3.wu_hbm = bf16[4096,1376]{1,0:T(8,128)(2,1)S(1)} custom-call(bf16[1376,4096]{1,0:T(8,128)(2,1)} %bitcast.26), custom_call_target="tpu_custom_call" | custom-call | flops 1442840576 | bytes 22544384 | tf_op jit(solution)/shard_map/turn/pallas_call | solution.py:57
  298.7 4.2 %copy-done.1 = bf16[4096,1376]{1,0:T(8,128)(2,1)} copy-done((bf16[4096,1376]{1,0:T(8,128)(2,1)}, bf16[4096,1376]{1,0:T(8,128)(2,1)S(1)}, u32[]{:S(2)}) %copy-start.1) | copy-done | bytes 11272216
  302.9 14.8 %collective-permute-done.30.refs_1_ = bf16[2,128,4096]{2,1,0:T(8,128)(2,1)S(1)} collective-permute-done((bf16[2,128,4096]{2,1,0:T(8,128)(2,1)S(1)}, bf16[2,128,4096]{2,1,0:T(8,128)(2,1)S(1)}, u32[]{:S(2)}, u32[]{:S(2)}) %collective-permute-start.30) | collective-permute-done | bytes 2097184 | tf_op jit(solution)/shard_map/ppermute | solution.py:629
  318.2 1.7 collective-permute-start.34
  321.8 3.0 collective-permute-done.33.refs_3_
  324.8 14.0 %kv_chunk.18 = (bf16[8,1025,4,128]{3,2,1,0:T(4,128)(2,1)}, bf16[8,1025,4,128]{3,2,1,0:T(4,128)(2,1)}, f32[14,8,3,8,128]{4,3,2,1,0:T(8,128)S(1)}) custom-call(bf16[2,128,4096]{2,1,0:T(8,128)(2,1)S(1)} %collective-permute-done.31.refs_0_, ...), custom_call_target="tpu_custom_call", output_to_operand_aliasing={{0}: (10, {}), {1}: (11, {}), {2}: (12, {})} | custom-call | flops 8589934592 | bytes 10485760 | tf_op jit(solution)/shard_map/kv_chunk/pallas_call | solution.py:462
  338.8 4.4 %collective-permute-done.34.refs_1_ = bf16[1,128,4096]{2,1,0:T(8,128)(2,1)S(1)} collective-permute-done((bf16[1,128,4096]{2,1,0:T(8,128)(2,1)S(1)}, bf16[1,128,4096]{2,1,0:T(8,128)(2,1)S(1)}, u32[]{:S(2)}, u32[]{:S(2)}) %collective-permute-start.34) | collective-permute-done | bytes 1048608 | tf_op jit(solution)/shard_map/ppermute | solution.py:629
  348.9 7.4 %kv_chunk.19 = (bf16[8,1025,4,128]{3,2,1,0:T(4,128)(2,1)}, bf16[8,1025,4,128]{3,2,1,0:T(4,128)(2,1)}, f32[14,8,3,8,128]{4,3,2,1,0:T(8,128)S(1)}) custom-call(bf16[1,128,4096]{2,1,0:T(8,128)(2,1)S(1)} %collective-permute-done.35.refs_0_, ...), custom_call_target="tpu_custom_call", output_to_operand_aliasing={{0}: (10, {}), {1}: (11, {}), {2}: (12, {})} | custom-call | flops 4294967296 | bytes 5242880 | tf_op jit(solution)/shard_map/kv_chunk/pallas_call | solution.py:462
  356.2 2.8 collective-permute-done.38.refs_1_
  359.6 1.7 collective-permute-start.42
  362.8 5.1 %kv_chunk.20 = (bf16[8,1025,4,128]{3,2,1,0:T(4,128)(2,1)}, bf16[8,1025,4,128]{3,2,1,0:T(4,128)(2,1)}, f32[14,8,3,8,128]{4,3,2,1,0:T(8,128)S(1)}) custom-call(bf16[1,64,4096]{2,1,0:T(8,128)(2,1)S(1)} %collective-permute-done.39.refs_0_, ...), custom_call_target="tpu_custom_call", output_to_operand_aliasing={{0}: (11, {}), {1}: (12, {}), {2}: (13, {})} | custom-call | flops 2147483648 | bytes 2621440 | tf_op jit(solution)/shard_map/kv_chunk/pallas_call | solution.py:462
  367.9 5.5 %collective-permute-done.42.refs_1_ = bf16[1,64,4096]{2,1,0:T(8,128)(2,1)S(1)} collective-permute-done((bf16[1,64,4096]{2,1,0:T(8,128)(2,1)S(1)}, bf16[1,64,4096]{2,1,0:T(8,128)(2,1)S(1)}, u32[]{:S(2)}, u32[]{:S(2)}) %collective-permute-start.42) | collective-permute-done | bytes 524320 | tf_op jit(solution)/shard_map/ppermute | solution.py:629
  377.5 3.6 kv_chunk.21
  381.1 22.5 %tail.1 = bf16[2,8,4096]{2,1,0:T(8,128)(2,1)S(1)} custom-call(f32[14,8,3,8,128]{4,3,2,1,0:T(8,128)S(1)} %get-tuple-element.194.stv, f32[3,8,8,128]{3,2,1,0:T(8,128)S(1)} %get-tuple-element.195.self_ref, bf16[16,512]{1,0:T(8,128)(2,1)S(1)} %fusion.1.xs_ref, bf16[1,4096]{1,0:T(2,128)(2,1)S(1)} %copy-done.6, bf16[512,4096]{1,0:T(8,128)(2,1)S(1)} %get-tuple-element.197.wo, ...), custom_call_target="tpu_custom_call" | custom-call | tf_op jit(solution)/shard_map/tail/pallas_call | solution.py:594
  (110 shorter events, 43.3 us)
Async XLA Ops:
  15.9 35.1 %collective-permute-start = (bf16[8,128,4096]{2,1,0:T(8,128)(2,1)}, bf16[8,128,4096]{2,1,0:T(8,128)(2,1)}, u32[]{:S(2)}, u32[]{:S(2)}) collective-permute-start(bf16[8,128,4096]{2,1,0:T(8,128)(2,1)} %get-tuple-element.103.refs_0_.refs_1_), channel_id=1, source_target_pairs={{0,1},{1,0},{2,3},{3,2},{4,5},{5,4},{6,7},{7,6}} | collective-permute-start | bytes 25165832 | tf_op jit(solution)/shard_map/ppermute | solution.py:629
  21.4 21.7 %copy-start.5 = (bf16[8,4096]{1,0:T(8,128)(2,1)S(1)}, bf16[8,4096]{1,0:T(8,128)(2,1)}, u32[]{:S(2)}) copy-start(bf16[8,4096]{1,0:T(8,128)(2,1)} %new_ref.1) | copy-start | bytes 196612
  21.5 8.6 %collective-permute-start.1 = (bf16[8,4096]{1,0:T(8,128)(2,1)S(1)}, bf16[8,4096]{1,0:T(8,128)(2,1)S(1)}, u32[]{:S(2)}, u32[]{:S(2)}) collective-permute-start(bf16[8,4096]{1,0:T(8,128)(2,1)S(1)} %bitcast.32), channel_id=1, source_target_pairs={{0,1},{1,0},{2,3},{3,2},{4,5},{5,4},{6,7},{7,6}} | collective-permute-start | bytes 196616 | tf_op jit(solution)/shard_map/ppermute | solution.py:629
  23.8 55.1 %collective-permute-start.7 = (bf16[1,64,4096]{2,1,0:T(8,128)(2,1)}, bf16[1,64,4096]{2,1,0:T(8,128)(2,1)S(1)}, u32[]{:S(2)}, u32[]{:S(2)}) collective-permute-start(bf16[1,64,4096]{2,1,0:T(8,128)(2,1)} %get-tuple-element.204), channel_id=1, source_target_pairs={{0,2},{1,3},{2,0},{3,1},{4,6},{5,7},{6,4},{7,5}} | collective-permute-start | bytes 1572872 | tf_op jit(solution)/shard_map/ppermute | solution.py:629
  30.1 5.9 %collective-permute-start.3 = (bf16[8,2048]{1,0:T(8,128)(2,1)S(1)}, bf16[8,2048]{1,0:T(8,128)(2,1)S(1)}, u32[]{:S(2)}, u32[]{:S(2)}) collective-permute-start(bf16[8,2048]{1,0:T(8,128)(2,1)S(1)} %dynamic-slice_add_fusion), channel_id=1, source_target_pairs={{0,4},{1,5},{2,6},{3,7},{4,0},{5,1},{6,2},{7,3}} | collective-permute-start | bytes 98312 | tf_op jit(solution)/shard_map/ppermute | solution.py:629
  32.8 7.4 %collective-permute-start.2 = (bf16[8,2048]{1,0:T(8,128)(2,1)S(1)}, bf16[8,2048]{1,0:T(8,128)(2,1)S(1)}, u32[]{:S(2)}, u32[]{:S(2)}) collective-permute-start(bf16[8,2048]{1,0:T(8,128)(2,1)S(1)} %dynamic-slice_add_fusion), channel_id=1, source_target_pairs={{0,2},{1,3},{2,0},{3,1},{4,6},{5,7},{6,4},{7,5}} | collective-permute-start | bytes 98312 | tf_op jit(solution)/shard_map/ppermute | solution.py:629
  34.2 7.5 %collective-permute-start.4 = (bf16[8,2048]{1,0:T(8,128)(2,1)S(1)}, bf16[8,2048]{1,0:T(8,128)(2,1)S(1)}, u32[]{:S(2)}, u32[]{:S(2)}) collective-permute-start(bf16[8,2048]{1,0:T(8,128)(2,1)S(1)} %dynamic-slice_add_fusion), channel_id=1, source_target_pairs={{0,6},{1,7},{2,4},{3,5},{4,2},{5,3},{6,0},{7,1}} | collective-permute-start | bytes 98312 | tf_op jit(solution)/shard_map/ppermute | solution.py:629
  36.0 42.9 %collective-permute-start.6 = (bf16[1,64,4096]{2,1,0:T(8,128)(2,1)}, bf16[1,64,4096]{2,1,0:T(8,128)(2,1)S(1)}, u32[]{:S(2)}, u32[]{:S(2)}) collective-permute-start(bf16[1,64,4096]{2,1,0:T(8,128)(2,1)} %get-tuple-element.205), channel_id=1, source_target_pairs={{0,4},{1,5},{2,6},{3,7},{4,0},{5,1},{6,2},{7,3}} | collective-permute-start | bytes 1572872 | tf_op jit(solution)/shard_map/ppermute | solution.py:629
  41.8 1.2 collective-permute-start.5
  78.9 4.3 %collective-permute-start.8 = (bf16[1,64,4096]{2,1,0:T(8,128)(2,1)S(1)}, bf16[1,64,4096]{2,1,0:T(8,128)(2,1)S(1)}, u32[]{:S(2)}, u32[]{:S(2)}) collective-permute-start(bf16[1,64,4096]{2,1,0:T(8,128)(2,1)S(1)} %collective-permute-done.6.refs_0_), channel_id=1, source_target_pairs={{0,1},{1,0},{2,3},{3,2},{4,5},{5,4},{6,7},{7,6}} | collective-permute-start | bytes 1572872 | tf_op jit(solution)/shard_map/ppermute | solution.py:629
  79.1 4.1 %collective-permute-start.9 = (bf16[1,64,4096]{2,1,0:T(8,128)(2,1)S(1)}, bf16[1,64,4096]{2,1,0:T(8,128)(2,1)S(1)}, u32[]{:S(2)}, u32[]{:S(2)}) collective-permute-start(bf16[1,64,4096]{2,1,0:T(8,128)(2,1)S(1)} %collective-permute-done.7.refs_1_), channel_id=1, source_target_pairs={{0,1},{1,0},{2,3},{3,2},{4,5},{5,4},{6,7},{7,6}} | collective-permute-start | bytes 1572872 | tf_op jit(solution)/shard_map/ppermute | solution.py:629
  81.2 14.0 %collective-permute-start.10 = (bf16[1,64,4096]{2,1,0:T(8,128)(2,1)S(1)}, bf16[1,64,4096]{2,1,0:T(8,128)(2,1)S(1)}, u32[]{:S(2)}, u32[]{:S(2)}) collective-permute-start(bf16[1,64,4096]{2,1,0:T(8,128)(2,1)S(1)} %get-tuple-element.125), channel_id=1, source_target_pairs={{0,4},{1,5},{2,6},{3,7},{4,0},{5,1},{6,2},{7,3}} | collective-permute-start | bytes 1572872 | tf_op jit(solution)/shard_map/ppermute | solution.py:629
  81.5 13.8 %collective-permute-start.11 = (bf16[1,64,4096]{2,1,0:T(8,128)(2,1)S(1)}, bf16[1,64,4096]{2,1,0:T(8,128)(2,1)S(1)}, u32[]{:S(2)}, u32[]{:S(2)}) collective-permute-start(bf16[1,64,4096]{2,1,0:T(8,128)(2,1)S(1)} %get-tuple-element.126), channel_id=1, source_target_pairs={{0,2},{1,3},{2,0},{3,1},{4,6},{5,7},{6,4},{7,5}} | collective-permute-start | bytes 1572872 | tf_op jit(solution)/shard_map/ppermute | solution.py:629
  83.2 15.7 %copy-start.8 = (bf16[2,128,4096]{2,1,0:T(8,128)(2,1)S(1)}, bf16[2,128,4096]{2,1,0:T(8,128)(2,1)}, u32[]{:S(2)}) copy-start(bf16[2,128,4096]{2,1,0:T(8,128)(2,1)} %copy-done.7) | copy-start | bytes 6291460
  95.2 3.7 collective-permute-start.12
  95.2 26.0 %collective-permute-start.14 = (bf16[1,128,4096]{2,1,0:T(8,128)(2,1)S(1)}, bf16[1,128,4096]{2,1,0:T(8,128)(2,1)S(1)}, u32[]{:S(2)}, u32[]{:S(2)}) collective-permute-start(bf16[1,128,4096]{2,1,0:T(8,128)(2,1)S(1)} %copy-done.12), channel_id=1, source_target_pairs={{0,4},{1,5},{2,6},{3,7},{4,0},{5,1},{6,2},{7,3}} | collective-permute-start | bytes 3145736 | tf_op jit(solution)/shard_map/ppermute | solution.py:629
  96.9 26.0 %collective-permute-start.15 = (bf16[1,128,4096]{2,1,0:T(8,128)(2,1)S(1)}, bf16[1,128,4096]{2,1,0:T(8,128)(2,1)S(1)}, u32[]{:S(2)}, u32[]{:S(2)}) collective-permute-start(bf16[1,128,4096]{2,1,0:T(8,128)(2,1)S(1)} %get-tuple-element.134), channel_id=1, source_target_pairs={{0,2},{1,3},{2,0},{3,1},{4,6},{5,7},{6,4},{7,5}} | collective-permute-start | bytes 3145736 | tf_op jit(solution)/shard_map/ppermute | solution.py:629
  98.4 1.9 collective-permute-start.13
  98.4 67.3 %collective-permute-start.18 = (bf16[2,128,4096]{2,1,0:T(8,128)(2,1)S(1)}, bf16[2,128,4096]{2,1,0:T(8,128)(2,1)S(1)}, u32[]{:S(2)}, u32[]{:S(2)}) collective-permute-start(bf16[2,128,4096]{2,1,0:T(8,128)(2,1)S(1)} %copy-done.10), channel_id=1, source_target_pairs={{0,4},{1,5},{2,6},{3,7},{4,0},{5,1},{6,2},{7,3}} | collective-permute-start | bytes 6291464 | tf_op jit(solution)/shard_map/ppermute | solution.py:629
  99.0 68.2 %collective-permute-start.19 = (bf16[2,128,4096]{2,1,0:T(8,128)(2,1)S(1)}, bf16[2,128,4096]{2,1,0:T(8,128)(2,1)S(1)}, u32[]{:S(2)}, u32[]{:S(2)}) collective-permute-start(bf16[2,128,4096]{2,1,0:T(8,128)(2,1)S(1)} %copy-done.8), channel_id=1, source_target_pairs={{0,2},{1,3},{2,0},{3,1},{4,6},{5,7},{6,4},{7,5}} | collective-permute-start | bytes 6291464 | tf_op jit(solution)/shard_map/ppermute | solution.py:629
  123.0 2.7 collective-permute-start.16
  123.0 4.2 %collective-permute-start.17 = (bf16[1,128,4096]{2,1,0:T(8,128)(2,1)S(1)}, bf16[1,128,4096]{2,1,0:T(8,128)(2,1)S(1)}, u32[]{:S(2)}, u32[]{:S(2)}) collective-permute-start(bf16[1,128,4096]{2,1,0:T(8,128)(2,1)S(1)} %collective-permute-done.15.refs_1_), channel_id=1, source_target_pairs={{0,1},{1,0},{2,3},{3,2},{4,5},{5,4},{6,7},{7,6}} | collective-permute-start | bytes 3145736 | tf_op jit(solution)/shard_map/ppermute | solution.py:629
  167.2 4.2 %collective-permute-start.20 = (bf16[2,128,4096]{2,1,0:T(8,128)(2,1)S(1)}, bf16[2,128,4096]{2,1,0:T(8,128)(2,1)S(1)}, u32[]{:S(2)}, u32[]{:S(2)}) collective-permute-start(bf16[2,128,4096]{2,1,0:T(8,128)(2,1)S(1)} %collective-permute-done.18.refs_0_), channel_id=1, source_target_pairs={{0,1},{1,0},{2,3},{3,2},{4,5},{5,4},{6,7},{7,6}} | collective-permute-start | bytes 6291464 | tf_op jit(solution)/shard_map/ppermute | solution.py:629
  167.2 7.2 %collective-permute-start.21 = (bf16[2,128,4096]{2,1,0:T(8,128)(2,1)S(1)}, bf16[2,128,4096]{2,1,0:T(8,128)(2,1)S(1)}, u32[]{:S(2)}, u32[]{:S(2)}) collective-permute-start(bf16[2,128,4096]{2,1,0:T(8,128)(2,1)S(1)} %collective-permute-done.19.refs_1_), channel_id=1, source_target_pairs={{0,1},{1,0},{2,3},{3,2},{4,5},{5,4},{6,7},{7,6}} | collective-permute-start | bytes 6291464 | tf_op jit(solution)/shard_map/ppermute | solution.py:629
  167.7 47.5 %collective-permute-start.23 = (bf16[2,128,4096]{2,1,0:T(8,128)(2,1)S(1)}, bf16[2,128,4096]{2,1,0:T(8,128)(2,1)S(1)}, u32[]{:S(2)}, u32[]{:S(2)}) collective-permute-start(bf16[2,128,4096]{2,1,0:T(8,128)(2,1)S(1)} %copy-done.10), channel_id=1, source_target_pairs={{0,2},{1,3},{2,0},{3,1},{4,6},{5,7},{6,4},{7,5}} | collective-permute-start | bytes 6291464 | tf_op jit(solution)/shard_map/ppermute | solution.py:629
  169.2 47.3 %collective-permute-start.22 = (bf16[2,128,4096]{2,1,0:T(8,128)(2,1)S(1)}, bf16[2,128,4096]{2,1,0:T(8,128)(2,1)S(1)}, u32[]{:S(2)}, u32[]{:S(2)}) collective-permute-start(bf16[2,128,4096]{2,1,0:T(8,128)(2,1)S(1)} %copy-done.8), channel_id=1, source_target_pairs={{0,4},{1,5},{2,6},{3,7},{4,0},{5,1},{6,2},{7,3}} | collective-permute-start | bytes 6291464 | tf_op jit(solution)/shard_map/ppermute | solution.py:629
  216.4 6.0 %collective-permute-start.24 = (bf16[2,128,4096]{2,1,0:T(8,128)(2,1)S(1)}, bf16[2,128,4096]{2,1,0:T(8,128)(2,1)S(1)}, u32[]{:S(2)}, u32[]{:S(2)}) collective-permute-start(bf16[2,128,4096]{2,1,0:T(8,128)(2,1)S(1)} %collective-permute-done.22.refs_0_), channel_id=1, source_target_pairs={{0,1},{1,0},{2,3},{3,2},{4,5},{5,4},{6,7},{7,6}} | collective-permute-start | bytes 6291464 | tf_op jit(solution)/shard_map/ppermute | solution.py:629
  216.4 7.2 %collective-permute-start.25 = (bf16[2,128,4096]{2,1,0:T(8,128)(2,1)S(1)}, bf16[2,128,4096]{2,1,0:T(8,128)(2,1)S(1)}, u32[]{:S(2)}, u32[]{:S(2)}) collective-permute-start(bf16[2,128,4096]{2,1,0:T(8,128)(2,1)S(1)} %collective-permute-done.23.refs_1_), channel_id=1, source_target_pairs={{0,1},{1,0},{2,3},{3,2},{4,5},{5,4},{6,7},{7,6}} | collective-permute-start | bytes 6291464 | tf_op jit(solution)/shard_map/ppermute | solution.py:629
  221.6 47.7 %collective-permute-start.27 = (bf16[2,128,4096]{2,1,0:T(8,128)(2,1)}, bf16[2,128,4096]{2,1,0:T(8,128)(2,1)S(1)}, u32[]{:S(2)}, u32[]{:S(2)}) collective-permute-start(bf16[2,128,4096]{2,1,0:T(8,128)(2,1)} %get-tuple-element.202), channel_id=1, source_target_pairs={{0,2},{1,3},{2,0},{3,1},{4,6},{5,7},{6,4},{7,5}} | collective-permute-start | bytes 6291464 | tf_op jit(solution)/shard_map/ppermute | solution.py:629
  222.1 47.5 %collective-permute-start.26 = (bf16[2,128,4096]{2,1,0:T(8,128)(2,1)}, bf16[2,128,4096]{2,1,0:T(8,128)(2,1)S(1)}, u32[]{:S(2)}, u32[]{:S(2)}) collective-permute-start(bf16[2,128,4096]{2,1,0:T(8,128)(2,1)} %get-tuple-element.203), channel_id=1, source_target_pairs={{0,4},{1,5},{2,6},{3,7},{4,0},{5,1},{6,2},{7,3}} | collective-permute-start | bytes 6291464 | tf_op jit(solution)/shard_map/ppermute | solution.py:629
  269.6 4.2 %collective-permute-start.28 = (bf16[2,128,4096]{2,1,0:T(8,128)(2,1)S(1)}, bf16[2,128,4096]{2,1,0:T(8,128)(2,1)S(1)}, u32[]{:S(2)}, u32[]{:S(2)}) collective-permute-start(bf16[2,128,4096]{2,1,0:T(8,128)(2,1)S(1)} %collective-permute-done.26.refs_0_), channel_id=1, source_target_pairs={{0,1},{1,0},{2,3},{3,2},{4,5},{5,4},{6,7},{7,6}} | collective-permute-start | bytes 6291464 | tf_op jit(solution)/shard_map/ppermute | solution.py:629
  269.6 7.2 %collective-permute-start.29 = (bf16[2,128,4096]{2,1,0:T(8,128)(2,1)S(1)}, bf16[2,128,4096]{2,1,0:T(8,128)(2,1)S(1)}, u32[]{:S(2)}, u32[]{:S(2)}) collective-permute-start(bf16[2,128,4096]{2,1,0:T(8,128)(2,1)S(1)} %collective-permute-done.27.refs_1_), channel_id=1, source_target_pairs={{0,1},{1,0},{2,3},{3,2},{4,5},{5,4},{6,7},{7,6}} | collective-permute-start | bytes 6291464 | tf_op jit(solution)/shard_map/ppermute | solution.py:629
  270.1 47.5 %collective-permute-start.30 = (bf16[2,128,4096]{2,1,0:T(8,128)(2,1)S(1)}, bf16[2,128,4096]{2,1,0:T(8,128)(2,1)S(1)}, u32[]{:S(2)}, u32[]{:S(2)}) collective-permute-start(bf16[2,128,4096]{2,1,0:T(8,128)(2,1)S(1)} %collective-permute-done.19.refs_1_), channel_id=1, source_target_pairs={{0,4},{1,5},{2,6},{3,7},{4,0},{5,1},{6,2},{7,3}} | collective-permute-start | bytes 6291464 | tf_op jit(solution)/shard_map/ppermute | solution.py:629
  270.4 47.3 %collective-permute-start.31 = (bf16[2,128,4096]{2,1,0:T(8,128)(2,1)S(1)}, bf16[2,128,4096]{2,1,0:T(8,128)(2,1)S(1)}, u32[]{:S(2)}, u32[]{:S(2)}) collective-permute-start(bf16[2,128,4096]{2,1,0:T(8,128)(2,1)S(1)} %collective-permute-done.18.refs_0_), channel_id=1, source_target_pairs={{0,2},{1,3},{2,0},{3,1},{4,6},{5,7},{6,4},{7,5}} | collective-permute-start | bytes 6291464 | tf_op jit(solution)/shard_map/ppermute | solution.py:629
  317.7 4.2 %collective-permute-start.32 = (bf16[2,128,4096]{2,1,0:T(8,128)(2,1)S(1)}, bf16[2,128,4096]{2,1,0:T(8,128)(2,1)S(1)}, u32[]{:S(2)}, u32[]{:S(2)}) collective-permute-start(bf16[2,128,4096]{2,1,0:T(8,128)(2,1)S(1)} %collective-permute-done.31.refs_0_), channel_id=1, source_target_pairs={{0,1},{1,0},{2,3},{3,2},{4,5},{5,4},{6,7},{7,6}} | collective-permute-start | bytes 6291464 | tf_op jit(solution)/shard_map/ppermute | solution.py:629
  317.7 7.2 %collective-permute-start.33 = (bf16[2,128,4096]{2,1,0:T(8,128)(2,1)S(1)}, bf16[2,128,4096]{2,1,0:T(8,128)(2,1)S(1)}, u32[]{:S(2)}, u32[]{:S(2)}) collective-permute-start(bf16[2,128,4096]{2,1,0:T(8,128)(2,1)S(1)} %collective-permute-done.30.refs_1_), channel_id=1, source_target_pairs={{0,1},{1,0},{2,3},{3,2},{4,5},{5,4},{6,7},{7,6}} | collective-permute-start | bytes 6291464 | tf_op jit(solution)/shard_map/ppermute | solution.py:629
  318.2 25.1 %collective-permute-start.34 = (bf16[1,128,4096]{2,1,0:T(8,128)(2,1)S(1)}, bf16[1,128,4096]{2,1,0:T(8,128)(2,1)S(1)}, u32[]{:S(2)}, u32[]{:S(2)}) collective-permute-start(bf16[1,128,4096]{2,1,0:T(8,128)(2,1)S(1)} %collective-permute-done.15.refs_1_), channel_id=1, source_target_pairs={{0,4},{1,5},{2,6},{3,7},{4,0},{5,1},{6,2},{7,3}} | collective-permute-start | bytes 3145736 | tf_op jit(solution)/shard_map/ppermute | solution.py:629
  319.9 24.8 %collective-permute-start.35 = (bf16[1,128,4096]{2,1,0:T(8,128)(2,1)S(1)}, bf16[1,128,4096]{2,1,0:T(8,128)(2,1)S(1)}, u32[]{:S(2)}, u32[]{:S(2)}) collective-permute-start(bf16[1,128,4096]{2,1,0:T(8,128)(2,1)S(1)} %collective-permute-done.14.refs_0_), channel_id=1, source_target_pairs={{0,2},{1,3},{2,0},{3,1},{4,6},{5,7},{6,4},{7,5}} | collective-permute-start | bytes 3145736 | tf_op jit(solution)/shard_map/ppermute | solution.py:629
  344.7 2.7 collective-permute-start.36
  344.7 4.2 %collective-permute-start.37 = (bf16[1,128,4096]{2,1,0:T(8,128)(2,1)S(1)}, bf16[1,128,4096]{2,1,0:T(8,128)(2,1)S(1)}, u32[]{:S(2)}, u32[]{:S(2)}) collective-permute-start(bf16[1,128,4096]{2,1,0:T(8,128)(2,1)S(1)} %collective-permute-done.34.refs_1_), channel_id=1, source_target_pairs={{0,1},{1,0},{2,3},{3,2},{4,5},{5,4},{6,7},{7,6}} | collective-permute-start | bytes 3145736 | tf_op jit(solution)/shard_map/ppermute | solution.py:629
  345.2 13.8 %collective-permute-start.38 = (bf16[1,64,4096]{2,1,0:T(8,128)(2,1)S(1)}, bf16[1,64,4096]{2,1,0:T(8,128)(2,1)S(1)}, u32[]{:S(2)}, u32[]{:S(2)}) collective-permute-start(bf16[1,64,4096]{2,1,0:T(8,128)(2,1)S(1)} %collective-permute-done.7.refs_1_), channel_id=1, source_target_pairs={{0,4},{1,5},{2,6},{3,7},{4,0},{5,1},{6,2},{7,3}} | collective-permute-start | bytes 1572872 | tf_op jit(solution)/shard_map/ppermute | solution.py:629
  345.5 13.6 %collective-permute-start.39 = (bf16[1,64,4096]{2,1,0:T(8,128)(2,1)S(1)}, bf16[1,64,4096]{2,1,0:T(8,128)(2,1)S(1)}, u32[]{:S(2)}, u32[]{:S(2)}) collective-permute-start(bf16[1,64,4096]{2,1,0:T(8,128)(2,1)S(1)} %collective-permute-done.6.refs_0_), channel_id=1, source_target_pairs={{0,2},{1,3},{2,0},{3,1},{4,6},{5,7},{6,4},{7,5}} | collective-permute-start | bytes 1572872 | tf_op jit(solution)/shard_map/ppermute | solution.py:629
  359.1 3.7 collective-permute-start.40
  359.1 3.7 collective-permute-start.41
  359.6 13.8 %collective-permute-start.42 = (bf16[1,64,4096]{2,1,0:T(8,128)(2,1)S(1)}, bf16[1,64,4096]{2,1,0:T(8,128)(2,1)S(1)}, u32[]{:S(2)}, u32[]{:S(2)}) collective-permute-start(bf16[1,64,4096]{2,1,0:T(8,128)(2,1)S(1)} %collective-permute-done.11.refs_1_), channel_id=1, source_target_pairs={{0,4},{1,5},{2,6},{3,7},{4,0},{5,1},{6,2},{7,3}} | collective-permute-start | bytes 1572872 | tf_op jit(solution)/shard_map/ppermute | solution.py:629
  361.3 13.6 %collective-permute-start.43 = (bf16[1,64,4096]{2,1,0:T(8,128)(2,1)S(1)}, bf16[1,64,4096]{2,1,0:T(8,128)(2,1)S(1)}, u32[]{:S(2)}, u32[]{:S(2)}) collective-permute-start(bf16[1,64,4096]{2,1,0:T(8,128)(2,1)S(1)} %collective-permute-done.10.refs_0_), channel_id=1, source_target_pairs={{0,2},{1,3},{2,0},{3,1},{4,6},{5,7},{6,4},{7,5}} | collective-permute-start | bytes 1572872 | tf_op jit(solution)/shard_map/ppermute | solution.py:629
  374.9 1.9 collective-permute-start.44
  374.9 2.7 collective-permute-start.45
  (12 other events, 68.0 us)

commit v13 on v12

--- a/solution.py
+++ b/solution.py
@@ -325,9 +325,12 @@
         return [pltpu.make_async_copy(src.at[pl.ds(b, 1)], dst.at[b, pl.ds(dst.shape[1] - 1, 1)], rest[12].at[idx, b])
                 for idx, (src, dst) in enumerate(zip(new_refs, (kc_ref, vc_ref))) for b in range(src.shape[0])]
 
+    in_place = n_steps == 1
+
     @when(step == 0)
     def _():
-        start_x(step, slot)
+        if not in_place:
+            start_x(step, slot)
         if with_new:
             for copy in new_copies():
                 copy.start()
@@ -341,8 +344,9 @@
         for copy in out_copies(slot, step - 2):
             copy.wait()
 
-    for copy in x_copies(0, slot, 0):
-        copy.wait()
+    if not in_place:
+        for copy in x_copies(0, slot, 0):
+            copy.wait()
     x_rows = x_buf.at[slot]
     if raw:
         lanes = [slice(c * HEAD_DIM, (c + 1) * HEAD_DIM) for c in range(x_buf.shape[3] // HEAD_DIM)]
@@ -351,11 +355,11 @@
                 at = pl.ds(pl.multiple_of(r * NORM_ROWS, NORM_ROWS), NORM_ROWS)
                 acc = [jnp.zeros((NORM_ROWS, HEAD_DIM), jnp.float32) for _ in range(2)]
                 for c, lane in enumerate(lanes):
-                    xf = x_rows[i, at, lane].astype(jnp.float32)
+                    xf = x_refs[i][0, at, lane].astype(jnp.float32)
                     acc[c % 2] += xf * xf
                 inv_rms = lax.rsqrt(jnp.sum(acc[0] + acc[1], axis=-1, keepdims=True) / x_buf.shape[3] + 1e-5)
                 for lane in lanes:
-                    xf = x_rows[i, at, lane].astype(jnp.float32)
+                    xf = x_refs[i][0, at, lane].astype(jnp.float32)
                     x_rows[i, at, lane] = (xf * inv_rms * gain_ref[:, lane].astype(jnp.float32)).astype(jnp.bfloat16)
                 return carry
 
@@ -363,7 +367,10 @@
 
     def col_tile(c, carry):
         cols = pl.ds(pl.multiple_of(c * COL_TILE, COL_TILE), COL_TILE) if n_steps > 1 else slice(c * COL_TILE, (c + 1) * COL_TILE)
-        normed = x_rows[...].reshape(n_tok, x_buf.shape[3])
+        if in_place and not raw:
+            normed = jnp.concatenate([x_ref[0] for x_ref in x_refs], axis=0)
+        else:
+            normed = x_rows[...].reshape(n_tok, x_buf.shape[3])
         kf = jnp.dot(normed, wk[:, cols], preferred_element_type=jnp.float32)
         vf = jnp.dot(normed, wv[:, cols], preferred_element_type=jnp.float32)
         v_buf[:, cols] = vf.astype(jnp.bfloat16)
@@ -442,7 +449,11 @@
     heads = width // HEAD_DIM
     any_spec = pl.BlockSpec(memory_space=pl.ANY)
     operands = [arr for group in groups for arr, _ in group]
-    in_specs = [any_spec] * len(operands) + [pl.BlockSpec(memory_space=pltpu.VMEM)] * 6
+    x_spec = any_spec
+    if n_steps == 1:
+        x_spec = pl.BlockSpec(memory_space=pltpu.VMEM)
+        operands = [pltpu.with_memory_space_constraint(arr, pltpu.VMEM) for arr in operands]
+    in_specs = [x_spec] * len(operands) + [pl.BlockSpec(memory_space=pltpu.VMEM)] * 6
     operands += [cos_tab, sin_tab, lengths, w_k, w_v, q_diag]
     if gain is not None:
         in_specs.append(pl.BlockSpec(memory_space=pltpu.VMEM))
@@ -499,7 +510,7 @@
     def peer_of(mask):
         return sum(lax.rem(me // bit + mask // bit, 2) * bit for bit in (1, 2, 4))
 
-    far_first = ((6, 7), (2, 3, 4, 5), (1,))
+    far_first = ((6,), (7, 2), (4, 5, 3), (1,))
     for mask in sum(far_first, ()):
         pl.semaphore_signal(barrier, inc=1, device_id={"model": peer_of(mask)}, device_id_type=MESH)
 

time: 405 us -> 405 us (level)
  no operation moved by 1% of the time
where the time goes in v13:
time: 405 us; the launch traced here: 404 us
  Pallas kernels  174 us (43%)
  waiting for transfers between devices  165 us (41%)
  starting transfers between devices  34 us (8%)
  local copies, waits for them, and re-layouts  20.6 us (5%)
  other arithmetic  5.18 us (1%)
  matrix products  4.57 us (1%)
    ppermute x46, waiting for transfers between devices, swap(): return lax.ppermute(arr, 'model', [(i, i ^ bit) for i in range(n_dev)])  165 us
    pallas_call x11, Pallas kernels, kv_call(): pl.pallas_call(functools.partial(kv_kernel, n_in, n_steps, masks, batches...  115 us
    ppermute x46, starting transfers between devices, swap(): return lax.ppermute(arr, 'model', [(i, i ^ bit) for i in range(n_dev)])  34 us
    pallas_call x1, Pallas kernels, tail_call(): pl.pallas_call(functools.partial(tail_kernel, n_dev, parts_of), out_shape...  22.4 us
    pallas_call x2, Pallas kernels, turn_call(): pl.pallas_call(turn_kernel, grid=(d // cols,), in_specs=[pl.BlockSpec((n,...  15.8 us
    unnamed x28, local copies, waits for them, and re-layouts  12.8 us
    pallas_call x1, Pallas kernels, norm_call(): pl.pallas_call(functools.partial(norm_kernel, outs_of), grid=(len(order),...  10.8 us
  transfers between devices with their start and end apart: 46, of which 32 were waited for; matrix products, arithmetic and copies ran while one was open for 4% of the time, Pallas kernels for 34%

profile of v13, /device:TPU:0, one launch (start us, length us, event | category | flops | bytes accessed | tf_op | source)
XLA Modules:
  0.0 404.0 jit_solution(15419545975309120922)
XLA Ops:
  1.4 10.8 %norm_rows.1 = (bf16[1,128,4096]{2,1,0:T(8,128)(2,1)S(1)}, bf16[1,128,4096]{2,1,0:T(8,128)(2,1)S(1)}, bf16[2,128,4096]{2,1,0:T(8,128)(2,1)S(1)}, bf16[2,128,4096]{2,1,0:T(8,128)(2,1)S(1)}, bf16[8,128,4096]{2,1,0:T(8,128)(2,1)}) custom-call(bf16[8,128,4096]{2,1,0:T(8,128)(2,1)} %x_hbm.1, bf16[1,4096]{1,0:T(2,128)(2,1)S(1)} %copy-done.2), custom_call_target="tpu_custom_call" | custom-call | flops 33554432 | bytes 25165824 | tf_op jit(solution)/shard_map/norm_rows/pallas_call | solution.py:180
  16.8 4.6 %fusion.2 = bf16[8,1,4096]{2,1,0:T(2,128)(2,1)S(1)} fusion(bf16[8,128,4096]{2,1,0:T(8,128)(2,1)} %x_hbm.1, pred[8,128,1]{1,0,2:T(8,128)(4,1)S(1)} %compare_bitcast_fusion), kind=kOutput, calls=%fused_computation.14 | convolution fusion | flops 8388608 | bytes 8455168 | tf_op jit(solution)/shard_map/bs,bsd->bd/dot_general | solution.py:675
  21.5 2.3 fusion.6
  23.8 3.0 collective-permute-start.7
  26.9 3.0 fusion
  30.1 2.7 collective-permute-start.3
  34.3 1.7 pad_maximum_fusion
  36.0 2.0 collective-permute-start.6
  38.0 2.1 collective-permute-done.2
  43.2 4.7 %keep.1 = (bf16[4096,512]{1,0:T(8,128)(2,1)S(1)}, bf16[4096,512]{1,0:T(8,128)(2,1)S(1)}, bf16[512,4096]{1,0:T(8,128)(2,1)S(1)}) custom-call(bf16[4096,512]{1,0:T(8,128)(2,1)} %bitcast.28, bf16[4096,512]{1,0:T(8,128)(2,1)} %bitcast.29, bf16[512,4096]{1,0:T(8,128)(2,1)} %bitcast.30), custom_call_target="tpu_custom_call" | custom-call | tf_op jit(solution)/shard_map/keep/pallas_call | solution.py:39
  47.9 3.1 query_rows.1
  51.0 27.9 %kv_chunk.11 = (bf16[8,1025,4,128]{3,2,1,0:T(4,128)(2,1)}, bf16[8,1025,4,128]{3,2,1,0:T(4,128)(2,1)}, f32[14,8,3,8,128]{4,3,2,1,0:T(8,128)S(1)}) custom-call(bf16[8,128,4096]{2,1,0:T(8,128)(2,1)} %get-tuple-element.103.refs_0_.refs_1_, bf16[8,128,4096]{2,1,0:T(8,128)(2,1)} %get-tuple-element.103.refs_0_.refs_1_, ...), custom_call_target="tpu_custom_call" | custom-call | flops 17179869184 | bytes 20971520 | tf_op jit(solution)/shard_map/kv_chunk/pallas_call | solution.py:473
  79.5 1.7 first_rows.1
  81.5 1.7 collective-permute-start.11
  83.2 4.8 %kv_chunk.12 = (bf16[8,1025,4,128]{3,2,1,0:T(4,128)(2,1)}, bf16[8,1025,4,128]{3,2,1,0:T(4,128)(2,1)}, f32[14,8,3,8,128]{4,3,2,1,0:T(8,128)S(1)}) custom-call(bf16[1,64,4096]{2,1,0:T(8,128)(2,1)S(1)} %collective-permute-done.6.refs_0_, ...), custom_call_target="tpu_custom_call", output_to_operand_aliasing={{0}: (11, {}), {1}: (12, {}), {2}: (13, {})} | custom-call | flops 2147483648 | bytes 2621440 | tf_op jit(solution)/shard_map/kv_chunk/pallas_call | solution.py:473
  88.0 7.2 %collective-permute-done.10.refs_0_ = bf16[1,64,4096]{2,1,0:T(8,128)(2,1)S(1)} collective-permute-done((bf16[1,64,4096]{2,1,0:T(8,128)(2,1)S(1)}, bf16[1,64,4096]{2,1,0:T(8,128)(2,1)S(1)}, u32[]{:S(2)}, u32[]{:S(2)}) %collective-permute-start.10) | collective-permute-done | bytes 524320 | tf_op jit(solution)/shard_map/ppermute | solution.py:640
  95.2 1.7 collective-permute-start.14
  100.3 3.3 kv_chunk.13
  103.7 17.6 %collective-permute-done.14.refs_0_ = bf16[1,128,4096]{2,1,0:T(8,128)(2,1)S(1)} collective-permute-done((bf16[1,128,4096]{2,1,0:T(8,128)(2,1)S(1)}, bf16[1,128,4096]{2,1,0:T(8,128)(2,1)S(1)}, u32[]{:S(2)}, u32[]{:S(2)}) %collective-permute-start.14) | collective-permute-done | bytes 1048608 | tf_op jit(solution)/shard_map/ppermute | solution.py:640
  121.3 1.7 collective-permute-done.15.refs_1_
  123.5 2.1 collective-permute-done.16.refs_2_
  127.1 7.4 %kv_chunk.14 = (bf16[8,1025,4,128]{3,2,1,0:T(4,128)(2,1)}, bf16[8,1025,4,128]{3,2,1,0:T(4,128)(2,1)}, f32[14,8,3,8,128]{4,3,2,1,0:T(8,128)S(1)}) custom-call(bf16[1,128,4096]{2,1,0:T(8,128)(2,1)S(1)} %collective-permute-done.14.refs_0_, ...), custom_call_target="tpu_custom_call", output_to_operand_aliasing={{0}: (10, {}), {1}: (11, {}), {2}: (12, {})} | custom-call | flops 4294967296 | bytes 5242880 | tf_op jit(solution)/shard_map/kv_chunk/pallas_call | solution.py:473
  134.5 31.2 %collective-permute-done.18.refs_0_ = bf16[2,128,4096]{2,1,0:T(8,128)(2,1)S(1)} collective-permute-done((bf16[2,128,4096]{2,1,0:T(8,128)(2,1)S(1)}, bf16[2,128,4096]{2,1,0:T(8,128)(2,1)S(1)}, u32[]{:S(2)}, u32[]{:S(2)}) %collective-permute-start.18) | collective-permute-done | bytes 2097184 | tf_op jit(solution)/shard_map/ppermute | solution.py:640
  171.3 3.0 collective-permute-done.21.refs_3_
  174.3 14.0 %kv_chunk.15 = (bf16[8,1025,4,128]{3,2,1,0:T(4,128)(2,1)}, bf16[8,1025,4,128]{3,2,1,0:T(4,128)(2,1)}, f32[14,8,3,8,128]{4,3,2,1,0:T(8,128)S(1)}) custom-call(bf16[2,128,4096]{2,1,0:T(8,128)(2,1)S(1)} %collective-permute-done.18.refs_0_, ...), custom_call_target="tpu_custom_call", output_to_operand_aliasing={{0}: (10, {}), {1}: (11, {}), {2}: (12, {})} | custom-call | flops 8589934592 | bytes 10485760 | tf_op jit(solution)/shard_map/kv_chunk/pallas_call | solution.py:473
  188.4 26.9 %collective-permute-done.23.refs_1_ = bf16[2,128,4096]{2,1,0:T(8,128)(2,1)S(1)} collective-permute-done((bf16[2,128,4096]{2,1,0:T(8,128)(2,1)S(1)}, bf16[2,128,4096]{2,1,0:T(8,128)(2,1)S(1)}, u32[]{:S(2)}, u32[]{:S(2)}) %collective-permute-start.23) | collective-permute-done | bytes 2097184 | tf_op jit(solution)/shard_map/ppermute | solution.py:640
  216.9 4.7 %fusion.5 = (bf16[2,128,4096]{2,1,0:T(8,128)(2,1)}, bf16[2,128,4096]{2,1,0:T(8,128)(2,1)}) fusion(bf16[8,128,4096]{2,1,0:T(8,128)(2,1)} %get-tuple-element.103.refs_0_.refs_1_), kind=kLoop, calls=%fused_computation.27 | loop fusion | bytes 8388608 | tf_op jit(solution)/shard_map/slice | solution.py:684
  223.6 14.0 %kv_chunk.16 = (bf16[8,1025,4,128]{3,2,1,0:T(4,128)(2,1)}, bf16[8,1025,4,128]{3,2,1,0:T(4,128)(2,1)}, f32[14,8,3,8,128]{4,3,2,1,0:T(8,128)S(1)}) custom-call(bf16[2,128,4096]{2,1,0:T(8,128)(2,1)S(1)} %collective-permute-done.22.refs_0_, ...), custom_call_target="tpu_custom_call", output_to_operand_aliasing={{0}: (10, {}), {1}: (11, {}), {2}: (12, {})} | custom-call | flops 8589934592 | bytes 10485760 | tf_op jit(solution)/shard_map/kv_chunk/pallas_call | solution.py:473
  237.6 7.9 %turn.2.wg_hbm = bf16[4096,1376]{1,0:T(8,128)(2,1)S(1)} custom-call(bf16[1376,4096]{1,0:T(8,128)(2,1)} %bitcast.25), custom_call_target="tpu_custom_call" | custom-call | flops 1442840576 | bytes 22544384 | tf_op jit(solution)/shard_map/turn/pallas_call | solution.py:57
  245.5 4.2 %copy-done = bf16[4096,1376]{1,0:T(8,128)(2,1)} copy-done((bf16[4096,1376]{1,0:T(8,128)(2,1)}, bf16[4096,1376]{1,0:T(8,128)(2,1)S(1)}, u32[]{:S(2)}) %copy-start) | copy-done | bytes 11272216
  249.7 19.6 %collective-permute-done.27.refs_1_ = bf16[2,128,4096]{2,1,0:T(8,128)(2,1)S(1)} collective-permute-done((bf16[2,128,4096]{2,1,0:T(8,128)(2,1)}, bf16[2,128,4096]{2,1,0:T(8,128)(2,1)S(1)}, u32[]{:S(2)}, u32[]{:S(2)}) %collective-permute-start.27) | collective-permute-done | bytes 2097184 | tf_op jit(solution)/shard_map/ppermute | solution.py:640
  270.4 1.7 collective-permute-start.31
  273.8 3.0 collective-permute-done.29.refs_3_
  276.8 14.0 %kv_chunk.17 = (bf16[8,1025,4,128]{3,2,1,0:T(4,128)(2,1)}, bf16[8,1025,4,128]{3,2,1,0:T(4,128)(2,1)}, f32[14,8,3,8,128]{4,3,2,1,0:T(8,128)S(1)}) custom-call(bf16[2,128,4096]{2,1,0:T(8,128)(2,1)S(1)} %collective-permute-done.26.refs_0_, ...), custom_call_target="tpu_custom_call", output_to_operand_aliasing={{0}: (10, {}), {1}: (11, {}), {2}: (12, {})} | custom-call | flops 8589934592 | bytes 10485760 | tf_op jit(solution)/shard_map/kv_chunk/pallas_call | solution.py:473
  290.8 7.9 %turn.3.wu_hbm = bf16[4096,1376]{1,0:T(8,128)(2,1)S(1)} custom-call(bf16[1376,4096]{1,0:T(8,128)(2,1)} %bitcast.26), custom_call_target="tpu_custom_call" | custom-call | flops 1442840576 | bytes 22544384 | tf_op jit(solution)/shard_map/turn/pallas_call | solution.py:57
  298.7 4.2 %copy-done.1 = bf16[4096,1376]{1,0:T(8,128)(2,1)} copy-done((bf16[4096,1376]{1,0:T(8,128)(2,1)}, bf16[4096,1376]{1,0:T(8,128)(2,1)S(1)}, u32[]{:S(2)}) %copy-start.1) | copy-done | bytes 11272216
  302.9 14.8 %collective-permute-done.30.refs_1_ = bf16[2,128,4096]{2,1,0:T(8,128)(2,1)S(1)} collective-permute-done((bf16[2,128,4096]{2,1,0:T(8,128)(2,1)S(1)}, bf16[2,128,4096]{2,1,0:T(8,128)(2,1)S(1)}, u32[]{:S(2)}, u32[]{:S(2)}) %collective-permute-start.30) | collective-permute-done | bytes 2097184 | tf_op jit(solution)/shard_map/ppermute | solution.py:640
  318.2 1.7 collective-permute-start.34
  321.8 3.0 collective-permute-done.33.refs_3_
  324.8 14.0 %kv_chunk.18 = (bf16[8,1025,4,128]{3,2,1,0:T(4,128)(2,1)}, bf16[8,1025,4,128]{3,2,1,0:T(4,128)(2,1)}, f32[14,8,3,8,128]{4,3,2,1,0:T(8,128)S(1)}) custom-call(bf16[2,128,4096]{2,1,0:T(8,128)(2,1)S(1)} %collective-permute-done.31.refs_0_, ...), custom_call_target="tpu_custom_call", output_to_operand_aliasing={{0}: (10, {}), {1}: (11, {}), {2}: (12, {})} | custom-call | flops 8589934592 | bytes 10485760 | tf_op jit(solution)/shard_map/kv_chunk/pallas_call | solution.py:473
  338.8 4.4 %collective-permute-done.34.refs_1_ = bf16[1,128,4096]{2,1,0:T(8,128)(2,1)S(1)} collective-permute-done((bf16[1,128,4096]{2,1,0:T(8,128)(2,1)S(1)}, bf16[1,128,4096]{2,1,0:T(8,128)(2,1)S(1)}, u32[]{:S(2)}, u32[]{:S(2)}) %collective-permute-start.34) | collective-permute-done | bytes 1048608 | tf_op jit(solution)/shard_map/ppermute | solution.py:640
  348.9 7.4 %kv_chunk.19 = (bf16[8,1025,4,128]{3,2,1,0:T(4,128)(2,1)}, bf16[8,1025,4,128]{3,2,1,0:T(4,128)(2,1)}, f32[14,8,3,8,128]{4,3,2,1,0:T(8,128)S(1)}) custom-call(bf16[1,128,4096]{2,1,0:T(8,128)(2,1)S(1)} %collective-permute-done.35.refs_0_, ...), custom_call_target="tpu_custom_call", output_to_operand_aliasing={{0}: (10, {}), {1}: (11, {}), {2}: (12, {})} | custom-call | flops 4294967296 | bytes 5242880 | tf_op jit(solution)/shard_map/kv_chunk/pallas_call | solution.py:473
  356.2 2.8 collective-permute-done.38.refs_1_
  359.6 1.7 collective-permute-start.42
  362.8 5.0 %kv_chunk.20 = (bf16[8,1025,4,128]{3,2,1,0:T(4,128)(2,1)}, bf16[8,1025,4,128]{3,2,1,0:T(4,128)(2,1)}, f32[14,8,3,8,128]{4,3,2,1,0:T(8,128)S(1)}) custom-call(bf16[1,64,4096]{2,1,0:T(8,128)(2,1)S(1)} %collective-permute-done.39.refs_0_, ...), custom_call_target="tpu_custom_call", output_to_operand_aliasing={{0}: (11, {}), {1}: (12, {}), {2}: (13, {})} | custom-call | flops 2147483648 | bytes 2621440 | tf_op jit(solution)/shard_map/kv_chunk/pallas_call | solution.py:473
  367.8 5.6 %collective-permute-done.42.refs_1_ = bf16[1,64,4096]{2,1,0:T(8,128)(2,1)S(1)} collective-permute-done((bf16[1,64,4096]{2,1,0:T(8,128)(2,1)S(1)}, bf16[1,64,4096]{2,1,0:T(8,128)(2,1)S(1)}, u32[]{:S(2)}, u32[]{:S(2)}) %collective-permute-start.42) | collective-permute-done | bytes 524320 | tf_op jit(solution)/shard_map/ppermute | solution.py:640
  377.5 3.4 kv_chunk.21
  380.9 22.4 %tail.1 = bf16[2,8,4096]{2,1,0:T(8,128)(2,1)S(1)} custom-call(f32[14,8,3,8,128]{4,3,2,1,0:T(8,128)S(1)} %get-tuple-element.194.stv, f32[3,8,8,128]{3,2,1,0:T(8,128)S(1)} %get-tuple-element.195.self_ref, bf16[16,512]{1,0:T(8,128)(2,1)S(1)} %fusion.1.xs_ref, bf16[1,4096]{1,0:T(2,128)(2,1)S(1)} %copy-done.6, bf16[512,4096]{1,0:T(8,128)(2,1)S(1)} %get-tuple-element.197.wo, ...), custom_call_target="tpu_custom_call" | custom-call | tf_op jit(solution)/shard_map/tail/pallas_call | solution.py:605
  (110 shorter events, 43.3 us)
Async XLA Ops:
  15.9 35.1 %collective-permute-start = (bf16[8,128,4096]{2,1,0:T(8,128)(2,1)}, bf16[8,128,4096]{2,1,0:T(8,128)(2,1)}, u32[]{:S(2)}, u32[]{:S(2)}) collective-permute-start(bf16[8,128,4096]{2,1,0:T(8,128)(2,1)} %get-tuple-element.103.refs_0_.refs_1_), channel_id=1, source_target_pairs={{0,1},{1,0},{2,3},{3,2},{4,5},{5,4},{6,7},{7,6}} | collective-permute-start | bytes 25165832 | tf_op jit(solution)/shard_map/ppermute | solution.py:640
  21.4 21.7 %copy-start.5 = (bf16[8,4096]{1,0:T(8,128)(2,1)S(1)}, bf16[8,4096]{1,0:T(8,128)(2,1)}, u32[]{:S(2)}) copy-start(bf16[8,4096]{1,0:T(8,128)(2,1)} %new_ref.1) | copy-start | bytes 196612
  21.5 8.6 %collective-permute-start.1 = (bf16[8,4096]{1,0:T(8,128)(2,1)S(1)}, bf16[8,4096]{1,0:T(8,128)(2,1)S(1)}, u32[]{:S(2)}, u32[]{:S(2)}) collective-permute-start(bf16[8,4096]{1,0:T(8,128)(2,1)S(1)} %bitcast.32), channel_id=1, source_target_pairs={{0,1},{1,0},{2,3},{3,2},{4,5},{5,4},{6,7},{7,6}} | collective-permute-start | bytes 196616 | tf_op jit(solution)/shard_map/ppermute | solution.py:640
  23.8 55.1 %collective-permute-start.7 = (bf16[1,64,4096]{2,1,0:T(8,128)(2,1)}, bf16[1,64,4096]{2,1,0:T(8,128)(2,1)S(1)}, u32[]{:S(2)}, u32[]{:S(2)}) collective-permute-start(bf16[1,64,4096]{2,1,0:T(8,128)(2,1)} %get-tuple-element.204), channel_id=1, source_target_pairs={{0,2},{1,3},{2,0},{3,1},{4,6},{5,7},{6,4},{7,5}} | collective-permute-start | bytes 1572872 | tf_op jit(solution)/shard_map/ppermute | solution.py:640
  30.1 5.9 %collective-permute-start.3 = (bf16[8,2048]{1,0:T(8,128)(2,1)S(1)}, bf16[8,2048]{1,0:T(8,128)(2,1)S(1)}, u32[]{:S(2)}, u32[]{:S(2)}) collective-permute-start(bf16[8,2048]{1,0:T(8,128)(2,1)S(1)} %dynamic-slice_add_fusion), channel_id=1, source_target_pairs={{0,4},{1,5},{2,6},{3,7},{4,0},{5,1},{6,2},{7,3}} | collective-permute-start | bytes 98312 | tf_op jit(solution)/shard_map/ppermute | solution.py:640
  32.8 7.4 %collective-permute-start.2 = (bf16[8,2048]{1,0:T(8,128)(2,1)S(1)}, bf16[8,2048]{1,0:T(8,128)(2,1)S(1)}, u32[]{:S(2)}, u32[]{:S(2)}) collective-permute-start(bf16[8,2048]{1,0:T(8,128)(2,1)S(1)} %dynamic-slice_add_fusion), channel_id=1, source_target_pairs={{0,2},{1,3},{2,0},{3,1},{4,6},{5,7},{6,4},{7,5}} | collective-permute-start | bytes 98312 | tf_op jit(solution)/shard_map/ppermute | solution.py:640
  34.2 7.5 %collective-permute-start.4 = (bf16[8,2048]{1,0:T(8,128)(2,1)S(1)}, bf16[8,2048]{1,0:T(8,128)(2,1)S(1)}, u32[]{:S(2)}, u32[]{:S(2)}) collective-permute-start(bf16[8,2048]{1,0:T(8,128)(2,1)S(1)} %dynamic-slice_add_fusion), channel_id=1, source_target_pairs={{0,6},{1,7},{2,4},{3,5},{4,2},{5,3},{6,0},{7,1}} | collective-permute-start | bytes 98312 | tf_op jit(solution)/shard_map/ppermute | solution.py:640
  36.0 42.9 %collective-permute-start.6 = (bf16[1,64,4096]{2,1,0:T(8,128)(2,1)}, bf16[1,64,4096]{2,1,0:T(8,128)(2,1)S(1)}, u32[]{:S(2)}, u32[]{:S(2)}) collective-permute-start(bf16[1,64,4096]{2,1,0:T(8,128)(2,1)} %get-tuple-element.205), channel_id=1, source_target_pairs={{0,4},{1,5},{2,6},{3,7},{4,0},{5,1},{6,2},{7,3}} | collective-permute-start | bytes 1572872 | tf_op jit(solution)/shard_map/ppermute | solution.py:640
  41.8 1.2 collective-permute-start.5
  78.9 4.3 %collective-permute-start.8 = (bf16[1,64,4096]{2,1,0:T(8,128)(2,1)S(1)}, bf16[1,64,4096]{2,1,0:T(8,128)(2,1)S(1)}, u32[]{:S(2)}, u32[]{:S(2)}) collective-permute-start(bf16[1,64,4096]{2,1,0:T(8,128)(2,1)S(1)} %collective-permute-done.6.refs_0_), channel_id=1, source_target_pairs={{0,1},{1,0},{2,3},{3,2},{4,5},{5,4},{6,7},{7,6}} | collective-permute-start | bytes 1572872 | tf_op jit(solution)/shard_map/ppermute | solution.py:640
  79.1 4.1 %collective-permute-start.9 = (bf16[1,64,4096]{2,1,0:T(8,128)(2,1)S(1)}, bf16[1,64,4096]{2,1,0:T(8,128)(2,1)S(1)}, u32[]{:S(2)}, u32[]{:S(2)}) collective-permute-start(bf16[1,64,4096]{2,1,0:T(8,128)(2,1)S(1)} %collective-permute-done.7.refs_1_), channel_id=1, source_target_pairs={{0,1},{1,0},{2,3},{3,2},{4,5},{5,4},{6,7},{7,6}} | collective-permute-start | bytes 1572872 | tf_op jit(solution)/shard_map/ppermute | solution.py:640
  81.2 14.0 %collective-permute-start.10 = (bf16[1,64,4096]{2,1,0:T(8,128)(2,1)S(1)}, bf16[1,64,4096]{2,1,0:T(8,128)(2,1)S(1)}, u32[]{:S(2)}, u32[]{:S(2)}) collective-permute-start(bf16[1,64,4096]{2,1,0:T(8,128)(2,1)S(1)} %get-tuple-element.125), channel_id=1, source_target_pairs={{0,4},{1,5},{2,6},{3,7},{4,0},{5,1},{6,2},{7,3}} | collective-permute-start | bytes 1572872 | tf_op jit(solution)/shard_map/ppermute | solution.py:640
  81.5 13.8 %collective-permute-start.11 = (bf16[1,64,4096]{2,1,0:T(8,128)(2,1)S(1)}, bf16[1,64,4096]{2,1,0:T(8,128)(2,1)S(1)}, u32[]{:S(2)}, u32[]{:S(2)}) collective-permute-start(bf16[1,64,4096]{2,1,0:T(8,128)(2,1)S(1)} %get-tuple-element.126), channel_id=1, source_target_pairs={{0,2},{1,3},{2,0},{3,1},{4,6},{5,7},{6,4},{7,5}} | collective-permute-start | bytes 1572872 | tf_op jit(solution)/shard_map/ppermute | solution.py:640
  83.2 15.7 %copy-start.8 = (bf16[2,128,4096]{2,1,0:T(8,128)(2,1)S(1)}, bf16[2,128,4096]{2,1,0:T(8,128)(2,1)}, u32[]{:S(2)}) copy-start(bf16[2,128,4096]{2,1,0:T(8,128)(2,1)} %copy-done.7) | copy-start | bytes 6291460
  95.2 3.7 collective-permute-start.12
  95.2 26.0 %collective-permute-start.14 = (bf16[1,128,4096]{2,1,0:T(8,128)(2,1)S(1)}, bf16[1,128,4096]{2,1,0:T(8,128)(2,1)S(1)}, u32[]{:S(2)}, u32[]{:S(2)}) collective-permute-start(bf16[1,128,4096]{2,1,0:T(8,128)(2,1)S(1)} %copy-done.12), channel_id=1, source_target_pairs={{0,4},{1,5},{2,6},{3,7},{4,0},{5,1},{6,2},{7,3}} | collective-permute-start | bytes 3145736 | tf_op jit(solution)/shard_map/ppermute | solution.py:640
  96.9 26.0 %collective-permute-start.15 = (bf16[1,128,4096]{2,1,0:T(8,128)(2,1)S(1)}, bf16[1,128,4096]{2,1,0:T(8,128)(2,1)S(1)}, u32[]{:S(2)}, u32[]{:S(2)}) collective-permute-start(bf16[1,128,4096]{2,1,0:T(8,128)(2,1)S(1)} %get-tuple-element.134), channel_id=1, source_target_pairs={{0,2},{1,3},{2,0},{3,1},{4,6},{5,7},{6,4},{7,5}} | collective-permute-start | bytes 3145736 | tf_op jit(solution)/shard_map/ppermute | solution.py:640
  98.4 1.9 collective-permute-start.13
  98.4 67.3 %collective-permute-start.18 = (bf16[2,128,4096]{2,1,0:T(8,128)(2,1)S(1)}, bf16[2,128,4096]{2,1,0:T(8,128)(2,1)S(1)}, u32[]{:S(2)}, u32[]{:S(2)}) collective-permute-start(bf16[2,128,4096]{2,1,0:T(8,128)(2,1)S(1)} %copy-done.10), channel_id=1, source_target_pairs={{0,4},{1,5},{2,6},{3,7},{4,0},{5,1},{6,2},{7,3}} | collective-permute-start | bytes 6291464 | tf_op jit(solution)/shard_map/ppermute | solution.py:640
  99.0 68.2 %collective-permute-start.19 = (bf16[2,128,4096]{2,1,0:T(8,128)(2,1)S(1)}, bf16[2,128,4096]{2,1,0:T(8,128)(2,1)S(1)}, u32[]{:S(2)}, u32[]{:S(2)}) collective-permute-start(bf16[2,128,4096]{2,1,0:T(8,128)(2,1)S(1)} %copy-done.8), channel_id=1, source_target_pairs={{0,2},{1,3},{2,0},{3,1},{4,6},{5,7},{6,4},{7,5}} | collective-permute-start | bytes 6291464 | tf_op jit(solution)/shard_map/ppermute | solution.py:640
  123.0 2.7 collective-permute-start.16
  123.0 4.2 %collective-permute-start.17 = (bf16[1,128,4096]{2,1,0:T(8,128)(2,1)S(1)}, bf16[1,128,4096]{2,1,0:T(8,128)(2,1)S(1)}, u32[]{:S(2)}, u32[]{:S(2)}) collective-permute-start(bf16[1,128,4096]{2,1,0:T(8,128)(2,1)S(1)} %collective-permute-done.15.refs_1_), channel_id=1, source_target_pairs={{0,1},{1,0},{2,3},{3,2},{4,5},{5,4},{6,7},{7,6}} | collective-permute-start | bytes 3145736 | tf_op jit(solution)/shard_map/ppermute | solution.py:640
  167.2 4.2 %collective-permute-start.20 = (bf16[2,128,4096]{2,1,0:T(8,128)(2,1)S(1)}, bf16[2,128,4096]{2,1,0:T(8,128)(2,1)S(1)}, u32[]{:S(2)}, u32[]{:S(2)}) collective-permute-start(bf16[2,128,4096]{2,1,0:T(8,128)(2,1)S(1)} %collective-permute-done.18.refs_0_), channel_id=1, source_target_pairs={{0,1},{1,0},{2,3},{3,2},{4,5},{5,4},{6,7},{7,6}} | collective-permute-start | bytes 6291464 | tf_op jit(solution)/shard_map/ppermute | solution.py:640
  167.2 7.2 %collective-permute-start.21 = (bf16[2,128,4096]{2,1,0:T(8,128)(2,1)S(1)}, bf16[2,128,4096]{2,1,0:T(8,128)(2,1)S(1)}, u32[]{:S(2)}, u32[]{:S(2)}) collective-permute-start(bf16[2,128,4096]{2,1,0:T(8,128)(2,1)S(1)} %collective-permute-done.19.refs_1_), channel_id=1, source_target_pairs={{0,1},{1,0},{2,3},{3,2},{4,5},{5,4},{6,7},{7,6}} | collective-permute-start | bytes 6291464 | tf_op jit(solution)/shard_map/ppermute | solution.py:640
  167.7 47.5 %collective-permute-start.23 = (bf16[2,128,4096]{2,1,0:T(8,128)(2,1)S(1)}, bf16[2,128,4096]{2,1,0:T(8,128)(2,1)S(1)}, u32[]{:S(2)}, u32[]{:S(2)}) collective-permute-start(bf16[2,128,4096]{2,1,0:T(8,128)(2,1)S(1)} %copy-done.10), channel_id=1, source_target_pairs={{0,2},{1,3},{2,0},{3,1},{4,6},{5,7},{6,4},{7,5}} | collective-permute-start | bytes 6291464 | tf_op jit(solution)/shard_map/ppermute | solution.py:640
  169.2 47.3 %collective-permute-start.22 = (bf16[2,128,4096]{2,1,0:T(8,128)(2,1)S(1)}, bf16[2,128,4096]{2,1,0:T(8,128)(2,1)S(1)}, u32[]{:S(2)}, u32[]{:S(2)}) collective-permute-start(bf16[2,128,4096]{2,1,0:T(8,128)(2,1)S(1)} %copy-done.8), channel_id=1, source_target_pairs={{0,4},{1,5},{2,6},{3,7},{4,0},{5,1},{6,2},{7,3}} | collective-permute-start | bytes 6291464 | tf_op jit(solution)/shard_map/ppermute | solution.py:640
  216.4 6.0 %collective-permute-start.24 = (bf16[2,128,4096]{2,1,0:T(8,128)(2,1)S(1)}, bf16[2,128,4096]{2,1,0:T(8,128)(2,1)S(1)}, u32[]{:S(2)}, u32[]{:S(2)}) collective-permute-start(bf16[2,128,4096]{2,1,0:T(8,128)(2,1)S(1)} %collective-permute-done.22.refs_0_), channel_id=1, source_target_pairs={{0,1},{1,0},{2,3},{3,2},{4,5},{5,4},{6,7},{7,6}} | collective-permute-start | bytes 6291464 | tf_op jit(solution)/shard_map/ppermute | solution.py:640
  216.4 7.2 %collective-permute-start.25 = (bf16[2,128,4096]{2,1,0:T(8,128)(2,1)S(1)}, bf16[2,128,4096]{2,1,0:T(8,128)(2,1)S(1)}, u32[]{:S(2)}, u32[]{:S(2)}) collective-permute-start(bf16[2,128,4096]{2,1,0:T(8,128)(2,1)S(1)} %collective-permute-done.23.refs_1_), channel_id=1, source_target_pairs={{0,1},{1,0},{2,3},{3,2},{4,5},{5,4},{6,7},{7,6}} | collective-permute-start | bytes 6291464 | tf_op jit(solution)/shard_map/ppermute | solution.py:640
  221.6 47.7 %collective-permute-start.27 = (bf16[2,128,4096]{2,1,0:T(8,128)(2,1)}, bf16[2,128,4096]{2,1,0:T(8,128)(2,1)S(1)}, u32[]{:S(2)}, u32[]{:S(2)}) collective-permute-start(bf16[2,128,4096]{2,1,0:T(8,128)(2,1)} %get-tuple-element.202), channel_id=1, source_target_pairs={{0,2},{1,3},{2,0},{3,1},{4,6},{5,7},{6,4},{7,5}} | collective-permute-start | bytes 6291464 | tf_op jit(solution)/shard_map/ppermute | solution.py:640
  222.1 47.5 %collective-permute-start.26 = (bf16[2,128,4096]{2,1,0:T(8,128)(2,1)}, bf16[2,128,4096]{2,1,0:T(8,128)(2,1)S(1)}, u32[]{:S(2)}, u32[]{:S(2)}) collective-permute-start(bf16[2,128,4096]{2,1,0:T(8,128)(2,1)} %get-tuple-element.203), channel_id=1, source_target_pairs={{0,4},{1,5},{2,6},{3,7},{4,0},{5,1},{6,2},{7,3}} | collective-permute-start | bytes 6291464 | tf_op jit(solution)/shard_map/ppermute | solution.py:640
  269.6 4.2 %collective-permute-start.28 = (bf16[2,128,4096]{2,1,0:T(8,128)(2,1)S(1)}, bf16[2,128,4096]{2,1,0:T(8,128)(2,1)S(1)}, u32[]{:S(2)}, u32[]{:S(2)}) collective-permute-start(bf16[2,128,4096]{2,1,0:T(8,128)(2,1)S(1)} %collective-permute-done.26.refs_0_), channel_id=1, source_target_pairs={{0,1},{1,0},{2,3},{3,2},{4,5},{5,4},{6,7},{7,6}} | collective-permute-start | bytes 6291464 | tf_op jit(solution)/shard_map/ppermute | solution.py:640
  269.6 7.2 %collective-permute-start.29 = (bf16[2,128,4096]{2,1,0:T(8,128)(2,1)S(1)}, bf16[2,128,4096]{2,1,0:T(8,128)(2,1)S(1)}, u32[]{:S(2)}, u32[]{:S(2)}) collective-permute-start(bf16[2,128,4096]{2,1,0:T(8,128)(2,1)S(1)} %collective-permute-done.27.refs_1_), channel_id=1, source_target_pairs={{0,1},{1,0},{2,3},{3,2},{4,5},{5,4},{6,7},{7,6}} | collective-permute-start | bytes 6291464 | tf_op jit(solution)/shard_map/ppermute | solution.py:640
  270.1 47.5 %collective-permute-start.30 = (bf16[2,128,4096]{2,1,0:T(8,128)(2,1)S(1)}, bf16[2,128,4096]{2,1,0:T(8,128)(2,1)S(1)}, u32[]{:S(2)}, u32[]{:S(2)}) collective-permute-start(bf16[2,128,4096]{2,1,0:T(8,128)(2,1)S(1)} %collective-permute-done.19.refs_1_), channel_id=1, source_target_pairs={{0,4},{1,5},{2,6},{3,7},{4,0},{5,1},{6,2},{7,3}} | collective-permute-start | bytes 6291464 | tf_op jit(solution)/shard_map/ppermute | solution.py:640
  270.4 47.3 %collective-permute-start.31 = (bf16[2,128,4096]{2,1,0:T(8,128)(2,1)S(1)}, bf16[2,128,4096]{2,1,0:T(8,128)(2,1)S(1)}, u32[]{:S(2)}, u32[]{:S(2)}) collective-permute-start(bf16[2,128,4096]{2,1,0:T(8,128)(2,1)S(1)} %collective-permute-done.18.refs_0_), channel_id=1, source_target_pairs={{0,2},{1,3},{2,0},{3,1},{4,6},{5,7},{6,4},{7,5}} | collective-permute-start | bytes 6291464 | tf_op jit(solution)/shard_map/ppermute | solution.py:640
  317.7 4.2 %collective-permute-start.32 = (bf16[2,128,4096]{2,1,0:T(8,128)(2,1)S(1)}, bf16[2,128,4096]{2,1,0:T(8,128)(2,1)S(1)}, u32[]{:S(2)}, u32[]{:S(2)}) collective-permute-start(bf16[2,128,4096]{2,1,0:T(8,128)(2,1)S(1)} %collective-permute-done.31.refs_0_), channel_id=1, source_target_pairs={{0,1},{1,0},{2,3},{3,2},{4,5},{5,4},{6,7},{7,6}} | collective-permute-start | bytes 6291464 | tf_op jit(solution)/shard_map/ppermute | solution.py:640
  317.7 7.2 %collective-permute-start.33 = (bf16[2,128,4096]{2,1,0:T(8,128)(2,1)S(1)}, bf16[2,128,4096]{2,1,0:T(8,128)(2,1)S(1)}, u32[]{:S(2)}, u32[]{:S(2)}) collective-permute-start(bf16[2,128,4096]{2,1,0:T(8,128)(2,1)S(1)} %collective-permute-done.30.refs_1_), channel_id=1, source_target_pairs={{0,1},{1,0},{2,3},{3,2},{4,5},{5,4},{6,7},{7,6}} | collective-permute-start | bytes 6291464 | tf_op jit(solution)/shard_map/ppermute | solution.py:640
  318.2 25.1 %collective-permute-start.34 = (bf16[1,128,4096]{2,1,0:T(8,128)(2,1)S(1)}, bf16[1,128,4096]{2,1,0:T(8,128)(2,1)S(1)}, u32[]{:S(2)}, u32[]{:S(2)}) collective-permute-start(bf16[1,128,4096]{2,1,0:T(8,128)(2,1)S(1)} %collective-permute-done.15.refs_1_), channel_id=1, source_target_pairs={{0,4},{1,5},{2,6},{3,7},{4,0},{5,1},{6,2},{7,3}} | collective-permute-start | bytes 3145736 | tf_op jit(solution)/shard_map/ppermute | solution.py:640
  319.9 24.8 %collective-permute-start.35 = (bf16[1,128,4096]{2,1,0:T(8,128)(2,1)S(1)}, bf16[1,128,4096]{2,1,0:T(8,128)(2,1)S(1)}, u32[]{:S(2)}, u32[]{:S(2)}) collective-permute-start(bf16[1,128,4096]{2,1,0:T(8,128)(2,1)S(1)} %collective-permute-done.14.refs_0_), channel_id=1, source_target_pairs={{0,2},{1,3},{2,0},{3,1},{4,6},{5,7},{6,4},{7,5}} | collective-permute-start | bytes 3145736 | tf_op jit(solution)/shard_map/ppermute | solution.py:640
  344.7 2.7 collective-permute-start.36
  344.7 4.2 %collective-permute-start.37 = (bf16[1,128,4096]{2,1,0:T(8,128)(2,1)S(1)}, bf16[1,128,4096]{2,1,0:T(8,128)(2,1)S(1)}, u32[]{:S(2)}, u32[]{:S(2)}) collective-permute-start(bf16[1,128,4096]{2,1,0:T(8,128)(2,1)S(1)} %collective-permute-done.34.refs_1_), channel_id=1, source_target_pairs={{0,1},{1,0},{2,3},{3,2},{4,5},{5,4},{6,7},{7,6}} | collective-permute-start | bytes 3145736 | tf_op jit(solution)/shard_map/ppermute | solution.py:640
  345.2 13.8 %collective-permute-start.38 = (bf16[1,64,4096]{2,1,0:T(8,128)(2,1)S(1)}, bf16[1,64,4096]{2,1,0:T(8,128)(2,1)S(1)}, u32[]{:S(2)}, u32[]{:S(2)}) collective-permute-start(bf16[1,64,4096]{2,1,0:T(8,128)(2,1)S(1)} %collective-permute-done.7.refs_1_), channel_id=1, source_target_pairs={{0,4},{1,5},{2,6},{3,7},{4,0},{5,1},{6,2},{7,3}} | collective-permute-start | bytes 1572872 | tf_op jit(solution)/shard_map/ppermute | solution.py:640
  345.5 13.6 %collective-permute-start.39 = (bf16[1,64,4096]{2,1,0:T(8,128)(2,1)S(1)}, bf16[1,64,4096]{2,1,0:T(8,128)(2,1)S(1)}, u32[]{:S(2)}, u32[]{:S(2)}) collective-permute-start(bf16[1,64,4096]{2,1,0:T(8,128)(2,1)S(1)} %collective-permute-done.6.refs_0_), channel_id=1, source_target_pairs={{0,2},{1,3},{2,0},{3,1},{4,6},{5,7},{6,4},{7,5}} | collective-permute-start | bytes 1572872 | tf_op jit(solution)/shard_map/ppermute | solution.py:640
  359.1 3.7 collective-permute-start.40
  359.1 3.7 collective-permute-start.41
  359.6 13.8 %collective-permute-start.42 = (bf16[1,64,4096]{2,1,0:T(8,128)(2,1)S(1)}, bf16[1,64,4096]{2,1,0:T(8,128)(2,1)S(1)}, u32[]{:S(2)}, u32[]{:S(2)}) collective-permute-start(bf16[1,64,4096]{2,1,0:T(8,128)(2,1)S(1)} %collective-permute-done.11.refs_1_), channel_id=1, source_target_pairs={{0,4},{1,5},{2,6},{3,7},{4,0},{5,1},{6,2},{7,3}} | collective-permute-start | bytes 1572872 | tf_op jit(solution)/shard_map/ppermute | solution.py:640
  361.3 13.6 %collective-permute-start.43 = (bf16[1,64,4096]{2,1,0:T(8,128)(2,1)S(1)}, bf16[1,64,4096]{2,1,0:T(8,128)(2,1)S(1)}, u32[]{:S(2)}, u32[]{:S(2)}) collective-permute-start(bf16[1,64,4096]{2,1,0:T(8,128)(2,1)S(1)} %collective-permute-done.10.refs_0_), channel_id=1, source_target_pairs={{0,2},{1,3},{2,0},{3,1},{4,6},{5,7},{6,4},{7,5}} | collective-permute-start | bytes 1572872 | tf_op jit(solution)/shard_map/ppermute | solution.py:640
  374.9 1.9 collective-permute-start.44
  374.9 2.7 collective-permute-start.45
  (12 other events, 67.8 us)

commit v14 on v13

--- a/solution.py
+++ b/solution.py
@@ -510,7 +510,7 @@
     def peer_of(mask):
         return sum(lax.rem(me // bit + mask // bit, 2) * bit for bit in (1, 2, 4))
 
-    far_first = ((6,), (7, 2), (4, 5, 3), (1,))
+    far_first = ((6, 7), (2, 3, 4, 5), (1,))
     for mask in sum(far_first, ()):
         pl.semaphore_signal(barrier, inc=1, device_id={"model": peer_of(mask)}, device_id_type=MESH)
 
@@ -563,11 +563,11 @@
         copies.append((send(0, mask, ps1.at[peer_of(mask)], pr1.at[mask - 1]), mask))
         copies[-1][0].start()
     sent = exchange(0, xs_ref[...].astype(jnp.float32) + ps1[me], copies, pr1, xo1, xg1)
-    sq = jnp.zeros((n_rows, 1), jnp.float32)
+    squares = jnp.zeros((n_rows, cols), jnp.float32)
     for j in range(n_dev):
         xf = xg1[j].astype(jnp.float32)
-        sq += jnp.sum(xf * xf, axis=-1, keepdims=True)
-    inv_rms = lax.rsqrt(sq / d_model + 1e-5)
+        squares += xf * xf
+    inv_rms = lax.rsqrt(jnp.sum(squares, axis=-1, keepdims=True) / d_model + 1e-5)
     for j in range(n_dev):
         at = slice(j * cols, (j + 1) * cols)
         n_buf[:, at] = (xg1[j].astype(jnp.float32) * inv_rms * gain_ref[:, at].astype(jnp.float32)).astype(jnp.bfloat16)

time: 405 us -> 405 us (level)
  no operation moved by 1% of the time
where the time goes in v14:
time: 405 us; the launch traced here: 404 us
  Pallas kernels  174 us (43%)
  waiting for transfers between devices  165 us (41%)
  starting transfers between devices  34 us (8%)
  local copies, waits for them, and re-layouts  20.6 us (5%)
  other arithmetic  5.18 us (1%)
  matrix products  4.57 us (1%)
    ppermute x46, waiting for transfers between devices, swap(): return lax.ppermute(arr, 'model', [(i, i ^ bit) for i in range(n_dev)])  165 us
    pallas_call x11, Pallas kernels, kv_call(): pl.pallas_call(functools.partial(kv_kernel, n_in, n_steps, masks, batches...  115 us
    ppermute x46, starting transfers between devices, swap(): return lax.ppermute(arr, 'model', [(i, i ^ bit) for i in range(n_dev)])  34 us
    pallas_call x1, Pallas kernels, tail_call(): pl.pallas_call(functools.partial(tail_kernel, n_dev, parts_of), out_shape...  22.5 us
    pallas_call x2, Pallas kernels, turn_call(): pl.pallas_call(turn_kernel, grid=(d // cols,), in_specs=[pl.BlockSpec((n,...  15.8 us
    unnamed x28, local copies, waits for them, and re-layouts  12.8 us
    pallas_call x1, Pallas kernels, norm_call(): pl.pallas_call(functools.partial(norm_kernel, outs_of), grid=(len(order),...  10.8 us
  transfers between devices with their start and end apart: 46, of which 32 were waited for; matrix products, arithmetic and copies ran while one was open for 4% of the time, Pallas kernels for 34%

profile of v14, /device:TPU:0, one launch (start us, length us, event | category | flops | bytes accessed | tf_op | source)
XLA Modules:
  0.0 404.1 jit_solution(6912018428303929998)
XLA Ops:
  1.4 10.8 %norm_rows.1 = (bf16[1,128,4096]{2,1,0:T(8,128)(2,1)S(1)}, bf16[1,128,4096]{2,1,0:T(8,128)(2,1)S(1)}, bf16[2,128,4096]{2,1,0:T(8,128)(2,1)S(1)}, bf16[2,128,4096]{2,1,0:T(8,128)(2,1)S(1)}, bf16[8,128,4096]{2,1,0:T(8,128)(2,1)}) custom-call(bf16[8,128,4096]{2,1,0:T(8,128)(2,1)} %x_hbm.1, bf16[1,4096]{1,0:T(2,128)(2,1)S(1)} %copy-done.2), custom_call_target="tpu_custom_call" | custom-call | flops 33554432 | bytes 25165824 | tf_op jit(solution)/shard_map/norm_rows/pallas_call | solution.py:180
  16.8 4.6 %fusion.2 = bf16[8,1,4096]{2,1,0:T(2,128)(2,1)S(1)} fusion(bf16[8,128,4096]{2,1,0:T(8,128)(2,1)} %x_hbm.1, pred[8,128,1]{1,0,2:T(8,128)(4,1)S(1)} %compare_bitcast_fusion), kind=kOutput, calls=%fused_computation.14 | convolution fusion | flops 8388608 | bytes 8455168 | tf_op jit(solution)/shard_map/bs,bsd->bd/dot_general | solution.py:675
  21.5 2.3 fusion.6
  23.8 3.0 collective-permute-start.7
  26.9 3.0 fusion
  30.1 2.7 collective-permute-start.3
  34.3 1.7 pad_maximum_fusion
  36.0 2.0 collective-permute-start.6
  38.0 2.1 collective-permute-done.2
  43.2 4.7 %keep.1 = (bf16[4096,512]{1,0:T(8,128)(2,1)S(1)}, bf16[4096,512]{1,0:T(8,128)(2,1)S(1)}, bf16[512,4096]{1,0:T(8,128)(2,1)S(1)}) custom-call(bf16[4096,512]{1,0:T(8,128)(2,1)} %bitcast.28, bf16[4096,512]{1,0:T(8,128)(2,1)} %bitcast.29, bf16[512,4096]{1,0:T(8,128)(2,1)} %bitcast.30), custom_call_target="tpu_custom_call" | custom-call | tf_op jit(solution)/shard_map/keep/pallas_call | solution.py:39
  47.9 3.1 query_rows.1
  51.0 27.9 %kv_chunk.11 = (bf16[8,1025,4,128]{3,2,1,0:T(4,128)(2,1)}, bf16[8,1025,4,128]{3,2,1,0:T(4,128)(2,1)}, f32[14,8,3,8,128]{4,3,2,1,0:T(8,128)S(1)}) custom-call(bf16[8,128,4096]{2,1,0:T(8,128)(2,1)} %get-tuple-element.103.refs_0_.refs_1_, bf16[8,128,4096]{2,1,0:T(8,128)(2,1)} %get-tuple-element.103.refs_0_.refs_1_, ...), custom_call_target="tpu_custom_call" | custom-call | flops 17179869184 | bytes 20971520 | tf_op jit(solution)/shard_map/kv_chunk/pallas_call | solution.py:473
  79.5 1.7 first_rows.1
  81.5 1.7 collective-permute-start.11
  83.2 4.8 %kv_chunk.12 = (bf16[8,1025,4,128]{3,2,1,0:T(4,128)(2,1)}, bf16[8,1025,4,128]{3,2,1,0:T(4,128)(2,1)}, f32[14,8,3,8,128]{4,3,2,1,0:T(8,128)S(1)}) custom-call(bf16[1,64,4096]{2,1,0:T(8,128)(2,1)S(1)} %collective-permute-done.6.refs_0_, ...), custom_call_target="tpu_custom_call", output_to_operand_aliasing={{0}: (11, {}), {1}: (12, {}), {2}: (13, {})} | custom-call | flops 2147483648 | bytes 2621440 | tf_op jit(solution)/shard_map/kv_chunk/pallas_call | solution.py:473
  88.0 7.2 %collective-permute-done.10.refs_0_ = bf16[1,64,4096]{2,1,0:T(8,128)(2,1)S(1)} collective-permute-done((bf16[1,64,4096]{2,1,0:T(8,128)(2,1)S(1)}, bf16[1,64,4096]{2,1,0:T(8,128)(2,1)S(1)}, u32[]{:S(2)}, u32[]{:S(2)}) %collective-permute-start.10) | collective-permute-done | bytes 524320 | tf_op jit(solution)/shard_map/ppermute | solution.py:640
  95.2 1.7 collective-permute-start.14
  100.3 3.3 kv_chunk.13
  103.7 17.6 %collective-permute-done.14.refs_0_ = bf16[1,128,4096]{2,1,0:T(8,128)(2,1)S(1)} collective-permute-done((bf16[1,128,4096]{2,1,0:T(8,128)(2,1)S(1)}, bf16[1,128,4096]{2,1,0:T(8,128)(2,1)S(1)}, u32[]{:S(2)}, u32[]{:S(2)}) %collective-permute-start.14) | collective-permute-done | bytes 1048608 | tf_op jit(solution)/shard_map/ppermute | solution.py:640
  121.3 1.7 collective-permute-done.15.refs_1_
  123.5 2.1 collective-permute-done.16.refs_2_
  127.1 7.4 %kv_chunk.14 = (bf16[8,1025,4,128]{3,2,1,0:T(4,128)(2,1)}, bf16[8,1025,4,128]{3,2,1,0:T(4,128)(2,1)}, f32[14,8,3,8,128]{4,3,2,1,0:T(8,128)S(1)}) custom-call(bf16[1,128,4096]{2,1,0:T(8,128)(2,1)S(1)} %collective-permute-done.14.refs_0_, ...), custom_call_target="tpu_custom_call", output_to_operand_aliasing={{0}: (10, {}), {1}: (11, {}), {2}: (12, {})} | custom-call | flops 4294967296 | bytes 5242880 | tf_op jit(solution)/shard_map/kv_chunk/pallas_call | solution.py:473
  134.5 31.2 %collective-permute-done.18.refs_0_ = bf16[2,128,4096]{2,1,0:T(8,128)(2,1)S(1)} collective-permute-done((bf16[2,128,4096]{2,1,0:T(8,128)(2,1)S(1)}, bf16[2,128,4096]{2,1,0:T(8,128)(2,1)S(1)}, u32[]{:S(2)}, u32[]{:S(2)}) %collective-permute-start.18) | collective-permute-done | bytes 2097184 | tf_op jit(solution)/shard_map/ppermute | solution.py:640
  171.3 3.0 collective-permute-done.21.refs_3_
  174.3 14.0 %kv_chunk.15 = (bf16[8,1025,4,128]{3,2,1,0:T(4,128)(2,1)}, bf16[8,1025,4,128]{3,2,1,0:T(4,128)(2,1)}, f32[14,8,3,8,128]{4,3,2,1,0:T(8,128)S(1)}) custom-call(bf16[2,128,4096]{2,1,0:T(8,128)(2,1)S(1)} %collective-permute-done.18.refs_0_, ...), custom_call_target="tpu_custom_call", output_to_operand_aliasing={{0}: (10, {}), {1}: (11, {}), {2}: (12, {})} | custom-call | flops 8589934592 | bytes 10485760 | tf_op jit(solution)/shard_map/kv_chunk/pallas_call | solution.py:473
  188.4 26.9 %collective-permute-done.23.refs_1_ = bf16[2,128,4096]{2,1,0:T(8,128)(2,1)S(1)} collective-permute-done((bf16[2,128,4096]{2,1,0:T(8,128)(2,1)S(1)}, bf16[2,128,4096]{2,1,0:T(8,128)(2,1)S(1)}, u32[]{:S(2)}, u32[]{:S(2)}) %collective-permute-start.23) | collective-permute-done | bytes 2097184 | tf_op jit(solution)/shard_map/ppermute | solution.py:640
  216.9 4.7 %fusion.5 = (bf16[2,128,4096]{2,1,0:T(8,128)(2,1)}, bf16[2,128,4096]{2,1,0:T(8,128)(2,1)}) fusion(bf16[8,128,4096]{2,1,0:T(8,128)(2,1)} %get-tuple-element.103.refs_0_.refs_1_), kind=kLoop, calls=%fused_computation.27 | loop fusion | bytes 8388608 | tf_op jit(solution)/shard_map/slice | solution.py:684
  223.6 14.0 %kv_chunk.16 = (bf16[8,1025,4,128]{3,2,1,0:T(4,128)(2,1)}, bf16[8,1025,4,128]{3,2,1,0:T(4,128)(2,1)}, f32[14,8,3,8,128]{4,3,2,1,0:T(8,128)S(1)}) custom-call(bf16[2,128,4096]{2,1,0:T(8,128)(2,1)S(1)} %collective-permute-done.22.refs_0_, ...), custom_call_target="tpu_custom_call", output_to_operand_aliasing={{0}: (10, {}), {1}: (11, {}), {2}: (12, {})} | custom-call | flops 8589934592 | bytes 10485760 | tf_op jit(solution)/shard_map/kv_chunk/pallas_call | solution.py:473
  237.6 7.9 %turn.2.wg_hbm = bf16[4096,1376]{1,0:T(8,128)(2,1)S(1)} custom-call(bf16[1376,4096]{1,0:T(8,128)(2,1)} %bitcast.25), custom_call_target="tpu_custom_call" | custom-call | flops 1442840576 | bytes 22544384 | tf_op jit(solution)/shard_map/turn/pallas_call | solution.py:57
  245.5 4.2 %copy-done = bf16[4096,1376]{1,0:T(8,128)(2,1)} copy-done((bf16[4096,1376]{1,0:T(8,128)(2,1)}, bf16[4096,1376]{1,0:T(8,128)(2,1)S(1)}, u32[]{:S(2)}) %copy-start) | copy-done | bytes 11272216
  249.7 19.6 %collective-permute-done.27.refs_1_ = bf16[2,128,4096]{2,1,0:T(8,128)(2,1)S(1)} collective-permute-done((bf16[2,128,4096]{2,1,0:T(8,128)(2,1)}, bf16[2,128,4096]{2,1,0:T(8,128)(2,1)S(1)}, u32[]{:S(2)}, u32[]{:S(2)}) %collective-permute-start.27) | collective-permute-done | bytes 2097184 | tf_op jit(solution)/shard_map/ppermute | solution.py:640
  270.4 1.7 collective-permute-start.31
  273.8 3.0 collective-permute-done.29.refs_3_
  276.8 14.0 %kv_chunk.17 = (bf16[8,1025,4,128]{3,2,1,0:T(4,128)(2,1)}, bf16[8,1025,4,128]{3,2,1,0:T(4,128)(2,1)}, f32[14,8,3,8,128]{4,3,2,1,0:T(8,128)S(1)}) custom-call(bf16[2,128,4096]{2,1,0:T(8,128)(2,1)S(1)} %collective-permute-done.26.refs_0_, ...), custom_call_target="tpu_custom_call", output_to_operand_aliasing={{0}: (10, {}), {1}: (11, {}), {2}: (12, {})} | custom-call | flops 8589934592 | bytes 10485760 | tf_op jit(solution)/shard_map/kv_chunk/pallas_call | solution.py:473
  290.8 7.9 %turn.3.wu_hbm = bf16[4096,1376]{1,0:T(8,128)(2,1)S(1)} custom-call(bf16[1376,4096]{1,0:T(8,128)(2,1)} %bitcast.26), custom_call_target="tpu_custom_call" | custom-call | flops 1442840576 | bytes 22544384 | tf_op jit(solution)/shard_map/turn/pallas_call | solution.py:57
  298.7 4.2 %copy-done.1 = bf16[4096,1376]{1,0:T(8,128)(2,1)} copy-done((bf16[4096,1376]{1,0:T(8,128)(2,1)}, bf16[4096,1376]{1,0:T(8,128)(2,1)S(1)}, u32[]{:S(2)}) %copy-start.1) | copy-done | bytes 11272216
  302.9 14.8 %collective-permute-done.30.refs_1_ = bf16[2,128,4096]{2,1,0:T(8,128)(2,1)S(1)} collective-permute-done((bf16[2,128,4096]{2,1,0:T(8,128)(2,1)S(1)}, bf16[2,128,4096]{2,1,0:T(8,128)(2,1)S(1)}, u32[]{:S(2)}, u32[]{:S(2)}) %collective-permute-start.30) | collective-permute-done | bytes 2097184 | tf_op jit(solution)/shard_map/ppermute | solution.py:640
  318.2 1.7 collective-permute-start.34
  321.8 3.0 collective-permute-done.33.refs_3_
  324.8 14.0 %kv_chunk.18 = (bf16[8,1025,4,128]{3,2,1,0:T(4,128)(2,1)}, bf16[8,1025,4,128]{3,2,1,0:T(4,128)(2,1)}, f32[14,8,3,8,128]{4,3,2,1,0:T(8,128)S(1)}) custom-call(bf16[2,128,4096]{2,1,0:T(8,128)(2,1)S(1)} %collective-permute-done.31.refs_0_, ...), custom_call_target="tpu_custom_call", output_to_operand_aliasing={{0}: (10, {}), {1}: (11, {}), {2}: (12, {})} | custom-call | flops 8589934592 | bytes 10485760 | tf_op jit(solution)/shard_map/kv_chunk/pallas_call | solution.py:473
  338.8 4.4 %collective-permute-done.34.refs_1_ = bf16[1,128,4096]{2,1,0:T(8,128)(2,1)S(1)} collective-permute-done((bf16[1,128,4096]{2,1,0:T(8,128)(2,1)S(1)}, bf16[1,128,4096]{2,1,0:T(8,128)(2,1)S(1)}, u32[]{:S(2)}, u32[]{:S(2)}) %collective-permute-start.34) | collective-permute-done | bytes 1048608 | tf_op jit(solution)/shard_map/ppermute | solution.py:640
  348.9 7.4 %kv_chunk.19 = (bf16[8,1025,4,128]{3,2,1,0:T(4,128)(2,1)}, bf16[8,1025,4,128]{3,2,1,0:T(4,128)(2,1)}, f32[14,8,3,8,128]{4,3,2,1,0:T(8,128)S(1)}) custom-call(bf16[1,128,4096]{2,1,0:T(8,128)(2,1)S(1)} %collective-permute-done.35.refs_0_, ...), custom_call_target="tpu_custom_call", output_to_operand_aliasing={{0}: (10, {}), {1}: (11, {}), {2}: (12, {})} | custom-call | flops 4294967296 | bytes 5242880 | tf_op jit(solution)/shard_map/kv_chunk/pallas_call | solution.py:473
  356.2 2.8 collective-permute-done.38.refs_1_
  359.6 1.7 collective-permute-start.42
  362.8 5.0 %kv_chunk.20 = (bf16[8,1025,4,128]{3,2,1,0:T(4,128)(2,1)}, bf16[8,1025,4,128]{3,2,1,0:T(4,128)(2,1)}, f32[14,8,3,8,128]{4,3,2,1,0:T(8,128)S(1)}) custom-call(bf16[1,64,4096]{2,1,0:T(8,128)(2,1)S(1)} %collective-permute-done.39.refs_0_, ...), custom_call_target="tpu_custom_call", output_to_operand_aliasing={{0}: (11, {}), {1}: (12, {}), {2}: (13, {})} | custom-call | flops 2147483648 | bytes 2621440 | tf_op jit(solution)/shard_map/kv_chunk/pallas_call | solution.py:473
  367.8 5.6 %collective-permute-done.42.refs_1_ = bf16[1,64,4096]{2,1,0:T(8,128)(2,1)S(1)} collective-permute-done((bf16[1,64,4096]{2,1,0:T(8,128)(2,1)S(1)}, bf16[1,64,4096]{2,1,0:T(8,128)(2,1)S(1)}, u32[]{:S(2)}, u32[]{:S(2)}) %collective-permute-start.42) | collective-permute-done | bytes 524320 | tf_op jit(solution)/shard_map/ppermute | solution.py:640
  377.5 3.4 kv_chunk.21
  380.9 22.5 %tail.1 = bf16[2,8,4096]{2,1,0:T(8,128)(2,1)S(1)} custom-call(f32[14,8,3,8,128]{4,3,2,1,0:T(8,128)S(1)} %get-tuple-element.194.stv, f32[3,8,8,128]{3,2,1,0:T(8,128)S(1)} %get-tuple-element.195.self_ref, bf16[16,512]{1,0:T(8,128)(2,1)S(1)} %fusion.1.xs_ref, bf16[1,4096]{1,0:T(2,128)(2,1)S(1)} %copy-done.6, bf16[512,4096]{1,0:T(8,128)(2,1)S(1)} %get-tuple-element.197.wo, ...), custom_call_target="tpu_custom_call" | custom-call | tf_op jit(solution)/shard_map/tail/pallas_call | solution.py:605
  (110 shorter events, 43.3 us)
Async XLA Ops:
  15.9 35.1 %collective-permute-start = (bf16[8,128,4096]{2,1,0:T(8,128)(2,1)}, bf16[8,128,4096]{2,1,0:T(8,128)(2,1)}, u32[]{:S(2)}, u32[]{:S(2)}) collective-permute-start(bf16[8,128,4096]{2,1,0:T(8,128)(2,1)} %get-tuple-element.103.refs_0_.refs_1_), channel_id=1, source_target_pairs={{0,1},{1,0},{2,3},{3,2},{4,5},{5,4},{6,7},{7,6}} | collective-permute-start | bytes 25165832 | tf_op jit(solution)/shard_map/ppermute | solution.py:640
  21.4 21.7 %copy-start.5 = (bf16[8,4096]{1,0:T(8,128)(2,1)S(1)}, bf16[8,4096]{1,0:T(8,128)(2,1)}, u32[]{:S(2)}) copy-start(bf16[8,4096]{1,0:T(8,128)(2,1)} %new_ref.1) | copy-start | bytes 196612
  21.5 8.6 %collective-permute-start.1 = (bf16[8,4096]{1,0:T(8,128)(2,1)S(1)}, bf16[8,4096]{1,0:T(8,128)(2,1)S(1)}, u32[]{:S(2)}, u32[]{:S(2)}) collective-permute-start(bf16[8,4096]{1,0:T(8,128)(2,1)S(1)} %bitcast.32), channel_id=1, source_target_pairs={{0,1},{1,0},{2,3},{3,2},{4,5},{5,4},{6,7},{7,6}} | collective-permute-start | bytes 196616 | tf_op jit(solution)/shard_map/ppermute | solution.py:640
  23.8 55.1 %collective-permute-start.7 = (bf16[1,64,4096]{2,1,0:T(8,128)(2,1)}, bf16[1,64,4096]{2,1,0:T(8,128)(2,1)S(1)}, u32[]{:S(2)}, u32[]{:S(2)}) collective-permute-start(bf16[1,64,4096]{2,1,0:T(8,128)(2,1)} %get-tuple-element.204), channel_id=1, source_target_pairs={{0,2},{1,3},{2,0},{3,1},{4,6},{5,7},{6,4},{7,5}} | collective-permute-start | bytes 1572872 | tf_op jit(solution)/shard_map/ppermute | solution.py:640
  30.1 5.9 %collective-permute-start.3 = (bf16[8,2048]{1,0:T(8,128)(2,1)S(1)}, bf16[8,2048]{1,0:T(8,128)(2,1)S(1)}, u32[]{:S(2)}, u32[]{:S(2)}) collective-permute-start(bf16[8,2048]{1,0:T(8,128)(2,1)S(1)} %dynamic-slice_add_fusion), channel_id=1, source_target_pairs={{0,4},{1,5},{2,6},{3,7},{4,0},{5,1},{6,2},{7,3}} | collective-permute-start | bytes 98312 | tf_op jit(solution)/shard_map/ppermute | solution.py:640
  32.8 7.4 %collective-permute-start.2 = (bf16[8,2048]{1,0:T(8,128)(2,1)S(1)}, bf16[8,2048]{1,0:T(8,128)(2,1)S(1)}, u32[]{:S(2)}, u32[]{:S(2)}) collective-permute-start(bf16[8,2048]{1,0:T(8,128)(2,1)S(1)} %dynamic-slice_add_fusion), channel_id=1, source_target_pairs={{0,2},{1,3},{2,0},{3,1},{4,6},{5,7},{6,4},{7,5}} | collective-permute-start | bytes 98312 | tf_op jit(solution)/shard_map/ppermute | solution.py:640
  34.2 7.5 %collective-permute-start.4 = (bf16[8,2048]{1,0:T(8,128)(2,1)S(1)}, bf16[8,2048]{1,0:T(8,128)(2,1)S(1)}, u32[]{:S(2)}, u32[]{:S(2)}) collective-permute-start(bf16[8,2048]{1,0:T(8,128)(2,1)S(1)} %dynamic-slice_add_fusion), channel_id=1, source_target_pairs={{0,6},{1,7},{2,4},{3,5},{4,2},{5,3},{6,0},{7,1}} | collective-permute-start | bytes 98312 | tf_op jit(solution)/shard_map/ppermute | solution.py:640
  36.0 42.9 %collective-permute-start.6 = (bf16[1,64,4096]{2,1,0:T(8,128)(2,1)}, bf16[1,64,4096]{2,1,0:T(8,128)(2,1)S(1)}, u32[]{:S(2)}, u32[]{:S(2)}) collective-permute-start(bf16[1,64,4096]{2,1,0:T(8,128)(2,1)} %get-tuple-element.205), channel_id=1, source_target_pairs={{0,4},{1,5},{2,6},{3,7},{4,0},{5,1},{6,2},{7,3}} | collective-permute-start | bytes 1572872 | tf_op jit(solution)/shard_map/ppermute | solution.py:640
  41.8 1.2 collective-permute-start.5
  78.9 4.3 %collective-permute-start.8 = (bf16[1,64,4096]{2,1,0:T(8,128)(2,1)S(1)}, bf16[1,64,4096]{2,1,0:T(8,128)(2,1)S(1)}, u32[]{:S(2)}, u32[]{:S(2)}) collective-permute-start(bf16[1,64,4096]{2,1,0:T(8,128)(2,1)S(1)} %collective-permute-done.6.refs_0_), channel_id=1, source_target_pairs={{0,1},{1,0},{2,3},{3,2},{4,5},{5,4},{6,7},{7,6}} | collective-permute-start | bytes 1572872 | tf_op jit(solution)/shard_map/ppermute | solution.py:640
  79.1 4.1 %collective-permute-start.9 = (bf16[1,64,4096]{2,1,0:T(8,128)(2,1)S(1)}, bf16[1,64,4096]{2,1,0:T(8,128)(2,1)S(1)}, u32[]{:S(2)}, u32[]{:S(2)}) collective-permute-start(bf16[1,64,4096]{2,1,0:T(8,128)(2,1)S(1)} %collective-permute-done.7.refs_1_), channel_id=1, source_target_pairs={{0,1},{1,0},{2,3},{3,2},{4,5},{5,4},{6,7},{7,6}} | collective-permute-start | bytes 1572872 | tf_op jit(solution)/shard_map/ppermute | solution.py:640
  81.2 14.0 %collective-permute-start.10 = (bf16[1,64,4096]{2,1,0:T(8,128)(2,1)S(1)}, bf16[1,64,4096]{2,1,0:T(8,128)(2,1)S(1)}, u32[]{:S(2)}, u32[]{:S(2)}) collective-permute-start(bf16[1,64,4096]{2,1,0:T(8,128)(2,1)S(1)} %get-tuple-element.125), channel_id=1, source_target_pairs={{0,4},{1,5},{2,6},{3,7},{4,0},{5,1},{6,2},{7,3}} | collective-permute-start | bytes 1572872 | tf_op jit(solution)/shard_map/ppermute | solution.py:640
  81.5 13.8 %collective-permute-start.11 = (bf16[1,64,4096]{2,1,0:T(8,128)(2,1)S(1)}, bf16[1,64,4096]{2,1,0:T(8,128)(2,1)S(1)}, u32[]{:S(2)}, u32[]{:S(2)}) collective-permute-start(bf16[1,64,4096]{2,1,0:T(8,128)(2,1)S(1)} %get-tuple-element.126), channel_id=1, source_target_pairs={{0,2},{1,3},{2,0},{3,1},{4,6},{5,7},{6,4},{7,5}} | collective-permute-start | bytes 1572872 | tf_op jit(solution)/shard_map/ppermute | solution.py:640
  83.2 15.7 %copy-start.8 = (bf16[2,128,4096]{2,1,0:T(8,128)(2,1)S(1)}, bf16[2,128,4096]{2,1,0:T(8,128)(2,1)}, u32[]{:S(2)}) copy-start(bf16[2,128,4096]{2,1,0:T(8,128)(2,1)} %copy-done.7) | copy-start | bytes 6291460
  95.2 3.7 collective-permute-start.12
  95.2 26.0 %collective-permute-start.14 = (bf16[1,128,4096]{2,1,0:T(8,128)(2,1)S(1)}, bf16[1,128,4096]{2,1,0:T(8,128)(2,1)S(1)}, u32[]{:S(2)}, u32[]{:S(2)}) collective-permute-start(bf16[1,128,4096]{2,1,0:T(8,128)(2,1)S(1)} %copy-done.12), channel_id=1, source_target_pairs={{0,4},{1,5},{2,6},{3,7},{4,0},{5,1},{6,2},{7,3}} | collective-permute-start | bytes 3145736 | tf_op jit(solution)/shard_map/ppermute | solution.py:640
  96.9 26.0 %collective-permute-start.15 = (bf16[1,128,4096]{2,1,0:T(8,128)(2,1)S(1)}, bf16[1,128,4096]{2,1,0:T(8,128)(2,1)S(1)}, u32[]{:S(2)}, u32[]{:S(2)}) collective-permute-start(bf16[1,128,4096]{2,1,0:T(8,128)(2,1)S(1)} %get-tuple-element.134), channel_id=1, source_target_pairs={{0,2},{1,3},{2,0},{3,1},{4,6},{5,7},{6,4},{7,5}} | collective-permute-start | bytes 3145736 | tf_op jit(solution)/shard_map/ppermute | solution.py:640
  98.4 1.9 collective-permute-start.13
  98.4 67.3 %collective-permute-start.18 = (bf16[2,128,4096]{2,1,0:T(8,128)(2,1)S(1)}, bf16[2,128,4096]{2,1,0:T(8,128)(2,1)S(1)}, u32[]{:S(2)}, u32[]{:S(2)}) collective-permute-start(bf16[2,128,4096]{2,1,0:T(8,128)(2,1)S(1)} %copy-done.10), channel_id=1, source_target_pairs={{0,4},{1,5},{2,6},{3,7},{4,0},{5,1},{6,2},{7,3}} | collective-permute-start | bytes 6291464 | tf_op jit(solution)/shard_map/ppermute | solution.py:640
  99.0 68.2 %collective-permute-start.19 = (bf16[2,128,4096]{2,1,0:T(8,128)(2,1)S(1)}, bf16[2,128,4096]{2,1,0:T(8,128)(2,1)S(1)}, u32[]{:S(2)}, u32[]{:S(2)}) collective-permute-start(bf16[2,128,4096]{2,1,0:T(8,128)(2,1)S(1)} %copy-done.8), channel_id=1, source_target_pairs={{0,2},{1,3},{2,0},{3,1},{4,6},{5,7},{6,4},{7,5}} | collective-permute-start | bytes 6291464 | tf_op jit(solution)/shard_map/ppermute | solution.py:640
  123.0 2.7 collective-permute-start.16
  123.0 4.2 %collective-permute-start.17 = (bf16[1,128,4096]{2,1,0:T(8,128)(2,1)S(1)}, bf16[1,128,4096]{2,1,0:T(8,128)(2,1)S(1)}, u32[]{:S(2)}, u32[]{:S(2)}) collective-permute-start(bf16[1,128,4096]{2,1,0:T(8,128)(2,1)S(1)} %collective-permute-done.15.refs_1_), channel_id=1, source_target_pairs={{0,1},{1,0},{2,3},{3,2},{4,5},{5,4},{6,7},{7,6}} | collective-permute-start | bytes 3145736 | tf_op jit(solution)/shard_map/ppermute | solution.py:640
  167.2 4.2 %collective-permute-start.20 = (bf16[2,128,4096]{2,1,0:T(8,128)(2,1)S(1)}, bf16[2,128,4096]{2,1,0:T(8,128)(2,1)S(1)}, u32[]{:S(2)}, u32[]{:S(2)}) collective-permute-start(bf16[2,128,4096]{2,1,0:T(8,128)(2,1)S(1)} %collective-permute-done.18.refs_0_), channel_id=1, source_target_pairs={{0,1},{1,0},{2,3},{3,2},{4,5},{5,4},{6,7},{7,6}} | collective-permute-start | bytes 6291464 | tf_op jit(solution)/shard_map/ppermute | solution.py:640
  167.2 7.2 %collective-permute-start.21 = (bf16[2,128,4096]{2,1,0:T(8,128)(2,1)S(1)}, bf16[2,128,4096]{2,1,0:T(8,128)(2,1)S(1)}, u32[]{:S(2)}, u32[]{:S(2)}) collective-permute-start(bf16[2,128,4096]{2,1,0:T(8,128)(2,1)S(1)} %collective-permute-done.19.refs_1_), channel_id=1, source_target_pairs={{0,1},{1,0},{2,3},{3,2},{4,5},{5,4},{6,7},{7,6}} | collective-permute-start | bytes 6291464 | tf_op jit(solution)/shard_map/ppermute | solution.py:640
  167.7 47.5 %collective-permute-start.23 = (bf16[2,128,4096]{2,1,0:T(8,128)(2,1)S(1)}, bf16[2,128,4096]{2,1,0:T(8,128)(2,1)S(1)}, u32[]{:S(2)}, u32[]{:S(2)}) collective-permute-start(bf16[2,128,4096]{2,1,0:T(8,128)(2,1)S(1)} %copy-done.10), channel_id=1, source_target_pairs={{0,2},{1,3},{2,0},{3,1},{4,6},{5,7},{6,4},{7,5}} | collective-permute-start | bytes 6291464 | tf_op jit(solution)/shard_map/ppermute | solution.py:640
  169.2 47.3 %collective-permute-start.22 = (bf16[2,128,4096]{2,1,0:T(8,128)(2,1)S(1)}, bf16[2,128,4096]{2,1,0:T(8,128)(2,1)S(1)}, u32[]{:S(2)}, u32[]{:S(2)}) collective-permute-start(bf16[2,128,4096]{2,1,0:T(8,128)(2,1)S(1)} %copy-done.8), channel_id=1, source_target_pairs={{0,4},{1,5},{2,6},{3,7},{4,0},{5,1},{6,2},{7,3}} | collective-permute-start | bytes 6291464 | tf_op jit(solution)/shard_map/ppermute | solution.py:640
  216.4 6.0 %collective-permute-start.24 = (bf16[2,128,4096]{2,1,0:T(8,128)(2,1)S(1)}, bf16[2,128,4096]{2,1,0:T(8,128)(2,1)S(1)}, u32[]{:S(2)}, u32[]{:S(2)}) collective-permute-start(bf16[2,128,4096]{2,1,0:T(8,128)(2,1)S(1)} %collective-permute-done.22.refs_0_), channel_id=1, source_target_pairs={{0,1},{1,0},{2,3},{3,2},{4,5},{5,4},{6,7},{7,6}} | collective-permute-start | bytes 6291464 | tf_op jit(solution)/shard_map/ppermute | solution.py:640
  216.4 7.2 %collective-permute-start.25 = (bf16[2,128,4096]{2,1,0:T(8,128)(2,1)S(1)}, bf16[2,128,4096]{2,1,0:T(8,128)(2,1)S(1)}, u32[]{:S(2)}, u32[]{:S(2)}) collective-permute-start(bf16[2,128,4096]{2,1,0:T(8,128)(2,1)S(1)} %collective-permute-done.23.refs_1_), channel_id=1, source_target_pairs={{0,1},{1,0},{2,3},{3,2},{4,5},{5,4},{6,7},{7,6}} | collective-permute-start | bytes 6291464 | tf_op jit(solution)/shard_map/ppermute | solution.py:640
  221.6 47.7 %collective-permute-start.27 = (bf16[2,128,4096]{2,1,0:T(8,128)(2,1)}, bf16[2,128,4096]{2,1,0:T(8,128)(2,1)S(1)}, u32[]{:S(2)}, u32[]{:S(2)}) collective-permute-start(bf16[2,128,4096]{2,1,0:T(8,128)(2,1)} %get-tuple-element.202), channel_id=1, source_target_pairs={{0,2},{1,3},{2,0},{3,1},{4,6},{5,7},{6,4},{7,5}} | collective-permute-start | bytes 6291464 | tf_op jit(solution)/shard_map/ppermute | solution.py:640
  222.1 47.5 %collective-permute-start.26 = (bf16[2,128,4096]{2,1,0:T(8,128)(2,1)}, bf16[2,128,4096]{2,1,0:T(8,128)(2,1)S(1)}, u32[]{:S(2)}, u32[]{:S(2)}) collective-permute-start(bf16[2,128,4096]{2,1,0:T(8,128)(2,1)} %get-tuple-element.203), channel_id=1, source_target_pairs={{0,4},{1,5},{2,6},{3,7},{4,0},{5,1},{6,2},{7,3}} | collective-permute-start | bytes 6291464 | tf_op jit(solution)/shard_map/ppermute | solution.py:640
  269.6 4.2 %collective-permute-start.28 = (bf16[2,128,4096]{2,1,0:T(8,128)(2,1)S(1)}, bf16[2,128,4096]{2,1,0:T(8,128)(2,1)S(1)}, u32[]{:S(2)}, u32[]{:S(2)}) collective-permute-start(bf16[2,128,4096]{2,1,0:T(8,128)(2,1)S(1)} %collective-permute-done.26.refs_0_), channel_id=1, source_target_pairs={{0,1},{1,0},{2,3},{3,2},{4,5},{5,4},{6,7},{7,6}} | collective-permute-start | bytes 6291464 | tf_op jit(solution)/shard_map/ppermute | solution.py:640
  269.6 7.2 %collective-permute-start.29 = (bf16[2,128,4096]{2,1,0:T(8,128)(2,1)S(1)}, bf16[2,128,4096]{2,1,0:T(8,128)(2,1)S(1)}, u32[]{:S(2)}, u32[]{:S(2)}) collective-permute-start(bf16[2,128,4096]{2,1,0:T(8,128)(2,1)S(1)} %collective-permute-done.27.refs_1_), channel_id=1, source_target_pairs={{0,1},{1,0},{2,3},{3,2},{4,5},{5,4},{6,7},{7,6}} | collective-permute-start | bytes 6291464 | tf_op jit(solution)/shard_map/ppermute | solution.py:640
  270.1 47.5 %collective-permute-start.30 = (bf16[2,128,4096]{2,1,0:T(8,128)(2,1)S(1)}, bf16[2,128,4096]{2,1,0:T(8,128)(2,1)S(1)}, u32[]{:S(2)}, u32[]{:S(2)}) collective-permute-start(bf16[2,128,4096]{2,1,0:T(8,128)(2,1)S(1)} %collective-permute-done.19.refs_1_), channel_id=1, source_target_pairs={{0,4},{1,5},{2,6},{3,7},{4,0},{5,1},{6,2},{7,3}} | collective-permute-start | bytes 6291464 | tf_op jit(solution)/shard_map/ppermute | solution.py:640
  270.4 47.3 %collective-permute-start.31 = (bf16[2,128,4096]{2,1,0:T(8,128)(2,1)S(1)}, bf16[2,128,4096]{2,1,0:T(8,128)(2,1)S(1)}, u32[]{:S(2)}, u32[]{:S(2)}) collective-permute-start(bf16[2,128,4096]{2,1,0:T(8,128)(2,1)S(1)} %collective-permute-done.18.refs_0_), channel_id=1, source_target_pairs={{0,2},{1,3},{2,0},{3,1},{4,6},{5,7},{6,4},{7,5}} | collective-permute-start | bytes 6291464 | tf_op jit(solution)/shard_map/ppermute | solution.py:640
  317.7 4.2 %collective-permute-start.32 = (bf16[2,128,4096]{2,1,0:T(8,128)(2,1)S(1)}, bf16[2,128,4096]{2,1,0:T(8,128)(2,1)S(1)}, u32[]{:S(2)}, u32[]{:S(2)}) collective-permute-start(bf16[2,128,4096]{2,1,0:T(8,128)(2,1)S(1)} %collective-permute-done.31.refs_0_), channel_id=1, source_target_pairs={{0,1},{1,0},{2,3},{3,2},{4,5},{5,4},{6,7},{7,6}} | collective-permute-start | bytes 6291464 | tf_op jit(solution)/shard_map/ppermute | solution.py:640
  317.7 7.2 %collective-permute-start.33 = (bf16[2,128,4096]{2,1,0:T(8,128)(2,1)S(1)}, bf16[2,128,4096]{2,1,0:T(8,128)(2,1)S(1)}, u32[]{:S(2)}, u32[]{:S(2)}) collective-permute-start(bf16[2,128,4096]{2,1,0:T(8,128)(2,1)S(1)} %collective-permute-done.30.refs_1_), channel_id=1, source_target_pairs={{0,1},{1,0},{2,3},{3,2},{4,5},{5,4},{6,7},{7,6}} | collective-permute-start | bytes 6291464 | tf_op jit(solution)/shard_map/ppermute | solution.py:640
  318.2 25.1 %collective-permute-start.34 = (bf16[1,128,4096]{2,1,0:T(8,128)(2,1)S(1)}, bf16[1,128,4096]{2,1,0:T(8,128)(2,1)S(1)}, u32[]{:S(2)}, u32[]{:S(2)}) collective-permute-start(bf16[1,128,4096]{2,1,0:T(8,128)(2,1)S(1)} %collective-permute-done.15.refs_1_), channel_id=1, source_target_pairs={{0,4},{1,5},{2,6},{3,7},{4,0},{5,1},{6,2},{7,3}} | collective-permute-start | bytes 3145736 | tf_op jit(solution)/shard_map/ppermute | solution.py:640
  319.9 24.8 %collective-permute-start.35 = (bf16[1,128,4096]{2,1,0:T(8,128)(2,1)S(1)}, bf16[1,128,4096]{2,1,0:T(8,128)(2,1)S(1)}, u32[]{:S(2)}, u32[]{:S(2)}) collective-permute-start(bf16[1,128,4096]{2,1,0:T(8,128)(2,1)S(1)} %collective-permute-done.14.refs_0_), channel_id=1, source_target_pairs={{0,2},{1,3},{2,0},{3,1},{4,6},{5,7},{6,4},{7,5}} | collective-permute-start | bytes 3145736 | tf_op jit(solution)/shard_map/ppermute | solution.py:640
  344.7 2.7 collective-permute-start.36
  344.7 4.2 %collective-permute-start.37 = (bf16[1,128,4096]{2,1,0:T(8,128)(2,1)S(1)}, bf16[1,128,4096]{2,1,0:T(8,128)(2,1)S(1)}, u32[]{:S(2)}, u32[]{:S(2)}) collective-permute-start(bf16[1,128,4096]{2,1,0:T(8,128)(2,1)S(1)} %collective-permute-done.34.refs_1_), channel_id=1, source_target_pairs={{0,1},{1,0},{2,3},{3,2},{4,5},{5,4},{6,7},{7,6}} | collective-permute-start | bytes 3145736 | tf_op jit(solution)/shard_map/ppermute | solution.py:640
  345.2 13.8 %collective-permute-start.38 = (bf16[1,64,4096]{2,1,0:T(8,128)(2,1)S(1)}, bf16[1,64,4096]{2,1,0:T(8,128)(2,1)S(1)}, u32[]{:S(2)}, u32[]{:S(2)}) collective-permute-start(bf16[1,64,4096]{2,1,0:T(8,128)(2,1)S(1)} %collective-permute-done.7.refs_1_), channel_id=1, source_target_pairs={{0,4},{1,5},{2,6},{3,7},{4,0},{5,1},{6,2},{7,3}} | collective-permute-start | bytes 1572872 | tf_op jit(solution)/shard_map/ppermute | solution.py:640
  345.5 13.6 %collective-permute-start.39 = (bf16[1,64,4096]{2,1,0:T(8,128)(2,1)S(1)}, bf16[1,64,4096]{2,1,0:T(8,128)(2,1)S(1)}, u32[]{:S(2)}, u32[]{:S(2)}) collective-permute-start(bf16[1,64,4096]{2,1,0:T(8,128)(2,1)S(1)} %collective-permute-done.6.refs_0_), channel_id=1, source_target_pairs={{0,2},{1,3},{2,0},{3,1},{4,6},{5,7},{6,4},{7,5}} | collective-permute-start | bytes 1572872 | tf_op jit(solution)/shard_map/ppermute | solution.py:640
  359.1 3.7 collective-permute-start.40
  359.1 3.7 collective-permute-start.41
  359.6 13.8 %collective-permute-start.42 = (bf16[1,64,4096]{2,1,0:T(8,128)(2,1)S(1)}, bf16[1,64,4096]{2,1,0:T(8,128)(2,1)S(1)}, u32[]{:S(2)}, u32[]{:S(2)}) collective-permute-start(bf16[1,64,4096]{2,1,0:T(8,128)(2,1)S(1)} %collective-permute-done.11.refs_1_), channel_id=1, source_target_pairs={{0,4},{1,5},{2,6},{3,7},{4,0},{5,1},{6,2},{7,3}} | collective-permute-start | bytes 1572872 | tf_op jit(solution)/shard_map/ppermute | solution.py:640
  361.3 13.6 %collective-permute-start.43 = (bf16[1,64,4096]{2,1,0:T(8,128)(2,1)S(1)}, bf16[1,64,4096]{2,1,0:T(8,128)(2,1)S(1)}, u32[]{:S(2)}, u32[]{:S(2)}) collective-permute-start(bf16[1,64,4096]{2,1,0:T(8,128)(2,1)S(1)} %collective-permute-done.10.refs_0_), channel_id=1, source_target_pairs={{0,2},{1,3},{2,0},{3,1},{4,6},{5,7},{6,4},{7,5}} | collective-permute-start | bytes 1572872 | tf_op jit(solution)/shard_map/ppermute | solution.py:640
  374.9 1.9 collective-permute-start.44
  374.9 2.7 collective-permute-start.45
  (12 other events, 67.8 us)
